TPU v7x, 32 devices: a whole 2x2x4 slice. The times are simulated.
32 devices in a mesh: dp: 2 (over x), row: 4 (over y, core), col: 4 (over z).
Axes of the slice: x: 2, y: 2, z: 4, core: 2. Of those that a mesh axis runs over, the one named last changes fastest.
Arguments:
- tokens: bfloat16 [16384, 1024], P(('dp', 'row'), 'col'), may hold values from -6 to 6
- condition: bfloat16 [16, 1024], P('dp', 'row'), may hold values from -6 to 6
- modulation_weight: bfloat16 [1024, 6, 1024], P('row', None, 'col'), may hold values from -0.1875 to 0.1875
- modulation_bias: bfloat16 [6, 1024], P(None, 'col'), may hold values from -2 to 2
- input_weight: bfloat16 [1024, 3, 1024], P('col', None, 'row'), may hold values from -0.1875 to 0.1875
- input_bias: bfloat16 [2, 1024], P(None, 'row'), may hold values from -2 to 2
- output_weight: bfloat16 [1024, 1024], P('row', 'col'), may hold values from -1.5 to 1.5
- output_bias: bfloat16 [1024], P('col'), may hold values from -3 to 3
- expand_weight: bfloat16 [1024, 4096], P('col', 'row'), may hold values from -0.1875 to 0.1875
- expand_bias: bfloat16 [4096], P('row'), may hold values from -2 to 2
- shrink_weight: bfloat16 [4096, 1024], P('row', 'col'), may hold values from -0.09375 to 0.09375
- shrink_bias: bfloat16 [1024], P('col'), may hold values from -3 to 3
- cotangent: bfloat16 [16384, 1024], P(('dp', 'row'), 'col'), may hold values from -6 to 6
Outputs:
- layer_output: bfloat16 [16384, 1024], P(('dp', 'row'), 'col')
- tokens_gradient: float32 [16384, 1024], P(('dp', 'row'), 'col')
- condition_gradient: float32 [16, 1024], P('dp', 'row')
- modulation_weight_gradient: float32 [1024, 6, 1024], P('row', None, 'col')
- modulation_bias_gradient: float32 [6, 1024], P(None, 'col')
- input_weight_gradient: float32 [1024, 3, 1024], P('col', None, 'row')
- input_bias_gradient: float32 [2, 1024], P(None, 'row')
- output_weight_gradient: float32 [1024, 1024], P('row', 'col')
- output_bias_gradient: float32 [1024], P('col')
- expand_weight_gradient: float32 [1024, 4096], P('col', 'row')
- expand_bias_gradient: float32 [4096], P('row')
- shrink_weight_gradient: float32 [4096, 1024], P('row', 'col')
- shrink_bias_gradient: float32 [1024], P('col')
All inputs are finite; a program needn't handle non-finite values.
Results may differ from a plain program's by a relative error of at most 0.01.
The roundings to bfloat16 on the way count: a program that leaves them out, or rounds other values in their place, can miss the bound.
Values may be sent and summed in bfloat16 or wider, within the bound.
No kernel may reach another device: no remote copies, remote signals or barrier semaphores. Data moves between devices by JAX's collectives and lax.ppermute only.
A program may use at most 192 MiB of HBM per device.

v0:
```python
import jax
import jax.numpy as jnp
from jax import lax
from jax.sharding import PartitionSpec as P

HEAD_DIM = 64
LENGTH = 1024


EPS = 1e-06


def gelu_tanh(values):
    return (
        0.5
        * values
        * (1.0 + jnp.tanh(0.7978845608028654 * (values + 0.044715 * values * values * values)))
    )


def contract(left, right):
    return lax.dot_general(
        left, right, (((0,), (0,)), ((), ())), preferred_element_type=jnp.float32
    )


def by_latent(values, factor):
    shaped = values.reshape(factor.shape[0], -1, values.shape[-1])
    return (shaped * factor[:, None, :]).reshape(values.shape)


def modulate(normed, shifts, scaling):
    shaped = normed.reshape(shifts.shape[0], -1, normed.shape[-1])
    return (shaped * (1.0 + scaling[:, None, :]) + shifts[:, None, :]).reshape(normed.shape)


def latent_sums(values, groups):
    return jnp.sum(values.reshape(groups, -1, values.shape[-1]), axis=1)


def feature_sums(totals, squares):
    return lax.psum((totals, squares), "col")


def normalize(values):
    features = values.shape[1] * lax.axis_size("col")
    totals, squares = feature_sums(jnp.sum(values, axis=1), jnp.sum(values * values, axis=1))
    average = totals / features
    inverse = lax.rsqrt(squares / features - average * average + EPS)
    return ((values - average[:, None]) * inverse[:, None], inverse)


def norm_back(incoming, normed, inverse):
    features = incoming.shape[1] * lax.axis_size("col")
    totals, crossed = feature_sums(jnp.sum(incoming, axis=1), jnp.sum(incoming * normed, axis=1))
    return inverse[:, None] * (
        incoming - totals[:, None] / features - normed * (crossed[:, None] / features)
    )


def row_gather(values):
    return lax.all_gather(values, "row", axis=0, tiled=True)


def attend_forward(pieces):
    queries, key_rows, values = pieces
    scores = jnp.einsum(
        "qhd,khd->hqk", queries, key_rows, preferred_element_type=jnp.float32
    ) * HEAD_DIM ** (-0.5)
    highest = jnp.max(scores, axis=2, keepdims=True)
    weights = jnp.exp(scores - highest)
    totals = jnp.sum(weights, axis=2, keepdims=True)
    probability = (weights / totals).astype(jnp.bfloat16)
    attended = jnp.einsum("hqk,khd->qhd", probability, values, preferred_element_type=jnp.float32)
    return (attended, (highest + jnp.log(totals))[:, :, 0])


def attend_backward(pieces):
    queries, key_rows, values, logsum, incoming = pieces
    scores = jnp.einsum(
        "qhd,khd->hqk", queries, key_rows, preferred_element_type=jnp.float32
    ) * HEAD_DIM ** (-0.5)
    probability = jnp.exp(scores - logsum[:, :, None])
    mixing_back = jnp.einsum("qhd,khd->hqk", incoming, values, preferred_element_type=jnp.float32)
    value_back = jnp.einsum(
        "hqk,qhd->khd",
        probability.astype(jnp.bfloat16),
        incoming,
        preferred_element_type=jnp.float32,
    )
    centred = jnp.sum(probability * mixing_back, axis=2, keepdims=True)
    score_back = (probability * (mixing_back - centred)).astype(jnp.bfloat16)
    query_back = jnp.einsum(
        "hqk,khd->qhd", score_back, key_rows, preferred_element_type=jnp.float32
    ) * HEAD_DIM ** (-0.5)
    key_back = jnp.einsum(
        "hqk,qhd->khd", score_back, queries, preferred_element_type=jnp.float32
    ) * HEAD_DIM ** (-0.5)
    return jnp.stack([query_back, key_back, value_back], axis=1).astype(jnp.bfloat16)


def body(
    tokens,
    condition,
    modulation_weight,
    modulation_bias,
    input_weight,
    input_bias,
    output_weight,
    output_bias,
    expand_weight,
    expand_bias,
    shrink_weight,
    shrink_bias,
    cotangent,
):
    rows_here = tokens.shape[0]
    width_here = tokens.shape[1]
    latents_row = rows_here // LENGTH
    inner_here = input_weight.shape[2]
    heads_here = inner_here // HEAD_DIM
    input_block = input_weight.reshape(width_here, -1)
    modulator = modulation_weight.reshape(modulation_weight.shape[0], -1)

    def project_in(local_rows, block):
        gathered = row_gather(local_rows)
        share = gathered.shape[0] // lax.axis_size("col")

        def partial_rows(start, number):
            return jnp.dot(gathered, block, preferred_element_type=jnp.float32)

        return (
            gathered,
            lax.psum_scatter(
                partial_rows(jnp.int32(0), share * lax.axis_size("col")),
                "col",
                scatter_dimension=0,
                tiled=True,
            ),
        )

    def project_out(local_cols, block):
        gathered = lax.all_gather(local_cols, "col", axis=0, tiled=True)

        def partial_rows(start, number):
            return jnp.dot(gathered, block, preferred_element_type=jnp.float32)

        return (
            gathered,
            lax.psum_scatter(
                partial_rows(jnp.int32(0), rows_here * lax.axis_size("row")),
                "row",
                scatter_dimension=0,
                tiled=True,
            ),
        )

    condition_float = condition.astype(jnp.float32)
    silu_low = jax.nn.silu(condition_float).astype(jnp.bfloat16)
    modulation = lax.psum_scatter(
        jnp.dot(silu_low, modulator, preferred_element_type=jnp.float32),
        "row",
        scatter_dimension=0,
        tiled=True,
    )
    modulation = modulation.reshape(latents_row, 6, width_here) + modulation_bias.astype(
        jnp.float32
    )
    shift_one = modulation[:, 0]
    scale_one = modulation[:, 1]
    gate_one = modulation[:, 2]
    shift_two = modulation[:, 3]
    scale_two = modulation[:, 4]
    gate_two = modulation[:, 5]
    residual = tokens.astype(jnp.float32)
    normed_one, inverse_one = normalize(residual)
    modulated_one = modulate(normed_one, shift_one, scale_one).astype(jnp.bfloat16)
    gathered_one, projected = project_in(modulated_one, input_block)
    cols_here = projected.shape[0]
    projected = projected.reshape(cols_here, 3, inner_here)
    bias_float = input_bias.astype(jnp.float32)
    heads_shape = (cols_here // LENGTH, LENGTH, heads_here, HEAD_DIM)
    query_heads = (projected[:, 0] + bias_float[0]).astype(jnp.bfloat16).reshape(heads_shape)
    key_heads = projected[:, 1].astype(jnp.bfloat16).reshape(heads_shape)
    value_heads = (projected[:, 2] + bias_float[1]).astype(jnp.bfloat16).reshape(heads_shape)
    attended, logsum = lax.map(attend_forward, (query_heads, key_heads, value_heads))
    attended_low = attended.reshape(cols_here, inner_here).astype(jnp.bfloat16)
    gathered_attended, branch_one = project_out(attended_low, output_weight)
    branch_one = branch_one + output_bias.astype(jnp.float32)
    middle = residual + by_latent(branch_one, gate_one)
    normed_two, inverse_two = normalize(middle)
    modulated_two = modulate(normed_two, shift_two, scale_two).astype(jnp.bfloat16)
    gathered_two, expanded = project_in(modulated_two, expand_weight)
    expanded = expanded + expand_bias.astype(jnp.float32)
    hidden_low = gelu_tanh(expanded).astype(jnp.bfloat16)
    gathered_hidden, branch_two = project_out(hidden_low, shrink_weight)
    branch_two = branch_two + shrink_bias.astype(jnp.float32)
    layer_output = (middle + by_latent(branch_two, gate_two)).astype(jnp.bfloat16)
    upstream = cotangent.astype(jnp.float32)
    gate_two_back = latent_sums(branch_two * upstream, latents_row)
    branch_two_back = by_latent(upstream, gate_two).astype(jnp.bfloat16)
    gathered_down, hidden_back = project_in(branch_two_back, shrink_weight.T)
    shrink_weight_gradient = contract(gathered_hidden, gathered_down)
    shrink_bias_gradient = jnp.sum(gathered_down, axis=0, dtype=jnp.float32)
    gelu_value, gelu_pull = jax.vjp(gelu_tanh, expanded)
    expanded_back = gelu_pull(hidden_back)[0].astype(jnp.bfloat16)
    gathered_expanded, modulated_back_two = project_out(expanded_back, expand_weight.T)
    expand_weight_gradient = contract(gathered_two, gathered_expanded)
    expand_bias_gradient = jnp.sum(gathered_expanded, axis=0, dtype=jnp.float32)
    shift_two_back = latent_sums(modulated_back_two, latents_row)
    scale_two_back = latent_sums(modulated_back_two * normed_two, latents_row)
    middle_back = upstream + norm_back(
        by_latent(modulated_back_two, 1.0 + scale_two), normed_two, inverse_two
    )
    gate_one_back = latent_sums(branch_one * middle_back, latents_row)
    branch_one_back = by_latent(middle_back, gate_one).astype(jnp.bfloat16)
    gathered_middle, attended_back = project_in(branch_one_back, output_weight.T)
    output_weight_gradient = contract(gathered_attended, gathered_middle)
    output_bias_gradient = jnp.sum(gathered_middle, axis=0, dtype=jnp.float32)
    attended_back = attended_back.astype(jnp.bfloat16).reshape(heads_shape)
    stacked_back = lax.map(
        attend_backward, (query_heads, key_heads, value_heads, logsum, attended_back)
    )
    stacked_back = stacked_back.reshape(cols_here, 3 * inner_here)
    gathered_stacked, modulated_back_one = project_out(stacked_back, input_block.T)
    input_weight_gradient = contract(gathered_one, gathered_stacked).reshape(input_weight.shape)
    column_totals = jnp.sum(gathered_stacked, axis=0, dtype=jnp.float32).reshape(3, inner_here)
    input_bias_gradient = jnp.stack([column_totals[0], column_totals[2]])
    shift_one_back = latent_sums(modulated_back_one, latents_row)
    scale_one_back = latent_sums(modulated_back_one * normed_one, latents_row)
    tokens_gradient = middle_back + norm_back(
        by_latent(modulated_back_one, 1.0 + scale_one), normed_one, inverse_one
    )
    modulation_back = jnp.stack(
        [
            shift_one_back,
            scale_one_back,
            gate_one_back,
            shift_two_back,
            scale_two_back,
            gate_two_back,
        ],
        axis=1,
    ).astype(jnp.bfloat16)
    gathered_modulation = row_gather(modulation_back.reshape(latents_row, -1))
    modulation_weight_gradient = contract(silu_low, gathered_modulation).reshape(
        modulation_weight.shape
    )
    modulation_bias_gradient = jnp.sum(gathered_modulation, axis=0, dtype=jnp.float32).reshape(
        6, width_here
    )
    silu_back = lax.psum(
        jnp.dot(gathered_modulation, modulator.T, preferred_element_type=jnp.float32), "col"
    )
    silu_value, silu_pull = jax.vjp(jax.nn.silu, condition_float)
    condition_gradient = silu_pull(silu_back)[0]
    summed = lax.psum(
        (
            modulation_weight_gradient,
            modulation_bias_gradient,
            input_weight_gradient,
            input_bias_gradient,
            output_weight_gradient,
            output_bias_gradient,
            expand_weight_gradient,
            expand_bias_gradient,
            shrink_weight_gradient,
            shrink_bias_gradient,
        ),
        "dp",
    )
    return (
        layer_output,
        tokens_gradient,
        condition_gradient,
        summed[0],
        summed[1],
        summed[2],
        summed[3],
        summed[4],
        summed[5],
        summed[6],
        summed[7],
        summed[8],
        summed[9],
    )


def solution(mesh):
    placed = (
        P(("dp", "row"), "col"),
        P("dp", "row"),
        P("row", None, "col"),
        P(None, "col"),
        P("col", None, "row"),
        P(None, "row"),
        P("row", "col"),
        P("col"),
        P("col", "row"),
        P("row"),
        P("row", "col"),
        P("col"),
        P(("dp", "row"), "col"),
    )
    return jax.shard_map(
        body,
        mesh=mesh,
        in_specs=placed,
        out_specs=(
            P(("dp", "row"), "col"),
            P(("dp", "row"), "col"),
            P("dp", "row"),
            P("row", None, "col"),
            P(None, "col"),
            P("col", None, "row"),
            P(None, "row"),
            P("row", "col"),
            P("col"),
            P("col", "row"),
            P("row"),
            P("row", "col"),
            P("col"),
        ),
        check_vma=False,
    )
```

profile of v0, /device:TPU:0, one launch (start us, length us, event | category | flops | bytes accessed | tf_op | source)
XLA Modules:
  0.0 3410.5 jit_solution(3242845162846547682)
XLA Ops:
  12.4 13.2 all-reduce
  28.2 19.0 all-reduce.4
  49.0 31.7 all-gather.10.cloned.1.call-done
  80.7 14.0 fusion.89
  95.5 413.7 %reduce-scatter.9.cloned.1.call-done = f32[2048,768]{1,0:T(8,128)} async-done(((f32[8192,768]{1,0:T(8,128)}), f32[2048,768]{1,0:T(8,128)}) %reduce-scatter.9.cloned.1.call-update) | async-done | bytes 6291472 | tf_op jit(solution)/shard_map/reduce_scatter | solution.py:134
  509.2 6.6 copy.81
  539.2 51.5 %while.22 = (s32[]{:T(128)}, bf16[2,1024,4,64]{1,3,2,0:T(8,128)(2,1)}, f32[2,4,1024]{2,1,0:T(4,128)S(1)}, bf16[2,1024,4,64]{1,3,2,0:T(8,128)(2,1)}, bf16[2,1024,...) while((s32[]{:T(128)}, bf16[2,1024,4,64]{1,3,2,0:T(8,128)(2,1)}, ...), condition=%wide.region_9.10_spmd, body=%wide.region_6.9_spmd.sunk | while | flops 1111486464 | bytes 65669292 | solution.py:186
  539.7 8.1 multiply_reduce_fusion.6
  547.8 8.7 fusion.148
  556.5 7.7 fusion.149
  565.2 8.1 multiply_reduce_fusion.6
  573.3 8.7 fusion.148
  582.0 7.7 fusion.149
  594.3 82.7 %all-gather.12.cloned.1.call-done = bf16[8192,256]{0,1:T(8,128)(2,1)} async-done(((bf16[2048,256]{0,1:T(8,128)(2,1)}), bf16[8192,256]{0,1:T(8,128)(2,1)}) %all-gather.12.cloned.1.call-update) | async-done | bytes 4194320 | tf_op jit(solution)/shard_map/all_gather | solution.py:143
  677.0 6.7 fusion.90
  687.0 67.2 %reduce-scatter.11.cloned.1.call-done = f32[2048,256]{1,0:T(8,128)} async-done(((f32[8192,256]{1,0:T(8,128)}), f32[2048,256]{1,0:T(8,128)}) %reduce-scatter.11.cloned.1.call-update) | async-done | bytes 2097168 | tf_op jit(solution)/shard_map/reduce_scatter | solution.py:150
  757.7 18.7 all-reduce.3
  779.2 11.5 all-gather.18.cloned.1.call-done
  790.7 16.8 fusion.93
  807.6 19.6 all-gather.14.cloned.1.call-done
  827.2 15.9 fusion.91
  843.8 537.8 %reduce-scatter.17.cloned.1.call-done = f32[2048,1024]{1,0:T(8,128)} async-done(((f32[8192,1024]{1,0:T(8,128)}), f32[2048,1024]{1,0:T(8,128)}) %reduce-scatter.17.cloned.1.call-update) | async-done | bytes 8388624 | tf_op jit(solution)/shard_map/reduce_scatter | solution.py:134
  1381.6 555.3 %reduce-scatter.13.cloned.1.call-done = f32[2048,1024]{1,0:T(8,128)} async-done(((f32[8192,1024]{1,0:T(8,128)}), f32[2048,1024]{1,0:T(8,128)}) %reduce-scatter.13.cloned.1.call-update) | async-done | bytes 8388624 | tf_op jit(solution)/shard_map/reduce_scatter | solution.py:134
  1937.0 13.1 fusion.52
  1951.0 286.8 %all-gather.16.cloned.1.call-done = bf16[8192,1024]{1,0:T(8,128)(2,1)} async-done(((bf16[2048,1024]{1,0:T(8,128)(2,1)}), bf16[8192,1024]{1,0:T(8,128)(2,1)}) %all-gather.16.cloned.1.call-update) | async-done | bytes 16777232 | tf_op jit(solution)/shard_map/all_gather | solution.py:143
  2237.8 14.2 fusion.92
  2252.0 272.2 %all-gather.20.cloned.1.call-done = bf16[8192,1024]{1,0:T(8,128)(2,1)} async-done(((bf16[2048,1024]{1,0:T(8,128)(2,1)}), bf16[8192,1024]{1,0:T(8,128)(2,1)}) %all-gather.20.cloned.1.call-update) | async-done | bytes 16777232 | tf_op jit(solution)/shard_map/all_gather | solution.py:143
  2524.2 15.1 fusion.94
  2539.9 56.8 %reduce-scatter.15.cloned.1.call-done = f32[2048,256]{1,0:T(8,128)} async-done(((f32[8192,256]{1,0:T(8,128)}), f32[2048,256]{1,0:T(8,128)}) %reduce-scatter.15.cloned.1.call-update) | async-done | bytes 2097168 | tf_op jit(solution)/shard_map/reduce_scatter | solution.py:150
  2596.7 74.4 %reduce-scatter.19.cloned.1.call-done = f32[2048,256]{1,0:T(8,128)} async-done(((f32[8192,256]{1,0:T(8,128)}), f32[2048,256]{1,0:T(8,128)}) %reduce-scatter.19.cloned.1.call-update) | async-done | bytes 2097168 | tf_op jit(solution)/shard_map/reduce_scatter | solution.py:150
  2675.2 18.7 all-reduce.2
  2702.0 31.4 all-gather.22.cloned.1.call-done
  2733.4 6.7 fusion.95
  2740.2 144.6 %reduce-scatter.21.cloned.1.call-done = f32[2048,256]{1,0:T(8,128)} async-done(((f32[8192,256]{1,0:T(8,128)}), f32[2048,256]{1,0:T(8,128)}) %reduce-scatter.21.cloned.1.call-update) | async-done | bytes 2097168 | tf_op jit(solution)/shard_map/reduce_scatter | solution.py:134
  2895.9 61.1 %while.23 = (s32[]{:T(128)}, bf16[2,1024,3,4,64]{1,4,3,2,0:T(8,128)(2,1)}, bf16[2,1024,4,64]{1,3,2,0:T(8,128)(2,1)S(1)}, bf16[2,1024,4,64]{1,3,2,0:T(8,128)(2,1)...) while((s32[]{:T(128)}, ...), condition=%wide.region_26.27_spmd, body=%wide.region_24.26_spmd.sunk | while | flops 2740711424 | bytes 159762672 | solution.py:221
  2903.1 9.2 multiply_reduce_fusion.7
  2912.3 7.9 multiply_convert_fusion.3
  2933.6 9.2 multiply_reduce_fusion.7
  2942.8 7.9 multiply_convert_fusion.3
  2964.9 219.0 %all-gather.24.cloned.1.call-done = bf16[8192,768]{0,1:T(8,128)(2,1)} async-done(((bf16[2048,768]{0,1:T(8,128)(2,1)}), bf16[8192,768]{0,1:T(8,128)(2,1)}) %all-gather.24.cloned.1.call-update) | async-done | bytes 12582928 | tf_op jit(solution)/shard_map/all_gather | solution.py:143
  3183.9 11.4 fusion.96
  3195.4 14.9 fusion.99
  3210.3 9.5 fusion.100
  3229.1 36.3 %reduce-scatter.23.cloned.1.call-done = f32[2048,256]{1,0:T(8,128)} async-done(((f32[8192,256]{1,0:T(8,128)}), f32[2048,256]{1,0:T(8,128)}) %reduce-scatter.23.cloned.1.call-update) | async-done | bytes 2097168 | tf_op jit(solution)/shard_map/reduce_scatter | solution.py:150
  3277.6 10.7 convert_reduce_fusion
  3298.9 18.9 all-reduce.1
  3321.6 8.8 all-reduce.5
  3331.0 64.4 %all-reduce.9.cloned.1.call-done = (f32[256,6,256]{0,2,1:T(8,128)}, f32[256,3,256]{0,2,1:T(8,128)}, f32[256,256]{1,0:T(8,128)}, f32[256,1024]{1,0:T(8,128)}, f32[1024,256]{1,0:T(8,128)}) async-done(((f32[256,6,256]{0,2,1:T(8,128)}, f32[256,3,256]{0,2,1:T(8,128)}, f32[256,256]{1,0:T(8,128)}, f32[256,1024]{1,0:T(8,128)}, f32[1024,256]{1,0:T(8,128)}), (f32[256,6,256]{0,2,1:T(8,128)}, f32[256,3,256]{0,2,1:T(8,128)}, ...) | async-done | bytes 4718608 | tf_op jit(solution)/shard_map/psum | solution.py:257
  (243 shorter events, 152.6 us)
Async XLA Ops:
  7.2 783.5 %copy-start = (bf16[1024,256]{1,0:T(8,128)(2,1)S(1)}, bf16[1024,256]{1,0:T(8,128)(2,1)}, u32[]{:S(2)}) copy-start(bf16[1024,256]{1,0:T(8,128)(2,1)} %param.27) | copy-start | bytes 1572868
  7.2 40.0 %copy-start.3 = (bf16[2048,256]{1,0:T(8,128)(2,1)S(1)}, bf16[2048,256]{1,0:T(8,128)(2,1)}, u32[]{:S(2)}) copy-start(bf16[2048,256]{1,0:T(8,128)(2,1)} %param.17) | copy-start | bytes 3145732
  7.2 41.6 %copy-start.23 = (bf16[256,3,256]{2,0,1:T(8,128)(2,1)S(1)}, bf16[256,3,256]{2,0,1:T(8,128)(2,1)}, u32[]{:S(2)}) copy-start(bf16[256,3,256]{2,0,1:T(8,128)(2,1)} %param.21) | copy-start | bytes 1179652
  7.2 73.4 %all-gather.10.cloned.1.call-start = ((), (), s32[]{:S(2)}) async-start(), calls=%async_computation.8 | async-start | bytes 5242880 | tf_op jit(solution)/shard_map/all_gather | solution.py:62
  11.3 83.3 %copy-start.10 = (bf16[256,6,256]{0,2,1:T(8,128)(2,1)}, bf16[256,6,256]{0,2,1:T(8,128)(2,1)S(1)}, u32[]{:S(2)}) copy-start(bf16[256,6,256]{0,2,1:T(8,128)(2,1)S(1)} %copy.79) | copy-start | bytes 2359300
  47.2 47.5 %copy-start.27 = (f32[2048]{0:T(1024)}, f32[2048]{0:T(1024)S(1)}, u32[]{:S(2)}) copy-start(f32[2048]{0:T(1024)S(1)} %get-tuple-element.253) | copy-start | bytes 24580
  47.2 47.4 %copy-start.29 = (f32[2048]{0:T(1024)}, f32[2048]{0:T(1024)S(1)}, u32[]{:S(2)}) copy-start(f32[2048]{0:T(1024)S(1)} %get-tuple-element.254) | copy-start | bytes 24580
  47.2 47.4 %copy-start.32 = (f32[2,256]{1,0:T(2,128)}, f32[2,256]{1,0:T(2,128)S(1)}, u32[]{:S(2)}) copy-start(f32[2,256]{1,0:T(2,128)S(1)} %get-tuple-element.260) | copy-start | bytes 6148
  48.8 460.5 %reduce-scatter.9.cloned.1.call-start = ((), (), s32[]{:S(2)}) async-start(), calls=%async_computation.9 | async-start | bytes 31457280 | tf_op jit(solution)/shard_map/reduce_scatter | solution.py:134
  49.0 45.6 %copy-start.15 = (bf16[256,3,256]{0,2,1:T(8,128)(2,1)}, bf16[256,3,256]{0,2,1:T(8,128)(2,1)S(1)}, u32[]{:S(2)}) copy-start(bf16[256,3,256]{0,2,1:T(8,128)(2,1)S(1)} %copy.80) | copy-start | bytes 1179652
  94.7 582.3 %all-gather.12.cloned.1.call-start = ((), (), s32[]{:S(2)}) async-start(), calls=%async_computation.10 | async-start | bytes 5242880 | tf_op jit(solution)/shard_map/all_gather | solution.py:143
  547.8 8.7 copy-start.8
  547.8 8.7 copy-start.19
  573.3 8.7 copy-start.8
  573.3 8.7 copy-start.19
  590.7 86.3 %copy-start.22 = (bf16[256,256]{1,0:T(8,128)(2,1)S(1)}, bf16[256,256]{1,0:T(8,128)(2,1)}, u32[]{:S(2)}) copy-start(bf16[256,256]{1,0:T(8,128)(2,1)} %param.23) | copy-start | bytes 393220
  594.3 159.9 %reduce-scatter.11.cloned.1.call-start = ((), (), s32[]{:S(2)}) async-start(), calls=%async_computation.11 | async-start | bytes 10485760 | tf_op jit(solution)/shard_map/reduce_scatter | solution.py:150
  683.8 106.9 %all-gather.18.cloned.1.call-start = ((), (), s32[]{:S(2)}) async-start(), calls=%async_computation.16 | async-start | bytes 5242880 | tf_op jit(solution)/shard_map/all_gather | solution.py:62
  686.8 140.4 %all-gather.14.cloned.1.call-start = ((), (), s32[]{:S(2)}) async-start(), calls=%async_computation.12 | async-start | bytes 5242880 | tf_op jit(solution)/shard_map/all_gather | solution.py:62
  779.2 602.5 %reduce-scatter.17.cloned.1.call-start = ((), (), s32[]{:S(2)}) async-start(), calls=%async_computation.17 | async-start | bytes 41943040 | tf_op jit(solution)/shard_map/reduce_scatter | solution.py:134
  807.5 19.7 copy-start.21
  807.5 1129.5 %reduce-scatter.13.cloned.1.call-start = ((), (), s32[]{:S(2)}) async-start(), calls=%async_computation.13 | async-start | bytes 41943040 | tf_op jit(solution)/shard_map/reduce_scatter | solution.py:134
  843.1 1394.6 %all-gather.16.cloned.1.call-start = ((), (), s32[]{:S(2)}) async-start(), calls=%async_computation.14 | async-start | bytes 20971520 | tf_op jit(solution)/shard_map/all_gather | solution.py:143
  1950.1 574.1 %all-gather.20.cloned.1.call-start = ((), (), s32[]{:S(2)}) async-start(), calls=%async_computation.18 | async-start | bytes 20971520 | tf_op jit(solution)/shard_map/all_gather | solution.py:143
  1950.7 646.0 %reduce-scatter.15.cloned.1.call-start = ((), (), s32[]{:S(2)}) async-start(), calls=%async_computation.15 | async-start | bytes 10485760 | tf_op jit(solution)/shard_map/reduce_scatter | solution.py:150
  2251.9 419.1 %reduce-scatter.19.cloned.1.call-start = ((), (), s32[]{:S(2)}) async-start(), calls=%async_computation.19 | async-start | bytes 10485760 | tf_op jit(solution)/shard_map/reduce_scatter | solution.py:150
  2539.3 194.1 %all-gather.22.cloned.1.call-start = ((), (), s32[]{:S(2)}) async-start(), calls=%async_computation.20 | async-start | bytes 5242880 | tf_op jit(solution)/shard_map/all_gather | solution.py:62
  2701.6 183.2 %reduce-scatter.21.cloned.1.call-start = ((), (), s32[]{:S(2)}) async-start(), calls=%async_computation.21 | async-start | bytes 10485760 | tf_op jit(solution)/shard_map/reduce_scatter | solution.py:134
  2740.1 443.8 %all-gather.24.cloned.1.call-start = ((), (), s32[]{:S(2)}) async-start(), calls=%async_computation.22 | async-start | bytes 15728640 | tf_op jit(solution)/shard_map/all_gather | solution.py:143
  2962.1 221.8 %copy-start.16 = (bf16[256,3,256]{0,2,1:T(8,128)(2,1)S(1)}, bf16[256,3,256]{0,2,1:T(8,128)(2,1)}, u32[]{:S(2)}) copy-start(bf16[256,3,256]{0,2,1:T(8,128)(2,1)} %copy-done.15) | copy-start | bytes 1179652
  2964.8 300.6 %reduce-scatter.23.cloned.1.call-start = ((), (), s32[]{:S(2)}) async-start(), calls=%async_computation.23 | async-start | bytes 10485760 | tf_op jit(solution)/shard_map/reduce_scatter | solution.py:150
  3195.3 200.1 %all-reduce.9.cloned.1.call-start = ((), (), s32[]{:S(2)}) async-start(), calls=%async_computation.24 | async-start | bytes 9437184 | tf_op jit(solution)/shard_map/psum | solution.py:257
  3195.4 14.9 copy-start.2
  3210.3 9.5 copy-start.6
  3210.3 9.5 copy-start.12
  3210.3 11.5 slice-start
  3210.3 11.7 slice-start.1
  3224.7 40.7 %copy-start.4 = (bf16[2048,256]{1,0:T(8,128)(2,1)S(1)}, bf16[2048,256]{1,0:T(8,128)(2,1)}, u32[]{:S(2)}) copy-start(bf16[2048,256]{1,0:T(8,128)(2,1)} %param.17) | copy-start | bytes 3145732
  3224.7 40.7 %copy-start.28 = (f32[2048]{0:T(1024)S(1)}, f32[2048]{0:T(1024)}, u32[]{:S(2)}) copy-start(f32[2048]{0:T(1024)} %copy-done.27) | copy-start | bytes 24580
  3224.7 40.7 %copy-start.30 = (f32[2048]{0:T(1024)S(1)}, f32[2048]{0:T(1024)}, u32[]{:S(2)}) copy-start(f32[2048]{0:T(1024)} %copy-done.29) | copy-start | bytes 24580
  3224.7 42.7 %copy-start.41 = (bf16[2,256]{1,0:T(2,128)(2,1)S(1)}, bf16[2,256]{1,0:T(2,128)(2,1)}, u32[]{:S(2)}) copy-start(bf16[2,256]{1,0:T(2,128)(2,1)} %get-tuple-element.241) | copy-start | bytes 3076
  3224.7 42.7 %copy-start.40 = (bf16[2,256]{1,0:T(2,128)(2,1)S(1)}, bf16[2,256]{1,0:T(2,128)(2,1)}, u32[]{:S(2)}) copy-start(bf16[2,256]{1,0:T(2,128)(2,1)} %get-tuple-element.176) | copy-start | bytes 3076
  3224.7 42.7 %copy-start.39 = (bf16[2,256]{1,0:T(2,128)(2,1)S(1)}, bf16[2,256]{1,0:T(2,128)(2,1)}, u32[]{:S(2)}) copy-start(bf16[2,256]{1,0:T(2,128)(2,1)} %get-tuple-element.175) | copy-start | bytes 3076
  3224.7 42.7 %copy-start.38 = (bf16[2,256]{1,0:T(2,128)(2,1)S(1)}, bf16[2,256]{1,0:T(2,128)(2,1)}, u32[]{:S(2)}) copy-start(bf16[2,256]{1,0:T(2,128)(2,1)} %get-tuple-element.244) | copy-start | bytes 3076
  3224.7 48.0 %copy-start.31 = (bf16[8,256]{1,0:T(8,128)(2,1)S(1)}, bf16[8,256]{1,0:T(8,128)(2,1)}, u32[]{:S(2)}) copy-start(bf16[8,256]{1,0:T(8,128)(2,1)} %param.18) | copy-start | bytes 12292
  3277.6 10.7 copy-start.7
  3289.4 9.3 copy-start.11
  3395.4 8.1 copy-start.1
  (25 other events, 71.6 us)
Sparse Core Ops, SparseCore 0:
  48.9 31.7 all-gather.9
  94.8 414.3 reduce-scatter.8
  594.4 82.5 all-gather.11
  683.9 70.2 reduce-scatter.10
  756.2 34.4 all-gather.17
  792.7 34.4 all-gather.13
  829.6 552.0 reduce-scatter.16
  1384.1 552.7 reduce-scatter.12
  1950.2 287.4 all-gather.15
  2239.2 284.9 all-gather.19
  2526.8 69.8 reduce-scatter.14
  2599.3 71.6 reduce-scatter.18
  2701.7 31.6 all-gather.21
  2740.3 144.4 reduce-scatter.20
  2965.0 218.9 all-gather.23
  3195.5 69.9 reduce-scatter.22
  3274.4 120.9 all-reduce.8
where the time goes:
time: 3420 us; the launch traced here: 3410 us
  waiting for transfers between devices  2910 us (85%)
  matrix products  206 us (6%)
  other arithmetic  107 us (3%)
  blocking collectives  103 us (3%)
  local copies, waits for them, and re-layouts  71 us (2%)
    reduce_scatter x4, waiting for transfers between devices, project_in(): lax.psum_scatter(partial_rows(jnp.int32(0), share * lax.axis_size('col'))...  1650 us
    all_gather x4, waiting for transfers between devices, project_out(): gathered = lax.all_gather(local_cols, 'col', axis=0, tiled=True)  861 us
    reduce_scatter x4, waiting for transfers between devices, project_out(): lax.psum_scatter(partial_rows(jnp.int32(0), rows_here * lax.axis_size('ro...  235 us
    dot_general x8, matrix products, partial_rows(): return jnp.dot(gathered, block, preferred_element_type=jnp.float32)  101 us
    all_gather x4, waiting for transfers between devices, row_gather(): return lax.all_gather(values, 'row', axis=0, tiled=True)  94.2 us
    psum x4, blocking collectives, feature_sums(): return lax.psum((totals, squares), 'col')  75.3 us
  transfers between devices with their start and end apart: 17, of which 17 were waited for; matrix products, arithmetic and copies ran while one was open for 4% of the time, Pallas kernels for 0%

commit v1 on v0

v1 whole, which is shorter than its diff:
```python
import functools
import math

import jax
import jax.numpy as jnp
from jax import lax
from jax.experimental import pallas as pl
from jax.experimental.pallas import tpu as pltpu
from jax.sharding import Mesh
from jax.sharding import PartitionSpec as P

HEAD_DIM = 64
LENGTH = 1024
EPS = 1e-06
LANES = 128
SCALE = HEAD_DIM ** (-0.5)
SCALE_LOG2 = SCALE * math.log2(math.e)
ROWS = ("y", "core")
COLS = ("lat", "sub")
NT = (((1,), (1,)), ((), ()))
F32 = jnp.float32
BF16 = jnp.bfloat16
VMEM_LIMIT = 56 * 1024 * 1024


def dot(left, right):
    return jnp.dot(left, right, preferred_element_type=F32)


def dot_nt(left, right):
    return lax.dot_general(left, right, NT, preferred_element_type=F32)


def gelu_tanh(values):
    return (
        0.5
        * values
        * (1.0 + jnp.tanh(0.7978845608028654 * (values + 0.044715 * values * values * values)))
    )


def gelu_slope(values):
    inner = jnp.tanh(0.7978845608028654 * (values + 0.044715 * values * values * values))
    rate = 0.7978845608028654 * (1.0 + 3 * 0.044715 * values * values)
    return 0.5 * (1.0 + inner) + 0.5 * values * (1.0 - inner * inner) * rate


def whole(shape):
    return pl.BlockSpec(shape, lambda *_: (0,) * len(shape))


def block(shape, column=0, first=0, step=1):
    return pl.BlockSpec((None, *shape), lambda b: (first + step * b, 0, column))


def call(kernel, grid, in_specs, out_specs, out_shape, scratch=(), flops=0, moved=0, exps=0):
    return pl.pallas_call(
        kernel,
        grid=grid,
        in_specs=in_specs,
        out_specs=out_specs,
        out_shape=out_shape,
        scratch_shapes=list(scratch),
        compiler_params=pltpu.CompilerParams(vmem_limit_bytes=VMEM_LIMIT),
        cost_estimate=pl.CostEstimate(flops=flops, bytes_accessed=moved, transcendentals=exps),
    )


def shaped(shape, dtype):
    return jax.ShapeDtypeStruct(shape, dtype)


def project(left, blocks, bias):
    number, features, _ = blocks.shape
    rows = left.shape[0]

    def kernel(a, g, c, q, kv):
        out = dot(a[...], g[...]) + c[...]
        q[...] = out[:, :LANES].astype(BF16)
        kv[...] = out[:, LANES:].astype(BF16)

    return call(
        kernel,
        (number,),
        [whole(left.shape), block((features, 3 * LANES)), block((1, 3 * LANES))],
        [block((rows, LANES)), block((rows, 2 * LANES))],
        [shaped((number, rows, LANES), BF16), shaped((number, rows, 2 * LANES), BF16)],
        flops=2 * rows * features * number * 3 * LANES,
        moved=2 * number * features * 3 * LANES,
    )(left, blocks, bias)


def expand(left, blocks, bias):
    number, features, _ = blocks.shape
    rows, width = left.shape[0], bias.shape[-1]

    def kernel(a, g, c, e, h):
        out = dot(a[...], g[...]) + c[...]
        e[...] = out
        h[...] = gelu_tanh(out).astype(BF16)

    return call(
        kernel,
        (number,),
        [whole(left.shape), block((features, width)), block((1, width))],
        [block((rows, width)), block((rows, width))],
        [shaped((number, rows, width), F32), shaped((number, rows, width), BF16)],
        flops=2 * rows * features * number * width,
        moved=number * width * (2 * features + 6 * rows),
    )(left, blocks, bias)


def hidden_backward(left, blocks, expanded):
    number, rows, width = expanded.shape
    features = left.shape[1]

    def kernel(a, g, e, back, sums):
        out = (dot(a[...], g[...]) * gelu_slope(e[...])).astype(BF16)
        back[...] = out
        sums[...] = jnp.sum(out.astype(F32), axis=0, keepdims=True)

    return call(
        kernel,
        (number,),
        [whole(left.shape), block((features, width)), block((rows, width))],
        [block((rows, width)), block((1, width))],
        [shaped((number, rows, width), BF16), shaped((number, 1, width), F32)],
        flops=2 * rows * features * number * width,
        moved=number * width * (2 * features + 6 * rows),
    )(left, blocks, expanded)


def attended_backward(left, blocks, column):
    number, features, _ = blocks.shape
    rows = left.shape[0]

    def kernel(a, g, out):
        out[...] = dot(a[...], g[...]).astype(BF16)

    return call(
        kernel,
        (number,),
        [whole(left.shape), block((features, LANES), column)],
        block((rows, LANES)),
        shaped((number, rows, LANES), BF16),
        flops=2 * rows * features * number * LANES,
        moved=number * LANES * (2 * features + 2 * rows),
    )(left, blocks)


def contract(terms, extras, finish, outs):
    number, rows, _ = terms[0][0].shape
    features = terms[0][1].shape[1]
    count, more = len(terms), len(extras)

    def kernel(*refs):
        lefts, rights = refs[:count], refs[count : 2 * count]
        given = refs[2 * count : 2 * count + more]
        results, total = refs[2 * count + more : -1], refs[-1]
        out = dot_nt(lefts[0][...], rights[0][...])
        for left, right in zip(lefts[1:], rights[1:]):
            out = out + dot_nt(left[...], right[...])
        step = pl.program_id(0)

        @pl.when(step == 0)
        def _():
            total[...] = out

        @pl.when(step > 0)
        def _():
            total[...] += out

        @pl.when(step == number - 1)
        def _():
            finish(total, given, results)

    return call(
        kernel,
        (number,),
        [block(left.shape[1:]) for left, _, _ in terms]
        + [block((features, left.shape[2]), column) for left, _, column in terms]
        + [whole(extra.shape) for extra in extras],
        [whole(out.shape) for out in outs],
        outs,
        scratch=[pltpu.VMEM((rows, features), F32)],
        flops=2 * rows * features * number * sum(left.shape[2] for left, _, _ in terms),
        moved=number * sum(2 * left.shape[2] * (features + rows) for left, _, _ in terms),
    )(*[left for left, _, _ in terms], *[right for _, right, _ in terms], *extras)


def by_rows(rows, sums, features, work):
    tile = min(rows, 64)

    def step(i, totals):
        found = work(pl.ds(pl.multiple_of(i * tile, tile), tile))
        return tuple(
            total + jnp.sum(one.reshape(-1, 8, features), axis=0)
            for total, one in zip(totals, found)
        )

    zero = jnp.zeros((8, features), F32)
    totals = lax.fori_loop(0, rows // tile, step, (zero,) * sums)
    return [jnp.sum(total, axis=0, keepdims=True) for total in totals]


def normalize(values):
    average = jnp.mean(values, axis=1, keepdims=True)
    inverse = lax.rsqrt(
        jnp.mean(values * values, axis=1, keepdims=True) - average * average + EPS
    )
    return (values - average) * inverse, inverse


def norm_back(incoming, normed, inverse):
    return inverse * (
        incoming
        - jnp.mean(incoming, axis=1, keepdims=True)
        - normed * jnp.mean(incoming * normed, axis=1, keepdims=True)
    )


def finish_middle(total, given, results):
    tokens, vectors = given
    branch, middle, low = results
    rows, features = total.shape
    shift, scale, gate = vectors[3:4], 1.0 + vectors[4:5], vectors[2:3]
    bias = vectors[6:7]

    def work(here):
        one = total[here, :] + bias
        branch[here, :] = one
        values = tokens[here, :].astype(F32) + gate * one
        middle[here, :] = values
        low[here, :] = (normalize(values)[0] * scale + shift).astype(BF16)
        return ()

    by_rows(rows, 0, features, work)


def finish_output(total, given, results):
    middle, cotangent, vectors = given
    output, sums = results
    rows, features = total.shape
    gate, bias = vectors[5:6], vectors[7:8]

    def work(here):
        two = total[here, :] + bias
        output[here, :] = (middle[here, :] + gate * two).astype(BF16)
        return (two * cotangent[here, :].astype(F32),)

    (gate_back,) = by_rows(rows, 1, features, work)
    sums[...] = gate_back


def finish_middle_back(total, given, results):
    middle, branch, cotangent, vectors = given
    middle_back, low, sums = results
    rows, features = total.shape
    gate, scale = vectors[2:3], 1.0 + vectors[4:5]

    def work(here):
        back = total[here, :]
        normed, inverse = normalize(middle[here, :])
        out = cotangent[here, :].astype(F32) + norm_back(back * scale, normed, inverse)
        middle_back[here, :] = out
        rounded = (gate * out).astype(BF16)
        low[here, :] = rounded
        return back, back * normed, branch[here, :] * out, rounded.astype(F32)

    sums[...] = jnp.concatenate(by_rows(rows, 4, features, work), axis=0)


def finish_tokens_back(total, given, results):
    tokens, middle_back, vectors = given
    tokens_back, sums = results
    rows, features = total.shape
    scale = 1.0 + vectors[1:2]

    def work(here):
        back = total[here, :]
        normed, inverse = normalize(tokens[here, :].astype(F32))
        out = middle_back[here, :] + norm_back(back * scale, normed, inverse)
        tokens_back[here, :] = out.astype(BF16)
        return back, back * normed

    sums[...] = jnp.concatenate(by_rows(rows, 2, features, work), axis=0)


def gradients(pairs, adds=(), first=0, step=1, count=None, halves=False):
    features, rows = pairs[0][0].shape
    parts = [one for _, parts in pairs for one in parts]
    width = sum(one.shape[2] for one in parts)
    count = parts[0].shape[0] if count is None else count
    lefts, rights, extra = len(pairs), len(parts), len(adds)

    def kernel(*refs):
        left_refs = refs[:lefts]
        right_refs = list(refs[lefts : lefts + rights])
        add_refs = refs[lefts + rights : lefts + rights + extra]
        outs = refs[lefts + rights + extra :]
        start = 0
        for left, (_, own) in zip(left_refs, pairs):
            for _ in own:
                right = right_refs.pop(0)
                here = slice(start, start + right.shape[1])
                out = dot(left[...], right[...])
                for add in add_refs:
                    out = out + add[:, here].astype(F32)
                out = out.astype(BF16)
                if halves:
                    outs[0][:, here] = out[: features // 2]
                    outs[1][:, here] = out[features // 2 :]
                else:
                    outs[0][:, here] = out
                start += right.shape[1]

    if halves:
        out_specs = [whole((features // 2, width))] * 2
        outs = [shaped((features // 2, width), BF16)] * 2
    else:
        out_specs = [block((features, width))]
        outs = [shaped((count, features, width), BF16)]
    got = call(
        kernel,
        (count,),
        [whole(left.shape) for left, _ in pairs]
        + [block(one.shape[1:], 0, first, step) for one in parts]
        + [block(add.shape[1:], 0, one, two) for add, one, two in adds],
        out_specs,
        outs,
        flops=2 * rows * features * count * width,
        moved=count * width * features * 2 * (1 + extra),
    )(*[left for left, _ in pairs], *parts, *[add for add, _, _ in adds])
    return got if halves else got[0]


def attend(queries, pieces):
    number, rows, _ = queries.shape
    count = len(pieces)
    keys = sum(piece.shape[1] for piece in pieces)
    tile = min(rows, 256)

    def kernel(*refs):
        query, kv = refs[0], refs[1 : 1 + count]
        out_ref, log_ref = refs[1 + count :]
        head = lax.broadcasted_iota(jnp.int32, (1, LANES), 1) < HEAD_DIM
        for start in range(0, rows, tile):
            here = slice(start, start + tile)
            both = query[here, :]
            outs, logs = [], []
            for keep in (head, ~head):
                one = jnp.where(keep, both, jnp.zeros_like(both))
                scores = [dot_nt(one, piece[:, :LANES]) for piece in kv]
                top = functools.reduce(
                    jnp.maximum, [jnp.max(s, axis=1, keepdims=True) for s in scores]
                )
                weights = [jnp.exp2((s - top) * SCALE_LOG2) for s in scores]
                total = sum(jnp.sum(w, axis=1, keepdims=True) for w in weights)
                inverse = 1.0 / total
                out = sum(
                    dot((w * inverse).astype(BF16), piece[:, LANES:])
                    for w, piece in zip(weights, kv)
                )
                outs.append(out)
                logs.append(top * SCALE_LOG2 + jnp.log(total) * math.log2(math.e))
            out_ref[here, :] = jnp.where(head, outs[0], outs[1]).astype(BF16)
            table = jnp.where(head, logs[0], logs[1]).T
            log_ref[0:1, here] = table[0:1]
            log_ref[1:2, here] = table[HEAD_DIM : HEAD_DIM + 1]

    return call(
        kernel,
        (number,),
        [block((rows, LANES))] + [block((piece.shape[1], 2 * LANES)) for piece in pieces],
        [block((rows, LANES)), block((2, rows))],
        [shaped((number, rows, LANES), BF16), shaped((number, 2, rows), F32)],
        flops=number * 2 * 2 * 2 * rows * keys * 256,
        exps=number * 2 * rows * keys,
        moved=number * 2 * LANES * (2 * rows + 2 * keys),
    )(queries, *pieces)


def attend_back(queries, pieces, logs, incoming, kinds, first=0, number=None):
    number = queries.shape[0] if number is None else number
    rows = queries.shape[1]
    count = len(pieces)
    keys = sum(piece.shape[1] for piece in pieces)
    tile = min(rows, 256)

    def kernel(*refs):
        query, back_ref, log_ref = refs[:3]
        kv = refs[3 : 3 + count]
        query_back = refs[3 + count]
        kv_back = refs[4 + count : 4 + 2 * count]
        sums, scratch = refs[4 + 2 * count], refs[5 + 2 * count :]
        head = lax.broadcasted_iota(jnp.int32, (1, LANES), 1) < HEAD_DIM
        turned = [piece[:, :LANES].T for piece in kv]
        top = lax.broadcasted_iota(jnp.int32, (LANES, 1), 0) < HEAD_DIM
        query_sum = jnp.zeros((1, LANES), F32)
        for start in range(0, rows, tile):
            here = slice(start, start + tile)
            backs = []
            for index, keep in enumerate((head, ~head)):
                zero = jnp.zeros((tile, LANES), BF16)
                one = jnp.where(keep, query[here, :], zero)
                back = jnp.where(keep, back_ref[here, :], zero)
                log = log_ref[index : index + 1, here]
                chances, mixes = [], []
                for piece in kv:
                    scores = dot_nt(piece[:, :LANES], one)
                    chances.append(jnp.exp2(scores * SCALE_LOG2 - log))
                    mixes.append(dot_nt(piece[:, LANES:], back))
                centre = sum(
                    jnp.sum(p * m, axis=0, keepdims=True) for p, m in zip(chances, mixes)
                )
                total = None
                for i in range(count):
                    score_back = (chances[i] * (mixes[i] - centre)).astype(BF16)
                    key_back = dot(score_back, one) * SCALE
                    value_back = dot(chances[i].astype(BF16), back)
                    if start == 0 and index == 0:
                        scratch[i][:, :LANES] = key_back
                        scratch[i][:, LANES:] = value_back
                    else:
                        scratch[i][:, :LANES] += key_back
                        scratch[i][:, LANES:] += value_back
                    term = dot(turned[i], score_back)
                    total = term if total is None else total + term
                backs.append(total)
            both = (jnp.where(top, backs[0], backs[1]).T * SCALE).astype(BF16)
            query_back[here, :] = both
            query_sum = query_sum + jnp.sum(both.astype(F32), axis=0, keepdims=True)
        sums[...] = query_sum
        for out, held in zip(kv_back, scratch):
            out[...] = held[...].astype(out.dtype)

    here = dict(first=first)
    return call(
        kernel,
        (number,),
        [block((rows, LANES), **here), block((rows, LANES), **here), block((2, rows), **here)]
        + [block((piece.shape[1], 2 * LANES), **here) for piece in pieces],
        [block((rows, LANES))]
        + [block((piece.shape[1], 2 * LANES)) for piece in pieces]
        + [block((1, LANES))],
        [shaped((number, rows, LANES), BF16)]
        + [
            shaped((number, piece.shape[1], 2 * LANES), kind)
            for piece, kind in zip(pieces, kinds)
        ]
        + [shaped((number, 1, LANES), F32)],
        scratch=[pltpu.VMEM((piece.shape[1], 2 * LANES), F32) for piece in pieces],
        flops=number * 2 * 5 * 2 * rows * keys * 256,
        exps=number * 2 * rows * keys,
        moved=number * 2 * LANES * (4 * rows + 8 * keys),
    )(queries, incoming, logs, *pieces)


class Plain:
    def __init__(self, sizes):
        self.latents, self.parts, self.width = sizes
        self.row = lax.axis_size("y") * lax.axis_size("core")
        self.col = lax.axis_size("lat") * lax.axis_size("sub")

    def scatter(self, values):
        rows, width = values.shape
        shaped_in = values.reshape(self.latents, 2, LENGTH // 2, width)
        halves = lax.all_to_all(shaped_in, "core", 1, 0, tiled=True)
        pieces = halves.reshape(self.col, -1, width)
        pieces = lax.all_to_all(pieces, COLS, 0, 0, tiled=True)
        return pieces.transpose(1, 0, 2).reshape(-1, self.col * width)

    def collect(self, values):
        rows, features = values.shape
        pieces = values.reshape(rows, self.col, -1).transpose(1, 0, 2)
        pieces = lax.all_to_all(pieces, COLS, 0, 0, tiled=True)
        halves = pieces.reshape(2 * self.latents, 1, LENGTH // 2, -1)
        back = lax.all_to_all(halves, "core", 0, 1, tiled=True)
        return back.reshape(-1, features // self.col)

    def modulation(self, partial, bias, row_bias, col_bias):
        group = 2 * self.latents
        ours = lax.psum(partial, "core").reshape(-1, group, partial.shape[1])
        ours = lax.psum_scatter(ours, "y", scatter_dimension=0, tiled=True)[0] + bias
        sent = jnp.repeat(ours, self.col // group, axis=0)
        got = lax.all_to_all(sent, COLS, 0, 0, tiled=True)
        got = got.reshape(self.col, 6, -1).transpose(1, 0, 2).reshape(6, -1)
        cols = lax.all_gather(col_bias, COLS, axis=1, tiled=True)
        every = lax.all_gather(row_bias, ROWS, axis=0)
        return jnp.concatenate([got, cols], axis=0), [
            every.reshape(self.row * self.parts, 1, -1)
        ]

    def own_parts(self, parts):
        return parts

    def gather(self, parts, order):
        every = lax.all_gather(parts, COLS, axis=1, tiled=True)
        return [lax.all_gather(every, ROWS, axis=0, tiled=True)]

    def share(self, kv):
        return [[lax.all_gather(kv[0], ("core", "sub"), axis=1, tiled=True)]]

    def kinds(self):
        return [F32]

    def give_back(self, backs):
        return [
            lax.psum_scatter(
                backs[0][0], ("core", "sub"), scatter_dimension=1, tiled=True
            ).astype(BF16)
        ]

    def reduce(self, pairs, order):
        grads = gradients(pairs[0]).astype(F32)
        grads = lax.psum_scatter(grads, ROWS, scatter_dimension=0, tiled=True)
        grads = lax.psum_scatter(grads, COLS, scatter_dimension=1, tiled=True)
        return lax.psum(grads, "dp")

    def small(self, vectors, row_sums, col_sums):
        every = ("dp", *ROWS, *COLS)
        group = 2 * self.latents
        total = lax.psum(vectors, ("core", "sub")).astype(BF16)
        mine = lax.all_gather(total[:, None], "lat", axis=1, tiled=True)
        mine = lax.all_gather(mine, "y", axis=1, tiled=True)
        mine = lax.all_gather(mine, "dp", axis=1, tiled=True)
        col = lax.axis_index("lat") * lax.axis_size("sub") + lax.axis_index("sub")
        cut = lax.dynamic_slice_in_dim(mine, col * self.width, self.width, axis=2)
        cut = cut.transpose(1, 0, 2).reshape(mine.shape[1], -1)
        rows = lax.psum(row_sums[0], every).reshape(self.row, self.parts, -1)
        row = lax.axis_index("y") * 2 + lax.axis_index("core")
        rows = lax.dynamic_index_in_dim(rows, row, 0, keepdims=False)
        cols = lax.psum(col_sums, every)
        cols = lax.dynamic_slice_in_dim(cols, col * self.width, self.width, axis=1)
        return cut, rows, cols

    def both_groups(self, values):
        return lax.all_gather(values, "dp", axis=0, tiled=True)


class Cube(Plain):
    def __init__(self, sizes):
        super().__init__(sizes)
        self.x = lax.axis_index("dp")
        self.y = lax.axis_index("y")
        self.c = lax.axis_index("core")
        self.z = lax.axis_index("lat")

    def swap(self, values, axis):
        return lax.ppermute(values, axis, [(0, 1), (1, 0)])

    def along(self, values, bits):
        return lax.ppermute(values, "lat", [(i, i ^ bits) for i in range(4)])

    def scatter(self, values):
        rows, width = values.shape
        halves = values.reshape(self.latents, 2, LENGTH // 2, width)
        keep = lax.dynamic_index_in_dim(halves, self.c, 1, keepdims=False)
        send = lax.dynamic_index_in_dim(halves, 1 - self.c, 1, keepdims=False)
        every = jnp.concatenate([keep, self.swap(send, "core")], axis=0)
        pieces = []
        for bits in range(4):
            latent = self.z ^ bits
            index = ((latent // 2) ^ self.c) * 2 + latent % 2
            piece = lax.dynamic_index_in_dim(every, index, 0, keepdims=False)
            pieces.append(piece if bits == 0 else self.along(piece, bits))
        return jnp.concatenate(pieces, axis=1)

    def collect(self, values):
        rows, features = values.shape
        width = features // 4
        pieces = [values[:, i * width : (i + 1) * width] for i in range(4)]
        pieces = [p if bits == 0 else self.along(p, bits) for bits, p in enumerate(pieces)]
        every = jnp.stack(pieces)

        def latents(core):
            return jnp.stack(
                [
                    lax.dynamic_index_in_dim(every, self.z ^ (2 * core + i), 0, keepdims=False)
                    for i in range(2)
                ]
            )

        keep = latents(self.c)
        got = self.swap(latents(1 - self.c), "core")
        first = jnp.where(self.c == 0, keep, got)
        second = jnp.where(self.c == 0, got, keep)
        return jnp.stack([first, second], axis=1).reshape(-1, width)

    def modulation(self, partial, bias, row_bias, col_bias):
        span = partial.shape[1]
        own = row_bias.reshape(1, -1)
        got = self.swap(jnp.concatenate([partial, own], axis=0), "core")
        ours, other = partial + got[:-1], got[-1:]
        halves = ours.reshape(2, 4, span)
        keep = lax.dynamic_index_in_dim(halves, self.y, 0, keepdims=False)
        send = lax.dynamic_index_in_dim(halves, 1 - self.y, 0, keepdims=False)
        got = self.swap(jnp.concatenate([send, own, other], axis=0), "y")
        ours = keep + got[:4] + bias
        rows = jnp.stack([own, got[4:5], other, got[5:6]]).reshape(2, 2, 2, -1)
        flip = jnp.stack([rows[:, :, 1], rows[:, :, 0]], axis=2)
        rows = jnp.where(self.x == 0, rows, flip).transpose(0, 2, 1, 3).reshape(2, 4, 1, -1)
        pieces = []
        for bits in range(4):
            piece = lax.dynamic_index_in_dim(ours, self.z ^ bits, 0, keepdims=False)
            piece = jnp.concatenate([piece.reshape(6, -1), col_bias], axis=0)
            pieces.append(piece if bits == 0 else self.along(piece, bits))
        return jnp.concatenate(pieces, axis=1), [rows[0], rows[1]]

    def own_parts(self, parts):
        return lax.dynamic_index_in_dim(parts, self.x, 0, keepdims=False)

    def gather(self, part, order):
        part = jnp.concatenate([part, self.along(part, 1)], axis=0)
        part = jnp.concatenate([part, self.along(part, 2)], axis=0)
        first, second = ("y", "dp") if order == "yx" else ("dp", "y")
        pair = jnp.stack([part, self.swap(part, first)])
        other = self.swap(pair, second)
        four = jnp.stack([pair, other], axis=0 if order == "yx" else 1)
        four = four.reshape(4, *part.shape)
        return [four, self.swap(four, "core")]

    def share(self, kv):
        return [[kv[0], self.swap(kv[1], "core")], [kv[1], self.swap(kv[0], "core")]]

    def kinds(self):
        return [F32, BF16]

    def give_back(self, backs):
        got = [self.swap(backs[1][1], "core"), self.swap(backs[0][1], "core")]
        return [(own[0] + one.astype(F32)).astype(BF16) for own, one in zip(backs, got)]

    def reduce(self, pairs, order):
        near = self.swap(gradients(pairs[1]), "core")
        if order == "xy":
            axes, first, step, last = ("dp", "y"), 2, 1, 1
        else:
            axes, first, step, last = ("y", "dp"), 1, 2, 2
        sent = gradients(pairs[0], [(near, first, step)], first, step, 2)
        second = self.swap(sent, axes[0])
        sent = gradients(pairs[0], [(near, last, 1), (second, 1, 1)], last, 1, 1)
        third = self.swap(sent, axes[1])
        low, high = gradients(
            pairs[0], [(near, 0, 1), (second, 0, 1), (third, 0, 1)], 0, 1, 1, halves=True
        )
        low = low.astype(F32) + self.along(high, 2).astype(F32)
        rows = low.shape[0] // 2
        own = (low[:rows] + self.along(low[rows:].astype(BF16), 1).astype(F32)).astype(BF16)
        other = self.swap(own, "dp")
        return jnp.stack(
            [jnp.where(self.x == 0, own, other), jnp.where(self.x == 0, other, own)]
        ).astype(F32)

    def small(self, vectors, row_sums, col_sums):
        span = row_sums[0].shape[-1]
        features = vectors.shape[1]

        def flat(*parts):
            return jnp.concatenate([part.reshape(-1, LANES) for part in parts], axis=0)

        def cut(message, *shapes):
            parts, start = [], 0
            for shape in shapes:
                size = math.prod(shape) // LANES
                parts.append(message[start : start + size].reshape(shape))
                start += size
            return parts

        rows0, rows1 = (one.reshape(2, 2, span) for one in row_sums)
        got = self.swap(flat(rows1, col_sums, vectors), "core")
        got = cut(got, rows1.shape, col_sums.shape, vectors.shape)
        rows, cols = rows0 + got[0], col_sums + got[1]
        mine = (vectors + got[2]).astype(BF16).astype(F32)
        got = self.swap(flat(rows[:, 1], cols, mine), "y")
        got = cut(got, (2, span), cols.shape, mine.shape)
        rows, cols = rows[:, 0] + got[0], cols + got[1]
        pair = jnp.stack([mine, got[2]])
        got = self.swap(flat(rows, cols, pair), "dp")
        got = cut(got, rows.shape, cols.shape, pair.shape)
        rows = rows + jnp.stack([got[0][1], got[0][0]])
        rows = jnp.where(self.x == 0, rows, jnp.stack([rows[1], rows[0]]))
        cols = cols + got[1]
        four = jnp.stack([pair, got[2]]).reshape(4, 6, features)
        width = self.width
        found = []
        for bits in range(4):
            here = slice(bits * width, (bits + 1) * width)
            piece = [four[:, :, here], cols[:, here], rows]
            if bits:
                got = self.along(flat(*piece), bits)
                piece = cut(got, *[part.shape for part in piece])
            found.append(piece)
        tree = [(found[0][i] + found[1][i]) + (found[2][i] + found[3][i]) for i in (1, 2)]
        every = jnp.stack([one[0] for one in found])
        every = every.reshape(16, -1)
        place = lax.broadcasted_iota(jnp.int32, (16, 16), 0)
        held = lax.broadcasted_iota(jnp.int32, (16, 16), 1)
        latent = (
            (((held // 2) % 2) ^ self.x) * 8 + ((held % 2) ^ self.y) * 4 + ((held // 4) ^ self.z)
        )
        chosen = (latent == place).astype(F32)
        every = jnp.dot(chosen, every, precision=lax.Precision.HIGHEST).astype(BF16)
        return every, tree[1], tree[0]

    def both_groups(self, values):
        got = self.swap(values, "dp")
        return jnp.where(
            self.x == 0,
            jnp.concatenate([values, got], axis=0),
            jnp.concatenate([got, values], axis=0),
        )


def body(
    fast,
    tokens,
    condition,
    modulation_weight,
    modulation_bias,
    input_weight,
    input_bias,
    output_weight,
    output_bias,
    expand_weight,
    expand_bias,
    shrink_weight,
    shrink_bias,
    cotangent,
):
    width = tokens.shape[1]
    inner = input_weight.shape[2]
    parts = inner // LANES
    units = expand_weight.shape[1] // parts
    sizes = (tokens.shape[0] // LENGTH, parts, width)
    net = (Cube if fast else Plain)(sizes)

    own_in = net.own_parts(
        input_weight.reshape(width, 3, parts, LANES)
        .transpose(2, 0, 1, 3)
        .reshape(parts, width, 3 * LANES)
    )
    own_out = net.own_parts(output_weight.reshape(parts, LANES, width).transpose(0, 2, 1))
    own_expand = net.own_parts(expand_weight.reshape(width, parts, units).transpose(1, 0, 2))
    own_shrink = net.own_parts(shrink_weight.reshape(parts, units, width).transpose(0, 2, 1))
    out_column = units // LANES

    condition_float = condition.astype(F32)
    silu_low = jax.nn.silu(condition_float).astype(BF16)
    modulator = modulation_weight.reshape(modulation_weight.shape[0], -1)
    row_bias = jnp.concatenate(
        [
            input_bias.reshape(2, parts, LANES).transpose(1, 0, 2).reshape(parts, -1),
            expand_bias.reshape(parts, units),
        ],
        axis=1,
    ).astype(F32)
    vectors, row_biases = net.modulation(
        dot(silu_low, modulator),
        modulation_bias.astype(F32).reshape(1, -1),
        row_bias,
        jnp.stack([output_bias, shrink_bias]).astype(F32),
    )
    mine = net.scatter(tokens)
    in_bufs = net.gather(own_in, "yx")
    out_bufs = net.gather(jnp.concatenate([own_expand, own_out], axis=-1), "xy")
    shrink_bufs = net.gather(own_shrink, "yx")
    back = net.scatter(cotangent)
    rows = mine.shape[0]
    features = mine.shape[1]
    in_biases = [
        jnp.concatenate(
            [one[..., :LANES], jnp.zeros_like(one[..., :LANES]), one[..., LANES : 2 * LANES]],
            axis=-1,
        )
        for one in row_biases
    ]
    expand_biases = [one[..., 2 * LANES :] for one in row_biases]

    normed, _ = normalize(mine.astype(F32))
    low_one = (normed * (1.0 + vectors[1:2]) + vectors[0:1]).astype(BF16)
    queries, own_kv = [], []
    for buf, bias in zip(in_bufs, in_biases):
        one, two = project(low_one, buf, bias)
        queries.append(one)
        own_kv.append(two)
    kv = net.share(own_kv)
    attended, logs = [], []
    for one, pieces in zip(queries, kv):
        out, log = attend(one, pieces)
        attended.append(out)
        logs.append(log)
    branch_one, middle, low_two = contract(
        [(one, buf, out_column) for one, buf in zip(attended, out_bufs)],
        [mine, vectors],
        finish_middle,
        [
            shaped((rows, features), F32),
            shaped((rows, features), F32),
            shaped((rows, features), BF16),
        ],
    )
    expanded, hidden = [], []
    for buf, bias in zip(out_bufs, expand_biases):
        one, two = expand(low_two, buf, bias)
        expanded.append(one)
        hidden.append(two)
    output, gate_two_back = contract(
        [(one, buf, 0) for one, buf in zip(hidden, shrink_bufs)],
        [middle, back, vectors],
        finish_output,
        [shaped((rows, features), BF16), shaped((1, features), F32)],
    )

    branch_two_back = (vectors[5:6] * back.astype(F32)).astype(BF16)
    shrink_sum = jnp.sum(branch_two_back.astype(F32), axis=0, keepdims=True)
    turned_two_back = branch_two_back.T
    shrink_parts = net.reduce([[(turned_two_back, [one])] for one in hidden], "xy")
    expanded_back, expand_sums = [], []
    for buf, one in zip(shrink_bufs, expanded):
        two, sums = hidden_backward(branch_two_back, buf, one)
        expanded_back.append(two)
        expand_sums.append(sums)
    middle_back, branch_one_back, sums_two = contract(
        [(one, buf, 0) for one, buf in zip(expanded_back, out_bufs)],
        [middle, branch_one, back, vectors],
        finish_middle_back,
        [
            shaped((rows, features), F32),
            shaped((rows, features), BF16),
            shaped((4, features), F32),
        ],
    )
    turned_two, turned_one_back = low_two.T, branch_one_back.T
    out_parts = net.reduce(
        [
            [(turned_two, [one]), (turned_one_back, [two])]
            for one, two in zip(expanded_back, attended)
        ],
        "yx",
    )
    incoming = [attended_backward(branch_one_back, buf, out_column) for buf in out_bufs]
    query_back, backs, query_sums = [], [], []
    for one, pieces, log, two in zip(queries, kv, logs, incoming):
        got = attend_back(one, pieces, log, two, net.kinds())
        query_back.append(got[0])
        backs.append(got[1:-1])
        query_sums.append(got[-1])
    kv_back = net.give_back(backs)
    value_sums = [
        jnp.sum(one[:, :, LANES:].astype(F32), axis=1, keepdims=True) for one in kv_back
    ]
    turned_one = low_one.T
    in_parts = net.reduce(
        [[(turned_one, [one, two])] for one, two in zip(query_back, kv_back)], "xy"
    )
    tokens_back, sums_one = contract(
        [(one, buf, 0) for one, buf in zip(query_back, in_bufs)]
        + [(one[:, :, :LANES], buf, 1) for one, buf in zip(kv_back, in_bufs)]
        + [(one[:, :, LANES:], buf, 2) for one, buf in zip(kv_back, in_bufs)],
        [mine, middle_back, vectors],
        finish_tokens_back,
        [shaped((rows, features), BF16), shaped((2, features), F32)],
    )

    summed = jnp.concatenate([sums_one, sums_two[2:3], sums_two[0:2], gate_two_back], axis=0)
    row_sums = [
        jnp.concatenate([one, two, three], axis=-1)
        for one, two, three in zip(query_sums, value_sums, expand_sums)
    ]
    col_sums = jnp.concatenate([sums_two[3:4], shrink_sum], axis=0)
    every, row_found, col_found = net.small(summed, row_sums, col_sums)
    silu_all = net.both_groups(silu_low)
    modulation_weight_gradient = lax.dot_general(
        silu_all, every, (((0,), (0,)), ((), ())), preferred_element_type=F32
    ).reshape(modulation_weight.shape)
    modulation_bias_gradient = jnp.sum(every.astype(F32), axis=0).reshape(6, width)
    groups = condition.shape[0]
    ours = lax.dynamic_slice_in_dim(every, lax.axis_index("dp") * groups, groups, axis=0)
    silu_back = lax.psum(dot_nt(ours, modulator), COLS)
    silu_pull = jax.vjp(jax.nn.silu, condition_float)[1]
    condition_gradient = silu_pull(silu_back)[0]

    return (
        net.collect(output),
        net.collect(tokens_back).astype(F32),
        condition_gradient,
        modulation_weight_gradient,
        modulation_bias_gradient,
        in_parts.reshape(parts, width, 3, LANES)
        .transpose(1, 2, 0, 3)
        .reshape(input_weight.shape),
        row_found[:, : 2 * LANES]
        .reshape(parts, 2, LANES)
        .transpose(1, 0, 2)
        .reshape(input_bias.shape),
        out_parts[:, :, units:].transpose(0, 2, 1).reshape(output_weight.shape),
        col_found[0],
        out_parts[:, :, :units].transpose(1, 0, 2).reshape(expand_weight.shape),
        row_found[:, 2 * LANES :].reshape(expand_bias.shape),
        shrink_parts.transpose(0, 2, 1).reshape(shrink_weight.shape),
        col_found[1],
    )


def solution(mesh):
    dp, row, col = (mesh.shape[name] for name in ("dp", "row", "col"))

    def run(*arrays):
        latents = arrays[0].shape[0] // (dp * row * LENGTH)
        group = 2 * latents
        refined = Mesh(
            mesh.devices.reshape(dp, row // 2, 2, group, col // group),
            ("dp", "y", "core", "lat", "sub"),
        )
        fast = (dp, row, col, latents) == (2, 4, 4, 2)
        token = P(("dp", *ROWS), COLS)
        weights = (
            P(ROWS, None, COLS),
            P(None, COLS),
            P(COLS, None, ROWS),
            P(None, ROWS),
            P(ROWS, COLS),
            P(COLS),
            P(COLS, ROWS),
            P(ROWS),
            P(ROWS, COLS),
            P(COLS),
        )
        given = P("dp", ROWS)
        return jax.shard_map(
            functools.partial(body, fast),
            mesh=refined,
            in_specs=(token, given, *weights, token),
            out_specs=(token, token, given, *weights),
            check_vma=False,
        )(*arrays)

    return run
```

time: 3420 us -> 766 us (0.22)
  waiting for transfers between devices: 2910 us -> 311 us
  Pallas kernels: 0 us -> 217 us
  matrix products: 206 us -> 1.13 us
  blocking collectives: 103 us -> 9.51 us
  starting transfers between devices: 1.32 us -> 78.5 us
  other arithmetic: 107 us -> 60 us
    reduce_scatter x8 -> x0, waiting for transfers between devices: 1890 us -> none  [the longest x4 1650 us: project_in(): lax.psum_scatter(partial_rows(jnp.int32(0), share * lax.axis_size('col'))...]
    all_gather x8 -> x0, waiting for transfers between devices: 955 us -> none  [the longest x4 861 us: project_out(): gathered = lax.all_gather(local_cols, 'col', axis=0, tiled=True)]
    ppermute x0 -> x65, waiting for transfers between devices: none -> 311 us  [the longest x35 187 us: swap(): return lax.ppermute(values, axis, [(0, 1), (1, 0)])]
    pallas_call x0 -> x28, Pallas kernels: none -> 217 us  [the longest x12 57.8 us: gradients(): call(kernel, (count,), [whole(left.shape) for left, _ in pairs] + [block(...]
    dot_general x29 -> x4, matrix products: 206 us -> 1.13 us  [the longest x1 0.41 us: body(): lax.dot_general(silu_all, every, (((0,), (0,)), ((), ())), preferred_elem...]
    ppermute x0 -> x65, starting transfers between devices: none -> 78.5 us  [the longest x30 54.7 us: along(): return lax.ppermute(values, 'lat', [(i, i ^ bits) for i in range(4)])]
    psum x5 -> x1, blocking collectives: 84.2 us -> 9.51 us  [body(): silu_back = lax.psum(dot_nt(ours, modulator), COLS)]
    psum x1 -> x0, waiting for transfers between devices: 64.4 us -> none  [body(): lax.psum((modulation_weight_gradient, modulation_bias_gradient, input_wei...]
  transfers between devices with their start and end apart: 17 -> 65, of which waited for: 17 -> 26; matrix products, arithmetic and copies ran while one was open for 4% -> 16% of each run, Pallas kernels for 0% -> 24%
where the time goes in v1:
time: 766 us; the launch traced here: 755 us
  waiting for transfers between devices  311 us (41%)
  Pallas kernels  217 us (28%)
  starting transfers between devices  78.5 us (10%)
  local copies, waits for them, and re-layouts  75 us (10%)
  other arithmetic  60 us (8%)
  blocking collectives  9.51 us (1%)
    ppermute x35, waiting for transfers between devices, swap(): return lax.ppermute(values, axis, [(0, 1), (1, 0)])  187 us
    ppermute x30, waiting for transfers between devices, along(): return lax.ppermute(values, 'lat', [(i, i ^ bits) for i in range(4)])  124 us
    pallas_call x12, Pallas kernels, gradients(): call(kernel, (count,), [whole(left.shape) for left, _ in pairs] + [block(...  57.8 us
    ppermute x30, starting transfers between devices, along(): return lax.ppermute(values, 'lat', [(i, i ^ bits) for i in range(4)])  54.7 us
    pallas_call x4, Pallas kernels, contract(): call(kernel, (number,), [block(left.shape[1:]) for left, _, _ in terms] +...  48.2 us
    pallas_call x2, Pallas kernels, attend_back(): call(kernel, (number,), [block((rows, LANES), **here), block((rows, LANES...  35.2 us
    pallas_call x2, Pallas kernels, attend(): call(kernel, (number,), [block((rows, LANES))] + [block((piece.shape[1],...  24 us
    ppermute x35, starting transfers between devices, swap(): return lax.ppermute(values, axis, [(0, 1), (1, 0)])  23.8 us
  transfers between devices with their start and end apart: 65, of which 26 were waited for; matrix products, arithmetic and copies ran while one was open for 16% of the time, Pallas kernels for 24%

profile of v1, /device:TPU:0, one launch (start us, length us, event | category | flops | bytes accessed | tf_op | source)
XLA Modules:
  0.0 755.2 jit_solution(16939212046904714888)
XLA Ops:
  6.3 7.7 %collective-permute-done.16 = bf16[256,640]{1,0:T(8,128)(2,1)S(1)} collective-permute-done((bf16[256,640]{1,0:T(8,128)(2,1)S(1)}, bf16[256,640]{1,0:T(8,128)(2,1)S(1)}, u32[]{:S(2)}, u32[]{:S(2)}) %collective-permute-start.16) | collective-permute-done | bytes 327712 | tf_op jit(solution)/shard_map/ppermute | solution.py:553
  20.7 25.3 %collective-permute-done.17 = bf16[512,640]{1,0:T(8,128)(2,1)} collective-permute-done((bf16[512,640]{1,0:T(8,128)(2,1)}, bf16[512,640]{1,0:T(8,128)(2,1)}, u32[]{:S(2)}, u32[]{:S(2)}) %collective-permute-start.17) | collective-permute-done | bytes 655392 | tf_op jit(solution)/shard_map/ppermute | solution.py:553
  56.8 21.5 %collective-permute-done.18 = bf16[1024,640]{1,0:T(8,128)(2,1)} collective-permute-done((bf16[1024,640]{1,0:T(8,128)(2,1)S(1)}, bf16[1024,640]{1,0:T(8,128)(2,1)}, u32[]{:S(2)}, u32[]{:S(2)}) %collective-permute-start.18) | collective-permute-done | bytes 1310752 | tf_op jit(solution)/shard_map/ppermute | solution.py:550
  87.1 20.8 %collective-permute-done.22 = bf16[512,512]{1,0:T(8,128)(2,1)S(1)} collective-permute-done((bf16[512,512]{1,0:T(8,128)(2,1)S(1)}, bf16[512,512]{1,0:T(8,128)(2,1)S(1)}, u32[]{:S(2)}, u32[]{:S(2)}) %collective-permute-start.22) | collective-permute-done | bytes 524320 | tf_op jit(solution)/shard_map/ppermute | solution.py:553
  111.3 47.5 %collective-permute-done.11 = bf16[1024,384]{1,0:T(8,128)(2,1)S(1)} collective-permute-done((bf16[1024,384]{1,0:T(8,128)(2,1)S(1)}, bf16[1024,384]{1,0:T(8,128)(2,1)S(1)}, u32[]{:S(2)}, u32[]{:S(2)}) %collective-permute-start.11) | collective-permute-done | bytes 786464 | tf_op jit(solution)/shard_map/ppermute | solution.py:550
  169.2 10.3 %collective-permute-done.5 = f32[6,1536]{1,0:T(8,128)S(1)} collective-permute-done((f32[6,1536]{1,0:T(8,128)S(1)}, f32[6,1536]{1,0:T(8,128)S(1)}, u32[]{:S(2)}, u32[]{:S(2)}) %collective-permute-start.5) | collective-permute-done | bytes 36896 | tf_op jit(solution)/shard_map/ppermute | solution.py:550
  189.5 9.0 %collective-permute-done.12 = bf16[2,1024,384]{2,1,0:T(8,128)(2,1)} collective-permute-done((bf16[2,1024,384]{2,1,0:T(8,128)(2,1)}, bf16[2,1024,384]{2,1,0:T(8,128)(2,1)}, u32[]{:S(2)}, u32[]{:S(2)}) %collective-permute-start.12) | collective-permute-done | bytes 1572896 | tf_op jit(solution)/shard_map/ppermute | solution.py:550
  204.2 32.5 %collective-permute-done.24 = bf16[2,1024,512]{2,1,0:T(8,128)(2,1)} collective-permute-done((bf16[2,1024,512]{2,1,0:T(8,128)(2,1)}, bf16[2,1024,512]{2,1,0:T(8,128)(2,1)}, u32[]{:S(2)}, u32[]{:S(2)}) %collective-permute-start.24) | collective-permute-done | bytes 2097184 | tf_op jit(solution)/shard_map/ppermute | solution.py:550
  236.7 4.7 pad_maximum_fusion.1
  241.4 6.3 collective-permute-start.8
  254.4 8.7 %collective-permute-done.1 = bf16[512,256]{0,1:T(8,128)(2,1)S(1)} collective-permute-done((bf16[512,256]{0,1:T(8,128)(2,1)S(1)}, bf16[512,256]{0,1:T(8,128)(2,1)S(1)}, u32[]{:S(2)}, u32[]{:S(2)}) %collective-permute-start.1) | collective-permute-done | bytes 262176 | tf_op jit(solution)/shard_map/ppermute | solution.py:553
  266.0 6.2 collective-permute-start.27
  278.9 5.7 shard_map.228
  285.8 6.4 collective-permute-start.28
  297.3 5.7 shard_map.229
  303.0 7.9 %collective-permute-done.28 = bf16[512,256]{0,1:T(8,128)(2,1)} collective-permute-done((bf16[512,256]{0,1:T(8,128)(2,1)}, bf16[512,256]{0,1:T(8,128)(2,1)}, u32[]{:S(2)}, u32[]{:S(2)}) %collective-permute-start.28) | collective-permute-done | bytes 262176 | tf_op jit(solution)/shard_map/ppermute | solution.py:553
  318.9 12.0 %shard_map.231 = (bf16[4,512,128]{2,1,0:T(8,128)(2,1)}, f32[4,2,512]{2,1,0:T(2,128)}) custom-call(bf16[4,512,128]{2,1,0:T(8,128)(2,1)} %get-tuple-element.57.refs_0_, bf16[4,512,256]{2,1,0:T(8,128)(2,1)} %get-tuple-element.55.refs_1_.refs_3_, bf16[4,512,256]{2,1,0:T(8,128)(2,1)} %collective-permute-done.15.refs_2_.refs_4_), custom_call_target="tpu_custom_call" | custom-call | flops 4294967296 | bytes 3145728 | tf_op jit(solution)/shard_map/pallas_call | solution.py:371
  331.8 12.0 %shard_map.230 = (bf16[4,512,128]{2,1,0:T(8,128)(2,1)}, f32[4,2,512]{2,1,0:T(2,128)}) custom-call(bf16[4,512,128]{2,1,0:T(8,128)(2,1)} %get-tuple-element.53.refs_0_, bf16[4,512,256]{2,1,0:T(8,128)(2,1)} %get-tuple-element.54.refs_1_.refs_3_, bf16[4,512,256]{2,1,0:T(8,128)(2,1)} %copy-done.57), custom_call_target="tpu_custom_call" | custom-call | flops 4294967296 | bytes 3145728 | tf_op jit(solution)/shard_map/pallas_call | solution.py:371
  343.8 9.3 %shard_map.232 = (f32[512,1024]{1,0:T(8,128)}, f32[512,1024]{1,0:T(8,128)}, bf16[512,1024]{1,0:T(8,128)(2,1)}) custom-call(bf16[4,512,128]{2,1,0:T(8,128)(2,1)} %get-tuple-element.56.refs_0_.refs_3_, bf16[4,512,128]{2,1,0:T(8,128)(2,1)} %get-tuple-element.58.refs_1_.refs_3_, bf16[4,1024,640]{2,1,0:T(8,128)(2,1)} %bitcast.38.refs_2_.g, ...), custom_call_target="tpu_custom_call" | custom-call | flops 1073741824 | bytes 3145728 | tf_op jit(solution)/shard_map/pallas_call | solution.py:177
  355.4 7.4 shard_map.233
  362.8 8.3 %shard_map.236 = (bf16[4,512,512]{2,1,0:T(8,128)(2,1)}, f32[4,1,512]{2,1,0:T(1,128)}) custom-call(bf16[512,1024]{1,0:T(8,128)(2,1)} %copy.96.a, bf16[4,1024,512]{2,1,0:T(8,128)(2,1)} %bitcast.47.refs_2_.g, f32[4,512,512]{2,1,0:T(8,128)} %get-tuple-element.64.e), custom_call_target="tpu_custom_call" | custom-call | flops 2147483648 | bytes 10485760 | tf_op jit(solution)/shard_map/pallas_call | solution.py:122
  371.1 7.4 shard_map.234
  378.5 8.5 %shard_map.237 = (bf16[4,512,512]{2,1,0:T(8,128)(2,1)}, f32[4,1,512]{2,1,0:T(1,128)}) custom-call(bf16[512,1024]{1,0:T(8,128)(2,1)} %copy.96.a, bf16[4,1024,512]{2,1,0:T(8,128)(2,1)} %collective-permute-done.25.refs_3_.g, f32[4,512,512]{2,1,0:T(8,128)} %get-tuple-element.66.e), custom_call_target="tpu_custom_call" | custom-call | flops 2147483648 | bytes 10485760 | tf_op jit(solution)/shard_map/pallas_call | solution.py:122
  387.0 14.1 %shard_map.238 = (f32[512,1024]{1,0:T(8,128)}, bf16[512,1024]{1,0:T(8,128)(2,1)}, f32[4,1024]{1,0:T(4,128)}) custom-call(bf16[4,512,512]{2,1,0:T(8,128)(2,1)} %get-tuple-element.65.refs_0_.refs_2_, bf16[4,512,512]{2,1,0:T(8,128)(2,1)} %get-tuple-element.67.refs_1_.refs_2_, bf16[4,1024,640]{2,1,0:T(8,128)(2,1)} %bitcast.38.refs_2_.g, ...), custom_call_target="tpu_custom_call" | custom-call | flops 4294967296 | bytes 12582912 | tf_op jit(solution)/shard_map/pallas_call | solution.py:177
  401.2 4.6 shard_map.239.refs_1_
  407.1 5.9 shard_map.252
  413.5 10.8 %shard_map.235 = (bf16[512,1024]{1,0:T(8,128)(2,1)}, f32[1,1024]{1,0:T(1,128)}) custom-call(bf16[4,512,512]{2,1,0:T(8,128)(2,1)} %get-tuple-element.60.refs_0_.refs_1_, bf16[4,512,512]{2,1,0:T(8,128)(2,1)} %get-tuple-element.61.refs_1_, bf16[4,1024,512]{2,1,0:T(8,128)(2,1)} %bitcast.47.refs_2_.g, bf16[4,1024,512]{2,1,0:T(8,128)(2,1)} %collective-permute-done.25.refs_3_.g, ...), custom_call_target="tpu_custom_call" | custom-call | flops 4294967296 | bytes 12582912 | tf_op jit(solution)/shard_map/pallas_call | solution.py:177
  426.7 5.8 collective-permute-start.31
  432.5 4.5 shard_map.241.refs_1_
  437.0 17.5 %shard_map.242 = (bf16[4,512,128]{2,1,0:T(8,128)(2,1)}, f32[4,512,256]{2,1,0:T(8,128)}, bf16[4,512,256]{2,1,0:T(8,128)(2,1)}, f32[4,1,128]{2,1,0:T(1,128)}) custom-call(bf16[4,512,128]{2,1,0:T(8,128)(2,1)} %get-tuple-element.57.refs_0_, bf16[4,512,128]{2,1,0:T(8,128)(2,1)} %shard_map.241.refs_1_, f32[4,2,512]{2,1,0:T(2,128)} %get-tuple-element.72.refs_2_, ...), custom_call_target="tpu_custom_call" | custom-call | flops 10737418240 | bytes 10485760 | tf_op jit(solution)/shard_map/pallas_call | solution.py:438
  454.6 17.7 %shard_map.240 = (bf16[4,512,128]{2,1,0:T(8,128)(2,1)}, f32[4,512,256]{2,1,0:T(8,128)}, bf16[4,512,256]{2,1,0:T(8,128)(2,1)}, f32[4,1,128]{2,1,0:T(1,128)}) custom-call(bf16[4,512,128]{2,1,0:T(8,128)(2,1)} %get-tuple-element.53.refs_0_, bf16[4,512,128]{2,1,0:T(8,128)(2,1)} %shard_map.239.refs_1_, f32[4,2,512]{2,1,0:T(2,128)} %get-tuple-element.70.refs_2_, ...), custom_call_target="tpu_custom_call" | custom-call | flops 10737418240 | bytes 10485760 | tf_op jit(solution)/shard_map/pallas_call | solution.py:438
  474.0 7.4 shard_map.248
  488.5 14.0 %shard_map.243 = (bf16[512,1024]{1,0:T(8,128)(2,1)}, f32[2,1024]{1,0:T(2,128)}) custom-call(bf16[4,512,128]{2,1,0:T(8,128)(2,1)} %get-tuple-element.71.refs_0_.refs_1_, bf16[4,512,128]{2,1,0:T(8,128)(2,1)} %get-tuple-element.73.refs_1_, bf16[4,512,128]{2,1,0:T(8,128)(2,1)} %get-tuple-element.164.refs_2_, bf16[4,512,128]{2,1,0:T(8,128)(2,1)} %get-tuple-element.162.refs_3_, ...), custom_call_target="tpu_custom_call" | custom-call | flops 3221225472 | bytes 9437184 | tf_op jit(solution)/shard_map/pallas_call | solution.py:177
  503.5 5.8 shard_map.244
  544.2 5.5 shard_map.249
  568.1 4.4 shard_map.253
  575.2 28.3 %collective-permute-done.48.refs_4_ = bf16[2,1024,384]{2,1,0:T(8,128)(2,1)} collective-permute-done((bf16[2,1024,384]{2,1,0:T(8,128)(2,1)}, bf16[2,1024,384]{2,1,0:T(8,128)(2,1)}, u32[]{:S(2)}, u32[]{:S(2)}) %collective-permute-start.48) | collective-permute-done | bytes 1572896 | tf_op jit(solution)/shard_map/ppermute | solution.py:550
  612.6 9.5 %psum.7 = f32[8,256]{1,0:T(8,128)S(1)} all-reduce(f32[8,256]{1,0:T(8,128)S(1)} %fusion.27), channel_id=1, replica_groups=mesh['dp'=2,'y'=2,'core'=2,'lat'=4,'sub'=1] {'lat','sub'}, use_global_device_ids=true, to_apply=%region_5.6 | all-reduce | flops 2048 | bytes 16384 | tf_op jit(solution)/shard_map/psum | solution.py:879
  624.6 19.1 %collective-permute-done.60.refs_3_ = bf16[2,1024,512]{2,1,0:T(8,128)(2,1)S(1)} collective-permute-done((bf16[2,1024,512]{2,1,0:T(8,128)(2,1)}, bf16[2,1024,512]{2,1,0:T(8,128)(2,1)S(1)}, u32[]{:S(2)}, u32[]{:S(2)}) %collective-permute-start.60) | collective-permute-done | bytes 2097184 | tf_op jit(solution)/shard_map/ppermute | solution.py:550
  656.3 4.8 shard_map.250
  664.5 6.0 collective-permute-done.50
  680.0 9.0 %collective-permute-done.55.refs_6_ = bf16[1,1024,640]{2,1,0:T(8,128)(2,1)S(1)} collective-permute-done((bf16[1,1024,640]{2,1,0:T(8,128)(2,1)}, bf16[1,1024,640]{2,1,0:T(8,128)(2,1)S(1)}, u32[]{:S(2)}, u32[]{:S(2)}) %collective-permute-start.55) | collective-permute-done | bytes 1310752 | tf_op jit(solution)/shard_map/ppermute | solution.py:550
  690.0 4.9 shard_map.251
  698.3 18.7 %collective-permute-done.62 = bf16[512,512]{1,0:T(8,128)(2,1)S(1)} collective-permute-done((bf16[512,512]{1,0:T(8,128)(2,1)}, bf16[512,512]{1,0:T(8,128)(2,1)S(1)}, u32[]{:S(2)}, u32[]{:S(2)}) %collective-permute-start.62) | collective-permute-done | bytes 524320 | tf_op jit(solution)/shard_map/ppermute | solution.py:553
  717.2 12.5 %collective-permute-done.56 = bf16[512,640]{1,0:T(8,128)(2,1)S(1)} collective-permute-done((bf16[512,640]{1,0:T(8,128)(2,1)}, bf16[512,640]{1,0:T(8,128)(2,1)S(1)}, u32[]{:S(2)}, u32[]{:S(2)}) %collective-permute-start.56) | collective-permute-done | bytes 655392 | tf_op jit(solution)/shard_map/ppermute | solution.py:553
  730.0 5.3 collective-permute-done.63
  737.3 5.0 collective-permute-done.57
  745.1 7.0 collective-permute-done.58
  (448 shorter events, 213.4 us)
Async XLA Ops:
  14.9 31.2 %collective-permute-start.17 = (bf16[512,640]{1,0:T(8,128)(2,1)}, bf16[512,640]{1,0:T(8,128)(2,1)}, u32[]{:S(2)}, u32[]{:S(2)}) collective-permute-start(bf16[512,640]{1,0:T(8,128)(2,1)} %pad_maximum_fusion.14), channel_id=1, source_target_pairs={{0,2},{1,3},{2,0},{3,1},{4,6},{5,7},{6,4},{7,5},{8,10},{9,11},{10,... | collective-permute-start | bytes 1966088 | tf_op jit(solution)/shard_map/ppermute | solution.py:553
  17.8 65.4 %collective-permute-start.21 = (bf16[256,512]{1,0:T(8,128)(2,1)S(1)}, bf16[256,512]{1,0:T(8,128)(2,1)}, u32[]{:S(2)}, u32[]{:S(2)}) collective-permute-start(bf16[256,512]{1,0:T(8,128)(2,1)S(1)} %bitcast.211), channel_id=1, source_target_pairs={{0,1},{1,0},{2,3},{3,2},{4,5},{5,4},{6,7},{7,6},{8,9},{9,8},{10,11... | collective-permute-start | bytes 786440 | tf_op jit(solution)/shard_map/ppermute | solution.py:553
  19.9 35.2 %collective-permute-start.9 = (bf16[256,384]{1,0:T(8,128)(2,1)S(1)}, bf16[256,384]{1,0:T(8,128)(2,1)}, u32[]{:S(2)}, u32[]{:S(2)}) collective-permute-start(bf16[256,384]{1,0:T(8,128)(2,1)S(1)} %bitcast.217), channel_id=1, source_target_pairs={{0,1},{1,0},{2,3},{3,2},{4,5},{5,4},{6,7},{7,6},{8,9},{9,8},{10,11... | collective-permute-start | bytes 589832 | tf_op jit(solution)/shard_map/ppermute | solution.py:553
  48.4 29.9 %collective-permute-start.18 = (bf16[1024,640]{1,0:T(8,128)(2,1)S(1)}, bf16[1024,640]{1,0:T(8,128)(2,1)}, u32[]{:S(2)}, u32[]{:S(2)}) collective-permute-start(bf16[1024,640]{1,0:T(8,128)(2,1)S(1)} %get-tuple-element.150), channel_id=1, source_target_pairs={{0,16},{16,0},{1,17},{17,1},{2,18},{18,2},{3,19},{19,3},{4,20},{20... | collective-permute-start | bytes 3932168 | tf_op jit(solution)/shard_map/ppermute | solution.py:550
  53.9 193.8 %collective-permute-start = (bf16[2,512,256]{1,2,0:T(8,128)(2,1)}, bf16[2,512,256]{1,2,0:T(8,128)(2,1)}, u32[]{:S(2)}, u32[]{:S(2)}) collective-permute-start(bf16[2,512,256]{1,2,0:T(8,128)(2,1)} %bitcast.2), channel_id=1, source_target_pairs={{0,4},{4,0},{1,5},{5,1},{2,6},{6,2},{3,7},{7,3},{8,12},{12,8},{9,1... | collective-permute-start | bytes 1572872 | tf_op jit(solution)/shard_map/ppermute | solution.py:550
  56.8 27.5 %collective-permute-start.10 = (bf16[512,384]{1,0:T(8,128)(2,1)}, bf16[512,384]{1,0:T(8,128)(2,1)}, u32[]{:S(2)}, u32[]{:S(2)}) collective-permute-start(bf16[512,384]{1,0:T(8,128)(2,1)} %pad_maximum_fusion.21), channel_id=1, source_target_pairs={{0,2},{1,3},{2,0},{3,1},{4,6},{5,7},{6,4},{7,5},{8,10},{9,11},{10,... | collective-permute-start | bytes 1179656 | tf_op jit(solution)/shard_map/ppermute | solution.py:553
  82.0 102.4 %collective-permute-start.19 = (bf16[2,1024,640]{2,1,0:T(8,128)(2,1)}, bf16[2,1024,640]{2,1,0:T(8,128)(2,1)}, u32[]{:S(2)}, u32[]{:S(2)}) collective-permute-start(bf16[2,1024,640]{2,1,0:T(8,128)(2,1)} %get-tuple-element.144), channel_id=1, source_target_pairs={{0,8},{8,0},{1,9},{9,1},{2,10},{10,2},{3,11},{11,3},{4,12},{12,4},... | collective-permute-start | bytes 7864328 | tf_op jit(solution)/shard_map/ppermute | solution.py:550
  84.2 23.8 %collective-permute-start.22 = (bf16[512,512]{1,0:T(8,128)(2,1)S(1)}, bf16[512,512]{1,0:T(8,128)(2,1)S(1)}, u32[]{:S(2)}, u32[]{:S(2)}) collective-permute-start(bf16[512,512]{1,0:T(8,128)(2,1)S(1)} %pad_maximum_fusion.16), channel_id=1, source_target_pairs={{0,2},{1,3},{2,0},{3,1},{4,6},{5,7},{6,4},{7,5},{8,10},{9,11},{10,... | collective-permute-start | bytes 1572872 | tf_op jit(solution)/shard_map/ppermute | solution.py:553
  85.5 73.4 %collective-permute-start.11 = (bf16[1024,384]{1,0:T(8,128)(2,1)S(1)}, bf16[1024,384]{1,0:T(8,128)(2,1)S(1)}, u32[]{:S(2)}, u32[]{:S(2)}) collective-permute-start(bf16[1024,384]{1,0:T(8,128)(2,1)S(1)} %get-tuple-element.190), channel_id=1, source_target_pairs={{0,8},{8,0},{1,9},{9,1},{2,10},{10,2},{3,11},{11,3},{4,12},{12,4},... | collective-permute-start | bytes 2359304 | tf_op jit(solution)/shard_map/ppermute | solution.py:550
  110.3 69.2 %collective-permute-start.23 = (bf16[1024,512]{1,0:T(8,128)(2,1)}, bf16[1024,512]{1,0:T(8,128)(2,1)}, u32[]{:S(2)}, u32[]{:S(2)}) collective-permute-start(bf16[1024,512]{1,0:T(8,128)(2,1)} %get-tuple-element.182), channel_id=1, source_target_pairs={{0,8},{8,0},{1,9},{9,1},{2,10},{10,2},{3,11},{11,3},{4,12},{12,4},... | collective-permute-start | bytes 3145736 | tf_op jit(solution)/shard_map/ppermute | solution.py:550
  160.8 37.6 %collective-permute-start.12 = (bf16[2,1024,384]{2,1,0:T(8,128)(2,1)}, bf16[2,1024,384]{2,1,0:T(8,128)(2,1)}, u32[]{:S(2)}, u32[]{:S(2)}) collective-permute-start(bf16[2,1024,384]{2,1,0:T(8,128)(2,1)} %get-tuple-element.148), channel_id=1, source_target_pairs={{0,16},{16,0},{1,17},{17,1},{2,18},{18,2},{3,19},{19,3},{4,20},{20... | collective-permute-start | bytes 4718600 | tf_op jit(solution)/shard_map/ppermute | solution.py:550
  162.0 17.5 %collective-permute-start.5 = (f32[6,1536]{1,0:T(8,128)S(1)}, f32[6,1536]{1,0:T(8,128)S(1)}, u32[]{:S(2)}, u32[]{:S(2)}) collective-permute-start(f32[6,1536]{1,0:T(8,128)S(1)} %pad_maximum_fusion.31), channel_id=1, source_target_pairs={{0,8},{8,0},{1,9},{9,1},{2,10},{10,2},{3,11},{11,3},{4,12},{12,4},... | collective-permute-start | bytes 110600 | tf_op jit(solution)/shard_map/ppermute | solution.py:550
  183.3 53.4 %collective-permute-start.24 = (bf16[2,1024,512]{2,1,0:T(8,128)(2,1)}, bf16[2,1024,512]{2,1,0:T(8,128)(2,1)}, u32[]{:S(2)}, u32[]{:S(2)}) collective-permute-start(bf16[2,1024,512]{2,1,0:T(8,128)(2,1)} %get-tuple-element.146), channel_id=1, source_target_pairs={{0,16},{16,0},{1,17},{17,1},{2,18},{18,2},{3,19},{19,3},{4,20},{20... | collective-permute-start | bytes 6291464 | tf_op jit(solution)/shard_map/ppermute | solution.py:550
  189.4 154.4 %collective-permute-start.20 = (bf16[4,1024,640]{2,1,0:T(8,128)(2,1)}, bf16[4,1024,640]{2,1,0:T(8,128)(2,1)}, u32[]{:S(2)}, u32[]{:S(2)}) collective-permute-start(bf16[4,1024,640]{2,1,0:T(8,128)(2,1)} %bitcast.38.refs_2_.g), channel_id=1, source_target_pairs={{0,4},{4,0},{1,5},{5,1},{2,6},{6,2},{3,7},{7,3},{8,12},{12,8},{9,1... | collective-permute-start | bytes 15728648 | tf_op jit(solution)/shard_map/ppermute | solution.py:550
  200.2 92.0 %collective-permute-start.13 = (bf16[4,1024,384]{2,1,0:T(8,128)(2,1)S(1)}, bf16[4,1024,384]{2,1,0:T(8,128)(2,1)}, u32[]{:S(2)}, u32[]{:S(2)}) collective-permute-start(bf16[4,1024,384]{2,1,0:T(8,128)(2,1)S(1)} %bitcast.186), channel_id=1, source_target_pairs={{0,4},{4,0},{1,5},{5,1},{2,6},{6,2},{3,7},{7,3},{8,12},{12,8},{9,1... | collective-permute-start | bytes 9437192 | tf_op jit(solution)/shard_map/ppermute | solution.py:550
  204.2 48.4 %collective-permute-start.26 = (bf16[2,512,256]{1,2,0:T(8,128)(2,1)}, bf16[2,512,256]{1,2,0:T(8,128)(2,1)S(1)}, u32[]{:S(2)}, u32[]{:S(2)}) collective-permute-start(bf16[2,512,256]{1,2,0:T(8,128)(2,1)} %bitcast.234), channel_id=1, source_target_pairs={{0,4},{4,0},{1,5},{5,1},{2,6},{6,2},{3,7},{7,3},{8,12},{12,8},{9,1... | collective-permute-start | bytes 1572872 | tf_op jit(solution)/shard_map/ppermute | solution.py:550
  247.7 130.8 %collective-permute-start.25 = (bf16[4,1024,512]{2,1,0:T(8,128)(2,1)}, bf16[4,1024,512]{2,1,0:T(8,128)(2,1)}, u32[]{:S(2)}, u32[]{:S(2)}) collective-permute-start(bf16[4,1024,512]{2,1,0:T(8,128)(2,1)} %bitcast.47.refs_2_.g), channel_id=1, source_target_pairs={{0,4},{4,0},{1,5},{5,1},{2,6},{6,2},{3,7},{7,3},{8,12},{12,8},{9,1... | collective-permute-start | bytes 12582920 | tf_op jit(solution)/shard_map/ppermute | solution.py:550
  249.4 13.8 %collective-permute-start.1 = (bf16[512,256]{0,1:T(8,128)(2,1)S(1)}, bf16[512,256]{0,1:T(8,128)(2,1)S(1)}, u32[]{:S(2)}, u32[]{:S(2)}) collective-permute-start(bf16[512,256]{0,1:T(8,128)(2,1)S(1)} %get-tuple-element.184), channel_id=1, source_target_pairs={{0,1},{1,0},{2,3},{3,2},{4,5},{5,4},{6,7},{7,6},{8,9},{9,8},{10,11... | collective-permute-start | bytes 786440 | tf_op jit(solution)/shard_map/ppermute | solution.py:553
  252.6 13.4 %collective-permute-start.2 = (bf16[512,256]{0,1:T(8,128)(2,1)S(1)}, bf16[512,256]{0,1:T(8,128)(2,1)S(1)}, u32[]{:S(2)}, u32[]{:S(2)}) collective-permute-start(bf16[512,256]{0,1:T(8,128)(2,1)S(1)} %get-tuple-element.185), channel_id=1, source_target_pairs={{0,2},{1,3},{2,0},{3,1},{4,6},{5,7},{6,4},{7,5},{8,10},{9,11},{10,... | collective-permute-start | bytes 786440 | tf_op jit(solution)/shard_map/ppermute | solution.py:553
  266.0 19.8 %collective-permute-start.27 = (bf16[512,256]{0,1:T(8,128)(2,1)}, bf16[512,256]{0,1:T(8,128)(2,1)}, u32[]{:S(2)}, u32[]{:S(2)}) collective-permute-start(bf16[512,256]{0,1:T(8,128)(2,1)} %get-tuple-element.176), channel_id=1, source_target_pairs={{0,1},{1,0},{2,3},{3,2},{4,5},{5,4},{6,7},{7,6},{8,9},{9,8},{10,11... | collective-permute-start | bytes 786440 | tf_op jit(solution)/shard_map/ppermute | solution.py:553
  284.6 34.2 %collective-permute-start.15 = (bf16[4,512,256]{2,1,0:T(8,128)(2,1)}, bf16[4,512,256]{2,1,0:T(8,128)(2,1)}, u32[]{:S(2)}, u32[]{:S(2)}) collective-permute-start(bf16[4,512,256]{2,1,0:T(8,128)(2,1)} %get-tuple-element.54.refs_1_.refs_3_), channel_id=1, source_target_pairs={{0,4},{4,0},{1,5},{5,1},{2,6},{6,2},{3,7},{7,3},{8,12},{12,8},{9,1... | collective-permute-start | bytes 3145736 | tf_op jit(solution)/shard_map/ppermute | solution.py:550
  285.8 25.1 %collective-permute-start.28 = (bf16[512,256]{0,1:T(8,128)(2,1)}, bf16[512,256]{0,1:T(8,128)(2,1)}, u32[]{:S(2)}, u32[]{:S(2)}) collective-permute-start(bf16[512,256]{0,1:T(8,128)(2,1)} %get-tuple-element.177), channel_id=1, source_target_pairs={{0,2},{1,3},{2,0},{3,1},{4,6},{5,7},{6,4},{7,5},{8,10},{9,11},{10,... | collective-permute-start | bytes 786440 | tf_op jit(solution)/shard_map/ppermute | solution.py:553
  292.2 18.7 %collective-permute-start.29 = (bf16[512,256]{0,1:T(8,128)(2,1)}, bf16[512,256]{0,1:T(8,128)(2,1)S(1)}, u32[]{:S(2)}, u32[]{:S(2)}) collective-permute-start(bf16[512,256]{0,1:T(8,128)(2,1)} %get-tuple-element.178), channel_id=1, source_target_pairs={{0,3},{1,2},{2,1},{3,0},{4,7},{5,6},{6,5},{7,4},{8,11},{9,10},{10,... | collective-permute-start | bytes 786440 | tf_op jit(solution)/shard_map/ppermute | solution.py:553
  310.9 20.0 %collective-permute-start.14 = (bf16[4,512,256]{2,1,0:T(8,128)(2,1)}, bf16[4,512,256]{2,1,0:T(8,128)(2,1)S(1)}, u32[]{:S(2)}, u32[]{:S(2)}) collective-permute-start(bf16[4,512,256]{2,1,0:T(8,128)(2,1)} %get-tuple-element.55.refs_1_.refs_3_), channel_id=1, source_target_pairs={{0,4},{4,0},{1,5},{5,1},{2,6},{6,2},{3,7},{7,3},{8,12},{12,8},{9,1... | collective-permute-start | bytes 3145736 | tf_op jit(solution)/shard_map/ppermute | solution.py:550
  413.0 155.1 %collective-permute-start.59 = (bf16[4,1024,512]{2,1,0:T(8,128)(2,1)}, bf16[4,1024,512]{2,1,0:T(8,128)(2,1)}, u32[]{:S(2)}, u32[]{:S(2)}) collective-permute-start(bf16[4,1024,512]{2,1,0:T(8,128)(2,1)} %shard_map.252), channel_id=1, source_target_pairs={{0,4},{4,0},{1,5},{5,1},{2,6},{6,2},{3,7},{7,3},{8,12},{12,8},{9,1... | collective-permute-start | bytes 12582920 | tf_op jit(solution)/shard_map/ppermute | solution.py:550
  425.6 46.7 %collective-permute-start.32 = (bf16[512,256]{1,0:T(8,128)(2,1)S(1)}, bf16[512,256]{1,0:T(8,128)(2,1)S(1)}, u32[]{:S(2)}, u32[]{:S(2)}) collective-permute-start(bf16[512,256]{1,0:T(8,128)(2,1)S(1)} %get-tuple-element.172), channel_id=1, source_target_pairs={{0,3},{1,2},{2,1},{3,0},{4,7},{5,6},{6,5},{7,4},{8,11},{9,10},{10,... | collective-permute-start | bytes 786440 | tf_op jit(solution)/shard_map/ppermute | solution.py:553
  426.7 46.2 %collective-permute-start.31 = (bf16[512,256]{1,0:T(8,128)(2,1)S(1)}, bf16[512,256]{1,0:T(8,128)(2,1)S(1)}, u32[]{:S(2)}, u32[]{:S(2)}) collective-permute-start(bf16[512,256]{1,0:T(8,128)(2,1)S(1)} %get-tuple-element.173), channel_id=1, source_target_pairs={{0,2},{1,3},{2,0},{3,1},{4,6},{5,7},{6,4},{7,5},{8,10},{9,11},{10,... | collective-permute-start | bytes 786440 | tf_op jit(solution)/shard_map/ppermute | solution.py:553
  432.5 40.3 %collective-permute-start.30 = (bf16[512,256]{1,0:T(8,128)(2,1)S(1)}, bf16[512,256]{1,0:T(8,128)(2,1)S(1)}, u32[]{:S(2)}, u32[]{:S(2)}) collective-permute-start(bf16[512,256]{1,0:T(8,128)(2,1)S(1)} %get-tuple-element.174), channel_id=1, source_target_pairs={{0,1},{1,0},{2,3},{3,2},{4,5},{5,4},{6,7},{7,6},{8,9},{9,8},{10,11... | collective-permute-start | bytes 786440 | tf_op jit(solution)/shard_map/ppermute | solution.py:553
  454.5 28.8 %collective-permute-start.34 = (bf16[4,512,256]{2,1,0:T(8,128)(2,1)}, bf16[4,512,256]{2,1,0:T(8,128)(2,1)S(1)}, u32[]{:S(2)}, u32[]{:S(2)}) collective-permute-start(bf16[4,512,256]{2,1,0:T(8,128)(2,1)} %get-tuple-element.75), channel_id=1, source_target_pairs={{0,4},{4,0},{1,5},{5,1},{2,6},{6,2},{3,7},{7,3},{8,12},{12,8},{9,1... | collective-permute-start | bytes 3145736 | tf_op jit(solution)/shard_map/ppermute | solution.py:550
  472.3 13.4 %collective-permute-start.35 = (bf16[4,512,256]{2,1,0:T(8,128)(2,1)}, bf16[4,512,256]{2,1,0:T(8,128)(2,1)S(1)}, u32[]{:S(2)}, u32[]{:S(2)}) collective-permute-start(bf16[4,512,256]{2,1,0:T(8,128)(2,1)} %get-tuple-element.77), channel_id=1, source_target_pairs={{0,4},{4,0},{1,5},{5,1},{2,6},{6,2},{3,7},{7,3},{8,12},{12,8},{9,1... | collective-permute-start | bytes 3145736 | tf_op jit(solution)/shard_map/ppermute | solution.py:550
  481.5 61.6 %collective-permute-start.53 = (bf16[4,1024,640]{2,1,0:T(8,128)(2,1)}, bf16[4,1024,640]{2,1,0:T(8,128)(2,1)}, u32[]{:S(2)}, u32[]{:S(2)}) collective-permute-start(bf16[4,1024,640]{2,1,0:T(8,128)(2,1)} %shard_map.248), channel_id=1, source_target_pairs={{0,4},{4,0},{1,5},{5,1},{2,6},{6,2},{3,7},{7,3},{8,12},{12,8},{9,1... | collective-permute-start | bytes 15728648 | tf_op jit(solution)/shard_map/ppermute | solution.py:550
  509.3 50.4 %collective-permute-start.47 = (bf16[4,1024,384]{2,1,0:T(8,128)(2,1)}, bf16[4,1024,384]{2,1,0:T(8,128)(2,1)S(1)}, u32[]{:S(2)}, u32[]{:S(2)}) collective-permute-start(bf16[4,1024,384]{2,1,0:T(8,128)(2,1)} %shard_map.244), channel_id=1, source_target_pairs={{0,4},{4,0},{1,5},{5,1},{2,6},{6,2},{3,7},{7,3},{8,12},{12,8},{9,1... | collective-permute-start | bytes 9437192 | tf_op jit(solution)/shard_map/ppermute | solution.py:550
  520.7 87.8 %collective-permute-start.38 = (bf16[512,256]{1,0:T(8,128)(2,1)}, bf16[512,256]{1,0:T(8,128)(2,1)}, u32[]{:S(2)}, u32[]{:S(2)}) collective-permute-start(bf16[512,256]{1,0:T(8,128)(2,1)} %get-tuple-element.158), channel_id=1, source_target_pairs={{0,3},{1,2},{2,1},{3,0},{4,7},{5,6},{6,5},{7,4},{8,11},{9,10},{10,... | collective-permute-start | bytes 786440 | tf_op jit(solution)/shard_map/ppermute | solution.py:553
  550.2 106.1 %collective-permute-start.54 = (bf16[2,1024,640]{2,1,0:T(8,128)(2,1)}, bf16[2,1024,640]{2,1,0:T(8,128)(2,1)}, u32[]{:S(2)}, u32[]{:S(2)}) collective-permute-start(bf16[2,1024,640]{2,1,0:T(8,128)(2,1)} %shard_map.249), channel_id=1, source_target_pairs={{0,8},{8,0},{1,9},{9,1},{2,10},{10,2},{3,11},{11,3},{4,12},{12,4},... | collective-permute-start | bytes 7864328 | tf_op jit(solution)/shard_map/ppermute | solution.py:550
  553.6 69.1 %collective-permute-start.37 = (bf16[512,256]{1,0:T(8,128)(2,1)}, bf16[512,256]{1,0:T(8,128)(2,1)}, u32[]{:S(2)}, u32[]{:S(2)}) collective-permute-start(bf16[512,256]{1,0:T(8,128)(2,1)} %get-tuple-element.159), channel_id=1, source_target_pairs={{0,2},{1,3},{2,0},{3,1},{4,6},{5,7},{6,4},{7,5},{8,10},{9,11},{10,... | collective-permute-start | bytes 786440 | tf_op jit(solution)/shard_map/ppermute | solution.py:553
  565.8 37.7 %collective-permute-start.48 = (bf16[2,1024,384]{2,1,0:T(8,128)(2,1)}, bf16[2,1024,384]{2,1,0:T(8,128)(2,1)}, u32[]{:S(2)}, u32[]{:S(2)}) collective-permute-start(bf16[2,1024,384]{2,1,0:T(8,128)(2,1)} %shard_map.245), channel_id=1, source_target_pairs={{0,16},{16,0},{1,17},{17,1},{2,18},{18,2},{3,19},{19,3},{4,20},{20... | collective-permute-start | bytes 4718600 | tf_op jit(solution)/shard_map/ppermute | solution.py:550
  572.4 71.3 %collective-permute-start.60 = (bf16[2,1024,512]{2,1,0:T(8,128)(2,1)}, bf16[2,1024,512]{2,1,0:T(8,128)(2,1)S(1)}, u32[]{:S(2)}, u32[]{:S(2)}) collective-permute-start(bf16[2,1024,512]{2,1,0:T(8,128)(2,1)} %shard_map.253), channel_id=1, source_target_pairs={{0,16},{16,0},{1,17},{17,1},{2,18},{18,2},{3,19},{19,3},{4,20},{20... | collective-permute-start | bytes 6291464 | tf_op jit(solution)/shard_map/ppermute | solution.py:550
  607.0 43.3 %collective-permute-start.49 = (bf16[1,1024,384]{2,1,0:T(8,128)(2,1)}, bf16[1,1024,384]{2,1,0:T(8,128)(2,1)S(1)}, u32[]{:S(2)}, u32[]{:S(2)}) collective-permute-start(bf16[1,1024,384]{2,1,0:T(8,128)(2,1)} %shard_map.246), channel_id=1, source_target_pairs={{0,8},{8,0},{1,9},{9,1},{2,10},{10,2},{3,11},{11,3},{4,12},{12,4},... | collective-permute-start | bytes 2359304 | tf_op jit(solution)/shard_map/ppermute | solution.py:550
  608.5 14.9 %collective-permute-start.36 = (bf16[512,256]{1,0:T(8,128)(2,1)S(1)}, bf16[512,256]{1,0:T(8,128)(2,1)}, u32[]{:S(2)}, u32[]{:S(2)}) collective-permute-start(bf16[512,256]{1,0:T(8,128)(2,1)S(1)} %copy-done.25), channel_id=1, source_target_pairs={{0,1},{1,0},{2,3},{3,2},{4,5},{5,4},{6,7},{7,6},{8,9},{9,8},{10,11... | collective-permute-start | bytes 786440 | tf_op jit(solution)/shard_map/ppermute | solution.py:553
  622.8 39.7 %collective-permute-start.46 = (bf16[8,256]{1,0:T(8,128)(2,1)S(1)}, bf16[8,256]{1,0:T(8,128)(2,1)S(1)}, u32[]{:S(2)}, u32[]{:S(2)}) collective-permute-start(bf16[8,256]{1,0:T(8,128)(2,1)S(1)} %get-tuple-element.244), channel_id=1, source_target_pairs={{0,16},{16,0},{1,17},{17,1},{2,18},{18,2},{3,19},{19,3},{4,20},{20... | collective-permute-start | bytes 12296 | tf_op jit(solution)/shard_map/ppermute | solution.py:550
  648.8 24.2 %collective-permute-start.61 = (bf16[1,1024,512]{2,1,0:T(8,128)(2,1)}, bf16[1,1024,512]{2,1,0:T(8,128)(2,1)}, u32[]{:S(2)}, u32[]{:S(2)}) collective-permute-start(bf16[1,1024,512]{2,1,0:T(8,128)(2,1)} %shard_map.254), channel_id=1, source_target_pairs={{0,8},{8,0},{1,9},{9,1},{2,10},{10,2},{3,11},{11,3},{4,12},{12,4},... | collective-permute-start | bytes 3145736 | tf_op jit(solution)/shard_map/ppermute | solution.py:550
  654.8 15.7 %collective-permute-start.50 = (bf16[512,384]{1,0:T(8,128)(2,1)}, bf16[512,384]{1,0:T(8,128)(2,1)}, u32[]{:S(2)}, u32[]{:S(2)}) collective-permute-start(bf16[512,384]{1,0:T(8,128)(2,1)} %get-tuple-element.88), channel_id=1, source_target_pairs={{0,2},{1,3},{2,0},{3,1},{4,6},{5,7},{6,4},{7,5},{8,10},{9,11},{10,... | collective-permute-start | bytes 1179656 | tf_op jit(solution)/shard_map/ppermute | solution.py:553
  661.0 28.0 %collective-permute-start.55 = (bf16[1,1024,640]{2,1,0:T(8,128)(2,1)}, bf16[1,1024,640]{2,1,0:T(8,128)(2,1)S(1)}, u32[]{:S(2)}, u32[]{:S(2)}) collective-permute-start(bf16[1,1024,640]{2,1,0:T(8,128)(2,1)} %shard_map.250), channel_id=1, source_target_pairs={{0,16},{16,0},{1,17},{17,1},{2,18},{18,2},{3,19},{19,3},{4,20},{20... | collective-permute-start | bytes 3932168 | tf_op jit(solution)/shard_map/ppermute | solution.py:550
  677.0 39.9 %collective-permute-start.62 = (bf16[512,512]{1,0:T(8,128)(2,1)}, bf16[512,512]{1,0:T(8,128)(2,1)S(1)}, u32[]{:S(2)}, u32[]{:S(2)}) collective-permute-start(bf16[512,512]{1,0:T(8,128)(2,1)} %get-tuple-element.92), channel_id=1, source_target_pairs={{0,2},{1,3},{2,0},{3,1},{4,6},{5,7},{6,4},{7,5},{8,10},{9,11},{10,... | collective-permute-start | bytes 1572872 | tf_op jit(solution)/shard_map/ppermute | solution.py:553
  679.4 18.6 %collective-permute-start.52 = (bf16[256,384]{1,0:T(8,128)(2,1)S(1)}, bf16[256,384]{1,0:T(8,128)(2,1)S(1)}, u32[]{:S(2)}, u32[]{:S(2)}) collective-permute-start(bf16[256,384]{1,0:T(8,128)(2,1)S(1)} %fusion.7), channel_id=1, source_target_pairs={{0,16},{16,0},{1,17},{17,1},{2,18},{18,2},{3,19},{19,3},{4,20},{20... | collective-permute-start | bytes 589832 | tf_op jit(solution)/shard_map/ppermute | solution.py:550
  695.0 34.8 %collective-permute-start.56 = (bf16[512,640]{1,0:T(8,128)(2,1)}, bf16[512,640]{1,0:T(8,128)(2,1)S(1)}, u32[]{:S(2)}, u32[]{:S(2)}) collective-permute-start(bf16[512,640]{1,0:T(8,128)(2,1)} %get-tuple-element.90), channel_id=1, source_target_pairs={{0,2},{1,3},{2,0},{3,1},{4,6},{5,7},{6,4},{7,5},{8,10},{9,11},{10,... | collective-permute-start | bytes 1966088 | tf_op jit(solution)/shard_map/ppermute | solution.py:553
  717.1 18.2 %collective-permute-start.63 = (bf16[256,512]{1,0:T(8,128)(2,1)S(1)}, bf16[256,512]{1,0:T(8,128)(2,1)S(1)}, u32[]{:S(2)}, u32[]{:S(2)}) collective-permute-start(bf16[256,512]{1,0:T(8,128)(2,1)S(1)} %slice.430), channel_id=1, source_target_pairs={{0,1},{1,0},{2,3},{3,2},{4,5},{5,4},{6,7},{7,6},{8,9},{9,8},{10,11... | collective-permute-start | bytes 786440 | tf_op jit(solution)/shard_map/ppermute | solution.py:553
  729.9 12.4 %collective-permute-start.57 = (bf16[256,640]{1,0:T(8,128)(2,1)S(1)}, bf16[256,640]{1,0:T(8,128)(2,1)S(1)}, u32[]{:S(2)}, u32[]{:S(2)}) collective-permute-start(bf16[256,640]{1,0:T(8,128)(2,1)S(1)} %slice.429), channel_id=1, source_target_pairs={{0,1},{1,0},{2,3},{3,2},{4,5},{5,4},{6,7},{7,6},{8,9},{9,8},{10,11... | collective-permute-start | bytes 983048 | tf_op jit(solution)/shard_map/ppermute | solution.py:553
  (77 other events, 859.2 us)

commit v2 on v1

v2 whole, which is shorter than its diff:
```python
import functools
import math

import jax
import jax.numpy as jnp
from jax import lax
from jax.experimental import pallas as pl
from jax.experimental.layout import Layout, with_layout_constraint
from jax.experimental.pallas import tpu as pltpu
from jax.sharding import Mesh
from jax.sharding import PartitionSpec as P

HEAD_DIM = 64
LENGTH = 1024
EPS = 1e-06
LANES = 128
SCALE = HEAD_DIM ** (-0.5)
SCALE_LOG2 = SCALE * math.log2(math.e)
ROWS = ("y", "core")
COLS = ("lat", "sub")
NT = (((1,), (1,)), ((), ()))
F32 = jnp.float32
BF16 = jnp.bfloat16
VMEM_LIMIT = 56 * 1024 * 1024
LAST = []


def dot(left, right):
    return jnp.dot(left, right, preferred_element_type=F32)


def dot_nt(left, right):
    return lax.dot_general(left, right, NT, preferred_element_type=F32)


def gelu_tanh(values):
    return (
        0.5
        * values
        * (1.0 + jnp.tanh(0.7978845608028654 * (values + 0.044715 * values * values * values)))
    )


def gelu_slope(values):
    inner = jnp.tanh(0.7978845608028654 * (values + 0.044715 * values * values * values))
    rate = 0.7978845608028654 * (1.0 + 3 * 0.044715 * values * values)
    return 0.5 * (1.0 + inner) + 0.5 * values * (1.0 - inner * inner) * rate


def whole(shape):
    return pl.BlockSpec(shape, lambda *_: (0,) * len(shape))


def fixed(shape):
    return pl.BlockSpec(
        shape, lambda *_: (0,) * len(shape), pipeline_mode=pl.Buffered(1)
    )


def block(shape, column=0, first=0, step=1):
    return pl.BlockSpec((None, *shape), lambda b, *_: (first + step * b, 0, column))


def tabled(shape, place, start=0):
    row, column = place

    def index(b, table):
        return table[row, b], 0, start if column is None else start + table[column, b]

    return pl.BlockSpec((None, *shape), index)


def call(name, kernel, grid, in_specs, out_specs, out_shape, scratch=(), table=None):
    run = pl.pallas_call(
        kernel,
        grid_spec=pltpu.PrefetchScalarGridSpec(
            num_scalar_prefetch=0 if table is None else 1,
            grid=grid,
            in_specs=in_specs,
            out_specs=out_specs,
            scratch_shapes=list(scratch),
        ),
        out_shape=out_shape,
        compiler_params=pltpu.CompilerParams(vmem_limit_bytes=VMEM_LIMIT),
        cost_estimate=pl.CostEstimate(flops=0, bytes_accessed=0, transcendentals=0),
        name=name,
    )

    def ordered(first, *others):
        first = after(first, *LAST)
        found = run(first, *others) if table is None else run(table, first, *others)
        LAST[:] = jax.tree.leaves(found)[:1]
        return found

    return ordered


def after(value, *others):
    return lax.optimization_barrier((value, *others))[0]


def shaped(shape, dtype):
    return jax.ShapeDtypeStruct(shape, dtype)


def project(left, query_blocks, kv_blocks, bias):
    number, features, _ = query_blocks.shape
    rows = left.shape[0]

    def kernel(a, g, h, c, query, kv):
        query[...] = (dot(a[...], g[...]) + c[:, :LANES]).astype(BF16)
        kv[:, :LANES] = dot(a[...], h[:, :LANES]).astype(BF16)
        kv[:, LANES:] = (dot(a[...], h[:, LANES:]) + c[:, LANES : 2 * LANES]).astype(BF16)

    return call(
        "project",
        kernel,
        (number,),
        [
            fixed(left.shape),
            block((features, LANES)),
            block((features, 2 * LANES)),
            block((1, bias.shape[-1])),
        ],
        [block((rows, LANES)), block((rows, 2 * LANES))],
        [shaped((number, rows, LANES), BF16), shaped((number, rows, 2 * LANES), BF16)],
    )(left, query_blocks, kv_blocks, bias)


def feed_forward(left, late, bias, parts, extras):
    number, _, width = bias.shape
    rows, features = left.shape

    def late_block(start):
        return pl.BlockSpec(
            (None, features, width), lambda b: (b // parts, 0, start + b % parts)
        )

    def kernel(a, g, h, c, middle, cotangent, vectors, expanded, hidden, output, sums, total):
        out = dot(a[...], g[...]) + c[...]
        expanded[...] = out
        low = gelu_tanh(out).astype(BF16)
        hidden[...] = low
        out = dot_nt(low, h[...])

        @pl.when(pl.program_id(0) == 0)
        def _():
            total[...] = out

        @pl.when(pl.program_id(0) > 0)
        def _():
            total[...] += out

        @pl.when(pl.program_id(0) == number - 1)
        def _():
            finish_output(total, (middle, cotangent, vectors), (output, sums))

    return call(
        "feed_forward",
        kernel,
        (number,),
        [fixed(left.shape), late_block(0), late_block(parts), block((1, width))]
        + [fixed(extra.shape) for extra in extras],
        [
            block((rows, width)),
            block((rows, width)),
            whole((rows, features)),
            whole((1, features)),
        ],
        [
            shaped((number, rows, width), F32),
            shaped((number, rows, width), BF16),
            shaped((rows, features), BF16),
            shaped((1, features), F32),
        ],
        scratch=[pltpu.VMEM((rows, features), F32)],
    )(left, late, late, bias, *extras)


def feed_back(name, low, turned, late, expanded, hidden, table, parts, extras, before, apart):
    _, rows, width = expanded.shape
    features = low.shape[1]
    number = table.shape[1]
    count = number // 2 if apart else 1
    more = [] if before is None else [before]

    def kernel(table_ref, *refs):
        low, turned_low, turned_in, shrink, grow, before_act, after_act = refs[:7]
        refs = list(refs[7:])
        start = [refs.pop(0) for _ in more]
        given = [refs.pop(0) for _ in extras]
        shrink_outs = [refs.pop(0) for _ in range(count)]
        expand_outs = [refs.pop(0) for _ in range(count)]
        sums = refs.pop(0)
        results, total = (refs[:-1], refs[-1]) if extras else (None, refs[0])
        step = pl.program_id(0)
        back = dot(low[...], shrink[...]) * gelu_slope(before_act[...])
        back = back.astype(BF16)
        sums[...] = jnp.sum(back.astype(F32), axis=0, keepdims=True)
        found = dot(turned_low[...], after_act[...]).astype(BF16)
        grown = dot(turned_in[...], back).astype(BF16)
        if apart:
            for index in range(count):

                @pl.when(step // 2 == index)
                def _():
                    shrink_outs[index][...] = found
                    expand_outs[index][...] = grown

        else:
            shrink_outs[0][...] = found
            expand_outs[0][...] = grown
        out = dot_nt(back, grow[...])

        @pl.when(step == 0)
        def _():
            total[...] = out + start[0][...] if start else out

        @pl.when(step > 0)
        def _():
            total[...] += out

        if extras:

            @pl.when(step == number - 1)
            def _():
                finish_middle_back(total, given, results)

    weight = (features, width)
    ends = [shaped((number, 1, width), F32)]
    end_specs = [block((1, width))]
    if extras:
        ends += [
            shaped((rows, features), F32),
            shaped((rows, features), BF16),
            shaped((features, rows), BF16),
            shaped((4, features), F32),
        ]
    else:
        ends += [shaped((rows, features), F32)]
    end_specs += [whole(one.shape) for one in ends[1:]]
    if apart:
        outs = [shaped((2, *weight), BF16)] * number
        out_specs = [
            pl.BlockSpec(
                (None, *weight), lambda b, _, at=at: (jnp.clip(b - 2 * at, 0, 1), 0, 0)
            )
            for at in range(count)
        ] * 2
    else:
        outs, out_specs = [shaped((number, *weight), BF16)] * 2, [block(weight)] * 2
    got = call(
        name,
        kernel,
        (number,),
        [
            fixed(low.shape),
            *[fixed(one.shape) for one in turned],
            tabled(weight, (1, 2), parts),
            tabled(weight, (1, 2), 0),
            tabled((rows, width), (0, None)),
            tabled((rows, width), (0, None)),
        ]
        + [fixed(one.shape) for one in (*more, *extras)],
        out_specs + end_specs,
        outs + ends,
        scratch=[pltpu.VMEM((rows, features), F32)] if extras else (),
        table=table,
    )(low, *turned, late, late, expanded, hidden, *more, *extras)
    return got[:count], got[count : 2 * count], got[2 * count :]


def add_up(name, blocks, upper=None):
    _, features, width = blocks[0][0][0].shape
    tile = min(features if upper is None else features // 2, 512)
    terms = [one for block_terms in blocks for one in block_terms]
    count = len(blocks)

    def kernel(*refs):
        if upper is not None:
            refs = refs[1:]
        given = list(refs[: len(terms)]) if upper is None else list(refs[: 2 * len(terms)])
        outs = refs[len(given) :]

        def total(number):
            return sum(given.pop(0)[...].astype(F32) for _ in range(number)).astype(BF16)

        if upper is None:
            for index, one in enumerate(blocks):
                outs[0][index] = total(len(one))
        else:
            for out in outs:
                out[...] = total(len(terms))

    def spec(index, side=None):
        if side is None:
            return pl.BlockSpec((None, tile, width), lambda i: (index, i, 0))
        half = features // 2 // tile
        if side == 0:
            return pl.BlockSpec((None, tile, width), lambda i, t: (index, t[0] * half + i, 0))
        return pl.BlockSpec((None, tile, width), lambda i, t: (index, (1 - t[0]) * half + i, 0))

    arrays = [array for array, _ in terms]
    if upper is None:
        return call(
            name,
            kernel,
            (features // tile,),
            [spec(index) for _, index in terms],
            pl.BlockSpec((count, tile, width), lambda i: (0, i, 0)),
            shaped((count, features, width), BF16),
        )(*arrays)
    return call(
        name,
        kernel,
        (features // 2 // tile,),
        [spec(index, 0) for _, index in terms] + [spec(index, 1) for _, index in terms],
        [pl.BlockSpec((tile, width), lambda i, _: (i, 0))] * 2,
        [shaped((features // 2, width), BF16)] * 2,
        table=jnp.full((1,), upper, jnp.int32),
    )(*arrays, *arrays)


def attended_backward(left, late, table, start):
    number = table.shape[1]
    rows, features = left.shape

    def kernel(_, a, g, out):
        out[...] = dot(a[...], g[...]).astype(BF16)

    return call(
        "attended_back",
        kernel,
        (number,),
        [fixed(left.shape), tabled((features, LANES), (0, 1), start)],
        block((rows, LANES)),
        shaped((number, rows, LANES), BF16),
        table=table,
    )(left, late)


def contract(name, terms, extras, finish, outs, table=None):
    number, rows, _ = terms[0][0].shape
    features = terms[0][1].shape[1]
    count, more = len(terms), len(extras)

    def kernel(*refs):
        refs = refs if table is None else refs[1:]
        lefts, rights = refs[:count], refs[count : 2 * count]
        given = refs[2 * count : 2 * count + more]
        results, total = refs[2 * count + more : -1], refs[-1]
        out = dot_nt(lefts[0][...], rights[0][...])
        for left, right in zip(lefts[1:], rights[1:]):
            out = out + dot_nt(left[...], right[...])
        step = pl.program_id(0)

        @pl.when(step == 0)
        def _():
            total[...] = out

        @pl.when(step > 0)
        def _():
            total[...] += out

        @pl.when(step == number - 1)
        def _():
            finish(total, given, results)

    return call(
        name,
        kernel,
        (number,),
        [block(left.shape[1:]) for left, _, _ in terms]
        + [where(features, left.shape[2]) for left, _, where in terms]
        + [fixed(extra.shape) for extra in extras],
        [whole(out.shape) for out in outs],
        outs,
        scratch=[pltpu.VMEM((rows, features), F32)],
        table=table,
    )(*[left for left, _, _ in terms], *[right for _, right, _ in terms], *extras)


def by_rows(rows, sums, features, work, tile=64):
    tile = min(rows, tile)

    def step(i, totals):
        found = work(pl.ds(pl.multiple_of(i * tile, tile), tile))
        return tuple(
            total + jnp.sum(one.reshape(-1, 8, features), axis=0)
            for total, one in zip(totals, found)
        )

    zero = jnp.zeros((8, features), F32)
    totals = lax.fori_loop(0, rows // tile, step, (zero,) * sums)
    return [jnp.sum(total, axis=0, keepdims=True) for total in totals]


def normalize(values):
    average = jnp.mean(values, axis=1, keepdims=True)
    inverse = lax.rsqrt(
        jnp.mean(values * values, axis=1, keepdims=True) - average * average + EPS
    )
    return (values - average) * inverse, inverse


def norm_back(incoming, normed, inverse):
    return inverse * (
        incoming
        - jnp.mean(incoming, axis=1, keepdims=True)
        - normed * jnp.mean(incoming * normed, axis=1, keepdims=True)
    )


def enter(tokens, vectors):
    rows, features = tokens.shape

    def kernel(tokens, vectors, low, turned):
        shift, scale = vectors[0:1], 1.0 + vectors[1:2]

        def work(here):
            values = normalize(tokens[here, :].astype(F32))[0] * scale + shift
            values = values.astype(BF16)
            low[here, :] = values
            turned[:, here] = values.T
            return ()

        by_rows(rows, 0, features, work, LANES)

    return call(
        "enter",
        kernel,
        (1,),
        [whole(tokens.shape), whole(vectors.shape)],
        [whole((rows, features)), whole((features, rows))],
        [shaped((rows, features), BF16), shaped((features, rows), BF16)],
    )(tokens, vectors)


def enter_back(cotangent, vectors):
    rows, features = cotangent.shape

    def kernel(cotangent, vectors, low, turned, sums):
        gate = vectors[5:6]

        def work(here):
            values = (gate * cotangent[here, :].astype(F32)).astype(BF16)
            low[here, :] = values
            turned[:, here] = values.T
            return (values.astype(F32),)

        (sums[...],) = by_rows(rows, 1, features, work, LANES)

    return call(
        "enter_back",
        kernel,
        (1,),
        [whole(cotangent.shape), whole(vectors.shape)],
        [whole((rows, features)), whole((features, rows)), whole((1, features))],
        [
            shaped((rows, features), BF16),
            shaped((features, rows), BF16),
            shaped((1, features), F32),
        ],
    )(cotangent, vectors)


def finish_middle(total, given, results):
    tokens, vectors = given
    branch, middle, low, turned = results
    rows, features = total.shape
    shift, scale, gate = vectors[3:4], 1.0 + vectors[4:5], vectors[2:3]
    bias = vectors[6:7]

    def work(here):
        one = total[here, :] + bias
        branch[here, :] = one
        values = tokens[here, :].astype(F32) + gate * one
        middle[here, :] = values
        values = (normalize(values)[0] * scale + shift).astype(BF16)
        low[here, :] = values
        turned[:, here] = values.T
        return ()

    by_rows(rows, 0, features, work, LANES)


def finish_output(total, given, results):
    middle, cotangent, vectors = given
    output, sums = results
    rows, features = total.shape
    gate, bias = vectors[5:6], vectors[7:8]

    def work(here):
        two = total[here, :] + bias
        output[here, :] = (middle[here, :] + gate * two).astype(BF16)
        return (two * cotangent[here, :].astype(F32),)

    (gate_back,) = by_rows(rows, 1, features, work)
    sums[...] = gate_back


def finish_middle_back(total, given, results):
    middle, branch, cotangent, vectors = given
    middle_back, low, turned, sums = results
    rows, features = total.shape
    gate, scale = vectors[2:3], 1.0 + vectors[4:5]

    def work(here):
        back = total[here, :]
        normed, inverse = normalize(middle[here, :])
        out = cotangent[here, :].astype(F32) + norm_back(back * scale, normed, inverse)
        middle_back[here, :] = out
        rounded = (gate * out).astype(BF16)
        low[here, :] = rounded
        turned[:, here] = rounded.T
        return back, back * normed, branch[here, :] * out, rounded.astype(F32)

    sums[...] = jnp.concatenate(by_rows(rows, 4, features, work, LANES), axis=0)


def finish_tokens_back(total, given, results):
    tokens, middle_back, vectors = given
    tokens_back, sums = results
    rows, features = total.shape
    scale = 1.0 + vectors[1:2]

    def work(here):
        back = total[here, :]
        normed, inverse = normalize(tokens[here, :].astype(F32))
        out = middle_back[here, :] + norm_back(back * scale, normed, inverse)
        tokens_back[here, :] = out.astype(BF16)
        return back, back * normed

    sums[...] = jnp.concatenate(by_rows(rows, 2, features, work), axis=0)


def chosen(parts):
    found = parts[0][...]
    for index, part in enumerate(parts[1:], 1):
        found = jnp.where(pl.program_id(0) == index, part[...], found)
    return found


def gradients(name, pairs, count, first=0, table=None, adds=(), form="one"):
    features, rows = pairs[0][0].shape
    parts = [one for _, parts in pairs for one in parts]
    width = sum(one.shape[2] for one in parts)
    lefts, rights = len(pairs), len(parts)
    given = [one for add in adds for one in add]

    def kernel(*refs):
        if table is not None:
            table_ref, *refs = refs
        left_refs = refs[:lefts]
        right_refs = list(refs[lefts : lefts + rights])
        add_refs = list(refs[lefts + rights : lefts + rights + len(given)])
        outs = refs[lefts + rights + len(given) :]
        found = []
        for left, (_, own) in zip(left_refs, pairs):
            for _ in own:
                found.append(dot(left[...], right_refs.pop(0)[...]))
        out = found[0] if len(found) == 1 else jnp.concatenate(found, axis=1)
        for add in adds:
            out = out + chosen([add_refs.pop(0) for _ in add]).astype(F32)
        out = out.astype(BF16)
        if form == "one":
            outs[0][...] = out
        elif form == "apart":
            for index, one in enumerate(outs):

                @pl.when(pl.program_id(0) == index)
                def _():
                    one[...] = out

        else:
            half = features // 2
            for index in range(2):

                @pl.when(table_ref[1, 0] == index)
                def _():
                    outs[index][...] = out[:half]
                    outs[1 - index][...] = out[half:]

    def right_spec(one):
        if table is None or form == "halves" and first is not None:
            return block(one.shape[1:], 0, first)
        return tabled(one.shape[1:], (0, None))

    def addend(one):
        array, index = one
        return pl.BlockSpec((None, *array.shape[1:]), lambda *_: (index, 0, 0))

    if form == "one":
        out_specs, shape = [block((features, width))], (count, features, width)
    else:
        shape = (features // (2 if form == "halves" else 1), width)
        out_specs = [whole(shape)] * (2 if form == "halves" else count)
    got = call(
        name,
        kernel,
        (count,),
        [fixed(left.shape) for left, _ in pairs]
        + [right_spec(one) for one in parts]
        + [addend(one) for one in given],
        out_specs,
        [shaped(shape, BF16)] * len(out_specs),
        table=table,
    )(*[left for left, _ in pairs], *parts, *[array for array, _ in given])
    return got[0] if form == "one" else got


def attend(queries, pieces):
    number, rows, _ = queries.shape
    count = len(pieces)
    keys = sum(piece.shape[1] for piece in pieces)
    tile = min(rows, 256)

    def kernel(*refs):
        query, kv = refs[0], refs[1 : 1 + count]
        out_ref, log_ref = refs[1 + count :]
        head = lax.broadcasted_iota(jnp.int32, (1, LANES), 1) < HEAD_DIM
        for start in range(0, rows, tile):
            here = slice(start, start + tile)
            both = query[here, :]
            outs, logs = [], []
            for keep in (head, ~head):
                one = jnp.where(keep, both, jnp.zeros_like(both))
                scores = [dot_nt(one, piece[:, :LANES]) for piece in kv]
                top = functools.reduce(
                    jnp.maximum, [jnp.max(s, axis=1, keepdims=True) for s in scores]
                )
                weights = [jnp.exp2((s - top) * SCALE_LOG2) for s in scores]
                total = sum(jnp.sum(w, axis=1, keepdims=True) for w in weights)
                inverse = 1.0 / total
                out = sum(
                    dot((w * inverse).astype(BF16), piece[:, LANES:])
                    for w, piece in zip(weights, kv)
                )
                outs.append(out)
                logs.append(top * SCALE_LOG2 + jnp.log(total) * math.log2(math.e))
            out_ref[here, :] = jnp.where(head, outs[0], outs[1]).astype(BF16)
            table = jnp.where(head, logs[0], logs[1]).T
            log_ref[0:1, here] = table[0:1]
            log_ref[1:2, here] = table[HEAD_DIM : HEAD_DIM + 1]

    return call(
        "attend",
        kernel,
        (number,),
        [block((rows, LANES))] + [block((piece.shape[1], 2 * LANES)) for piece in pieces],
        [block((rows, LANES)), block((2, rows))],
        [shaped((number, rows, LANES), BF16), shaped((number, 2, rows), F32)],
    )(queries, *pieces)


def attend_back(queries, pieces, logs, incoming, first, kinds):
    number, rows, _ = queries.shape
    count = len(pieces)
    keys = sum(piece.shape[1] for piece in pieces)
    tile = min(rows, 256)

    def kernel(*refs):
        query, back_ref, log_ref = refs[:3]
        kv = refs[3 : 3 + count]
        query_back = refs[3 + count]
        kv_back = refs[4 + count : 4 + 2 * count]
        sums, scratch = refs[4 + 2 * count], refs[5 + 2 * count :]
        head = lax.broadcasted_iota(jnp.int32, (1, LANES), 1) < HEAD_DIM
        turned = [piece[:, :LANES].T for piece in kv]
        top = lax.broadcasted_iota(jnp.int32, (LANES, 1), 0) < HEAD_DIM
        query_sum = jnp.zeros((1, LANES), F32)
        for start in range(0, rows, tile):
            here = slice(start, start + tile)
            backs = []
            for index, keep in enumerate((head, ~head)):
                zero = jnp.zeros((tile, LANES), BF16)
                one = jnp.where(keep, query[here, :], zero)
                back = jnp.where(keep, back_ref[here, :], zero)
                log = log_ref[index : index + 1, here]
                chances, mixes = [], []
                for piece in kv:
                    scores = dot_nt(piece[:, :LANES], one)
                    chances.append(jnp.exp2(scores * SCALE_LOG2 - log))
                    mixes.append(dot_nt(piece[:, LANES:], back))
                centre = sum(
                    jnp.sum(p * m, axis=0, keepdims=True) for p, m in zip(chances, mixes)
                )
                total = None
                for i in range(count):
                    score_back = (chances[i] * (mixes[i] - centre)).astype(BF16)
                    key_back = dot(score_back, one) * SCALE
                    value_back = dot(chances[i].astype(BF16), back)
                    if start == 0 and index == 0:
                        scratch[i][:, :LANES] = key_back
                        scratch[i][:, LANES:] = value_back
                    else:
                        scratch[i][:, :LANES] += key_back
                        scratch[i][:, LANES:] += value_back
                    term = dot(turned[i], score_back)
                    total = term if total is None else total + term
                backs.append(total)
            both = (jnp.where(top, backs[0], backs[1]).T * SCALE).astype(BF16)
            query_back[here, :] = both
            query_sum = query_sum + jnp.sum(both.astype(F32), axis=0, keepdims=True)
        sums[...] = query_sum
        for out, held in zip(kv_back, scratch):
            out[...] = held[...].astype(out.dtype)

    return call(
        "attend_back",
        kernel,
        (number,),
        [block((rows, LANES)), block((rows, LANES), first=first), block((2, rows))]
        + [block((piece.shape[1], 2 * LANES)) for piece in pieces],
        [block((rows, LANES))]
        + [block((piece.shape[1], 2 * LANES)) for piece in pieces]
        + [block((1, LANES))],
        [shaped((number, rows, LANES), BF16)]
        + [
            shaped((number, piece.shape[1], 2 * LANES), kind)
            for piece, kind in zip(pieces, kinds)
        ]
        + [shaped((number, 1, LANES), F32)],
        scratch=[pltpu.VMEM((piece.shape[1], 2 * LANES), F32) for piece in pieces],
    )(queries, incoming, logs, *pieces)


def block_at(features, width):
    return block((features, width))


class Steps:
    def __init__(self, steps):
        self.steps, self.result = steps, None
        self.got = next(steps)

    def step(self):
        if self.result is None:
            try:
                self.got = self.steps.send(self.got)
            except StopIteration as end:
                self.got = self.result = end.value

    def hold(self):
        LAST.extend(jax.tree.leaves(self.got))

    def behind(self, *values):
        (*values, self.got) = lax.optimization_barrier((*values, self.got))
        return values

    def finish(self):
        while self.result is None:
            self.step()
        return self.result


class Plain:
    def __init__(self, sizes):
        self.latents, self.parts, self.width = sizes
        self.row = lax.axis_size("y") * lax.axis_size("core")
        self.col = lax.axis_size("lat") * lax.axis_size("sub")

    def scatter(self, values, held=None):
        rows, width = values.shape
        shaped_in = values.reshape(self.latents, 2, LENGTH // 2, width)
        halves = lax.all_to_all(shaped_in, "core", 1, 0, tiled=True)
        pieces = halves.reshape(self.col, -1, width)
        pieces = lax.all_to_all(pieces, COLS, 0, 0, tiled=True)
        return pieces.transpose(1, 0, 2).reshape(-1, self.col * width), held

    def collect_start(self, values):
        rows = values.shape[0]
        pieces = values.reshape(rows, self.col, -1).transpose(1, 0, 2)
        return [lax.all_to_all(pieces, COLS, 0, 0, tiled=True)]

    def collect(self, pieces):
        (pieces,) = pieces
        halves = pieces.reshape(2 * self.latents, 1, LENGTH // 2, -1)
        back = lax.all_to_all(halves, "core", 0, 1, tiled=True)
        return back.reshape(-1, self.width)

    def modulation(self, partial, bias, row_bias, col_bias):
        group = 2 * self.latents
        ours = lax.psum(partial, "core").reshape(-1, group, partial.shape[1])
        ours = lax.psum_scatter(ours, "y", scatter_dimension=0, tiled=True)[0] + bias
        sent = jnp.repeat(ours, self.col // group, axis=0)
        got = lax.all_to_all(sent, COLS, 0, 0, tiled=True)
        got = got.reshape(self.col, 6, -1).transpose(1, 0, 2).reshape(6, -1)
        cols = lax.all_gather(col_bias, COLS, axis=1, tiled=True)
        every = lax.all_gather(row_bias, ROWS, axis=0)
        return jnp.concatenate([got, cols], axis=0), [
            every.reshape(self.row * self.parts, 1, -1)
        ]

    def gather(self, parts, held):
        del held
        every = lax.all_gather(parts, COLS, axis=1, tiled=True)
        every = lax.all_gather(every, ROWS, axis=0, tiled=True)
        return [every[:, :, :LANES]], [every[:, :, LANES:]]

    def gather_start(self, parts):
        return parts

    def gather_late(self, part):
        every = lax.all_gather(part, (*ROWS, *COLS), axis=0, tiled=True)
        return every.reshape(self.row, -1, part.shape[1])

    def expand_bias(self, row_bias, biases):
        every = lax.all_gather(row_bias, ROWS, axis=0)
        return every.reshape(self.row * self.parts, 1, -1)

    def with_units(self, row_sums, unit_sums):
        return [jnp.concatenate([row_sums[0], unit_sums[0]], axis=-1)]

    def tables(self):
        blocks = jnp.arange(self.row * self.parts, dtype=jnp.int32)
        return [jnp.stack([blocks // self.parts, blocks % self.parts])]


    def share(self, kv):
        return [[lax.all_gather(kv[0], ("core", "sub"), axis=1, tiled=True)]]

    def kinds(self):
        return [F32]

    PLACES = ((0, 0),)

    def give_back(self, backs, x):
        return [
            lax.psum_scatter(
                backs[0][0], ("core", "sub"), scatter_dimension=1, tiled=True
            ).astype(BF16)
        ]

    def sum_up(self, *args):
        return Steps(self.reduce(*args))

    def feed_back(self, low, turned, late, expanded, hidden, extras):
        blocks = jnp.arange(self.row * self.parts, dtype=jnp.int32)
        table = jnp.stack([blocks, blocks // self.parts, blocks % self.parts])
        shrink, grow, (sums, *ends) = feed_back(
            "feed_back",
            low,
            turned,
            late,
            expanded,
            hidden,
            table,
            self.parts,
            extras,
            None,
            False,
        )
        steps = [Steps(self.reduce_ready(one[0])) for one in (shrink, grow)]
        return steps, ends, [sums]

    def reduce(self, name, pairs):
        pairs = pairs[0]()
        grads = gradients(name, pairs, pairs[0][1][0].shape[0])
        return (yield from self.reduce_ready(grads))

    def reduce_ready(self, grads):
        grads = grads.astype(F32)
        grads = yield grads
        grads = lax.psum_scatter(grads, ROWS, scatter_dimension=0, tiled=True)
        grads = lax.psum_scatter(grads, COLS, scatter_dimension=1, tiled=True)
        return lax.psum(grads, "dp")

    def small(self, vectors, row_sums, col_sums):
        every = ("dp", *ROWS, *COLS)
        group = 2 * self.latents
        total = yield lax.psum(vectors, ("core", "sub"))
        total = total.astype(BF16)
        mine = lax.all_gather(total[:, None], "lat", axis=1, tiled=True)
        mine = lax.all_gather(mine, "y", axis=1, tiled=True)
        mine = lax.all_gather(mine, "dp", axis=1, tiled=True)
        col = lax.axis_index("lat") * lax.axis_size("sub") + lax.axis_index("sub")
        cut = lax.dynamic_slice_in_dim(mine, col * self.width, self.width, axis=2)
        cut = cut.transpose(1, 0, 2).reshape(mine.shape[1], -1)
        rows = lax.psum(row_sums[0], every).reshape(self.row, self.parts, -1)
        row = lax.axis_index("y") * 2 + lax.axis_index("core")
        rows = lax.dynamic_index_in_dim(rows, row, 0, keepdims=False)
        cols = lax.psum(col_sums, every)
        cols = lax.dynamic_slice_in_dim(cols, col * self.width, self.width, axis=1)
        return cut, rows, cols

    def col_sum(self, values):
        return lax.psum(values, COLS)

    def both_groups(self, values):
        return lax.all_gather(values, "dp", axis=0, tiled=True)


class Cube(Plain):
    PLACES = ((0, 0), (0, 1), (1, 0), (1, 1))

    def __init__(self, sizes):
        super().__init__(sizes)
        self.x = lax.axis_index("dp")
        self.y = lax.axis_index("y")
        self.c = lax.axis_index("core")
        self.z = lax.axis_index("lat")

    def swap(self, values, axis):
        return lax.ppermute(values, axis, [(0, 1), (1, 0)])

    def along(self, values, bits):
        return lax.ppermute(values, "lat", [(i, i ^ bits) for i in range(4)])

    def scatter(self, values, held=None):
        rows, width = values.shape
        halves = values.reshape(self.latents, 2, LENGTH // 2, width)
        keep = lax.dynamic_index_in_dim(halves, self.c, 1, keepdims=False)
        send = lax.dynamic_index_in_dim(halves, 1 - self.c, 1, keepdims=False)
        every = jnp.concatenate([keep, self.swap(send, "core")], axis=0)
        if held is not None:
            every, held = lax.optimization_barrier((every, held))
        pieces = []
        for bits in range(4):
            latent = self.z ^ bits
            index = ((latent // 2) ^ self.c) * 2 + latent % 2
            piece = lax.dynamic_index_in_dim(every, index, 0, keepdims=False)
            pieces.append(piece if bits == 0 else self.along(piece, bits))
        return jnp.concatenate(self.placed(pieces), axis=1), held

    def placed(self, pieces):
        odd, high = self.z % 2 == 1, self.z >= 2
        one, two, three, four = pieces
        one, two = jnp.where(odd, two, one), jnp.where(odd, one, two)
        three, four = jnp.where(odd, four, three), jnp.where(odd, three, four)
        return [
            jnp.where(high, three, one),
            jnp.where(high, four, two),
            jnp.where(high, one, three),
            jnp.where(high, two, four),
        ]

    def collect_start(self, values):
        width = self.width
        pieces = self.placed([values[:, i * width : (i + 1) * width] for i in range(4)])
        return [p if bits == 0 else self.along(p, bits) for bits, p in enumerate(pieces)]

    def collect(self, pieces):
        width = self.width
        every = jnp.stack(pieces)

        def latents(core):
            return jnp.stack(
                [
                    lax.dynamic_index_in_dim(every, self.z ^ (2 * core + i), 0, keepdims=False)
                    for i in range(2)
                ]
            )

        keep = latents(self.c)
        got = self.swap(latents(1 - self.c), "core")
        first = jnp.where(self.c == 0, keep, got)
        second = jnp.where(self.c == 0, got, keep)
        return jnp.stack([first, second], axis=1).reshape(-1, width)

    def modulation(self, partial, bias, row_bias, col_bias):
        span = partial.shape[1]
        own = row_bias.reshape(1, -1)
        got = self.swap(jnp.concatenate([partial, own], axis=0), "core")
        ours, other = partial + got[:-1], got[-1:]
        halves = ours.reshape(2, 4, span)
        keep = lax.dynamic_index_in_dim(halves, self.y, 0, keepdims=False)
        send = lax.dynamic_index_in_dim(halves, 1 - self.y, 0, keepdims=False)
        got = self.swap(jnp.concatenate([send, own, other], axis=0), "y")
        ours = keep + got[:4] + bias
        rows = jnp.stack([own, got[4:5], other, got[5:6]]).reshape(2, 2, 2, -1)
        flip = jnp.stack([rows[:, :, 1], rows[:, :, 0]], axis=2)
        rows = jnp.where(self.x == 0, rows, flip).transpose(2, 0, 1, 3)[:, :, :, None]
        pieces = []
        for bits in range(4):
            piece = lax.dynamic_index_in_dim(ours, self.z ^ bits, 0, keepdims=False)
            piece = jnp.concatenate([piece.reshape(6, -1), col_bias], axis=0)
            pieces.append(piece if bits == 0 else self.along(piece, bits))
        vectors = jnp.concatenate(self.placed(pieces), axis=1)
        return vectors, [rows[x, core] for x, core in self.PLACES]

    def gather_start(self, parts):
        part = lax.dynamic_index_in_dim(parts, self.x, 0, keepdims=False)
        odd, high = self.z % 2 == 1, self.z >= 2
        got = self.along(part, 1)
        part = jnp.concatenate([jnp.where(odd, got, part), jnp.where(odd, part, got)], axis=0)
        got = self.along(part, 2)
        part = jnp.concatenate(
            [jnp.where(high, got, part), jnp.where(high, part, got)], axis=0
        )

        return part

    def gather(self, part, held):
        one, two = part[:, :LANES], part[:, LANES:]
        one_pair = jnp.stack([one, self.swap(one, "dp")])
        near = jnp.stack([two, self.swap(two, "y")])
        near = after(near, one_pair, *held)
        far = self.swap(near, "dp")
        kv = [near, self.swap(near, "core"), far, self.swap(far, "core")]
        got = self.swap(one_pair, "y")
        near = jnp.stack([one_pair[0], got[0]])
        far = jnp.stack([one_pair[1], got[1]])
        queries = [near, self.swap(near, "core"), far, self.swap(far, "core")]
        return queries, kv

    def expand_bias(self, row_bias, biases):
        number = self.row * self.parts
        table = jnp.concatenate(self.tables(), axis=1)
        place = table[0] * self.parts + table[1]
        chosen = place[None, :] == lax.broadcasted_iota(jnp.int32, (number, number), 0)
        every = jnp.concatenate(biases, axis=0)[:, 0]
        found = jnp.dot(chosen.astype(F32), every, precision=lax.Precision.HIGHEST)
        return found[:, None]

    def with_units(self, row_sums, unit_sums):
        found = []
        for one, (x, core) in zip(row_sums, self.PLACES):
            units = unit_sums[1 - core][2 * x : 2 * x + 2]
            found.append(jnp.concatenate([one, units], axis=-1))
        return found

    def tables(self):
        side = jnp.arange(2, dtype=jnp.int32)
        return [
            jnp.stack(
                [(side ^ self.y) * 2 + (self.c ^ core), jnp.full((2,), self.x ^ x)]
            ).astype(jnp.int32)
            for x, core in self.PLACES
        ]

    def share(self, kv):
        return [
            [kv[2 * x + core], self.swap(kv[2 * x + 1 - core], "core")]
            for x, core in self.PLACES
        ]

    def kinds(self):
        return [F32, BF16]

    def give_back(self, backs, x):
        pair = backs[2 * x : 2 * x + 2]
        got = [self.swap(pair[1 - core][1], "core") for core in (0, 1)]
        return [(own[0] + one.astype(F32)).astype(BF16) for own, one in zip(pair, got)]

    def feed_back(self, low, turned, late, expanded, hidden, extras):
        tables = self.tables()
        found, sums, before = [], [], None
        for core in (1, 0):
            rows, parts = jnp.concatenate([tables[core], tables[2 + core]], axis=1)
            shrink, grow, (one, *ends) = feed_back(
                "feed_back",
                low,
                turned,
                late,
                expanded,
                hidden,
                jnp.stack([rows * self.parts + parts, rows, parts]),
                self.parts,
                [] if core else extras,
                before,
                core == 1,
            )
            if core:
                (before,) = ends
                found = [[self.swap(one, "core") for one in part] for part in (shrink, grow)]
            else:
                LAST.extend([one for part in found for one in part])
                steps = [
                    Steps(self.reduce_ready(name, near[0], far, order))
                    for name, near, far, order in (
                        ("d_shrink", shrink, found[0], "xy"),
                        ("d_expand", grow, found[1], "yx"),
                    )
                ]
            sums.append(one)
        return steps, ends, sums

    def reduce_ready(self, name, near, far, order):
        axes, one, two = (("dp", "y"), 2, 1) if order == "xy" else (("y", "dp"), 1, 2)
        far = [(far[x], y) for x in (0, 1) for y in (0, 1)]
        sent = add_up(name, [[(near, one), far[one]], [(near, 3), far[3]]])
        second = self.swap(sent, axes[0])
        second = yield second
        sent = add_up(name, [[(near, two), far[two], (second, 1)]])
        third = self.swap(sent, axes[1])
        third = yield third
        keep, send = add_up(
            name, [[(near, 0), far[0], (second, 0), (third, 0)]], upper=self.z // 2
        )
        return (yield from self.reduce_end(name, keep, send))

    def reduce_end(self, name, keep, other):
        got = lax.ppermute(other, "lat", [(0, 1), (3, 2)])
        got = yield got
        other = add_up(name + "_out", [[(other[None], 0), (got[None], 0)]])[0]
        got = lax.ppermute(other, "lat", [(1, 2), (2, 1)])
        got = yield got
        own, send = add_up(
            name + "_in", [[(keep[None], 0), (got[None], 0)]], upper=self.z % 2
        )
        got = self.along(send, 1)
        got = yield got
        own = (own.astype(F32) + got.astype(F32)).astype(BF16)
        got = self.swap(own, "dp")
        return jnp.stack(
            [jnp.where(self.x == 0, own, got), jnp.where(self.x == 0, got, own)]
        ).astype(F32)

    def reduce(self, name, pairs):
        def grads(places, adds=(), form="one"):
            x, y, core = places[0]
            table = None
            if form == "halves":
                table = jnp.full((2, 1), self.z // 2, jnp.int32)
            return gradients(name, pairs[2 * x + core](), len(places), y, table, adds, form)

        near = [None, None]
        for x in (1, 0):
            sent = grads([(x, 0, 1), (x, 1, 1)], form="apart")
            sent = yield [self.swap(one, "core") for one in sent]
            near[x] = [(one[None], 0) for one in sent]
            if x == 1:
                second = self.swap(grads([(1, 0, 0), (1, 1, 0)], [near[1]]), "dp")
                second = yield second
                second = [(second, 0), (second, 1)]
        third = self.swap(grads([(0, 1, 0)], [[near[0][1]], [second[1]]]), "y")
        third = yield third
        keep, send = grads(
            [(0, 0, 0)], [[near[0][0]], [second[0]], [(third, 0)]], form="halves"
        )
        return (yield from self.reduce_end(name, keep, send))

    def small(self, vectors, row_sums, col_sums):
        span = row_sums[0].shape[-1]
        features = vectors.shape[1]

        def flat(*parts):
            return jnp.concatenate([part.reshape(-1, LANES) for part in parts], axis=0)

        def cut(message, *shapes):
            parts, start = [], 0
            for shape in shapes:
                size = math.prod(shape) // LANES
                parts.append(message[start : start + size].reshape(shape))
                start += size
            return parts

        every = jnp.stack(row_sums).reshape(2, 2, 2, span)
        rows0, rows1 = every[:, 0], every[:, 1]
        got = yield self.swap(flat(rows1, col_sums, vectors), "core")
        got = cut(got, rows1.shape, col_sums.shape, vectors.shape)
        rows, cols = rows0 + got[0], col_sums + got[1]
        mine = (vectors + got[2]).astype(BF16).astype(F32)
        got = yield self.swap(flat(rows[:, 1], cols, mine), "y")
        got = cut(got, (2, span), cols.shape, mine.shape)
        rows, cols = rows[:, 0] + got[0], cols + got[1]
        pair = jnp.stack([mine, got[2]])
        got = yield self.swap(flat(rows, cols, pair), "dp")
        got = cut(got, rows.shape, cols.shape, pair.shape)
        rows = rows + jnp.stack([got[0][1], got[0][0]])
        rows = jnp.where(self.x == 0, rows, jnp.stack([rows[1], rows[0]]))
        cols = cols + got[1]
        four = jnp.stack([pair, got[2]]).reshape(4, 6, features)
        width = self.width

        def cuts(values):
            return self.placed(
                [values[..., i * width : (i + 1) * width] for i in range(4)]
            )

        found = []
        for bits, piece in enumerate(zip(cuts(four), cuts(cols))):
            piece = [*piece, rows]
            if bits:
                got = self.along(flat(*piece), bits)
                piece = cut(got, *[part.shape for part in piece])
            found.append(piece)
        tree = [(found[0][i] + found[1][i]) + (found[2][i] + found[3][i]) for i in (1, 2)]
        every = jnp.stack([one[0] for one in found])
        every = every.reshape(16, -1)
        place = lax.broadcasted_iota(jnp.int32, (16, 16), 0)
        held = lax.broadcasted_iota(jnp.int32, (16, 16), 1)
        latent = (
            (((held // 2) % 2) ^ self.x) * 8 + ((held % 2) ^ self.y) * 4 + ((held // 4) ^ self.z)
        )
        chosen = (latent == place).astype(F32)
        every = jnp.dot(chosen, every, precision=lax.Precision.HIGHEST).astype(BF16)
        return every, tree[1], tree[0]

    def col_sum(self, values):
        got = [values] + [self.along(values, bits) for bits in (1, 2, 3)]
        return (got[0] + got[1]) + (got[2] + got[3])

    def both_groups(self, values):
        got = self.swap(values, "dp")
        return jnp.where(
            self.x == 0,
            jnp.concatenate([values, got], axis=0),
            jnp.concatenate([got, values], axis=0),
        )


def body(
    fast,
    tokens,
    condition,
    modulation_weight,
    modulation_bias,
    input_weight,
    input_bias,
    output_weight,
    output_bias,
    expand_weight,
    expand_bias,
    shrink_weight,
    shrink_bias,
    cotangent,
):
    LAST.clear()
    width = tokens.shape[1]
    inner = input_weight.shape[2]
    parts = inner // LANES
    units = expand_weight.shape[1] // parts
    sizes = (tokens.shape[0] // LENGTH, parts, width)
    net = (Cube if fast else Plain)(sizes)

    own_in = (
        input_weight.reshape(width, 3, parts, LANES)
        .transpose(2, 0, 1, 3)
        .reshape(parts, width, 3 * LANES)
    )
    own_late = with_layout_constraint(
        jnp.concatenate([expand_weight, shrink_weight.T, output_weight.T], axis=1),
        Layout((0, 1)),
    )
    out_start = 2 * parts * units // LANES

    condition_float = condition.astype(F32)
    silu_low = jax.nn.silu(condition_float).astype(BF16)
    modulator = modulation_weight.reshape(modulation_weight.shape[0], -1)
    row_bias = jnp.concatenate(
        [
            input_bias.reshape(2, parts, LANES).transpose(1, 0, 2).reshape(parts, -1),
            expand_bias.reshape(parts, units),
        ],
        axis=1,
    ).astype(F32)
    late = net.gather_late(own_late)
    vectors, row_biases = net.modulation(
        dot(silu_low, modulator),
        modulation_bias.astype(F32).reshape(1, -1),
        row_bias,
        jnp.stack([output_bias, shrink_bias]).astype(F32),
    )
    own_in = net.gather_start(own_in)
    mine, own_in = net.scatter(tokens, own_in)
    query_bufs, kv_bufs = net.gather(own_in, [mine, vectors])
    rows = mine.shape[0]
    features = mine.shape[1]
    expand_biases = net.expand_bias(
        row_bias[:, 2 * LANES :], [one[..., 2 * LANES :] for one in row_biases]
    )
    tables = net.tables()

    low_one, turned_one = enter(mine, vectors)
    queries, own_kv = [], []
    for one, two, bias in zip(query_bufs, kv_bufs, row_biases):
        one, two = project(low_one, one, two, bias)
        queries.append(one)
        own_kv.append(two)
    kv = net.share(own_kv)
    back, _ = net.scatter(after(cotangent, own_kv[0]))
    attended, logs = [], []
    for one, pieces in zip(queries, kv):
        out, log = attend(one, pieces)
        attended.append(out)
        logs.append(log)

    branch_two_back, turned_two_back, shrink_sum = enter_back(back, vectors)

    def out_place(number):
        def place(features, width):
            return tabled((features, width), (2 * number, 2 * number + 1), out_start)

        return place

    branch_one, middle, low_two, turned_two = contract(
        "out",
        [(one, late, out_place(i)) for i, one in enumerate(attended)],
        [mine, vectors],
        finish_middle,
        [
            shaped((rows, features), F32),
            shaped((rows, features), F32),
            shaped((rows, features), BF16),
            shaped((features, rows), BF16),
        ],
        table=jnp.concatenate(tables, axis=0),
    )
    expanded, hidden, output, gate_two_back = feed_forward(
        low_two, late, expand_biases, parts, [middle, back, vectors]
    )
    output = net.collect_start(output)

    steps, ends, expand_sums = net.feed_back(
        branch_two_back,
        (turned_two_back, turned_two),
        late,
        expanded,
        hidden,
        [middle, branch_one, back, vectors],
    )
    middle_back, branch_one_back, turned_one_back, sums_two = ends
    shrink_steps, expand_steps = steps
    incoming = attended_backward(
        branch_one_back, late, jnp.concatenate(tables, axis=1), out_start
    )
    number = len(kv)
    query_back, backs, query_sums = [None] * number, [None] * number, [None] * number
    kv_back = [None] * number

    def attention_back(i):
        got = attend_back(
            queries[i], kv[i], logs[i], incoming, i * queries[i].shape[0], net.kinds()
        )
        query_back[i], backs[i], query_sums[i] = got[0], got[1:-1], got[-1]

    def kv_final(i):
        pair = net.give_back(backs, i // 2)
        kv_back[i : i + len(pair)] = pair

    def pair(i):
        return lambda: [
            (turned_one, [query_back[i], kv_back[i]]),
            (turned_one_back, [attended[i]]),
        ]

    half = number // 2
    for i in reversed(range(half, number)):
        attention_back(i)
    kv_final(half)
    in_steps = net.sum_up("d_in", [pair(j) for j in range(number)])
    shrink_steps.step()
    expand_steps.step()
    crossing = []
    if half:
        in_steps.step()
        crossing = [in_steps.got]
        for i in reversed(range(half)):
            if i == 0:
                shrink_steps.hold()
                expand_steps.hold()
            attention_back(i)
        shrink_steps.step()
        expand_steps.step()
        kv_final(0)
        in_steps.step()
        shrink_steps.step()
        in_steps.step()
        expand_steps.step()
    value_sums = [
        jnp.sum(one[:, :, LANES:].astype(F32), axis=1, keepdims=True) for one in kv_back
    ]
    LAST.extend(crossing)
    tokens_back, sums_one = contract(
        "tokens_back",
        [(one, buf, block_at) for one, buf in zip(query_back, query_bufs)]
        + [(one, buf, block_at) for one, buf in zip(kv_back, kv_bufs)],
        [mine, middle_back, vectors],
        finish_tokens_back,
        [shaped((rows, features), BF16), shaped((2, features), F32)],
    )
    summed = jnp.concatenate([sums_one, sums_two[2:3], sums_two[0:2], gate_two_back], axis=0)
    tokens_back = net.collect_start(tokens_back)
    shrink_steps.step()
    expand_steps.step()
    row_sums = [
        jnp.concatenate([one, two], axis=-1) for one, two in zip(query_sums, value_sums)
    ]
    row_sums = net.with_units(row_sums, expand_sums)
    col_sums = jnp.concatenate([sums_two[3:4], shrink_sum], axis=0)
    (summed,) = in_steps.behind(summed)
    small_steps = Steps(net.small(summed, row_sums, col_sums))
    in_steps.step()
    small_steps.step()
    LAST.extend(tokens_back[1:])
    small_steps.hold()
    in_steps.step()
    small_steps.step()
    small_steps.hold()
    in_steps.step()
    shrink_parts = shrink_steps.finish()
    expand_parts = expand_steps.finish()
    in_parts = in_steps.finish()

    every, row_found, col_found = small_steps.finish()
    silu_all = net.both_groups(silu_low)
    modulation_weight_gradient = lax.dot_general(
        silu_all, every, (((0,), (0,)), ((), ())), preferred_element_type=F32
    ).reshape(modulation_weight.shape)
    modulation_bias_gradient = jnp.sum(every.astype(F32), axis=0).reshape(6, width)
    groups = condition.shape[0]
    ours = lax.dynamic_slice_in_dim(every, lax.axis_index("dp") * groups, groups, axis=0)
    silu_back = net.col_sum(dot_nt(ours, modulator))
    silu_pull = jax.vjp(jax.nn.silu, condition_float)[1]
    condition_gradient = silu_pull(silu_back)[0]

    return (
        net.collect(output),
        net.collect(tokens_back).astype(F32),
        condition_gradient,
        modulation_weight_gradient,
        modulation_bias_gradient,
        in_parts[:, :, : 3 * LANES]
        .reshape(parts, width, 3, LANES)
        .transpose(1, 2, 0, 3)
        .reshape(input_weight.shape),
        row_found[:, : 2 * LANES]
        .reshape(parts, 2, LANES)
        .transpose(1, 0, 2)
        .reshape(input_bias.shape),
        in_parts[:, :, 3 * LANES :].transpose(0, 2, 1).reshape(output_weight.shape),
        col_found[0],
        expand_parts.transpose(1, 0, 2).reshape(expand_weight.shape),
        row_found[:, 2 * LANES :].reshape(expand_bias.shape),
        shrink_parts.transpose(0, 2, 1).reshape(shrink_weight.shape),
        col_found[1],
    )


def solution(mesh):
    dp, row, col = (mesh.shape[name] for name in ("dp", "row", "col"))

    def run(*arrays):
        latents = arrays[0].shape[0] // (dp * row * LENGTH)
        group = 2 * latents
        refined = Mesh(
            mesh.devices.reshape(dp, row // 2, 2, group, col // group),
            ("dp", "y", "core", "lat", "sub"),
        )
        fast = (dp, row, col, latents) == (2, 4, 4, 2)
        token = P(("dp", *ROWS), COLS)
        weights = (
            P(ROWS, None, COLS),
            P(None, COLS),
            P(COLS, None, ROWS),
            P(None, ROWS),
            P(ROWS, COLS),
            P(COLS),
            P(COLS, ROWS),
            P(ROWS),
            P(ROWS, COLS),
            P(COLS),
        )
        given = P("dp", ROWS)
        return jax.shard_map(
            functools.partial(body, fast),
            mesh=refined,
            in_specs=(token, given, *weights, token),
            out_specs=(token, token, given, *weights),
            check_vma=False,
        )(*arrays)

    return run
```

time: 766 us -> 546 us (0.71)
  waiting for transfers between devices: 311 us -> 116 us
  local copies, waits for them, and re-layouts: 75 us -> 36.3 us
  other arithmetic: 60 us -> 22.8 us
  Pallas kernels: 217 us -> 244 us
  starting transfers between devices: 78.5 us -> 105 us
  between operations: 2.5 us -> 16 us
  blocking collectives: 9.51 us -> 0 us
    ppermute x35 -> x43, waiting for transfers between devices: 187 us -> 33.6 us  [swap(): return lax.ppermute(values, axis, [(0, 1), (1, 0)])]
    ppermute x30 -> x26, waiting for transfers between devices: 124 us -> 74.4 us  [along(): return lax.ppermute(values, 'lat', [(i, i ^ bits) for i in range(4)])]
    pallas_call x28 -> x37, Pallas kernels: 217 us -> 244 us  [ordered(): found = run(first, *others) if table is None else run(table, first, *others)]
    another operation x11 -> x13, other arithmetic: 24.2 us -> 2.68 us  [the longest x1 0.86 us: gather(): near = jnp.stack([one_pair[0], got[0]])]
    ppermute x0 -> x6, starting transfers between devices: none -> 15 us  [the longest x3 12.7 us: reduce_end(): got = lax.ppermute(other, 'lat', [(0, 1), (3, 2)])]
    ppermute x30 -> x26, starting transfers between devices: 54.7 us -> 64.9 us  [along(): return lax.ppermute(values, 'lat', [(i, i ^ bits) for i in range(4)])]
    psum x1 -> x0, blocking collectives: 9.51 us -> none  [body(): silu_back = lax.psum(dot_nt(ours, modulator), COLS)]
    dynamic_slice x7 -> x2, local copies, waits for them, and re-layouts: 8.95 us -> 0.19 us  [gather_start(): part = lax.dynamic_index_in_dim(parts, self.x, 0, keepdims=False)]
  transfers between devices with their start and end apart: 65 -> 76, of which waited for: 26 -> 25; matrix products, arithmetic and copies ran while one was open for 16% -> 7% of each run, Pallas kernels for 24% -> 35%
where the time goes in v2:
time: 546 us; the launch traced here: 541 us
  Pallas kernels  244 us (45%)
  waiting for transfers between devices  116 us (21%)
  starting transfers between devices  105 us (19%)
  local copies, waits for them, and re-layouts  36.3 us (7%)
  other arithmetic  22.8 us (4%)
  between operations  16 us (3%)
    pallas_call x37, Pallas kernels, ordered(): found = run(first, *others) if table is None else run(table, first, *others)  244 us
    ppermute x26, waiting for transfers between devices, along(): return lax.ppermute(values, 'lat', [(i, i ^ bits) for i in range(4)])  74.4 us
    ppermute x26, starting transfers between devices, along(): return lax.ppermute(values, 'lat', [(i, i ^ bits) for i in range(4)])  64.9 us
    ppermute x43, waiting for transfers between devices, swap(): return lax.ppermute(values, axis, [(0, 1), (1, 0)])  33.6 us
    ppermute x43, starting transfers between devices, swap(): return lax.ppermute(values, axis, [(0, 1), (1, 0)])  25.6 us
    unnamed x169, local copies, waits for them, and re-layouts  22.3 us
    ppermute x3, starting transfers between devices, reduce_end(): got = lax.ppermute(other, 'lat', [(0, 1), (3, 2)])  12.7 us
  transfers between devices with their start and end apart: 76, of which 25 were waited for; matrix products, arithmetic and copies ran while one was open for 7% of the time, Pallas kernels for 35%

profile of v2, /device:TPU:0, one launch (start us, length us, event | category | flops | bytes accessed | tf_op | source)
XLA Modules:
  0.0 541.1 jit_solution(1591421641612729268)
XLA Ops:
  24.5 3.6 collective-permute-start.8
  33.8 18.9 %collective-permute-done.2 = bf16[512,384]{1,0:T(8,128)(2,1)S(1)} collective-permute-done((bf16[512,384]{1,0:T(8,128)(2,1)S(1)}, bf16[512,384]{1,0:T(8,128)(2,1)S(1)}, u32[]{:S(2)}, u32[]{:S(2)}) %collective-permute-start.2) | collective-permute-done | bytes 393248 | tf_op jit(solution)/shard_map/ppermute | solution.py:908
  61.6 6.8 %collective-permute-done.3 = bf16[512,256]{1,0:T(8,128)(2,1)S(1)} collective-permute-done((bf16[512,256]{1,0:T(8,128)(2,1)S(1)}, bf16[512,256]{1,0:T(8,128)(2,1)S(1)}, u32[]{:S(2)}, u32[]{:S(2)}) %collective-permute-start.3) | collective-permute-done | bytes 262176 | tf_op jit(solution)/shard_map/ppermute | solution.py:908
  68.4 15.1 %collective-permute-done.4 = bf16[512,256]{1,0:T(8,128)(2,1)S(1)} collective-permute-done((bf16[512,256]{1,0:T(8,128)(2,1)S(1)}, bf16[512,256]{1,0:T(8,128)(2,1)S(1)}, u32[]{:S(2)}, u32[]{:S(2)}) %collective-permute-start.4) | collective-permute-done | bytes 262176 | tf_op jit(solution)/shard_map/ppermute | solution.py:908
  88.2 3.9 enter.1
  92.1 11.9 %collective-permute-done.12 = bf16[2,1024,128]{2,1,0:T(8,128)(2,1)S(1)} collective-permute-done((bf16[2,1024,128]{2,1,0:T(8,128)(2,1)S(1)}, bf16[2,1024,128]{2,1,0:T(8,128)(2,1)S(1)}, u32[]{:S(2)}, u32[]{:S(2)}) %collective-permute-start.12) | collective-permute-done | bytes 524320 | tf_op jit(solution)/shard_map/ppermute | solution.py:905
  104.9 4.5 project.4
  121.7 4.4 project.5
  126.2 4.4 project.6
  131.2 4.4 project.7
  135.7 10.0 %collective-permute-done.22 = bf16[512,256]{1,0:T(8,128)(2,1)S(1)} collective-permute-done((bf16[512,256]{1,0:T(8,128)(2,1)S(1)}, bf16[512,256]{1,0:T(8,128)(2,1)S(1)}, u32[]{:S(2)}, u32[]{:S(2)}) %collective-permute-start.22) | collective-permute-done | bytes 262176 | tf_op jit(solution)/shard_map/ppermute | solution.py:908
  147.9 6.9 %attend.4 = (bf16[2,512,128]{2,1,0:T(8,128)(2,1)}, f32[2,2,512]{2,1,0:T(2,128)}) custom-call(bf16[2,512,128]{2,1,0:T(8,128)(2,1)} %get-tuple-element.202.refs_0_, bf16[2,512,256]{2,1,0:T(8,128)(2,1)} %get-tuple-element.144.refs_1_.refs_3_, bf16[2,512,256]{2,1,0:T(8,128)(2,1)} %copy-done.20), custom_call_target="tpu_custom_call" | custom-call | tf_op jit(solution)/shard_map/attend/pallas_call | solution.py:91
  155.6 6.9 %attend.5 = (bf16[2,512,128]{2,1,0:T(8,128)(2,1)}, f32[2,2,512]{2,1,0:T(2,128)}) custom-call(bf16[2,512,128]{2,1,0:T(8,128)(2,1)} %get-tuple-element.199.refs_0_, bf16[2,512,256]{2,1,0:T(8,128)(2,1)} %get-tuple-element.145.refs_1_.refs_3_, bf16[2,512,256]{2,1,0:T(8,128)(2,1)} %copy-done.21), custom_call_target="tpu_custom_call" | custom-call | tf_op jit(solution)/shard_map/attend/pallas_call | solution.py:91
  163.2 6.9 %attend.6 = (bf16[2,512,128]{2,1,0:T(8,128)(2,1)}, f32[2,2,512]{2,1,0:T(2,128)}) custom-call(bf16[2,512,128]{2,1,0:T(8,128)(2,1)} %get-tuple-element.185.refs_0_, bf16[2,512,256]{2,1,0:T(8,128)(2,1)} %get-tuple-element.151.refs_1_.refs_3_, bf16[2,512,256]{2,1,0:T(8,128)(2,1)} %copy-done.23), custom_call_target="tpu_custom_call" | custom-call | tf_op jit(solution)/shard_map/attend/pallas_call | solution.py:91
  171.0 7.4 %attend.7 = (bf16[2,512,128]{2,1,0:T(8,128)(2,1)}, f32[2,2,512]{2,1,0:T(2,128)}) custom-call(bf16[2,512,128]{2,1,0:T(8,128)(2,1)} %get-tuple-element.182.refs_0_, bf16[2,512,256]{2,1,0:T(8,128)(2,1)} %get-tuple-element.152.refs_1_.refs_3_, bf16[2,512,256]{2,1,0:T(8,128)(2,1)} %copy-done.24), custom_call_target="tpu_custom_call" | custom-call | tf_op jit(solution)/shard_map/attend/pallas_call | solution.py:91
  181.4 9.7 %out.1 = (f32[512,1024]{1,0:T(8,128)}, f32[512,1024]{1,0:T(8,128)}, bf16[512,1024]{1,0:T(8,128)(2,1)}, bf16[1024,512]{1,0:T(8,128)(2,1)}) custom-call(s32[8,2]{1,0:T(8,128)} %concatenate.104.refs_0_, bf16[2,512,128]{2,1,0:T(8,128)(2,1)} %get-tuple-element.158.refs_1_.refs_4_.refs_5_, bf16[2,512,128]{2,1,0:T(8,128)(2,1)} %get-tuple-element.149.refs_2_.refs_4_, ...), custom_call_target="tpu_custom_call" | custom-call | tf_op jit(solution)/shard_map/out/pallas_call | solution.py:91
  191.1 19.5 %feed_forward.1 = (f32[8,512,512]{2,1,0:T(8,128)}, bf16[8,512,512]{2,1,0:T(8,128)(2,1)}, bf16[512,1024]{1,0:T(8,128)(2,1)}, f32[1,1024]{1,0:T(1,128)}) custom-call(bf16[512,1024]{1,0:T(8,128)(2,1)} %get-tuple-element.161.a, bf16[4,1024,2304]{2,1,0:T(8,128)(2,1)} %bitcast.217, bf16[4,1024,2304]{2,1,0:T(8,128)(2,1)} %bitcast.218, ...), custom_call_target="tpu_custom_call" | custom-call | tf_op jit(solution)/shard_map/feed_forward/pallas_call | solution.py:91
  210.6 20.1 %feed_back.2 = (bf16[2,1024,512]{2,1,0:T(8,128)(2,1)}, bf16[2,1024,512]{2,1,0:T(8,128)(2,1)}, bf16[2,1024,512]{2,1,0:T(8,128)(2,1)}, bf16[2,1024,512]{2,1,0:T(8,...) custom-call(s32[3,4]{1,0:T(4,128)} %get-tuple-element.436.table_ref, bf16[512,1024]{1,0:T(8,128)(2,1)} %get-tuple-element.171.refs_0_, ...), custom_call_target="tpu_custom_call" | custom-call | tf_op jit(solution)/shard_map/feed_back/pallas_call | solution.py:91
  232.8 23.5 %feed_back.3 = (bf16[4,1024,512]{2,1,0:T(8,128)(2,1)}, bf16[4,1024,512]{2,1,0:T(8,128)(2,1)}, f32[4,1,512]{2,1,0:T(1,128)}, f32[512,1024]{1,0:T(8,128)}, bf16[51...) custom-call(s32[3,4]{1,0:T(4,128)} %get-tuple-element.435.table_ref, ...), custom_call_target="tpu_custom_call" | custom-call | tf_op jit(solution)/shard_map/feed_back/pallas_call | solution.py:91
  257.7 4.2 d_shrink.3
  262.7 3.4 d_expand.3
  267.4 8.1 %attended_back.1.refs_1_ = bf16[8,512,128]{2,1,0:T(8,128)(2,1)} custom-call(s32[2,8]{1,0:T(2,128)} %copy-done.64, bf16[512,1024]{1,0:T(8,128)(2,1)} %get-tuple-element.181.a, bf16[4,1024,2304]{2,1,0:T(8,128)(2,1)} %bitcast.223), custom_call_target="tpu_custom_call" | custom-call | tf_op jit(solution)/shard_map/attended_back/pallas_call | solution.py:91
  275.5 9.8 %attend_back.4 = (bf16[2,512,128]{2,1,0:T(8,128)(2,1)}, f32[2,512,256]{2,1,0:T(8,128)}, bf16[2,512,256]{2,1,0:T(8,128)(2,1)}, f32[2,1,128]{2,1,0:T(1,128)}) custom-call(bf16[2,512,128]{2,1,0:T(8,128)(2,1)} %get-tuple-element.182.refs_0_, bf16[8,512,128]{2,1,0:T(8,128)(2,1)} %attended_back.1.refs_1_, f32[2,2,512]{2,1,0:T(2,128)} %get-tuple-element.183.refs_2_, ...), custom_call_target="tpu_custom_call" | custom-call | tf_op jit(solution)/shard_map/attend_back/pallas_call | solution.py:91
  285.4 10.0 %attend_back.5 = (bf16[2,512,128]{2,1,0:T(8,128)(2,1)}, f32[2,512,256]{2,1,0:T(8,128)}, bf16[2,512,256]{2,1,0:T(8,128)(2,1)}, f32[2,1,128]{2,1,0:T(1,128)}) custom-call(bf16[2,512,128]{2,1,0:T(8,128)(2,1)} %get-tuple-element.185.refs_0_, bf16[8,512,128]{2,1,0:T(8,128)(2,1)} %attended_back.1.refs_1_, f32[2,2,512]{2,1,0:T(2,128)} %get-tuple-element.186.refs_2_, ...), custom_call_target="tpu_custom_call" | custom-call | tf_op jit(solution)/shard_map/attend_back/pallas_call | solution.py:91
  301.6 5.4 %d_in.5 = (bf16[1024,512]{1,0:T(8,128)(2,1)}, bf16[1024,512]{1,0:T(8,128)(2,1)}) custom-call(bf16[1024,512]{1,0:T(8,128)(2,1)} %get-tuple-element.239.refs_0_.refs_1_, bf16[1024,512]{1,0:T(8,128)(2,1)} %get-tuple-element.189.refs_1_.refs_2_, bf16[2,512,128]{2,1,0:T(8,128)(2,1)} %get-tuple-element.184.refs_2_.refs_3_, ...), custom_call_target="tpu_custom_call" | custom-call | tf_op jit(solution)/shard_map/d_in/pallas_call | solution.py:91
  307.0 3.2 collective-permute-done.36.refs_2_.refs_3_.refs_7_
  325.0 5.5 %d_in.6 = bf16[2,1024,512]{2,1,0:T(8,128)(2,1)} custom-call(bf16[1024,512]{1,0:T(8,128)(2,1)} %get-tuple-element.239.refs_0_.refs_1_, bf16[1024,512]{1,0:T(8,128)(2,1)} %get-tuple-element.189.refs_1_.refs_2_, bf16[2,512,128]{2,1,0:T(8,128)(2,1)} %get-tuple-element.187.refs_2_, bf16[2,512,256]{2,1,0:T(8,128)(2,1)} %add_convert_fusion.2.refs_3_.refs_6_, ...), custom_call_target="tpu_custom_call" | custom-call | tf_op jit(solution)/shard_map/d_in/pallas_call | solution.py:91
  331.2 9.8 %attend_back.6 = (bf16[2,512,128]{2,1,0:T(8,128)(2,1)}, f32[2,512,256]{2,1,0:T(8,128)}, bf16[2,512,256]{2,1,0:T(8,128)(2,1)}, f32[2,1,128]{2,1,0:T(1,128)}) custom-call(bf16[2,512,128]{2,1,0:T(8,128)(2,1)} %get-tuple-element.199.refs_0_, bf16[8,512,128]{2,1,0:T(8,128)(2,1)} %attended_back.1.refs_1_, f32[2,2,512]{2,1,0:T(2,128)} %get-tuple-element.200.refs_2_, ...), custom_call_target="tpu_custom_call" | custom-call | tf_op jit(solution)/shard_map/attend_back/pallas_call | solution.py:91
  341.0 4.9 collective-permute-done.42.refs_4_.refs_8_
  345.9 10.1 %attend_back.7 = (bf16[2,512,128]{2,1,0:T(8,128)(2,1)}, f32[2,512,256]{2,1,0:T(8,128)}, bf16[2,512,256]{2,1,0:T(8,128)(2,1)}, f32[2,1,128]{2,1,0:T(1,128)}) custom-call(bf16[2,512,128]{2,1,0:T(8,128)(2,1)} %get-tuple-element.202.refs_0_, bf16[8,512,128]{2,1,0:T(8,128)(2,1)} %attended_back.1.refs_1_, f32[2,2,512]{2,1,0:T(2,128)} %get-tuple-element.203.refs_2_, ...), custom_call_target="tpu_custom_call" | custom-call | tf_op jit(solution)/shard_map/attend_back/pallas_call | solution.py:91
  359.2 3.5 d_shrink.5
  362.7 3.6 d_expand.5
  366.3 6.4 %collective-permute-start.44 = (bf16[512,512]{1,0:T(8,128)(2,1)S(1)}, bf16[512,512]{1,0:T(8,128)(2,1)S(1)}, u32[]{:S(2)}, u32[]{:S(2)}) collective-permute-start(bf16[512,512]{1,0:T(8,128)(2,1)S(1)} %copy-done.41), channel_id=1, source_target_pairs={{0,1},{3,2},{4,5},{7,6},{8,9},{11,10},{12,13},{15,14},{16,17},{19,... | collective-permute-start | bytes 1572872 | tf_op jit(solution)/shard_map/ppermute | solution.py:1094
  373.7 5.5 %d_in.7 = (bf16[1024,512]{1,0:T(8,128)(2,1)}, bf16[1024,512]{1,0:T(8,128)(2,1)}) custom-call(bf16[1024,512]{1,0:T(8,128)(2,1)} %get-tuple-element.239.refs_0_.refs_1_, bf16[1024,512]{1,0:T(8,128)(2,1)} %get-tuple-element.189.refs_1_.refs_2_, bf16[2,512,128]{2,1,0:T(8,128)(2,1)} %get-tuple-element.201.refs_2_.refs_1_, ...), custom_call_target="tpu_custom_call" | custom-call | tf_op jit(solution)/shard_map/d_in/pallas_call | solution.py:91
  381.8 3.2 collective-permute-done.44
  391.3 4.3 d_in.8
  398.5 11.3 %tokens_back.1 = (bf16[512,1024]{1,0:T(8,128)(2,1)}, f32[2,1024]{1,0:T(2,128)}) custom-call(bf16[2,512,128]{2,1,0:T(8,128)(2,1)} %get-tuple-element.221.refs_2_.refs_0_.refs_3_, bf16[2,512,128]{2,1,0:T(8,128)(2,1)} %get-tuple-element.201.refs_2_.refs_1_, bf16[2,512,128]{2,1,0:T(8,128)(2,1)} %get-tuple-element.187.refs_2_, ...), custom_call_target="tpu_custom_call" | custom-call | tf_op jit(solution)/shard_map/tokens_back/pallas_call | solution.py:91
  412.8 3.7 collective-permute-start.73
  421.0 8.5 %collective-permute-done.73 = bf16[256,512]{1,0:T(8,128)(2,1)S(1)} collective-permute-done((bf16[256,512]{1,0:T(8,128)(2,1)}, bf16[256,512]{1,0:T(8,128)(2,1)S(1)}, u32[]{:S(2)}, u32[]{:S(2)}) %collective-permute-start.73) | collective-permute-done | bytes 262176 | tf_op jit(solution)/shard_map/ppermute | solution.py:908
  436.0 5.0 collective-permute-done.51
  444.8 10.9 %collective-permute-start.71 = (bf16[256,512]{1,0:T(8,128)(2,1)}, bf16[256,512]{1,0:T(8,128)(2,1)}, u32[]{:S(2)}, u32[]{:S(2)}) collective-permute-start(bf16[256,512]{1,0:T(8,128)(2,1)} %get-tuple-element.247), channel_id=1, source_target_pairs={{0,1},{1,0},{2,3},{3,2},{4,5},{5,4},{6,7},{7,6},{8,9},{9,8},{10,11... | collective-permute-start | bytes 786440 | tf_op jit(solution)/shard_map/ppermute | solution.py:908
  457.2 3.2 collective-permute-done.71
  469.3 3.1 collective-permute-done.56
  480.0 5.6 %d_in.9 = (bf16[512,512]{1,0:T(8,128)(2,1)}, bf16[512,512]{1,0:T(8,128)(2,1)}) custom-call(s32[2,1]{1,0:T(2,128)} %broadcast_in_dim.94.refs_0_, bf16[1024,512]{1,0:T(8,128)(2,1)} %get-tuple-element.239.refs_0_.refs_1_, bf16[1024,512]{1,0:T(8,128)(2,1)} %get-tuple-element.189.refs_1_.refs_2_, bf16[2,512,128]{2,1,0:T(8,128)(2,1)} %get-tuple-element.221.refs_2_.refs_0_.refs_3_, ...), custom_call_target="tpu_custom_call" | custom-call | tf_op jit(solution)/shard_map/d_in/pallas_call | solution.py:91
  485.6 4.0 collective-permute-start.67
  494.7 4.4 collective-permute-done.67
  505.6 13.9 %collective-permute-start.69 = (bf16[256,512]{1,0:T(8,128)(2,1)}, bf16[256,512]{1,0:T(8,128)(2,1)S(1)}, u32[]{:S(2)}, u32[]{:S(2)}) collective-permute-start(bf16[256,512]{1,0:T(8,128)(2,1)} %get-tuple-element.246), channel_id=1, source_target_pairs={{0,1},{1,0},{2,3},{3,2},{4,5},{5,4},{6,7},{7,6},{8,9},{9,8},{10,11... | collective-permute-start | bytes 786440 | tf_op jit(solution)/shard_map/ppermute | solution.py:908
  528.2 3.3 collective-permute-done.70
  (514 shorter events, 158.7 us)
Async XLA Ops:
  7.2 174.3 %all-gather.2.cloned.1.call-start = ((), (), s32[]{:S(2)}) async-start(), calls=%async_computation | async-start | bytes 20054016 | tf_op jit(solution)/shard_map/all_gather | solution.py:805
  16.3 17.4 %collective-permute-start = (bf16[2,512,256]{2,1,0:T(8,128)(2,1)S(1)}, bf16[2,512,256]{2,1,0:T(8,128)(2,1)S(1)}, u32[]{:S(2)}, u32[]{:S(2)}) collective-permute-start(bf16[2,512,256]{2,1,0:T(8,128)(2,1)S(1)} %get-tuple-element.358), channel_id=1, source_target_pairs={{0,4},{4,0},{1,5},{5,1},{2,6},{6,2},{3,7},{7,3},{8,12},{12,8},{9,1... | collective-permute-start | bytes 1572872 | tf_op jit(solution)/shard_map/ppermute | solution.py:905
  28.2 24.4 %collective-permute-start.2 = (bf16[512,384]{1,0:T(8,128)(2,1)S(1)}, bf16[512,384]{1,0:T(8,128)(2,1)S(1)}, u32[]{:S(2)}, u32[]{:S(2)}) collective-permute-start(bf16[512,384]{1,0:T(8,128)(2,1)S(1)} %pad_maximum_fusion.16), channel_id=1, source_target_pairs={{0,2},{1,3},{2,0},{3,1},{4,6},{5,7},{6,4},{7,5},{8,10},{9,11},{10,... | collective-permute-start | bytes 1179656 | tf_op jit(solution)/shard_map/ppermute | solution.py:908
  56.8 26.8 %collective-permute-start.4 = (bf16[512,256]{1,0:T(8,128)(2,1)S(1)}, bf16[512,256]{1,0:T(8,128)(2,1)S(1)}, u32[]{:S(2)}, u32[]{:S(2)}) collective-permute-start(bf16[512,256]{1,0:T(8,128)(2,1)S(1)} %get-tuple-element.355), channel_id=1, source_target_pairs={{0,2},{1,3},{2,0},{3,1},{4,6},{5,7},{6,4},{7,5},{8,10},{9,11},{10,... | collective-permute-start | bytes 786440 | tf_op jit(solution)/shard_map/ppermute | solution.py:908
  56.8 26.8 %collective-permute-start.5 = (bf16[512,256]{1,0:T(8,128)(2,1)S(1)}, bf16[512,256]{1,0:T(8,128)(2,1)S(1)}, u32[]{:S(2)}, u32[]{:S(2)}) collective-permute-start(bf16[512,256]{1,0:T(8,128)(2,1)S(1)} %get-tuple-element.354), channel_id=1, source_target_pairs={{0,1},{1,0},{2,3},{3,2},{4,5},{5,4},{6,7},{7,6},{8,9},{9,8},{10,11... | collective-permute-start | bytes 786440 | tf_op jit(solution)/shard_map/ppermute | solution.py:908
  59.1 25.7 %collective-permute-start.13 = (bf16[1024,256]{1,0:T(8,128)(2,1)S(1)}, bf16[1024,256]{1,0:T(8,128)(2,1)S(1)}, u32[]{:S(2)}, u32[]{:S(2)}) collective-permute-start(bf16[1024,256]{1,0:T(8,128)(2,1)S(1)} %get-tuple-element.360), channel_id=1, source_target_pairs={{0,8},{8,0},{1,9},{9,1},{2,10},{10,2},{3,11},{11,3},{4,12},{12,4},... | collective-permute-start | bytes 1572872 | tf_op jit(solution)/shard_map/ppermute | solution.py:905
  84.9 24.6 %collective-permute-start.16 = (bf16[2,1024,256]{2,1,0:T(8,128)(2,1)S(1)}, bf16[2,1024,256]{2,1,0:T(8,128)(2,1)}, u32[]{:S(2)}, u32[]{:S(2)}) collective-permute-start(bf16[2,1024,256]{2,1,0:T(8,128)(2,1)S(1)} %pad_maximum_fusion.3.h.refs_12_), channel_id=1, source_target_pairs={{0,16},{16,0},{1,17},{17,1},{2,18},{18,2},{3,19},{19,3},{4,20},{20... | collective-permute-start | bytes 3145736 | tf_op jit(solution)/shard_map/ppermute | solution.py:905
  86.0 18.1 %collective-permute-start.12 = (bf16[2,1024,128]{2,1,0:T(8,128)(2,1)S(1)}, bf16[2,1024,128]{2,1,0:T(8,128)(2,1)S(1)}, u32[]{:S(2)}, u32[]{:S(2)}) collective-permute-start(bf16[2,1024,128]{2,1,0:T(8,128)(2,1)S(1)} %copy-done.43), channel_id=1, source_target_pairs={{0,8},{8,0},{1,9},{9,1},{2,10},{10,2},{3,11},{11,3},{4,12},{12,4},... | collective-permute-start | bytes 1572872 | tf_op jit(solution)/shard_map/ppermute | solution.py:905
  92.1 26.7 %collective-permute-start.15 = (bf16[2,1024,256]{2,1,0:T(8,128)(2,1)S(1)}, bf16[2,1024,256]{2,1,0:T(8,128)(2,1)}, u32[]{:S(2)}, u32[]{:S(2)}) collective-permute-start(bf16[2,1024,256]{2,1,0:T(8,128)(2,1)S(1)} %pad_maximum_fusion.3.h.refs_12_), channel_id=1, source_target_pairs={{0,4},{4,0},{1,5},{5,1},{2,6},{6,2},{3,7},{7,3},{8,12},{12,8},{9,1... | collective-permute-start | bytes 3145736 | tf_op jit(solution)/shard_map/ppermute | solution.py:905
  109.5 21.2 %collective-permute-start.18 = (bf16[2,1024,256]{2,1,0:T(8,128)(2,1)}, bf16[2,1024,256]{2,1,0:T(8,128)(2,1)}, u32[]{:S(2)}, u32[]{:S(2)}) collective-permute-start(bf16[2,1024,256]{2,1,0:T(8,128)(2,1)} %collective-permute-done.16.h.refs_14_), channel_id=1, source_target_pairs={{0,4},{4,0},{1,5},{5,1},{2,6},{6,2},{3,7},{7,3},{8,12},{12,8},{9,1... | collective-permute-start | bytes 3145736 | tf_op jit(solution)/shard_map/ppermute | solution.py:905
  111.1 19.5 %collective-permute-start.17 = (bf16[2,1024,128]{2,1,0:T(8,128)(2,1)S(1)}, bf16[2,1024,128]{2,1,0:T(8,128)(2,1)}, u32[]{:S(2)}, u32[]{:S(2)}) collective-permute-start(bf16[2,1024,128]{2,1,0:T(8,128)(2,1)S(1)} %pad_maximum_fusion.11.g.refs_10_), channel_id=1, source_target_pairs={{0,4},{4,0},{1,5},{5,1},{2,6},{6,2},{3,7},{7,3},{8,12},{12,8},{9,1... | collective-permute-start | bytes 1572872 | tf_op jit(solution)/shard_map/ppermute | solution.py:905
  116.5 19.0 %collective-permute-start.21 = (bf16[512,256]{1,0:T(8,128)(2,1)S(1)}, bf16[512,256]{1,0:T(8,128)(2,1)S(1)}, u32[]{:S(2)}, u32[]{:S(2)}) collective-permute-start(bf16[512,256]{1,0:T(8,128)(2,1)S(1)} %get-tuple-element.350), channel_id=1, source_target_pairs={{0,3},{1,2},{2,1},{3,0},{4,7},{5,6},{6,5},{7,4},{8,11},{9,10},{10,... | collective-permute-start | bytes 786440 | tf_op jit(solution)/shard_map/ppermute | solution.py:908
  118.8 26.9 %collective-permute-start.22 = (bf16[512,256]{1,0:T(8,128)(2,1)S(1)}, bf16[512,256]{1,0:T(8,128)(2,1)S(1)}, u32[]{:S(2)}, u32[]{:S(2)}) collective-permute-start(bf16[512,256]{1,0:T(8,128)(2,1)S(1)} %get-tuple-element.351), channel_id=1, source_target_pairs={{0,2},{1,3},{2,0},{3,1},{4,6},{5,7},{6,4},{7,5},{8,10},{9,11},{10,... | collective-permute-start | bytes 786440 | tf_op jit(solution)/shard_map/ppermute | solution.py:908
  118.8 26.9 %collective-permute-start.23 = (bf16[512,256]{1,0:T(8,128)(2,1)S(1)}, bf16[512,256]{1,0:T(8,128)(2,1)S(1)}, u32[]{:S(2)}, u32[]{:S(2)}) collective-permute-start(bf16[512,256]{1,0:T(8,128)(2,1)S(1)} %get-tuple-element.349), channel_id=1, source_target_pairs={{0,1},{1,0},{2,3},{3,2},{4,5},{5,4},{6,7},{7,6},{8,9},{9,8},{10,11... | collective-permute-start | bytes 786440 | tf_op jit(solution)/shard_map/ppermute | solution.py:908
  130.6 24.2 %collective-permute-start.24 = (bf16[2,512,256]{2,1,0:T(8,128)(2,1)S(1)}, bf16[2,512,256]{2,1,0:T(8,128)(2,1)S(1)}, u32[]{:S(2)}, u32[]{:S(2)}) collective-permute-start(bf16[2,512,256]{2,1,0:T(8,128)(2,1)S(1)} %copy-done.18), channel_id=1, source_target_pairs={{0,4},{4,0},{1,5},{5,1},{2,6},{6,2},{3,7},{7,3},{8,12},{12,8},{9,1... | collective-permute-start | bytes 1572872 | tf_op jit(solution)/shard_map/ppermute | solution.py:905
  130.7 16.4 %collective-permute-start.19 = (bf16[2,512,256]{2,1,0:T(8,128)(2,1)S(1)}, bf16[2,512,256]{2,1,0:T(8,128)(2,1)S(1)}, u32[]{:S(2)}, u32[]{:S(2)}) collective-permute-start(bf16[2,512,256]{2,1,0:T(8,128)(2,1)S(1)} %copy-done.19), channel_id=1, source_target_pairs={{0,4},{4,0},{1,5},{5,1},{2,6},{6,2},{3,7},{7,3},{8,12},{12,8},{9,1... | collective-permute-start | bytes 1572872 | tf_op jit(solution)/shard_map/ppermute | solution.py:905
  135.5 34.6 %collective-permute-start.26 = (bf16[2,512,256]{2,1,0:T(8,128)(2,1)S(1)}, bf16[2,512,256]{2,1,0:T(8,128)(2,1)S(1)}, u32[]{:S(2)}, u32[]{:S(2)}) collective-permute-start(bf16[2,512,256]{2,1,0:T(8,128)(2,1)S(1)} %copy-done.22), channel_id=1, source_target_pairs={{0,4},{4,0},{1,5},{5,1},{2,6},{6,2},{3,7},{7,3},{8,12},{12,8},{9,1... | collective-permute-start | bytes 1572872 | tf_op jit(solution)/shard_map/ppermute | solution.py:905
  145.7 16.7 %collective-permute-start.25 = (bf16[2,512,256]{2,1,0:T(8,128)(2,1)}, bf16[2,512,256]{2,1,0:T(8,128)(2,1)S(1)}, u32[]{:S(2)}, u32[]{:S(2)}) collective-permute-start(bf16[2,512,256]{2,1,0:T(8,128)(2,1)} %get-tuple-element.152.refs_1_.refs_3_), channel_id=1, source_target_pairs={{0,4},{4,0},{1,5},{5,1},{2,6},{6,2},{3,7},{7,3},{8,12},{12,8},{9,1... | collective-permute-start | bytes 1572872 | tf_op jit(solution)/shard_map/ppermute | solution.py:905
  230.7 25.6 %collective-permute-start.31 = (bf16[2,1024,512]{2,1,0:T(8,128)(2,1)}, bf16[2,1024,512]{2,1,0:T(8,128)(2,1)S(1)}, u32[]{:S(2)}, u32[]{:S(2)}) collective-permute-start(bf16[2,1024,512]{2,1,0:T(8,128)(2,1)} %get-tuple-element.170), channel_id=1, source_target_pairs={{0,4},{4,0},{1,5},{5,1},{2,6},{6,2},{3,7},{7,3},{8,12},{12,8},{9,1... | collective-permute-start | bytes 6291464 | tf_op jit(solution)/shard_map/ppermute | solution.py:905
  232.2 24.1 %collective-permute-start.32 = (bf16[2,1024,512]{2,1,0:T(8,128)(2,1)}, bf16[2,1024,512]{2,1,0:T(8,128)(2,1)S(1)}, u32[]{:S(2)}, u32[]{:S(2)}) collective-permute-start(bf16[2,1024,512]{2,1,0:T(8,128)(2,1)} %get-tuple-element.176), channel_id=1, source_target_pairs={{0,4},{4,0},{1,5},{5,1},{2,6},{6,2},{3,7},{7,3},{8,12},{12,8},{9,1... | collective-permute-start | bytes 6291464 | tf_op jit(solution)/shard_map/ppermute | solution.py:905
  232.3 24.1 %collective-permute-start.33 = (bf16[2,1024,512]{2,1,0:T(8,128)(2,1)}, bf16[2,1024,512]{2,1,0:T(8,128)(2,1)S(1)}, u32[]{:S(2)}, u32[]{:S(2)}) collective-permute-start(bf16[2,1024,512]{2,1,0:T(8,128)(2,1)} %get-tuple-element.177), channel_id=1, source_target_pairs={{0,4},{4,0},{1,5},{5,1},{2,6},{6,2},{3,7},{7,3},{8,12},{12,8},{9,1... | collective-permute-start | bytes 6291464 | tf_op jit(solution)/shard_map/ppermute | solution.py:905
  232.7 23.7 %collective-permute-start.34 = (bf16[2,1024,512]{2,1,0:T(8,128)(2,1)}, bf16[2,1024,512]{2,1,0:T(8,128)(2,1)}, u32[]{:S(2)}, u32[]{:S(2)}) collective-permute-start(bf16[2,1024,512]{2,1,0:T(8,128)(2,1)} %get-tuple-element.178), channel_id=1, source_target_pairs={{0,4},{4,0},{1,5},{5,1},{2,6},{6,2},{3,7},{7,3},{8,12},{12,8},{9,1... | collective-permute-start | bytes 6291464 | tf_op jit(solution)/shard_map/ppermute | solution.py:905
  261.9 48.3 %collective-permute-start.36 = (bf16[2,1024,512]{2,1,0:T(8,128)(2,1)}, bf16[2,1024,512]{2,1,0:T(8,128)(2,1)}, u32[]{:S(2)}, u32[]{:S(2)}) collective-permute-start(bf16[2,1024,512]{2,1,0:T(8,128)(2,1)} %d_shrink.3), channel_id=1, source_target_pairs={{0,16},{16,0},{1,17},{17,1},{2,18},{18,2},{3,19},{19,3},{4,20},{20... | collective-permute-start | bytes 6291464 | tf_op jit(solution)/shard_map/ppermute | solution.py:905
  266.1 47.9 %collective-permute-start.37 = (bf16[2,1024,512]{2,1,0:T(8,128)(2,1)}, bf16[2,1024,512]{2,1,0:T(8,128)(2,1)S(1)}, u32[]{:S(2)}, u32[]{:S(2)}) collective-permute-start(bf16[2,1024,512]{2,1,0:T(8,128)(2,1)} %d_expand.3), channel_id=1, source_target_pairs={{0,8},{8,0},{1,9},{9,1},{2,10},{10,2},{3,11},{11,3},{4,12},{12,4},... | collective-permute-start | bytes 6291464 | tf_op jit(solution)/shard_map/ppermute | solution.py:905
  296.1 22.1 %collective-permute-start.27 = (bf16[512,256]{1,0:T(8,128)(2,1)S(1)}, bf16[512,256]{1,0:T(8,128)(2,1)S(1)}, u32[]{:S(2)}, u32[]{:S(2)}) collective-permute-start(bf16[512,256]{1,0:T(8,128)(2,1)S(1)} %get-tuple-element.343), channel_id=1, source_target_pairs={{0,1},{1,0},{2,3},{3,2},{4,5},{5,4},{6,7},{7,6},{8,9},{9,8},{10,11... | collective-permute-start | bytes 786440 | tf_op jit(solution)/shard_map/ppermute | solution.py:908
  297.2 21.3 %collective-permute-start.28 = (bf16[512,256]{1,0:T(8,128)(2,1)S(1)}, bf16[512,256]{1,0:T(8,128)(2,1)S(1)}, u32[]{:S(2)}, u32[]{:S(2)}) collective-permute-start(bf16[512,256]{1,0:T(8,128)(2,1)S(1)} %get-tuple-element.344), channel_id=1, source_target_pairs={{0,2},{1,3},{2,0},{3,1},{4,6},{5,7},{6,4},{7,5},{8,10},{9,11},{10,... | collective-permute-start | bytes 786440 | tf_op jit(solution)/shard_map/ppermute | solution.py:908
  299.3 20.3 %collective-permute-start.29 = (bf16[512,256]{1,0:T(8,128)(2,1)S(1)}, bf16[512,256]{1,0:T(8,128)(2,1)S(1)}, u32[]{:S(2)}, u32[]{:S(2)}) collective-permute-start(bf16[512,256]{1,0:T(8,128)(2,1)S(1)} %get-tuple-element.345), channel_id=1, source_target_pairs={{0,3},{1,2},{2,1},{3,0},{4,7},{5,6},{6,5},{7,4},{8,11},{9,10},{10,... | collective-permute-start | bytes 786440 | tf_op jit(solution)/shard_map/ppermute | solution.py:908
  318.6 27.4 %collective-permute-start.41 = (bf16[1,1024,512]{2,1,0:T(8,128)(2,1)S(1)}, bf16[1,1024,512]{2,1,0:T(8,128)(2,1)}, u32[]{:S(2)}, u32[]{:S(2)}) collective-permute-start(bf16[1,1024,512]{2,1,0:T(8,128)(2,1)S(1)} %copy-done.25), channel_id=1, source_target_pairs={{0,8},{8,0},{1,9},{9,1},{2,10},{10,2},{3,11},{11,3},{4,12},{12,4},... | collective-permute-start | bytes 3145736 | tf_op jit(solution)/shard_map/ppermute | solution.py:905
  319.6 26.3 %collective-permute-start.42 = (bf16[1,1024,512]{2,1,0:T(8,128)(2,1)}, bf16[1,1024,512]{2,1,0:T(8,128)(2,1)}, u32[]{:S(2)}, u32[]{:S(2)}) collective-permute-start(bf16[1,1024,512]{2,1,0:T(8,128)(2,1)} %d_expand.4), channel_id=1, source_target_pairs={{0,16},{16,0},{1,17},{17,1},{2,18},{18,2},{3,19},{19,3},{4,20},{20... | collective-permute-start | bytes 3145736 | tf_op jit(solution)/shard_map/ppermute | solution.py:905
  322.7 33.4 %collective-permute-start.30 = (bf16[2,512,256]{2,1,0:T(8,128)(2,1)}, bf16[2,512,256]{2,1,0:T(8,128)(2,1)}, u32[]{:S(2)}, u32[]{:S(2)}) collective-permute-start(bf16[2,512,256]{2,1,0:T(8,128)(2,1)} %pad_maximum_fusion.13), channel_id=1, source_target_pairs={{0,4},{4,0},{1,5},{5,1},{2,6},{6,2},{3,7},{7,3},{8,12},{12,8},{9,1... | collective-permute-start | bytes 1572872 | tf_op jit(solution)/shard_map/ppermute | solution.py:905
  330.5 59.5 %collective-permute-start.47 = (bf16[2,1024,512]{2,1,0:T(8,128)(2,1)}, bf16[2,1024,512]{2,1,0:T(8,128)(2,1)S(1)}, u32[]{:S(2)}, u32[]{:S(2)}) collective-permute-start(bf16[2,1024,512]{2,1,0:T(8,128)(2,1)} %d_in.6), channel_id=1, source_target_pairs={{0,16},{16,0},{1,17},{17,1},{2,18},{18,2},{3,19},{19,3},{4,20},{20... | collective-permute-start | bytes 6291464 | tf_op jit(solution)/shard_map/ppermute | solution.py:905
  356.0 16.7 %collective-permute-start.43 = (bf16[2,512,256]{2,1,0:T(8,128)(2,1)}, bf16[2,512,256]{2,1,0:T(8,128)(2,1)S(1)}, u32[]{:S(2)}, u32[]{:S(2)}) collective-permute-start(bf16[2,512,256]{2,1,0:T(8,128)(2,1)} %get-tuple-element.213), channel_id=1, source_target_pairs={{0,4},{4,0},{1,5},{5,1},{2,6},{6,2},{3,7},{7,3},{8,12},{12,8},{9,1... | collective-permute-start | bytes 1572872 | tf_op jit(solution)/shard_map/ppermute | solution.py:905
  358.7 22.9 %collective-permute-start.45 = (bf16[2,512,256]{2,1,0:T(8,128)(2,1)S(1)}, bf16[2,512,256]{2,1,0:T(8,128)(2,1)S(1)}, u32[]{:S(2)}, u32[]{:S(2)}) collective-permute-start(bf16[2,512,256]{2,1,0:T(8,128)(2,1)S(1)} %copy-done.74), channel_id=1, source_target_pairs={{0,4},{4,0},{1,5},{5,1},{2,6},{6,2},{3,7},{7,3},{8,12},{12,8},{9,1... | collective-permute-start | bytes 1572872 | tf_op jit(solution)/shard_map/ppermute | solution.py:905
  366.3 18.7 %collective-permute-start.44 = (bf16[512,512]{1,0:T(8,128)(2,1)S(1)}, bf16[512,512]{1,0:T(8,128)(2,1)S(1)}, u32[]{:S(2)}, u32[]{:S(2)}) collective-permute-start(bf16[512,512]{1,0:T(8,128)(2,1)S(1)} %copy-done.41), channel_id=1, source_target_pairs={{0,1},{3,2},{4,5},{7,6},{8,9},{11,10},{12,13},{15,14},{16,17},{19,... | collective-permute-start | bytes 1572872 | tf_op jit(solution)/shard_map/ppermute | solution.py:1094
  379.3 17.1 %collective-permute-start.48 = (bf16[512,512]{1,0:T(8,128)(2,1)}, bf16[512,512]{1,0:T(8,128)(2,1)}, u32[]{:S(2)}, u32[]{:S(2)}) collective-permute-start(bf16[512,512]{1,0:T(8,128)(2,1)} %get-tuple-element.208), channel_id=1, source_target_pairs={{0,1},{3,2},{4,5},{7,6},{8,9},{11,10},{12,13},{15,14},{16,17},{19,... | collective-permute-start | bytes 1572872 | tf_op jit(solution)/shard_map/ppermute | solution.py:1094
  387.9 22.0 %collective-permute-start.64 = (bf16[512,512]{1,0:T(8,128)(2,1)}, bf16[512,512]{1,0:T(8,128)(2,1)S(1)}, u32[]{:S(2)}, u32[]{:S(2)}) collective-permute-start(bf16[512,512]{1,0:T(8,128)(2,1)} %bitcast.259), channel_id=1, source_target_pairs={{1,2},{2,1},{5,6},{6,5},{9,10},{10,9},{13,14},{14,13},{17,18},{18,... | collective-permute-start | bytes 1572872 | tf_op jit(solution)/shard_map/ppermute | solution.py:1097
  395.6 66.8 %collective-permute-start.53 = (bf16[1,1024,512]{2,1,0:T(8,128)(2,1)}, bf16[1,1024,512]{2,1,0:T(8,128)(2,1)}, u32[]{:S(2)}, u32[]{:S(2)}) collective-permute-start(bf16[1,1024,512]{2,1,0:T(8,128)(2,1)} %d_in.8), channel_id=1, source_target_pairs={{0,8},{8,0},{1,9},{9,1},{2,10},{10,2},{3,11},{11,3},{4,12},{12,4},... | collective-permute-start | bytes 3145736 | tf_op jit(solution)/shard_map/ppermute | solution.py:905
  412.8 16.7 %collective-permute-start.73 = (bf16[256,512]{1,0:T(8,128)(2,1)}, bf16[256,512]{1,0:T(8,128)(2,1)S(1)}, u32[]{:S(2)}, u32[]{:S(2)}) collective-permute-start(bf16[256,512]{1,0:T(8,128)(2,1)} %get-tuple-element.248), channel_id=1, source_target_pairs={{0,1},{1,0},{2,3},{3,2},{4,5},{5,4},{6,7},{7,6},{8,9},{9,8},{10,11... | collective-permute-start | bytes 786440 | tf_op jit(solution)/shard_map/ppermute | solution.py:908
  416.6 18.1 %collective-permute-start.50 = (bf16[512,256]{1,0:T(8,128)(2,1)S(1)}, bf16[512,256]{1,0:T(8,128)(2,1)S(1)}, u32[]{:S(2)}, u32[]{:S(2)}) collective-permute-start(bf16[512,256]{1,0:T(8,128)(2,1)S(1)} %get-tuple-element.334), channel_id=1, source_target_pairs={{0,2},{1,3},{2,0},{3,1},{4,6},{5,7},{6,4},{7,5},{8,10},{9,11},{10,... | collective-permute-start | bytes 786440 | tf_op jit(solution)/shard_map/ppermute | solution.py:908
  419.5 21.4 %collective-permute-start.51 = (bf16[512,256]{1,0:T(8,128)(2,1)S(1)}, bf16[512,256]{1,0:T(8,128)(2,1)S(1)}, u32[]{:S(2)}, u32[]{:S(2)}) collective-permute-start(bf16[512,256]{1,0:T(8,128)(2,1)S(1)} %get-tuple-element.335), channel_id=1, source_target_pairs={{0,3},{1,2},{2,1},{3,0},{4,7},{5,6},{6,5},{7,4},{8,11},{9,10},{10,... | collective-permute-start | bytes 786440 | tf_op jit(solution)/shard_map/ppermute | solution.py:908
  432.7 46.4 %collective-permute-start.66 = (bf16[1024,512]{1,0:T(8,128)(2,1)}, bf16[1024,512]{1,0:T(8,128)(2,1)S(1)}, u32[]{:S(2)}, u32[]{:S(2)}) collective-permute-start(bf16[1024,512]{1,0:T(8,128)(2,1)} %get-tuple-element.214), channel_id=1, source_target_pairs={{0,4},{4,0},{1,5},{5,1},{2,6},{6,2},{3,7},{7,3},{8,12},{12,8},{9,1... | collective-permute-start | bytes 3145736 | tf_op jit(solution)/shard_map/ppermute | solution.py:905
  434.7 21.1 %collective-permute-start.74 = (bf16[256,512]{1,0:T(8,128)(2,1)S(1)}, bf16[256,512]{1,0:T(8,128)(2,1)S(1)}, u32[]{:S(2)}, u32[]{:S(2)}) collective-permute-start(bf16[256,512]{1,0:T(8,128)(2,1)S(1)} %add_convert_fusion.4), channel_id=1, source_target_pairs={{0,16},{16,0},{1,17},{17,1},{2,18},{18,2},{3,19},{19,3},{4,20},{20... | collective-permute-start | bytes 786440 | tf_op jit(solution)/shard_map/ppermute | solution.py:905
  442.0 20.6 %collective-permute-start.52 = (bf16[2,512,256]{2,1,0:T(8,128)(2,1)}, bf16[2,512,256]{2,1,0:T(8,128)(2,1)}, u32[]{:S(2)}, u32[]{:S(2)}) collective-permute-start(bf16[2,512,256]{2,1,0:T(8,128)(2,1)} %pad_maximum_fusion.15), channel_id=1, source_target_pairs={{0,4},{4,0},{1,5},{5,1},{2,6},{6,2},{3,7},{7,3},{8,12},{12,8},{9,1... | collective-permute-start | bytes 1572872 | tf_op jit(solution)/shard_map/ppermute | solution.py:905
  472.8 16.8 %collective-permute-start.58 = (f32[64,128]{1,0:T(8,128)S(1)}, f32[64,128]{1,0:T(8,128)S(1)}, u32[]{:S(2)}, u32[]{:S(2)}) collective-permute-start(f32[64,128]{1,0:T(8,128)S(1)} %get-tuple-element.407), channel_id=1, source_target_pairs={{0,2},{1,3},{2,0},{3,1},{4,6},{5,7},{6,4},{7,5},{8,10},{9,11},{10,... | collective-permute-start | bytes 98312 | tf_op jit(solution)/shard_map/ppermute | solution.py:908
  490.2 31.6 %collective-permute-start.60 = (f32[8,256]{1,0:T(8,128)S(1)}, f32[8,256]{1,0:T(8,128)S(1)}, u32[]{:S(2)}, u32[]{:S(2)}) collective-permute-start(f32[8,256]{1,0:T(8,128)S(1)} %fusion.10), channel_id=1, source_target_pairs={{0,1},{1,0},{2,3},{3,2},{4,5},{5,4},{6,7},{7,6},{8,9},{9,8},{10,11... | collective-permute-start | bytes 24584 | tf_op jit(solution)/shard_map/ppermute | solution.py:908
  490.2 31.6 %collective-permute-start.61 = (f32[8,256]{1,0:T(8,128)S(1)}, f32[8,256]{1,0:T(8,128)S(1)}, u32[]{:S(2)}, u32[]{:S(2)}) collective-permute-start(f32[8,256]{1,0:T(8,128)S(1)} %fusion.10), channel_id=1, source_target_pairs={{0,2},{1,3},{2,0},{3,1},{4,6},{5,7},{6,4},{7,5},{8,10},{9,11},{10,... | collective-permute-start | bytes 24584 | tf_op jit(solution)/shard_map/ppermute | solution.py:908
  493.1 28.8 %collective-permute-start.62 = (f32[8,256]{1,0:T(8,128)S(1)}, f32[8,256]{1,0:T(8,128)S(1)}, u32[]{:S(2)}, u32[]{:S(2)}) collective-permute-start(f32[8,256]{1,0:T(8,128)S(1)} %fusion.10), channel_id=1, source_target_pairs={{0,3},{1,2},{2,1},{3,0},{4,7},{5,6},{6,5},{7,4},{8,11},{9,10},{10,... | collective-permute-start | bytes 24584 | tf_op jit(solution)/shard_map/ppermute | solution.py:908
  505.6 18.5 %collective-permute-start.69 = (bf16[256,512]{1,0:T(8,128)(2,1)}, bf16[256,512]{1,0:T(8,128)(2,1)S(1)}, u32[]{:S(2)}, u32[]{:S(2)}) collective-permute-start(bf16[256,512]{1,0:T(8,128)(2,1)} %get-tuple-element.246), channel_id=1, source_target_pairs={{0,1},{1,0},{2,3},{3,2},{4,5},{5,4},{6,7},{7,6},{8,9},{9,8},{10,11... | collective-permute-start | bytes 786440 | tf_op jit(solution)/shard_map/ppermute | solution.py:908
  (103 other events, 717.8 us)
Sparse Core Ops, SparseCore 0:
  11.9 162.6 all-gather.1

commit v3 on v2

--- a/solution.py
+++ b/solution.py
@@ -101,6 +101,15 @@
 
 def shaped(shape, dtype):
     return jax.ShapeDtypeStruct(shape, dtype)
+
+
+def gate(values):
+    def kernel(given, out):
+        out[...] = given[...]
+
+    return call(
+        "gate", kernel, (1,), [whole(values.shape)], whole(values.shape), shaped(values.shape, values.dtype)
+    )(values)
 
 
 def project(left, query_blocks, kv_blocks, bias):
@@ -340,18 +349,22 @@
 
 
 def contract(name, terms, extras, finish, outs, table=None):
-    number, rows, _ = terms[0][0].shape
+    terms = [(left if isinstance(left, list) else [left], *more) for left, *more in terms]
+    number = max(len(left) * left[0].shape[0] for left, _, _ in terms)
+    rows = terms[0][0][0].shape[1]
     features = terms[0][1].shape[1]
     count, more = len(terms), len(extras)
+    given_lefts = [one for left, _, _ in terms for one in left]
 
     def kernel(*refs):
-        refs = refs if table is None else refs[1:]
-        lefts, rights = refs[:count], refs[count : 2 * count]
-        given = refs[2 * count : 2 * count + more]
-        results, total = refs[2 * count + more : -1], refs[-1]
-        out = dot_nt(lefts[0][...], rights[0][...])
+        refs = list(refs if table is None else refs[1:])
+        lefts = [chosen([refs.pop(0) for _ in left]) for left, _, _ in terms]
+        rights = refs[:count]
+        given = refs[count : count + more]
+        results, total = refs[count + more : -1], refs[-1]
+        out = dot_nt(lefts[0], rights[0][...])
         for left, right in zip(lefts[1:], rights[1:]):
-            out = out + dot_nt(left[...], right[...])
+            out = out + dot_nt(left, right[...])
         step = pl.program_id(0)
 
         @pl.when(step == 0)
@@ -370,14 +383,18 @@
         name,
         kernel,
         (number,),
-        [block(left.shape[1:]) for left, _, _ in terms]
-        + [where(features, left.shape[2]) for left, _, where in terms]
+        [
+            block(one.shape[1:], step=0 if len(left) > 1 else 1)
+            for left, _, _ in terms
+            for one in left
+        ]
+        + [where(features, left[0].shape[2]) for left, _, where in terms]
         + [fixed(extra.shape) for extra in extras],
         [whole(out.shape) for out in outs],
         outs,
         scratch=[pltpu.VMEM((rows, features), F32)],
         table=table,
-    )(*[left for left, _, _ in terms], *[right for _, right, _ in terms], *extras)
+    )(*given_lefts, *[right for _, right, _ in terms], *extras)
 
 
 def by_rows(rows, sums, features, work, tile=64):
@@ -541,16 +558,18 @@
     return found
 
 
-def gradients(name, pairs, count, first=0, table=None, adds=(), form="one"):
+def gradients(name, pairs, count, adds=(), form="one"):
     features, rows = pairs[0][0].shape
     parts = [one for _, parts in pairs for one in parts]
-    width = sum(one.shape[2] for one in parts)
+    width = sum(one.shape[2] for one, _ in parts)
     lefts, rights = len(pairs), len(parts)
-    given = [one for add in adds for one in add]
+    half = features // 2
+    split = [isinstance(add[0], list) for add in adds]
+    given = []
+    for add, two in zip(adds, split):
+        given += [(one[side][None], 0) for side in (0, 1) for one in add] if two else add
 
     def kernel(*refs):
-        if table is not None:
-            table_ref, *refs = refs
         left_refs = refs[:lefts]
         right_refs = list(refs[lefts : lefts + rights])
         add_refs = list(refs[lefts + rights : lefts + rights + len(given)])
@@ -560,31 +579,22 @@
             for _ in own:
                 found.append(dot(left[...], right_refs.pop(0)[...]))
         out = found[0] if len(found) == 1 else jnp.concatenate(found, axis=1)
-        for add in adds:
-            out = out + chosen([add_refs.pop(0) for _ in add]).astype(F32)
+        for add, two in zip(adds, split):
+            sides = [
+                chosen([add_refs.pop(0) for _ in add]).astype(F32)
+                for _ in range(2 if two else 1)
+            ]
+            out = out + (jnp.concatenate(sides, axis=0) if two else sides[0])
         out = out.astype(BF16)
         if form == "one":
             outs[0][...] = out
-        elif form == "apart":
-            for index, one in enumerate(outs):
+        else:
+            for index in range(count):
 
                 @pl.when(pl.program_id(0) == index)
                 def _():
-                    one[...] = out
-
-        else:
-            half = features // 2
-            for index in range(2):
-
-                @pl.when(table_ref[1, 0] == index)
-                def _():
-                    outs[index][...] = out[:half]
-                    outs[1 - index][...] = out[half:]
-
-    def right_spec(one):
-        if table is None or form == "halves" and first is not None:
-            return block(one.shape[1:], 0, first)
-        return tabled(one.shape[1:], (0, None))
+                    outs[2 * index][...] = out[:half]
+                    outs[2 * index + 1][...] = out[half:]
 
     def addend(one):
         array, index = one
@@ -593,19 +603,22 @@
     if form == "one":
         out_specs, shape = [block((features, width))], (count, features, width)
     else:
-        shape = (features // (2 if form == "halves" else 1), width)
-        out_specs = [whole(shape)] * (2 if form == "halves" else count)
+        shape = (half, width)
+        out_specs = [whole(shape)] * (2 * count)
     got = call(
         name,
         kernel,
         (count,),
         [fixed(left.shape) for left, _ in pairs]
-        + [right_spec(one) for one in parts]
+        + [block(one.shape[1:], 0, first) for one, first in parts]
         + [addend(one) for one in given],
         out_specs,
         [shaped(shape, BF16)] * len(out_specs),
-        table=table,
-    )(*[left for left, _ in pairs], *parts, *[array for array, _ in given])
+    )(
+        *[left for left, _ in pairs],
+        *[one for one, _ in parts],
+        *[array for array, _ in given],
+    )
     return got[0] if form == "one" else got
 
 
@@ -653,8 +666,8 @@
     )(queries, *pieces)
 
 
-def attend_back(queries, pieces, logs, incoming, first, kinds):
-    number, rows, _ = queries.shape
+def attend_back(queries, pieces, logs, incoming, first, kinds, begin, number):
+    rows = queries.shape[1]
     count = len(pieces)
     keys = sum(piece.shape[1] for piece in pieces)
     tile = min(rows, 256)
@@ -710,8 +723,12 @@
         "attend_back",
         kernel,
         (number,),
-        [block((rows, LANES)), block((rows, LANES), first=first), block((2, rows))]
-        + [block((piece.shape[1], 2 * LANES)) for piece in pieces],
+        [
+            block((rows, LANES), first=begin),
+            block((rows, LANES), first=first + begin),
+            block((2, rows), first=begin),
+        ]
+        + [block((piece.shape[1], 2 * LANES), first=begin) for piece in pieces],
         [block((rows, LANES))]
         + [block((piece.shape[1], 2 * LANES)) for piece in pieces]
         + [block((1, LANES))],
@@ -825,7 +842,7 @@
 
     PLACES = ((0, 0),)
 
-    def give_back(self, backs, x):
+    def give_back(self, backs):
         return [
             lax.psum_scatter(
                 backs[0][0], ("core", "sub"), scatter_dimension=1, tiled=True
@@ -855,8 +872,7 @@
         return steps, ends, [sums]
 
     def reduce(self, name, pairs):
-        pairs = pairs[0]()
-        grads = gradients(name, pairs, pairs[0][1][0].shape[0])
+        grads = gradients(name, pairs(0, 0, 0), self.row * self.parts)
         return (yield from self.reduce_ready(grads))
 
     def reduce_ready(self, grads):
@@ -916,12 +932,11 @@
         if held is not None:
             every, held = lax.optimization_barrier((every, held))
         pieces = []
-        for bits in range(4):
-            latent = self.z ^ bits
+        for latent in range(4):
             index = ((latent // 2) ^ self.c) * 2 + latent % 2
-            piece = lax.dynamic_index_in_dim(every, index, 0, keepdims=False)
-            pieces.append(piece if bits == 0 else self.along(piece, bits))
-        return jnp.concatenate(self.placed(pieces), axis=1), held
+            pieces.append(lax.dynamic_index_in_dim(every, index, 0, keepdims=False))
+        pieces = lax.all_to_all(jnp.stack(pieces), "lat", 0, 0, tiled=True)
+        return pieces.transpose(1, 0, 2).reshape(-1, 4 * width), held
 
     def placed(self, pieces):
         odd, high = self.z % 2 == 1, self.z >= 2
@@ -936,21 +951,15 @@
         ]
 
     def collect_start(self, values):
-        width = self.width
-        pieces = self.placed([values[:, i * width : (i + 1) * width] for i in range(4)])
-        return [p if bits == 0 else self.along(p, bits) for bits, p in enumerate(pieces)]
+        pieces = values.reshape(-1, 4, self.width).transpose(1, 0, 2)
+        return [lax.all_to_all(pieces, "lat", 0, 0, tiled=True)]
 
     def collect(self, pieces):
         width = self.width
-        every = jnp.stack(pieces)
+        every = pieces[0].reshape(2, 2, -1, width)
 
         def latents(core):
-            return jnp.stack(
-                [
-                    lax.dynamic_index_in_dim(every, self.z ^ (2 * core + i), 0, keepdims=False)
-                    for i in range(2)
-                ]
-            )
+            return lax.dynamic_index_in_dim(every, core, 0, keepdims=False)
 
         keep = latents(self.c)
         got = self.swap(latents(1 - self.c), "core")
@@ -1038,10 +1047,9 @@
     def kinds(self):
         return [F32, BF16]
 
-    def give_back(self, backs, x):
-        pair = backs[2 * x : 2 * x + 2]
-        got = [self.swap(pair[1 - core][1], "core") for core in (0, 1)]
-        return [(own[0] + one.astype(F32)).astype(BF16) for own, one in zip(pair, got)]
+    def give_back(self, backs):
+        got = [self.swap(backs[1 - core][1], "core") for core in (0, 1)]
+        return [(own[0] + one.astype(F32)).astype(BF16) for own, one in zip(backs, got)]
 
     def feed_back(self, low, turned, late, expanded, hidden, extras):
         tables = self.tables()
@@ -1069,8 +1077,8 @@
                 steps = [
                     Steps(self.reduce_ready(name, near[0], far, order))
                     for name, near, far, order in (
-                        ("d_shrink", shrink, found[0], "xy"),
-                        ("d_expand", grow, found[1], "yx"),
+                        ("d_shrink", shrink, found[0], "yx"),
+                        ("d_expand", grow, found[1], "xy"),
                     )
                 ]
             sums.append(one)
@@ -1080,56 +1088,34 @@
         axes, one, two = (("dp", "y"), 2, 1) if order == "xy" else (("y", "dp"), 1, 2)
         far = [(far[x], y) for x in (0, 1) for y in (0, 1)]
         sent = add_up(name, [[(near, one), far[one]], [(near, 3), far[3]]])
-        second = self.swap(sent, axes[0])
-        second = yield second
+        second = yield self.swap(sent, axes[0])
         sent = add_up(name, [[(near, two), far[two], (second, 1)]])
-        third = self.swap(sent, axes[1])
-        third = yield third
-        keep, send = add_up(
-            name, [[(near, 0), far[0], (second, 0), (third, 0)]], upper=self.z // 2
-        )
-        return (yield from self.reduce_end(name, keep, send))
-
-    def reduce_end(self, name, keep, other):
-        got = lax.ppermute(other, "lat", [(0, 1), (3, 2)])
-        got = yield got
-        other = add_up(name + "_out", [[(other[None], 0), (got[None], 0)]])[0]
-        got = lax.ppermute(other, "lat", [(1, 2), (2, 1)])
-        got = yield got
-        own, send = add_up(
-            name + "_in", [[(keep[None], 0), (got[None], 0)]], upper=self.z % 2
-        )
-        got = self.along(send, 1)
-        got = yield got
-        own = (own.astype(F32) + got.astype(F32)).astype(BF16)
-        got = self.swap(own, "dp")
+        third = yield self.swap(sent, axes[1])
+        terms = [(near, 0), far[0], (second, 0), (third, 0)]
+        return (yield from self.reduce_col(add_up(name, [terms])))
+
+    def reduce_col(self, blocks):
+        own = yield lax.psum_scatter(blocks[0], COLS, scatter_dimension=0, tiled=True)
+        got = yield self.swap(gate(own), "dp")
         return jnp.stack(
             [jnp.where(self.x == 0, own, got), jnp.where(self.x == 0, got, own)]
         ).astype(F32)
 
     def reduce(self, name, pairs):
-        def grads(places, adds=(), form="one"):
-            x, y, core = places[0]
-            table = None
-            if form == "halves":
-                table = jnp.full((2, 1), self.z // 2, jnp.int32)
-            return gradients(name, pairs[2 * x + core](), len(places), y, table, adds, form)
-
-        near = [None, None]
-        for x in (1, 0):
-            sent = grads([(x, 0, 1), (x, 1, 1)], form="apart")
-            sent = yield [self.swap(one, "core") for one in sent]
-            near[x] = [(one[None], 0) for one in sent]
-            if x == 1:
-                second = self.swap(grads([(1, 0, 0), (1, 1, 0)], [near[1]]), "dp")
-                second = yield second
-                second = [(second, 0), (second, 1)]
-        third = self.swap(grads([(0, 1, 0)], [[near[0][1]], [second[1]]]), "y")
-        third = yield third
-        keep, send = grads(
-            [(0, 0, 0)], [[near[0][0]], [second[0]], [(third, 0)]], form="halves"
-        )
-        return (yield from self.reduce_end(name, keep, send))
+        def grads(place, count, adds=(), form="one"):
+            return gradients(name, pairs(*place), count, adds, form)
+
+        def far(place, count):
+            sent = grads(place, count, form="apart")
+            return [self.swap(one, "core") for one in sent]
+
+        near = yield far((1, 0, 1), 2)
+        second = yield self.swap(grads((1, 0, 0), 2, [[near[:2], near[2:]]]), "dp")
+        near = yield far((0, 1, 1), 1)
+        last = yield far((0, 0, 1), 1)
+        third = yield self.swap(grads((0, 1, 0), 1, [[near], [(second, 1)]]), "y")
+        adds = [[last], [(second, 0)], [(third, 0)]]
+        return (yield from self.reduce_col(grads((0, 0, 0), 1, adds)))
 
     def small(self, vectors, row_sums, col_sums):
         span = row_sums[0].shape[-1]
@@ -1148,15 +1134,15 @@
 
         every = jnp.stack(row_sums).reshape(2, 2, 2, span)
         rows0, rows1 = every[:, 0], every[:, 1]
-        got = yield self.swap(flat(rows1, col_sums, vectors), "core")
+        got = yield self.swap(gate(flat(rows1, col_sums, vectors)), "core")
         got = cut(got, rows1.shape, col_sums.shape, vectors.shape)
         rows, cols = rows0 + got[0], col_sums + got[1]
         mine = (vectors + got[2]).astype(BF16).astype(F32)
-        got = yield self.swap(flat(rows[:, 1], cols, mine), "y")
+        got = yield self.swap(gate(flat(rows[:, 1], cols, mine)), "y")
         got = cut(got, (2, span), cols.shape, mine.shape)
         rows, cols = rows[:, 0] + got[0], cols + got[1]
         pair = jnp.stack([mine, got[2]])
-        got = yield self.swap(flat(rows, cols, pair), "dp")
+        got = yield self.swap(gate(flat(rows, cols, pair)), "dp")
         got = cut(got, rows.shape, cols.shape, pair.shape)
         rows = rows + jnp.stack([got[0][1], got[0][0]])
         rows = jnp.where(self.x == 0, rows, jnp.stack([rows[1], rows[0]]))
@@ -1263,6 +1249,9 @@
     )
     tables = net.tables()
 
+    silu_all = net.both_groups(silu_low)
+    LAST.append(silu_all)
+
     low_one, turned_one = enter(mine, vectors)
     queries, own_kv = [], []
     for one, two, bias in zip(query_bufs, kv_bufs, row_biases):
@@ -1301,7 +1290,6 @@
     expanded, hidden, output, gate_two_back = feed_forward(
         low_two, late, expand_biases, parts, [middle, back, vectors]
     )
-    output = net.collect_start(output)
 
     steps, ends, expand_sums = net.feed_back(
         branch_two_back,
@@ -1316,86 +1304,98 @@
     incoming = attended_backward(
         branch_one_back, late, jnp.concatenate(tables, axis=1), out_start
     )
+    output = net.collect_start(gate(output))
     number = len(kv)
-    query_back, backs, query_sums = [None] * number, [None] * number, [None] * number
-    kv_back = [None] * number
-
-    def attention_back(i):
+    blocks = queries[0].shape[0]
+    found = {}
+
+    def attention_back(i, begin, count):
         got = attend_back(
-            queries[i], kv[i], logs[i], incoming, i * queries[i].shape[0], net.kinds()
+            queries[i], kv[i], logs[i], incoming, i * blocks, net.kinds(), begin, count
         )
-        query_back[i], backs[i], query_sums[i] = got[0], got[1:-1], got[-1]
-
-    def kv_final(i):
-        pair = net.give_back(backs, i // 2)
-        kv_back[i : i + len(pair)] = pair
-
-    def pair(i):
-        return lambda: [
-            (turned_one, [query_back[i], kv_back[i]]),
-            (turned_one_back, [attended[i]]),
-        ]
-
-    half = number // 2
-    for i in reversed(range(half, number)):
-        attention_back(i)
-    kv_final(half)
-    in_steps = net.sum_up("d_in", [pair(j) for j in range(number)])
-    shrink_steps.step()
-    expand_steps.step()
-    crossing = []
-    if half:
-        in_steps.step()
-        crossing = [in_steps.got]
-        for i in reversed(range(half)):
-            if i == 0:
-                shrink_steps.hold()
-                expand_steps.hold()
-            attention_back(i)
+        found[i, begin] = [got[0], got[1:-1], got[-1]]
+
+    def kv_final(keys):
+        for key, one in zip(keys, net.give_back([found[key][1] for key in keys])):
+            found[key][1] = one
+
+    def pairs(x, y, core):
+        i = 2 * x + core
+        key, begin = ((i, 0), y) if (i, 1) not in found else ((i, y), 0)
+        heads = [(found[key][0], begin), (found[key][1], begin)]
+        return [(turned_one, heads), (turned_one_back, [(attended[i], y)])]
+
+    def every_block(i, which):
+        ones = [found[key][which] for key in sorted(found) if key[0] == i]
+        return ones if len(ones) > 1 else ones[0]
+
+    if number > 1:
+        attention_back(3, 0, 2)
+        attention_back(2, 0, 2)
+        LAST.extend(output)
+        shrink_steps.hold()
+        expand_steps.hold()
         shrink_steps.step()
         expand_steps.step()
-        kv_final(0)
+        kv_final([(2, 0), (3, 0)])
+        in_steps = net.sum_up("d_in", pairs)
+        attention_back(1, 1, 1)
         in_steps.step()
+        attention_back(0, 1, 1)
         shrink_steps.step()
+        kv_final([(0, 1), (1, 1)])
         in_steps.step()
+        attention_back(1, 0, 1)
+        attention_back(0, 0, 1)
         expand_steps.step()
-    value_sums = [
-        jnp.sum(one[:, :, LANES:].astype(F32), axis=1, keepdims=True) for one in kv_back
-    ]
-    LAST.extend(crossing)
+        kv_final([(0, 0), (1, 0)])
+        in_steps.step()
+        in_steps.step()
+    else:
+        attention_back(0, 0, blocks)
+        kv_final([(0, 0)])
+        in_steps = net.sum_up("d_in", pairs)
+    shrink_steps.hold()
     tokens_back, sums_one = contract(
         "tokens_back",
-        [(one, buf, block_at) for one, buf in zip(query_back, query_bufs)]
-        + [(one, buf, block_at) for one, buf in zip(kv_back, kv_bufs)],
+        [(every_block(i, 0), buf, block_at) for i, buf in enumerate(query_bufs)]
+        + [(every_block(i, 1), buf, block_at) for i, buf in enumerate(kv_bufs)],
         [mine, middle_back, vectors],
         finish_tokens_back,
         [shaped((rows, features), BF16), shaped((2, features), F32)],
     )
     summed = jnp.concatenate([sums_one, sums_two[2:3], sums_two[0:2], gate_two_back], axis=0)
-    tokens_back = net.collect_start(tokens_back)
-    shrink_steps.step()
-    expand_steps.step()
-    row_sums = [
-        jnp.concatenate([one, two], axis=-1) for one, two in zip(query_sums, value_sums)
-    ]
+
+    def value_sum(one):
+        return jnp.sum(one[:, :, LANES:].astype(F32), axis=1, keepdims=True)
+
+    row_sums = []
+    for i in range(number):
+        ones = [found[key] for key in sorted(found) if key[0] == i]
+        row_sums.append(
+            jnp.concatenate(
+                [
+                    jnp.concatenate([one[2], value_sum(one[1])], axis=-1)
+                    for one in ones
+                ]
+            )
+        )
     row_sums = net.with_units(row_sums, expand_sums)
     col_sums = jnp.concatenate([sums_two[3:4], shrink_sum], axis=0)
-    (summed,) = in_steps.behind(summed)
+    tokens_back = net.collect_start(gate(tokens_back))
     small_steps = Steps(net.small(summed, row_sums, col_sums))
     in_steps.step()
     small_steps.step()
-    LAST.extend(tokens_back[1:])
-    small_steps.hold()
-    in_steps.step()
+    LAST.extend(tokens_back)
     small_steps.step()
-    small_steps.hold()
+    shrink_steps.step()
+    expand_steps.step()
     in_steps.step()
     shrink_parts = shrink_steps.finish()
     expand_parts = expand_steps.finish()
     in_parts = in_steps.finish()
 
     every, row_found, col_found = small_steps.finish()
-    silu_all = net.both_groups(silu_low)
     modulation_weight_gradient = lax.dot_general(
         silu_all, every, (((0,), (0,)), ((), ())), preferred_element_type=F32
     ).reshape(modulation_weight.shape)

time: 546 us -> 521 us (0.954)
  starting transfers between devices: 105 us -> 70.6 us
  waiting for transfers between devices: 116 us -> 103 us
  other arithmetic: 22.8 us -> 32.7 us
  Pallas kernels: 244 us -> 250 us
    ppermute x26 -> x11, starting transfers between devices: 64.9 us -> 17.9 us  [along(): return lax.ppermute(values, 'lat', [(i, i ^ bits) for i in range(4)])]
    ppermute x26 -> x11, waiting for transfers between devices: 74.4 us -> 46.9 us  [along(): return lax.ppermute(values, 'lat', [(i, i ^ bits) for i in range(4)])]
    all_to_all x0 -> x4, starting transfers between devices: none -> 24.8 us  [the longest x2 16.2 us: collect_start(): return [lax.all_to_all(pieces, 'lat', 0, 0, tiled=True)]]
    all_to_all x0 -> x4, waiting for transfers between devices: none -> 15.8 us  [the longest x2 15.8 us: collect_start(): return [lax.all_to_all(pieces, 'lat', 0, 0, tiled=True)]]
    ppermute x6 -> x0, starting transfers between devices: 15 us -> none  [the longest x3 12.7 us: reduce_end(): got = lax.ppermute(other, 'lat', [(0, 1), (3, 2)])]
    ppermute x6 -> x0, waiting for transfers between devices: 7.59 us -> none  [the longest x3 7.58 us: reduce_end(): got = lax.ppermute(other, 'lat', [(0, 1), (3, 2)])]
    ppermute x43 -> x49, waiting for transfers between devices: 33.6 us -> 40.5 us  [swap(): return lax.ppermute(values, axis, [(0, 1), (1, 0)])]
    reshape x0 -> x4, local copies, waits for them, and re-layouts: none -> 6.77 us  [the longest x2 3.47 us: scatter(): return (pieces.transpose(1, 0, 2).reshape(-1, 4 * width), held)]
  transfers between devices with their start and end apart: 76 -> 68, of which waited for: 25 -> 16; matrix products, arithmetic and copies ran while one was open for 7% -> 11% of each run, Pallas kernels for 35% -> 37%
where the time goes in v3:
time: 521 us; the launch traced here: 514 us
  Pallas kernels  250 us (48%)
  waiting for transfers between devices  103 us (20%)
  starting transfers between devices  70.6 us (14%)
  local copies, waits for them, and re-layouts  40.4 us (8%)
  other arithmetic  32.7 us (6%)
  between operations  16.2 us (3%)
    pallas_call x42, Pallas kernels, ordered(): found = run(first, *others) if table is None else run(table, first, *others)  250 us
    ppermute x11, waiting for transfers between devices, along(): return lax.ppermute(values, 'lat', [(i, i ^ bits) for i in range(4)])  46.9 us
    ppermute x49, waiting for transfers between devices, swap(): return lax.ppermute(values, axis, [(0, 1), (1, 0)])  40.5 us
    ppermute x49, starting transfers between devices, swap(): return lax.ppermute(values, axis, [(0, 1), (1, 0)])  27.6 us
    unnamed x189, local copies, waits for them, and re-layouts  20.4 us
    ppermute x11, starting transfers between devices, along(): return lax.ppermute(values, 'lat', [(i, i ^ bits) for i in range(4)])  17.9 us
    all_to_all x2, starting transfers between devices, collect_start(): return [lax.all_to_all(pieces, 'lat', 0, 0, tiled=True)]  16.2 us
    all_to_all x2, waiting for transfers between devices, collect_start(): return [lax.all_to_all(pieces, 'lat', 0, 0, tiled=True)]  15.8 us
  transfers between devices with their start and end apart: 68, of which 16 were waited for; matrix products, arithmetic and copies ran while one was open for 11% of the time, Pallas kernels for 37%

profile of v3, /device:TPU:0, one launch (start us, length us, event | category | flops | bytes accessed | tf_op | source)
XLA Modules:
  0.0 514.1 jit_solution(10722953394957350854)
XLA Ops:
  13.4 2.8 collective-permute-start.1
  27.0 20.7 %collective-permute-done.2 = bf16[512,384]{1,0:T(8,128)(2,1)} collective-permute-done((bf16[512,384]{1,0:T(8,128)(2,1)S(1)}, bf16[512,384]{1,0:T(8,128)(2,1)}, u32[]{:S(2)}, u32[]{:S(2)}) %collective-permute-start.2) | collective-permute-done | bytes 393248 | tf_op jit(solution)/shard_map/ppermute | solution.py:924
  50.1 4.1 all-to-all-start
  55.5 3.9 collective-permute-start.6
  65.1 19.3 %collective-permute-done.6 = f32[8,256]{1,0:T(8,128)S(1)} collective-permute-done((f32[8,256]{1,0:T(8,128)S(1)}, f32[8,256]{1,0:T(8,128)S(1)}, u32[]{:S(2)}, u32[]{:S(2)}) %collective-permute-start.6) | collective-permute-done | bytes 8224 | tf_op jit(solution)/shard_map/ppermute | solution.py:924
  94.3 3.6 enter.1
  98.0 4.4 project.4
  104.8 9.5 %collective-permute-done.14.h.refs_18_ = bf16[2,1024,256]{2,1,0:T(8,128)(2,1)} collective-permute-done((bf16[2,1024,256]{2,1,0:T(8,128)(2,1)}, bf16[2,1024,256]{2,1,0:T(8,128)(2,1)}, u32[]{:S(2)}, u32[]{:S(2)}) %collective-permute-start.14) | collective-permute-done | bytes 1048608 | tf_op jit(solution)/shard_map/ppermute | solution.py:921
  115.5 4.5 all-to-all-start.1
  123.1 4.3 project.5
  127.5 4.4 project.6
  133.2 4.3 project.7
  139.6 6.9 %attend.4 = (bf16[2,512,128]{2,1,0:T(8,128)(2,1)}, f32[2,2,512]{2,1,0:T(2,128)}) custom-call(bf16[2,512,128]{2,1,0:T(8,128)(2,1)} %get-tuple-element.219.refs_0_, bf16[2,512,256]{2,1,0:T(8,128)(2,1)} %get-tuple-element.148.refs_1_.refs_3_, bf16[2,512,256]{2,1,0:T(8,128)(2,1)} %copy-done.10), custom_call_target="tpu_custom_call" | custom-call | tf_op jit(solution)/shard_map/attend/pallas_call | solution.py:91
  147.3 6.9 %attend.5 = (bf16[2,512,128]{2,1,0:T(8,128)(2,1)}, f32[2,2,512]{2,1,0:T(2,128)}) custom-call(bf16[2,512,128]{2,1,0:T(8,128)(2,1)} %get-tuple-element.217.refs_0_, bf16[2,512,256]{2,1,0:T(8,128)(2,1)} %get-tuple-element.149.refs_1_.refs_3_, bf16[2,512,256]{2,1,0:T(8,128)(2,1)} %copy-done.11), custom_call_target="tpu_custom_call" | custom-call | tf_op jit(solution)/shard_map/attend/pallas_call | solution.py:91
  157.4 6.9 %attend.6 = (bf16[2,512,128]{2,1,0:T(8,128)(2,1)}, f32[2,2,512]{2,1,0:T(2,128)}) custom-call(bf16[2,512,128]{2,1,0:T(8,128)(2,1)} %get-tuple-element.190.refs_0_, bf16[2,512,256]{2,1,0:T(8,128)(2,1)} %get-tuple-element.155.refs_1_.refs_3_, bf16[2,512,256]{2,1,0:T(8,128)(2,1)} %copy-done.23), custom_call_target="tpu_custom_call" | custom-call | tf_op jit(solution)/shard_map/attend/pallas_call | solution.py:91
  165.0 6.9 %attend.7 = (bf16[2,512,128]{2,1,0:T(8,128)(2,1)}, f32[2,2,512]{2,1,0:T(2,128)}) custom-call(bf16[2,512,128]{2,1,0:T(8,128)(2,1)} %get-tuple-element.187.refs_0_, bf16[2,512,256]{2,1,0:T(8,128)(2,1)} %get-tuple-element.156.refs_1_.refs_3_, bf16[2,512,256]{2,1,0:T(8,128)(2,1)} %copy-done.22), custom_call_target="tpu_custom_call" | custom-call | tf_op jit(solution)/shard_map/attend/pallas_call | solution.py:91
  171.9 3.1 enter_back.1
  175.0 9.9 %out.1 = (f32[512,1024]{1,0:T(8,128)}, f32[512,1024]{1,0:T(8,128)}, bf16[512,1024]{1,0:T(8,128)(2,1)}, bf16[1024,512]{1,0:T(8,128)(2,1)}) custom-call(s32[8,2]{1,0:T(8,128)} %concatenate.133.refs_0_, bf16[2,512,128]{2,1,0:T(8,128)(2,1)} %get-tuple-element.162.refs_1_.refs_4_, bf16[2,512,128]{2,1,0:T(8,128)(2,1)} %get-tuple-element.153.refs_2_.refs_4_, ...), custom_call_target="tpu_custom_call" | custom-call | tf_op jit(solution)/shard_map/out/pallas_call | solution.py:91
  184.8 19.5 %feed_forward.1 = (f32[8,512,512]{2,1,0:T(8,128)}, bf16[8,512,512]{2,1,0:T(8,128)(2,1)}, bf16[512,1024]{1,0:T(8,128)(2,1)}, f32[1,1024]{1,0:T(1,128)}) custom-call(bf16[512,1024]{1,0:T(8,128)(2,1)} %get-tuple-element.165.a, bf16[4,1024,2304]{2,1,0:T(8,128)(2,1)} %bitcast.239, bf16[4,1024,2304]{2,1,0:T(8,128)(2,1)} %bitcast.240, ...), custom_call_target="tpu_custom_call" | custom-call | tf_op jit(solution)/shard_map/feed_forward/pallas_call | solution.py:91
  204.4 20.1 %feed_back.2 = (bf16[2,1024,512]{2,1,0:T(8,128)(2,1)}, bf16[2,1024,512]{2,1,0:T(8,128)(2,1)}, bf16[2,1024,512]{2,1,0:T(8,128)(2,1)}, bf16[2,1024,512]{2,1,0:T(8,...) custom-call(s32[3,4]{1,0:T(4,128)} %get-tuple-element.423.table_ref, bf16[512,1024]{1,0:T(8,128)(2,1)} %get-tuple-element.174.refs_0_, ...), custom_call_target="tpu_custom_call" | custom-call | tf_op jit(solution)/shard_map/feed_back/pallas_call | solution.py:91
  225.5 23.3 %feed_back.3 = (bf16[4,1024,512]{2,1,0:T(8,128)(2,1)}, bf16[4,1024,512]{2,1,0:T(8,128)(2,1)}, f32[4,1,512]{2,1,0:T(1,128)}, f32[512,1024]{1,0:T(8,128)}, bf16[51...) custom-call(s32[3,4]{1,0:T(4,128)} %get-tuple-element.422.table_ref, ...), custom_call_target="tpu_custom_call" | custom-call | tf_op jit(solution)/shard_map/feed_back/pallas_call | solution.py:91
  250.2 4.1 d_shrink.3
  254.4 3.4 d_expand.3
  260.7 8.1 %attended_back.1.refs_1_ = bf16[8,512,128]{2,1,0:T(8,128)(2,1)} custom-call(s32[2,8]{1,0:T(2,128)} %copy-done.65, bf16[512,1024]{1,0:T(8,128)(2,1)} %get-tuple-element.184.a, bf16[4,1024,2304]{2,1,0:T(8,128)(2,1)} %bitcast.245), custom_call_target="tpu_custom_call" | custom-call | tf_op jit(solution)/shard_map/attended_back/pallas_call | solution.py:91
  273.4 9.1 %all-to-all-start.2 = ((bf16[4,512,256]{2,1,0:T(8,128)(2,1)}), bf16[4,512,256]{2,1,0:T(8,128)(2,1)}, u32[]{:S(2)}, u32[]{:S(2)}) async-start(bf16[4,512,256]{2,1,0:T(8,128)(2,1)} %bitcast.259), calls=%async_computation.2 | async-start | bytes 2097152 | tf_op jit(solution)/shard_map/all_to_all | solution.py:955
  282.5 10.1 %attend_back.6 = (bf16[2,512,128]{2,1,0:T(8,128)(2,1)}, f32[2,512,256]{2,1,0:T(8,128)}, bf16[2,512,256]{2,1,0:T(8,128)(2,1)}, f32[2,1,128]{2,1,0:T(1,128)}) custom-call(bf16[2,512,128]{2,1,0:T(8,128)(2,1)} %get-tuple-element.187.refs_0_, bf16[8,512,128]{2,1,0:T(8,128)(2,1)} %attended_back.1.refs_1_, f32[2,2,512]{2,1,0:T(2,128)} %get-tuple-element.188.refs_2_, ...), custom_call_target="tpu_custom_call" | custom-call | tf_op jit(solution)/shard_map/attend_back/pallas_call | solution.py:91
  292.6 9.7 %attend_back.7 = (bf16[2,512,128]{2,1,0:T(8,128)(2,1)}, f32[2,512,256]{2,1,0:T(8,128)}, bf16[2,512,256]{2,1,0:T(8,128)(2,1)}, f32[2,1,128]{2,1,0:T(1,128)}) custom-call(bf16[2,512,128]{2,1,0:T(8,128)(2,1)} %get-tuple-element.190.refs_0_, bf16[8,512,128]{2,1,0:T(8,128)(2,1)} %attended_back.1.refs_1_, f32[2,2,512]{2,1,0:T(2,128)} %get-tuple-element.191.refs_2_, ...), custom_call_target="tpu_custom_call" | custom-call | tf_op jit(solution)/shard_map/attend_back/pallas_call | solution.py:91
  304.0 4.6 all-to-all-done.2
  308.6 3.6 d_shrink.4
  317.6 5.6 %d_in.6 = (bf16[512,512]{1,0:T(8,128)(2,1)}, bf16[512,512]{1,0:T(8,128)(2,1)}, bf16[512,512]{1,0:T(8,128)(2,1)}, bf16[512,512]{1,0:T(8,128)(2,1)}) custom-call(bf16[1024,512]{1,0:T(8,128)(2,1)} %get-tuple-element.248.refs_0_, bf16[1024,512]{1,0:T(8,128)(2,1)} %get-tuple-element.196.refs_1_, bf16[2,512,128]{2,1,0:T(8,128)(2,1)} %get-tuple-element.189.refs_2_.refs_5_, ...), custom_call_target="tpu_custom_call" | custom-call | tf_op jit(solution)/shard_map/d_in/pallas_call | solution.py:91
  327.5 5.8 %attend_back.8 = (bf16[1,512,128]{2,1,0:T(8,128)(2,1)}, f32[1,512,256]{2,1,0:T(8,128)}, bf16[1,512,256]{2,1,0:T(8,128)(2,1)}, f32[1,1,128]{2,1,0:T(1,128)}) custom-call(bf16[2,512,128]{2,1,0:T(8,128)(2,1)} %get-tuple-element.217.refs_0_, bf16[8,512,128]{2,1,0:T(8,128)(2,1)} %attended_back.1.refs_1_, f32[2,2,512]{2,1,0:T(2,128)} %get-tuple-element.201.refs_2_, ...), custom_call_target="tpu_custom_call" | custom-call | tf_op jit(solution)/shard_map/attend_back/pallas_call | solution.py:91
  334.5 5.4 %d_in.7 = bf16[2,1024,512]{2,1,0:T(8,128)(2,1)} custom-call(bf16[1024,512]{1,0:T(8,128)(2,1)} %get-tuple-element.248.refs_0_, bf16[1024,512]{1,0:T(8,128)(2,1)} %get-tuple-element.196.refs_1_, bf16[2,512,128]{2,1,0:T(8,128)(2,1)} %get-tuple-element.192.refs_2_.refs_4_, bf16[2,512,256]{2,1,0:T(8,128)(2,1)} %add_convert_fusion.refs_3_.refs_10_, ...), custom_call_target="tpu_custom_call" | custom-call | tf_op jit(solution)/shard_map/d_in/pallas_call | solution.py:91
  339.9 5.8 %attend_back.9 = (bf16[1,512,128]{2,1,0:T(8,128)(2,1)}, f32[1,512,256]{2,1,0:T(8,128)}, bf16[1,512,256]{2,1,0:T(8,128)(2,1)}, f32[1,1,128]{2,1,0:T(1,128)}) custom-call(bf16[2,512,128]{2,1,0:T(8,128)(2,1)} %get-tuple-element.219.refs_0_, bf16[8,512,128]{2,1,0:T(8,128)(2,1)} %attended_back.1.refs_1_, f32[2,2,512]{2,1,0:T(2,128)} %get-tuple-element.210.refs_2_, ...), custom_call_target="tpu_custom_call" | custom-call | tf_op jit(solution)/shard_map/attend_back/pallas_call | solution.py:91
  345.8 3.3 d_shrink.5
  355.8 3.6 d_in.8
  359.4 5.8 %attend_back.10 = (bf16[1,512,128]{2,1,0:T(8,128)(2,1)}, f32[1,512,256]{2,1,0:T(8,128)}, bf16[1,512,256]{2,1,0:T(8,128)(2,1)}, f32[1,1,128]{2,1,0:T(1,128)}) custom-call(bf16[2,512,128]{2,1,0:T(8,128)(2,1)} %get-tuple-element.217.refs_0_, bf16[8,512,128]{2,1,0:T(8,128)(2,1)} %attended_back.1.refs_1_, f32[2,2,512]{2,1,0:T(2,128)} %get-tuple-element.201.refs_2_, ...), custom_call_target="tpu_custom_call" | custom-call | tf_op jit(solution)/shard_map/attend_back/pallas_call | solution.py:91
  366.1 5.8 %attend_back.11 = (bf16[1,512,128]{2,1,0:T(8,128)(2,1)}, f32[1,512,256]{2,1,0:T(8,128)}, bf16[1,512,256]{2,1,0:T(8,128)(2,1)}, f32[1,1,128]{2,1,0:T(1,128)}) custom-call(bf16[2,512,128]{2,1,0:T(8,128)(2,1)} %get-tuple-element.219.refs_0_, bf16[8,512,128]{2,1,0:T(8,128)(2,1)} %attended_back.1.refs_1_, f32[2,2,512]{2,1,0:T(2,128)} %get-tuple-element.210.refs_2_, ...), custom_call_target="tpu_custom_call" | custom-call | tf_op jit(solution)/shard_map/attend_back/pallas_call | solution.py:91
  371.9 3.8 collective-permute-done.37.refs_3_
  376.7 3.5 d_expand.5
  383.4 3.5 d_in.9
  386.9 12.6 %collective-permute-done.42.refs_7_ = bf16[2,1024,512]{2,1,0:T(8,128)(2,1)S(1)} collective-permute-done((bf16[2,1024,512]{2,1,0:T(8,128)(2,1)}, bf16[2,1024,512]{2,1,0:T(8,128)(2,1)S(1)}, u32[]{:S(2)}, u32[]{:S(2)}) %collective-permute-start.42) | collective-permute-done | bytes 2097184 | tf_op jit(solution)/shard_map/ppermute | solution.py:921
  400.9 4.3 d_in.10
  406.5 12.0 %tokens_back.1 = (bf16[512,1024]{1,0:T(8,128)(2,1)}, f32[2,1024]{1,0:T(2,128)}) custom-call(bf16[1,512,128]{2,1,0:T(8,128)(2,1)} %get-tuple-element.230.refs_0_.refs_2_, bf16[1,512,128]{2,1,0:T(8,128)(2,1)} %get-tuple-element.211.refs_2_.refs_1_, bf16[1,512,128]{2,1,0:T(8,128)(2,1)} %get-tuple-element.218.refs_2_, ...), custom_call_target="tpu_custom_call" | custom-call | tf_op jit(solution)/shard_map/tokens_back/pallas_call | solution.py:91
  426.6 7.1 %all-to-all-start.3 = ((bf16[4,512,256]{2,1,0:T(8,128)(2,1)}), bf16[4,512,256]{2,1,0:T(8,128)(2,1)S(1)}, u32[]{:S(2)}, u32[]{:S(2)}) async-start(bf16[4,512,256]{2,1,0:T(8,128)(2,1)} %bitcast.229), calls=%async_computation.4 | async-start | bytes 2097152 | tf_op jit(solution)/shard_map/all_to_all | solution.py:955
  437.7 4.8 d_in.11
  448.8 11.2 %all-to-all-done.3 = bf16[4,512,256]{2,1,0:T(8,128)(2,1)S(1)} async-done(((bf16[4,512,256]{2,1,0:T(8,128)(2,1)}), bf16[4,512,256]{2,1,0:T(8,128)(2,1)S(1)}, u32[]{:S(2)}, u32[]{:S(2)}) %all-to-all-start.3) | async-done | bytes 1048608 | tf_op jit(solution)/shard_map/all_to_all | solution.py:955
  473.4 4.9 collective-permute-done.51
  497.5 7.1 %collective-permute-done.57 = bf16[256,512]{1,0:T(8,128)(2,1)S(1)} collective-permute-done((bf16[256,512]{1,0:T(8,128)(2,1)}, bf16[256,512]{1,0:T(8,128)(2,1)S(1)}, u32[]{:S(2)}, u32[]{:S(2)}) %collective-permute-start.57) | collective-permute-done | bytes 262176 | tf_op jit(solution)/shard_map/ppermute | solution.py:921
  (522 shorter events, 139.8 us)
Async XLA Ops:
  7.2 167.8 %all-gather.2.cloned.1.call-start = ((), (), s32[]{:S(2)}) async-start(), calls=%async_computation.7 | async-start | bytes 20054016 | tf_op jit(solution)/shard_map/all_gather | solution.py:822
  13.4 9.8 %collective-permute-start.1 = (bf16[256,384]{1,0:T(8,128)(2,1)S(1)}, bf16[256,384]{1,0:T(8,128)(2,1)S(1)}, u32[]{:S(2)}, u32[]{:S(2)}) collective-permute-start(bf16[256,384]{1,0:T(8,128)(2,1)S(1)} %bitcast.276), channel_id=1, source_target_pairs={{0,1},{1,0},{2,3},{3,2},{4,5},{5,4},{6,7},{7,6},{8,9},{9,8},{10,11... | collective-permute-start | bytes 589832 | tf_op jit(solution)/shard_map/ppermute | solution.py:924
  16.3 10.6 %collective-permute-start = (bf16[2,512,256]{2,1,0:T(8,128)(2,1)S(1)}, bf16[2,512,256]{2,1,0:T(8,128)(2,1)S(1)}, u32[]{:S(2)}, u32[]{:S(2)}) collective-permute-start(bf16[2,512,256]{2,1,0:T(8,128)(2,1)S(1)} %get-tuple-element.339), channel_id=1, source_target_pairs={{0,4},{4,0},{1,5},{5,1},{2,6},{6,2},{3,7},{7,3},{8,12},{12,8},{9,1... | collective-permute-start | bytes 1572872 | tf_op jit(solution)/shard_map/ppermute | solution.py:921
  23.3 24.4 %collective-permute-start.2 = (bf16[512,384]{1,0:T(8,128)(2,1)S(1)}, bf16[512,384]{1,0:T(8,128)(2,1)}, u32[]{:S(2)}, u32[]{:S(2)}) collective-permute-start(bf16[512,384]{1,0:T(8,128)(2,1)S(1)} %pad_maximum_fusion.11), channel_id=1, source_target_pairs={{0,2},{1,3},{2,0},{3,1},{4,6},{5,7},{6,4},{7,5},{8,10},{9,11},{10,... | collective-permute-start | bytes 1179656 | tf_op jit(solution)/shard_map/ppermute | solution.py:924
  50.1 39.1 %all-to-all-start = ((bf16[4,512,256]{2,1,0:T(8,128)(2,1)}), bf16[4,512,256]{2,1,0:T(8,128)(2,1)S(1)}, u32[]{:S(2)}, u32[]{:S(2)}) async-start(bf16[4,512,256]{2,1,0:T(8,128)(2,1)} %pad_maximum_fusion.2), calls=%async_computation | async-start | bytes 2097152 | tf_op jit(solution)/shard_map/all_to_all | solution.py:938
  55.5 28.8 %collective-permute-start.6 = (f32[8,256]{1,0:T(8,128)S(1)}, f32[8,256]{1,0:T(8,128)S(1)}, u32[]{:S(2)}, u32[]{:S(2)}) collective-permute-start(f32[8,256]{1,0:T(8,128)S(1)} %get-tuple-element.415), channel_id=1, source_target_pairs={{0,3},{1,2},{2,1},{3,0},{4,7},{5,6},{6,5},{7,4},{8,11},{9,10},{10,... | collective-permute-start | bytes 24584 | tf_op jit(solution)/shard_map/ppermute | solution.py:924
  59.4 27.0 %collective-permute-start.7 = (f32[8,256]{1,0:T(8,128)S(1)}, f32[8,256]{1,0:T(8,128)S(1)}, u32[]{:S(2)}, u32[]{:S(2)}) collective-permute-start(f32[8,256]{1,0:T(8,128)S(1)} %get-tuple-element.414), channel_id=1, source_target_pairs={{0,2},{1,3},{2,0},{3,1},{4,6},{5,7},{6,4},{7,5},{8,10},{9,11},{10,... | collective-permute-start | bytes 24584 | tf_op jit(solution)/shard_map/ppermute | solution.py:924
  59.4 27.0 %collective-permute-start.8 = (f32[8,256]{1,0:T(8,128)S(1)}, f32[8,256]{1,0:T(8,128)S(1)}, u32[]{:S(2)}, u32[]{:S(2)}) collective-permute-start(f32[8,256]{1,0:T(8,128)S(1)} %get-tuple-element.413), channel_id=1, source_target_pairs={{0,1},{1,0},{2,3},{3,2},{4,5},{5,4},{6,7},{7,6},{8,9},{9,8},{10,11... | collective-permute-start | bytes 24584 | tf_op jit(solution)/shard_map/ppermute | solution.py:924
  60.9 26.1 %collective-permute-start.11 = (bf16[1024,256]{1,0:T(8,128)(2,1)}, bf16[1024,256]{1,0:T(8,128)(2,1)}, u32[]{:S(2)}, u32[]{:S(2)}) collective-permute-start(bf16[1024,256]{1,0:T(8,128)(2,1)} %get-tuple-element.341), channel_id=1, source_target_pairs={{0,8},{8,0},{1,9},{9,1},{2,10},{10,2},{3,11},{11,3},{4,12},{12,4},... | collective-permute-start | bytes 1572872 | tf_op jit(solution)/shard_map/ppermute | solution.py:921
  64.0 29.5 %collective-permute-start.10 = (bf16[2,1024,128]{2,1,0:T(8,128)(2,1)}, bf16[2,1024,128]{2,1,0:T(8,128)(2,1)S(1)}, u32[]{:S(2)}, u32[]{:S(2)}) collective-permute-start(bf16[2,1024,128]{2,1,0:T(8,128)(2,1)} %pad_maximum_fusion.8), channel_id=1, source_target_pairs={{0,8},{8,0},{1,9},{9,1},{2,10},{10,2},{3,11},{11,3},{4,12},{12,4},... | collective-permute-start | bytes 1572872 | tf_op jit(solution)/shard_map/ppermute | solution.py:921
  90.3 24.0 %collective-permute-start.14 = (bf16[2,1024,256]{2,1,0:T(8,128)(2,1)}, bf16[2,1024,256]{2,1,0:T(8,128)(2,1)}, u32[]{:S(2)}, u32[]{:S(2)}) collective-permute-start(bf16[2,1024,256]{2,1,0:T(8,128)(2,1)} %pad_maximum_fusion.3.h.refs_16_), channel_id=1, source_target_pairs={{0,16},{16,0},{1,17},{17,1},{2,18},{18,2},{3,19},{19,3},{4,20},{20... | collective-permute-start | bytes 3145736 | tf_op jit(solution)/shard_map/ppermute | solution.py:921
  103.2 19.1 %collective-permute-start.13 = (bf16[2,1024,256]{2,1,0:T(8,128)(2,1)}, bf16[2,1024,256]{2,1,0:T(8,128)(2,1)}, u32[]{:S(2)}, u32[]{:S(2)}) collective-permute-start(bf16[2,1024,256]{2,1,0:T(8,128)(2,1)} %pad_maximum_fusion.3.h.refs_16_), channel_id=1, source_target_pairs={{0,4},{4,0},{1,5},{5,1},{2,6},{6,2},{3,7},{7,3},{8,12},{12,8},{9,1... | collective-permute-start | bytes 3145736 | tf_op jit(solution)/shard_map/ppermute | solution.py:921
  114.4 18.1 %collective-permute-start.16 = (bf16[2,1024,256]{2,1,0:T(8,128)(2,1)}, bf16[2,1024,256]{2,1,0:T(8,128)(2,1)}, u32[]{:S(2)}, u32[]{:S(2)}) collective-permute-start(bf16[2,1024,256]{2,1,0:T(8,128)(2,1)} %collective-permute-done.14.h.refs_18_), channel_id=1, source_target_pairs={{0,4},{4,0},{1,5},{5,1},{2,6},{6,2},{3,7},{7,3},{8,12},{12,8},{9,1... | collective-permute-start | bytes 3145736 | tf_op jit(solution)/shard_map/ppermute | solution.py:921
  115.5 38.7 %all-to-all-start.1 = ((bf16[4,512,256]{2,1,0:T(8,128)(2,1)}), bf16[4,512,256]{2,1,0:T(8,128)(2,1)}, u32[]{:S(2)}, u32[]{:S(2)}) async-start(bf16[4,512,256]{2,1,0:T(8,128)(2,1)} %pad_maximum_fusion.4), calls=%async_computation.1 | async-start | bytes 2097152 | tf_op jit(solution)/shard_map/all_to_all | solution.py:938
  120.9 11.6 %collective-permute-start.15 = (bf16[2,1024,128]{2,1,0:T(8,128)(2,1)S(1)}, bf16[2,1024,128]{2,1,0:T(8,128)(2,1)S(1)}, u32[]{:S(2)}, u32[]{:S(2)}) collective-permute-start(bf16[2,1024,128]{2,1,0:T(8,128)(2,1)S(1)} %pad_maximum_fusion.10.g.refs_14_), channel_id=1, source_target_pairs={{0,4},{4,0},{1,5},{5,1},{2,6},{6,2},{3,7},{7,3},{8,12},{12,8},{9,1... | collective-permute-start | bytes 1572872 | tf_op jit(solution)/shard_map/ppermute | solution.py:921
  121.6 24.9 %collective-permute-start.19 = (bf16[2,512,256]{2,1,0:T(8,128)(2,1)S(1)}, bf16[2,512,256]{2,1,0:T(8,128)(2,1)S(1)}, u32[]{:S(2)}, u32[]{:S(2)}) collective-permute-start(bf16[2,512,256]{2,1,0:T(8,128)(2,1)S(1)} %copy-done.9), channel_id=1, source_target_pairs={{0,4},{4,0},{1,5},{5,1},{2,6},{6,2},{3,7},{7,3},{8,12},{12,8},{9,1... | collective-permute-start | bytes 1572872 | tf_op jit(solution)/shard_map/ppermute | solution.py:921
  132.4 31.9 %collective-permute-start.21 = (bf16[2,512,256]{2,1,0:T(8,128)(2,1)}, bf16[2,512,256]{2,1,0:T(8,128)(2,1)S(1)}, u32[]{:S(2)}, u32[]{:S(2)}) collective-permute-start(bf16[2,512,256]{2,1,0:T(8,128)(2,1)} %get-tuple-element.155.refs_1_.refs_3_), channel_id=1, source_target_pairs={{0,4},{4,0},{1,5},{5,1},{2,6},{6,2},{3,7},{7,3},{8,12},{12,8},{9,1... | collective-permute-start | bytes 1572872 | tf_op jit(solution)/shard_map/ppermute | solution.py:921
  137.6 19.0 %collective-permute-start.20 = (bf16[2,512,256]{2,1,0:T(8,128)(2,1)}, bf16[2,512,256]{2,1,0:T(8,128)(2,1)S(1)}, u32[]{:S(2)}, u32[]{:S(2)}) collective-permute-start(bf16[2,512,256]{2,1,0:T(8,128)(2,1)} %get-tuple-element.156.refs_1_.refs_3_), channel_id=1, source_target_pairs={{0,4},{4,0},{1,5},{5,1},{2,6},{6,2},{3,7},{7,3},{8,12},{12,8},{9,1... | collective-permute-start | bytes 1572872 | tf_op jit(solution)/shard_map/ppermute | solution.py:921
  224.5 24.4 %collective-permute-start.22 = (bf16[2,1024,512]{2,1,0:T(8,128)(2,1)}, bf16[2,1024,512]{2,1,0:T(8,128)(2,1)S(1)}, u32[]{:S(2)}, u32[]{:S(2)}) collective-permute-start(bf16[2,1024,512]{2,1,0:T(8,128)(2,1)} %get-tuple-element.173), channel_id=1, source_target_pairs={{0,4},{4,0},{1,5},{5,1},{2,6},{6,2},{3,7},{7,3},{8,12},{12,8},{9,1... | collective-permute-start | bytes 6291464 | tf_op jit(solution)/shard_map/ppermute | solution.py:921
  224.6 24.3 %collective-permute-start.23 = (bf16[2,1024,512]{2,1,0:T(8,128)(2,1)}, bf16[2,1024,512]{2,1,0:T(8,128)(2,1)}, u32[]{:S(2)}, u32[]{:S(2)}) collective-permute-start(bf16[2,1024,512]{2,1,0:T(8,128)(2,1)} %get-tuple-element.179), channel_id=1, source_target_pairs={{0,4},{4,0},{1,5},{5,1},{2,6},{6,2},{3,7},{7,3},{8,12},{12,8},{9,1... | collective-permute-start | bytes 6291464 | tf_op jit(solution)/shard_map/ppermute | solution.py:921
  225.0 23.9 %collective-permute-start.24 = (bf16[2,1024,512]{2,1,0:T(8,128)(2,1)}, bf16[2,1024,512]{2,1,0:T(8,128)(2,1)S(1)}, u32[]{:S(2)}, u32[]{:S(2)}) collective-permute-start(bf16[2,1024,512]{2,1,0:T(8,128)(2,1)} %get-tuple-element.180), channel_id=1, source_target_pairs={{0,4},{4,0},{1,5},{5,1},{2,6},{6,2},{3,7},{7,3},{8,12},{12,8},{9,1... | collective-permute-start | bytes 6291464 | tf_op jit(solution)/shard_map/ppermute | solution.py:921
  225.1 23.8 %collective-permute-start.25 = (bf16[2,1024,512]{2,1,0:T(8,128)(2,1)}, bf16[2,1024,512]{2,1,0:T(8,128)(2,1)S(1)}, u32[]{:S(2)}, u32[]{:S(2)}) collective-permute-start(bf16[2,1024,512]{2,1,0:T(8,128)(2,1)} %get-tuple-element.181), channel_id=1, source_target_pairs={{0,4},{4,0},{1,5},{5,1},{2,6},{6,2},{3,7},{7,3},{8,12},{12,8},{9,1... | collective-permute-start | bytes 6291464 | tf_op jit(solution)/shard_map/ppermute | solution.py:921
  257.8 50.8 %collective-permute-start.28 = (bf16[2,1024,512]{2,1,0:T(8,128)(2,1)}, bf16[2,1024,512]{2,1,0:T(8,128)(2,1)S(1)}, u32[]{:S(2)}, u32[]{:S(2)}) collective-permute-start(bf16[2,1024,512]{2,1,0:T(8,128)(2,1)} %d_expand.3), channel_id=1, source_target_pairs={{0,16},{16,0},{1,17},{17,1},{2,18},{18,2},{3,19},{19,3},{4,20},{20... | collective-permute-start | bytes 6291464 | tf_op jit(solution)/shard_map/ppermute | solution.py:921
  259.3 49.3 %collective-permute-start.27 = (bf16[2,1024,512]{2,1,0:T(8,128)(2,1)}, bf16[2,1024,512]{2,1,0:T(8,128)(2,1)}, u32[]{:S(2)}, u32[]{:S(2)}) collective-permute-start(bf16[2,1024,512]{2,1,0:T(8,128)(2,1)} %d_shrink.3), channel_id=1, source_target_pairs={{0,8},{8,0},{1,9},{9,1},{2,10},{10,2},{3,11},{11,3},{4,12},{12,4},... | collective-permute-start | bytes 6291464 | tf_op jit(solution)/shard_map/ppermute | solution.py:921
  273.4 35.2 %all-to-all-start.2 = ((bf16[4,512,256]{2,1,0:T(8,128)(2,1)}), bf16[4,512,256]{2,1,0:T(8,128)(2,1)}, u32[]{:S(2)}, u32[]{:S(2)}) async-start(bf16[4,512,256]{2,1,0:T(8,128)(2,1)} %bitcast.259), calls=%async_computation.2 | async-start | bytes 2097152 | tf_op jit(solution)/shard_map/all_to_all | solution.py:955
  282.5 124.0 %reduce-scatter.4.cloned.1.call-start = ((), (), s32[]{:S(2)}) async-start(), calls=%async_computation.8 | async-start | bytes 1310720 | tf_op jit(solution)/shard_map/reduce_scatter | solution.py:1098
  302.3 11.6 %collective-permute-start.29 = (bf16[2,512,256]{2,1,0:T(8,128)(2,1)}, bf16[2,512,256]{2,1,0:T(8,128)(2,1)S(1)}, u32[]{:S(2)}, u32[]{:S(2)}) collective-permute-start(bf16[2,512,256]{2,1,0:T(8,128)(2,1)} %get-tuple-element.198), channel_id=1, source_target_pairs={{0,4},{4,0},{1,5},{5,1},{2,6},{6,2},{3,7},{7,3},{8,12},{12,8},{9,1... | collective-permute-start | bytes 1572872 | tf_op jit(solution)/shard_map/ppermute | solution.py:921
  302.9 21.1 %collective-permute-start.30 = (bf16[2,512,256]{2,1,0:T(8,128)(2,1)}, bf16[2,512,256]{2,1,0:T(8,128)(2,1)}, u32[]{:S(2)}, u32[]{:S(2)}) collective-permute-start(bf16[2,512,256]{2,1,0:T(8,128)(2,1)} %get-tuple-element.205), channel_id=1, source_target_pairs={{0,4},{4,0},{1,5},{5,1},{2,6},{6,2},{3,7},{7,3},{8,12},{12,8},{9,1... | collective-permute-start | bytes 1572872 | tf_op jit(solution)/shard_map/ppermute | solution.py:921
  312.2 33.6 %collective-permute-start.35 = (bf16[1,1024,512]{2,1,0:T(8,128)(2,1)}, bf16[1,1024,512]{2,1,0:T(8,128)(2,1)}, u32[]{:S(2)}, u32[]{:S(2)}) collective-permute-start(bf16[1,1024,512]{2,1,0:T(8,128)(2,1)} %d_shrink.4), channel_id=1, source_target_pairs={{0,16},{16,0},{1,17},{17,1},{2,18},{18,2},{3,19},{19,3},{4,20},{20... | collective-permute-start | bytes 3145736 | tf_op jit(solution)/shard_map/ppermute | solution.py:921
  323.3 10.1 %collective-permute-start.31 = (bf16[512,512]{1,0:T(8,128)(2,1)}, bf16[512,512]{1,0:T(8,128)(2,1)S(1)}, u32[]{:S(2)}, u32[]{:S(2)}) collective-permute-start(bf16[512,512]{1,0:T(8,128)(2,1)} %get-tuple-element.199), channel_id=1, source_target_pairs={{0,4},{4,0},{1,5},{5,1},{2,6},{6,2},{3,7},{7,3},{8,12},{12,8},{9,1... | collective-permute-start | bytes 1572872 | tf_op jit(solution)/shard_map/ppermute | solution.py:921
  323.4 10.0 %collective-permute-start.32 = (bf16[512,512]{1,0:T(8,128)(2,1)}, bf16[512,512]{1,0:T(8,128)(2,1)S(1)}, u32[]{:S(2)}, u32[]{:S(2)}) collective-permute-start(bf16[512,512]{1,0:T(8,128)(2,1)} %get-tuple-element.206), channel_id=1, source_target_pairs={{0,4},{4,0},{1,5},{5,1},{2,6},{6,2},{3,7},{7,3},{8,12},{12,8},{9,1... | collective-permute-start | bytes 1572872 | tf_op jit(solution)/shard_map/ppermute | solution.py:921
  323.9 9.5 %collective-permute-start.33 = (bf16[512,512]{1,0:T(8,128)(2,1)}, bf16[512,512]{1,0:T(8,128)(2,1)S(1)}, u32[]{:S(2)}, u32[]{:S(2)}) collective-permute-start(bf16[512,512]{1,0:T(8,128)(2,1)} %get-tuple-element.207), channel_id=1, source_target_pairs={{0,4},{4,0},{1,5},{5,1},{2,6},{6,2},{3,7},{7,3},{8,12},{12,8},{9,1... | collective-permute-start | bytes 1572872 | tf_op jit(solution)/shard_map/ppermute | solution.py:921
  324.0 9.5 %collective-permute-start.34 = (bf16[512,512]{1,0:T(8,128)(2,1)}, bf16[512,512]{1,0:T(8,128)(2,1)}, u32[]{:S(2)}, u32[]{:S(2)}) collective-permute-start(bf16[512,512]{1,0:T(8,128)(2,1)} %get-tuple-element.208), channel_id=1, source_target_pairs={{0,4},{4,0},{1,5},{5,1},{2,6},{6,2},{3,7},{7,3},{8,12},{12,8},{9,1... | collective-permute-start | bytes 1572872 | tf_op jit(solution)/shard_map/ppermute | solution.py:921
  349.1 117.4 %reduce-scatter.8.cloned.1.call-start = ((), (), s32[]{:S(2)}) async-start(), calls=%async_computation.10 | async-start | bytes 1310720 | tf_op jit(solution)/shard_map/reduce_scatter | solution.py:1098
  350.3 25.4 %collective-permute-start.37 = (bf16[1,1024,512]{2,1,0:T(8,128)(2,1)}, bf16[1,1024,512]{2,1,0:T(8,128)(2,1)S(1)}, u32[]{:S(2)}, u32[]{:S(2)}) collective-permute-start(bf16[1,1024,512]{2,1,0:T(8,128)(2,1)} %d_expand.4), channel_id=1, source_target_pairs={{0,8},{8,0},{1,9},{9,1},{2,10},{10,2},{3,11},{11,3},{4,12},{12,4},... | collective-permute-start | bytes 3145736 | tf_op jit(solution)/shard_map/ppermute | solution.py:921
  351.1 14.6 %collective-permute-start.39 = (bf16[1,512,256]{2,1,0:T(8,128)(2,1)}, bf16[1,512,256]{2,1,0:T(8,128)(2,1)S(1)}, u32[]{:S(2)}, u32[]{:S(2)}) collective-permute-start(bf16[1,512,256]{2,1,0:T(8,128)(2,1)} %get-tuple-element.228), channel_id=1, source_target_pairs={{0,4},{4,0},{1,5},{5,1},{2,6},{6,2},{3,7},{7,3},{8,12},{12,8},{9,1... | collective-permute-start | bytes 786440 | tf_op jit(solution)/shard_map/ppermute | solution.py:921
  351.7 47.8 %collective-permute-start.42 = (bf16[2,1024,512]{2,1,0:T(8,128)(2,1)}, bf16[2,1024,512]{2,1,0:T(8,128)(2,1)S(1)}, u32[]{:S(2)}, u32[]{:S(2)}) collective-permute-start(bf16[2,1024,512]{2,1,0:T(8,128)(2,1)} %d_in.7), channel_id=1, source_target_pairs={{0,16},{16,0},{1,17},{17,1},{2,18},{18,2},{3,19},{19,3},{4,20},{20... | collective-permute-start | bytes 6291464 | tf_op jit(solution)/shard_map/ppermute | solution.py:921
  355.0 68.5 %collective-permute-start.26 = (bf16[2,512,256]{2,1,0:T(8,128)(2,1)}, bf16[2,512,256]{2,1,0:T(8,128)(2,1)}, u32[]{:S(2)}, u32[]{:S(2)}) collective-permute-start(bf16[2,512,256]{2,1,0:T(8,128)(2,1)} %dynamic-slice_bitcast_fusion.1), channel_id=1, source_target_pairs={{0,4},{4,0},{1,5},{5,1},{2,6},{6,2},{3,7},{7,3},{8,12},{12,8},{9,1... | collective-permute-start | bytes 1572872 | tf_op jit(solution)/shard_map/ppermute | solution.py:921
  365.3 15.0 %collective-permute-start.43 = (bf16[1,512,256]{2,1,0:T(8,128)(2,1)}, bf16[1,512,256]{2,1,0:T(8,128)(2,1)S(1)}, u32[]{:S(2)}, u32[]{:S(2)}) collective-permute-start(bf16[1,512,256]{2,1,0:T(8,128)(2,1)} %get-tuple-element.232), channel_id=1, source_target_pairs={{0,4},{4,0},{1,5},{5,1},{2,6},{6,2},{3,7},{7,3},{8,12},{12,8},{9,1... | collective-permute-start | bytes 786440 | tf_op jit(solution)/shard_map/ppermute | solution.py:921
  366.0 20.9 %collective-permute-start.40 = (bf16[512,512]{1,0:T(8,128)(2,1)}, bf16[512,512]{1,0:T(8,128)(2,1)}, u32[]{:S(2)}, u32[]{:S(2)}) collective-permute-start(bf16[512,512]{1,0:T(8,128)(2,1)} %get-tuple-element.216), channel_id=1, source_target_pairs={{0,4},{4,0},{1,5},{5,1},{2,6},{6,2},{3,7},{7,3},{8,12},{12,8},{9,1... | collective-permute-start | bytes 1572872 | tf_op jit(solution)/shard_map/ppermute | solution.py:921
  405.2 31.7 %collective-permute-start.48 = (bf16[1,1024,512]{2,1,0:T(8,128)(2,1)}, bf16[1,1024,512]{2,1,0:T(8,128)(2,1)}, u32[]{:S(2)}, u32[]{:S(2)}) collective-permute-start(bf16[1,1024,512]{2,1,0:T(8,128)(2,1)} %d_in.10), channel_id=1, source_target_pairs={{0,8},{8,0},{1,9},{9,1},{2,10},{10,2},{3,11},{11,3},{4,12},{12,4},... | collective-permute-start | bytes 3145736 | tf_op jit(solution)/shard_map/ppermute | solution.py:921
  423.6 10.1 %collective-permute-start.45 = (f32[88,128]{1,0:T(8,128)}, f32[88,128]{1,0:T(8,128)S(1)}, u32[]{:S(2)}, u32[]{:S(2)}) collective-permute-start(f32[88,128]{1,0:T(8,128)} %gate.10), channel_id=1, source_target_pairs={{0,4},{4,0},{1,5},{5,1},{2,6},{6,2},{3,7},{7,3},{8,12},{12,8},{9,1... | collective-permute-start | bytes 135176 | tf_op jit(solution)/shard_map/ppermute | solution.py:921
  424.9 12.0 %collective-permute-start.46 = (bf16[512,512]{1,0:T(8,128)(2,1)}, bf16[512,512]{1,0:T(8,128)(2,1)S(1)}, u32[]{:S(2)}, u32[]{:S(2)}) collective-permute-start(bf16[512,512]{1,0:T(8,128)(2,1)} %get-tuple-element.225), channel_id=1, source_target_pairs={{0,4},{4,0},{1,5},{5,1},{2,6},{6,2},{3,7},{7,3},{8,12},{12,8},{9,1... | collective-permute-start | bytes 1572872 | tf_op jit(solution)/shard_map/ppermute | solution.py:921
  425.4 11.4 %collective-permute-start.47 = (bf16[512,512]{1,0:T(8,128)(2,1)}, bf16[512,512]{1,0:T(8,128)(2,1)}, u32[]{:S(2)}, u32[]{:S(2)}) collective-permute-start(bf16[512,512]{1,0:T(8,128)(2,1)} %get-tuple-element.249), channel_id=1, source_target_pairs={{0,4},{4,0},{1,5},{5,1},{2,6},{6,2},{3,7},{7,3},{8,12},{12,8},{9,1... | collective-permute-start | bytes 1572872 | tf_op jit(solution)/shard_map/ppermute | solution.py:921
  426.6 33.4 %all-to-all-start.3 = ((bf16[4,512,256]{2,1,0:T(8,128)(2,1)}), bf16[4,512,256]{2,1,0:T(8,128)(2,1)S(1)}, u32[]{:S(2)}, u32[]{:S(2)}) async-start(bf16[4,512,256]{2,1,0:T(8,128)(2,1)} %bitcast.229), calls=%async_computation.4 | async-start | bytes 2097152 | tf_op jit(solution)/shard_map/all_to_all | solution.py:955
  433.7 60.3 %reduce-scatter.6.cloned.1.call-start = ((), (), s32[]{:S(2)}) async-start(), calls=%async_computation.9 | async-start | bytes 1310720 | tf_op jit(solution)/shard_map/reduce_scatter | solution.py:1098
  465.7 22.8 %collective-permute-start.59 = (bf16[256,512]{1,0:T(8,128)(2,1)}, bf16[256,512]{1,0:T(8,128)(2,1)}, u32[]{:S(2)}, u32[]{:S(2)}) collective-permute-start(bf16[256,512]{1,0:T(8,128)(2,1)} %gate.13), channel_id=1, source_target_pairs={{0,16},{16,0},{1,17},{17,1},{2,18},{18,2},{3,19},{19,3},{4,20},{20... | collective-permute-start | bytes 786440 | tf_op jit(solution)/shard_map/ppermute | solution.py:921
  468.2 22.7 %collective-permute-start.58 = (bf16[256,512]{1,0:T(8,128)(2,1)}, bf16[256,512]{1,0:T(8,128)(2,1)S(1)}, u32[]{:S(2)}, u32[]{:S(2)}) collective-permute-start(bf16[256,512]{1,0:T(8,128)(2,1)} %gate.14), channel_id=1, source_target_pairs={{0,16},{16,0},{1,17},{17,1},{2,18},{18,2},{3,19},{19,3},{4,20},{20... | collective-permute-start | bytes 786440 | tf_op jit(solution)/shard_map/ppermute | solution.py:921
  (105 other events, 657.3 us)
Sparse Core Ops, SparseCore 0:
  11.9 162.6 all-gather.1
  349.3 30.3 reduce-scatter.3
  382.0 28.6 reduce-scatter.7
  464.0 28.3 reduce-scatter.5

commit v4 on v3

--- a/solution.py
+++ b/solution.py
@@ -33,18 +33,11 @@
     return lax.dot_general(left, right, NT, preferred_element_type=F32)
 
 
-def gelu_tanh(values):
-    return (
-        0.5
-        * values
-        * (1.0 + jnp.tanh(0.7978845608028654 * (values + 0.044715 * values * values * values)))
-    )
-
-
-def gelu_slope(values):
-    inner = jnp.tanh(0.7978845608028654 * (values + 0.044715 * values * values * values))
-    rate = 0.7978845608028654 * (1.0 + 3 * 0.044715 * values * values)
-    return 0.5 * (1.0 + inner) + 0.5 * values * (1.0 - inner * inner) * rate
+def gelu_and_slope(values):
+    square = values * values
+    half = 0.5 + 0.5 * jnp.tanh(0.7978845608028654 * values * (1.0 + 0.044715 * square))
+    rate = (2 * 0.7978845608028654) * (1.0 + 3 * 0.044715 * square)
+    return values * half, half + values * (half - half * half) * rate
 
 
 def whole(shape):
@@ -136,19 +129,14 @@
     )(left, query_blocks, kv_blocks, bias)
 
 
-def feed_forward(left, late, bias, parts, extras):
+def feed_forward(left, late, bias, extras):
     number, _, width = bias.shape
     rows, features = left.shape
 
-    def late_block(start):
-        return pl.BlockSpec(
-            (None, features, width), lambda b: (b // parts, 0, start + b % parts)
-        )
-
-    def kernel(a, g, h, c, middle, cotangent, vectors, expanded, hidden, output, sums, total):
-        out = dot(a[...], g[...]) + c[...]
-        expanded[...] = out
-        low = gelu_tanh(out).astype(BF16)
+    def kernel(a, g, h, c, middle, vectors, slopes, hidden, branch, output, total):
+        low, slope = gelu_and_slope(dot(a[...], g[...]) + c[...])
+        slopes[...] = slope
+        low = low.astype(BF16)
         hidden[...] = low
         out = dot_nt(low, h[...])
 
@@ -162,63 +150,66 @@
 
         @pl.when(pl.program_id(0) == number - 1)
         def _():
-            finish_output(total, (middle, cotangent, vectors), (output, sums))
+            finish_output(total, (middle, vectors), (branch, output))
 
     return call(
         "feed_forward",
         kernel,
         (number,),
-        [fixed(left.shape), late_block(0), late_block(parts), block((1, width))]
+        [
+            fixed(left.shape),
+            block((features, width)),
+            block((features, width), 1),
+            block((1, width)),
+        ]
         + [fixed(extra.shape) for extra in extras],
         [
             block((rows, width)),
             block((rows, width)),
             whole((rows, features)),
-            whole((1, features)),
+            whole((rows, features)),
         ],
         [
             shaped((number, rows, width), F32),
             shaped((number, rows, width), BF16),
+            shaped((rows, features), F32),
             shaped((rows, features), BF16),
-            shaped((1, features), F32),
         ],
         scratch=[pltpu.VMEM((rows, features), F32)],
     )(left, late, late, bias, *extras)
 
 
-def feed_back(name, low, turned, late, expanded, hidden, table, parts, extras, before, apart):
-    _, rows, width = expanded.shape
+def feed_back(name, low, turned, late, slopes, hidden, table, parts, extras, before):
+    _, rows, width = slopes.shape
     features = low.shape[1]
     number = table.shape[1]
-    count = number // 2 if apart else 1
+    part = width // parts
     more = [] if before is None else [before]
 
     def kernel(table_ref, *refs):
-        low, turned_low, turned_in, shrink, grow, before_act, after_act = refs[:7]
+        low, turned_low, turned_in, shrink, grow, slope, after_act = refs[:7]
         refs = list(refs[7:])
         start = [refs.pop(0) for _ in more]
         given = [refs.pop(0) for _ in extras]
-        shrink_outs = [refs.pop(0) for _ in range(count)]
-        expand_outs = [refs.pop(0) for _ in range(count)]
+        shrink_outs = [refs.pop(0) for _ in range(parts)]
+        expand_outs = [refs.pop(0) for _ in range(parts)]
         sums = refs.pop(0)
         results, total = (refs[:-1], refs[-1]) if extras else (None, refs[0])
         step = pl.program_id(0)
-        back = dot(low[...], shrink[...]) * gelu_slope(before_act[...])
-        back = back.astype(BF16)
+        back = (dot(low[...], shrink[...]) * slope[...]).astype(BF16)
         sums[...] = jnp.sum(back.astype(F32), axis=0, keepdims=True)
-        found = dot(turned_low[...], after_act[...]).astype(BF16)
-        grown = dot(turned_in[...], back).astype(BF16)
-        if apart:
-            for index in range(count):
-
-                @pl.when(step // 2 == index)
+        side = table_ref[1, 0]
+        for place in range(parts):
+            here = slice(place * part, (place + 1) * part)
+            found = dot(turned_low[...], after_act[:, here]).astype(BF16)
+            grown = dot(turned_in[...], back[:, here]).astype(BF16)
+            for index in range(parts):
+
+                @pl.when(side == (place ^ index))
                 def _():
                     shrink_outs[index][...] = found
                     expand_outs[index][...] = grown
 
-        else:
-            shrink_outs[0][...] = found
-            expand_outs[0][...] = grown
         out = dot_nt(back, grow[...])
 
         @pl.when(step == 0)
@@ -235,9 +226,7 @@
             def _():
                 finish_middle_back(total, given, results)
 
-    weight = (features, width)
     ends = [shaped((number, 1, width), F32)]
-    end_specs = [block((1, width))]
     if extras:
         ends += [
             shaped((rows, features), F32),
@@ -247,17 +236,7 @@
         ]
     else:
         ends += [shaped((rows, features), F32)]
-    end_specs += [whole(one.shape) for one in ends[1:]]
-    if apart:
-        outs = [shaped((2, *weight), BF16)] * number
-        out_specs = [
-            pl.BlockSpec(
-                (None, *weight), lambda b, _, at=at: (jnp.clip(b - 2 * at, 0, 1), 0, 0)
-            )
-            for at in range(count)
-        ] * 2
-    else:
-        outs, out_specs = [shaped((number, *weight), BF16)] * 2, [block(weight)] * 2
+    outs = [shaped((number, features, part), BF16)] * (2 * parts)
     got = call(
         name,
         kernel,
@@ -265,18 +244,20 @@
         [
             fixed(low.shape),
             *[fixed(one.shape) for one in turned],
-            tabled(weight, (1, 2), parts),
-            tabled(weight, (1, 2), 0),
+            tabled((features, width), (0, None), 1),
+            tabled((features, width), (0, None), 0),
             tabled((rows, width), (0, None)),
             tabled((rows, width), (0, None)),
         ]
         + [fixed(one.shape) for one in (*more, *extras)],
-        out_specs + end_specs,
+        [block((features, part))] * (2 * parts)
+        + [block((1, width))]
+        + [whole(one.shape) for one in ends[1:]],
         outs + ends,
         scratch=[pltpu.VMEM((rows, features), F32)] if extras else (),
         table=table,
-    )(low, *turned, late, late, expanded, hidden, *more, *extras)
-    return got[:count], got[count : 2 * count], got[2 * count :]
+    )(low, *turned, late, late, slopes, hidden, *more, *extras)
+    return got[:parts], got[parts : 2 * parts], got[2 * parts :]
 
 
 def add_up(name, blocks, upper=None):
@@ -453,32 +434,33 @@
     )(tokens, vectors)
 
 
-def enter_back(cotangent, vectors):
+def enter_back(cotangent, branch, vectors):
     rows, features = cotangent.shape
 
-    def kernel(cotangent, vectors, low, turned, sums):
+    def kernel(cotangent, branch, vectors, low, turned, sums):
         gate = vectors[5:6]
 
         def work(here):
-            values = (gate * cotangent[here, :].astype(F32)).astype(BF16)
+            upstream = cotangent[here, :].astype(F32)
+            values = (gate * upstream).astype(BF16)
             low[here, :] = values
             turned[:, here] = values.T
-            return (values.astype(F32),)
-
-        (sums[...],) = by_rows(rows, 1, features, work, LANES)
+            return values.astype(F32), branch[here, :] * upstream
+
+        sums[...] = jnp.concatenate(by_rows(rows, 2, features, work, LANES), axis=0)
 
     return call(
         "enter_back",
         kernel,
         (1,),
-        [whole(cotangent.shape), whole(vectors.shape)],
-        [whole((rows, features)), whole((features, rows)), whole((1, features))],
+        [whole(cotangent.shape), whole(branch.shape), whole(vectors.shape)],
+        [whole((rows, features)), whole((features, rows)), whole((2, features))],
         [
             shaped((rows, features), BF16),
             shaped((features, rows), BF16),
-            shaped((1, features), F32),
+            shaped((2, features), F32),
         ],
-    )(cotangent, vectors)
+    )(cotangent, branch, vectors)
 
 
 def finish_middle(total, given, results):
@@ -502,18 +484,18 @@
 
 
 def finish_output(total, given, results):
-    middle, cotangent, vectors = given
-    output, sums = results
+    middle, vectors = given
+    branch, output = results
     rows, features = total.shape
     gate, bias = vectors[5:6], vectors[7:8]
 
     def work(here):
         two = total[here, :] + bias
+        branch[here, :] = two
         output[here, :] = (middle[here, :] + gate * two).astype(BF16)
-        return (two * cotangent[here, :].astype(F32),)
-
-    (gate_back,) = by_rows(rows, 1, features, work)
-    sums[...] = gate_back
+        return ()
+
+    by_rows(rows, 0, features, work)
 
 
 def finish_middle_back(total, given, results):
@@ -632,8 +614,9 @@
         query, kv = refs[0], refs[1 : 1 + count]
         out_ref, log_ref = refs[1 + count :]
         head = lax.broadcasted_iota(jnp.int32, (1, LANES), 1) < HEAD_DIM
-        for start in range(0, rows, tile):
-            here = slice(start, start + tile)
+
+        def step(i, _):
+            here = pl.ds(pl.multiple_of(i * tile, tile), tile)
             both = query[here, :]
             outs, logs = [], []
             for keep in (head, ~head):
@@ -655,6 +638,9 @@
             table = jnp.where(head, logs[0], logs[1]).T
             log_ref[0:1, here] = table[0:1]
             log_ref[1:2, here] = table[HEAD_DIM : HEAD_DIM + 1]
+            return 0
+
+        lax.fori_loop(0, rows // tile, step, 0)
 
     return call(
         "attend",
@@ -681,9 +667,11 @@
         head = lax.broadcasted_iota(jnp.int32, (1, LANES), 1) < HEAD_DIM
         turned = [piece[:, :LANES].T for piece in kv]
         top = lax.broadcasted_iota(jnp.int32, (LANES, 1), 0) < HEAD_DIM
-        query_sum = jnp.zeros((1, LANES), F32)
-        for start in range(0, rows, tile):
-            here = slice(start, start + tile)
+        for held in scratch:
+            held[...] = jnp.zeros_like(held)
+
+        def step(j, query_sum):
+            here = pl.ds(pl.multiple_of(j * tile, tile), tile)
             backs = []
             for index, keep in enumerate((head, ~head)):
                 zero = jnp.zeros((tile, LANES), BF16)
@@ -701,21 +689,16 @@
                 total = None
                 for i in range(count):
                     score_back = (chances[i] * (mixes[i] - centre)).astype(BF16)
-                    key_back = dot(score_back, one) * SCALE
-                    value_back = dot(chances[i].astype(BF16), back)
-                    if start == 0 and index == 0:
-                        scratch[i][:, :LANES] = key_back
-                        scratch[i][:, LANES:] = value_back
-                    else:
-                        scratch[i][:, :LANES] += key_back
-                        scratch[i][:, LANES:] += value_back
+                    scratch[i][:, :LANES] += dot(score_back, one) * SCALE
+                    scratch[i][:, LANES:] += dot(chances[i].astype(BF16), back)
                     term = dot(turned[i], score_back)
                     total = term if total is None else total + term
                 backs.append(total)
             both = (jnp.where(top, backs[0], backs[1]).T * SCALE).astype(BF16)
             query_back[here, :] = both
-            query_sum = query_sum + jnp.sum(both.astype(F32), axis=0, keepdims=True)
-        sums[...] = query_sum
+            return query_sum + jnp.sum(both.astype(F32), axis=0, keepdims=True)
+
+        sums[...] = lax.fori_loop(0, rows // tile, step, jnp.zeros((1, LANES), F32))
         for out, held in zip(kv_back, scratch):
             out[...] = held[...].astype(out.dtype)
 
@@ -810,13 +793,12 @@
         ]
 
     def gather(self, parts, held):
-        del held
         every = lax.all_gather(parts, COLS, axis=1, tiled=True)
         every = lax.all_gather(every, ROWS, axis=0, tiled=True)
-        return [every[:, :, :LANES]], [every[:, :, LANES:]]
-
-    def gather_start(self, parts):
-        return parts
+        return [every[:, :, :LANES]], [every[:, :, LANES:]], held
+
+    def gather_start(self, parts, held):
+        return parts, held
 
     def gather_late(self, part):
         every = lax.all_gather(part, (*ROWS, *COLS), axis=0, tiled=True)
@@ -852,24 +834,19 @@
     def sum_up(self, *args):
         return Steps(self.reduce(*args))
 
-    def feed_back(self, low, turned, late, expanded, hidden, extras):
-        blocks = jnp.arange(self.row * self.parts, dtype=jnp.int32)
-        table = jnp.stack([blocks, blocks // self.parts, blocks % self.parts])
+    def feed_back(self, low, turned, late, slopes, hidden, extras):
+        table = jnp.stack([jnp.arange(self.row, dtype=jnp.int32)] * 2) * jnp.array(
+            [[1], [0]], jnp.int32
+        )
         shrink, grow, (sums, *ends) = feed_back(
-            "feed_back",
-            low,
-            turned,
-            late,
-            expanded,
-            hidden,
-            table,
-            self.parts,
-            extras,
-            None,
-            False,
+            "feed_back", low, turned, late, slopes, hidden, table, self.parts, extras, None
         )
-        steps = [Steps(self.reduce_ready(one[0])) for one in (shrink, grow)]
-        return steps, ends, [sums]
+
+        def blocks(parts):
+            return jnp.stack(parts, axis=1).reshape(-1, *parts[0].shape[1:])
+
+        steps = [Steps(self.reduce_ready(blocks(one))) for one in (shrink, grow)]
+        return steps, ends, [sums.reshape(self.row * self.parts, 1, -1)]
 
     def reduce(self, name, pairs):
         grads = gradients(name, pairs(0, 0, 0), self.row * self.parts)
@@ -988,30 +965,32 @@
         vectors = jnp.concatenate(self.placed(pieces), axis=1)
         return vectors, [rows[x, core] for x, core in self.PLACES]
 
-    def gather_start(self, parts):
+    def gather_start(self, parts, held):
         part = lax.dynamic_index_in_dim(parts, self.x, 0, keepdims=False)
         odd, high = self.z % 2 == 1, self.z >= 2
         got = self.along(part, 1)
         part = jnp.concatenate([jnp.where(odd, got, part), jnp.where(odd, part, got)], axis=0)
+        part, held = lax.optimization_barrier((part, held))
         got = self.along(part, 2)
         part = jnp.concatenate(
             [jnp.where(high, got, part), jnp.where(high, part, got)], axis=0
         )
 
-        return part
+        return part, held
 
     def gather(self, part, held):
         one, two = part[:, :LANES], part[:, LANES:]
         one_pair = jnp.stack([one, self.swap(one, "dp")])
         near = jnp.stack([two, self.swap(two, "y")])
-        near = after(near, one_pair, *held)
+        near = after(near, one_pair)
         far = self.swap(near, "dp")
         kv = [near, self.swap(near, "core"), far, self.swap(far, "core")]
+        one_pair, held = lax.optimization_barrier((one_pair, held))
         got = self.swap(one_pair, "y")
         near = jnp.stack([one_pair[0], got[0]])
         far = jnp.stack([one_pair[1], got[1]])
         queries = [near, self.swap(near, "core"), far, self.swap(far, "core")]
-        return queries, kv
+        return queries, kv, held
 
     def expand_bias(self, row_bias, biases):
         number = self.row * self.parts
@@ -1051,23 +1030,22 @@
         got = [self.swap(backs[1 - core][1], "core") for core in (0, 1)]
         return [(own[0] + one.astype(F32)).astype(BF16) for own, one in zip(backs, got)]
 
-    def feed_back(self, low, turned, late, expanded, hidden, extras):
+    def feed_back(self, low, turned, late, slopes, hidden, extras):
         tables = self.tables()
         found, sums, before = [], [], None
         for core in (1, 0):
-            rows, parts = jnp.concatenate([tables[core], tables[2 + core]], axis=1)
+            rows = tables[core][0]
             shrink, grow, (one, *ends) = feed_back(
                 "feed_back",
                 low,
                 turned,
                 late,
-                expanded,
+                slopes,
                 hidden,
-                jnp.stack([rows * self.parts + parts, rows, parts]),
+                jnp.stack([rows, jnp.full((2,), self.x, jnp.int32)]),
                 self.parts,
                 [] if core else extras,
                 before,
-                core == 1,
             )
             if core:
                 (before,) = ends
@@ -1075,23 +1053,27 @@
             else:
                 LAST.extend([one for part in found for one in part])
                 steps = [
-                    Steps(self.reduce_ready(name, near[0], far, order))
+                    Steps(self.reduce_ready(name, near, far, order))
                     for name, near, far, order in (
                         ("d_shrink", shrink, found[0], "yx"),
                         ("d_expand", grow, found[1], "xy"),
                     )
                 ]
-            sums.append(one)
+            one = one.reshape(2, 1, self.parts, -1).transpose(2, 0, 1, 3)
+            one = jnp.where(self.x == 0, one, jnp.stack([one[1], one[0]]))
+            sums.append(one.reshape(4, 1, -1))
         return steps, ends, sums
 
     def reduce_ready(self, name, near, far, order):
         axes, one, two = (("dp", "y"), 2, 1) if order == "xy" else (("y", "dp"), 1, 2)
-        far = [(far[x], y) for x in (0, 1) for y in (0, 1)]
-        sent = add_up(name, [[(near, one), far[one]], [(near, 3), far[3]]])
+        near, far = (
+            [(part[x], y) for x in (0, 1) for y in (0, 1)] for part in (near, far)
+        )
+        sent = add_up(name, [[near[one], far[one]], [near[3], far[3]]])
         second = yield self.swap(sent, axes[0])
-        sent = add_up(name, [[(near, two), far[two], (second, 1)]])
+        sent = add_up(name, [[near[two], far[two], (second, 1)]])
         third = yield self.swap(sent, axes[1])
-        terms = [(near, 0), far[0], (second, 0), (third, 0)]
+        terms = [near[0], far[0], (second, 0), (third, 0)]
         return (yield from self.reduce_col(add_up(name, [terms])))
 
     def reduce_col(self, blocks):
@@ -1239,18 +1221,16 @@
         row_bias,
         jnp.stack([output_bias, shrink_bias]).astype(F32),
     )
-    own_in = net.gather_start(own_in)
+    silu_all = net.both_groups(silu_low)
+    own_in, (vectors, silu_all) = net.gather_start(own_in, (vectors, silu_all))
     mine, own_in = net.scatter(tokens, own_in)
-    query_bufs, kv_bufs = net.gather(own_in, [mine, vectors])
+    query_bufs, kv_bufs, mine = net.gather(own_in, mine)
     rows = mine.shape[0]
     features = mine.shape[1]
     expand_biases = net.expand_bias(
         row_bias[:, 2 * LANES :], [one[..., 2 * LANES :] for one in row_biases]
     )
     tables = net.tables()
-
-    silu_all = net.both_groups(silu_low)
-    LAST.append(silu_all)
 
     low_one, turned_one = enter(mine, vectors)
     queries, own_kv = [], []
@@ -1259,14 +1239,12 @@
         queries.append(one)
         own_kv.append(two)
     kv = net.share(own_kv)
-    back, _ = net.scatter(after(cotangent, own_kv[0]))
     attended, logs = [], []
     for one, pieces in zip(queries, kv):
         out, log = attend(one, pieces)
         attended.append(out)
         logs.append(log)
-
-    branch_two_back, turned_two_back, shrink_sum = enter_back(back, vectors)
+    back, (late, attended[-1]) = net.scatter(cotangent, (late, attended[-1]))
 
     def out_place(number):
         def place(features, width):
@@ -1287,15 +1265,17 @@
         ],
         table=jnp.concatenate(tables, axis=0),
     )
-    expanded, hidden, output, gate_two_back = feed_forward(
-        low_two, late, expand_biases, parts, [middle, back, vectors]
+    slopes, hidden, branch_two, output = feed_forward(
+        low_two, late, expand_biases.reshape(-1, 1, parts * units), [middle, vectors]
     )
+    branch_two_back, turned_two_back, sums_back = enter_back(back, branch_two, vectors)
+    shrink_sum, gate_two_back = sums_back[0:1], sums_back[1:2]
 
     steps, ends, expand_sums = net.feed_back(
         branch_two_back,
         (turned_two_back, turned_two),
         late,
-        expanded,
+        slopes,
         hidden,
         [middle, branch_one, back, vectors],
     )

time: 521 us -> 515 us (0.988)
  starting transfers between devices: 70.6 us -> 61.6 us
  other arithmetic: 32.7 us -> 24.7 us
  waiting for transfers between devices: 103 us -> 111 us
    ppermute x49, waiting for transfers between devices: 40.5 us -> 65.2 us  [swap(): return lax.ppermute(values, axis, [(0, 1), (1, 0)])]
    ppermute x11, waiting for transfers between devices: 46.9 us -> 23.4 us  [along(): return lax.ppermute(values, 'lat', [(i, i ^ bits) for i in range(4)])]
    all_to_all x2, waiting for transfers between devices: 0.01 us -> 11 us  [scatter(): pieces = lax.all_to_all(jnp.stack(pieces), 'lat', 0, 0, tiled=True)]
    all_to_all x2, starting transfers between devices: 16.2 us -> 9.83 us  [collect_start(): return [lax.all_to_all(pieces, 'lat', 0, 0, tiled=True)]]
    unnamed x189 -> x184, local copies, waits for them, and re-layouts: 20.4 us -> 18.7 us
  transfers between devices with their start and end apart: 68 -> 68, of which waited for: 16 -> 17; matrix products, arithmetic and copies ran while one was open for 11% -> 9% of each run, Pallas kernels for 37% -> 44%
where the time goes in v4:
time: 515 us; the launch traced here: 510 us
  Pallas kernels  254 us (49%)
  waiting for transfers between devices  111 us (22%)
  starting transfers between devices  61.6 us (12%)
  local copies, waits for them, and re-layouts  41.3 us (8%)
  other arithmetic  24.7 us (5%)
  between operations  16 us (3%)
    pallas_call x42, Pallas kernels, ordered(): found = run(first, *others) if table is None else run(table, first, *others)  254 us
    ppermute x49, waiting for transfers between devices, swap(): return lax.ppermute(values, axis, [(0, 1), (1, 0)])  65.2 us
    ppermute x49, starting transfers between devices, swap(): return lax.ppermute(values, axis, [(0, 1), (1, 0)])  26.7 us
    ppermute x11, waiting for transfers between devices, along(): return lax.ppermute(values, 'lat', [(i, i ^ bits) for i in range(4)])  23.4 us
    unnamed x184, local copies, waits for them, and re-layouts  18.7 us
    ppermute x11, starting transfers between devices, along(): return lax.ppermute(values, 'lat', [(i, i ^ bits) for i in range(4)])  17.1 us
    all_to_all x2, waiting for transfers between devices, scatter(): pieces = lax.all_to_all(jnp.stack(pieces), 'lat', 0, 0, tiled=True)  11 us
    all_to_all x2, waiting for transfers between devices, collect_start(): return [lax.all_to_all(pieces, 'lat', 0, 0, tiled=True)]  11 us
  transfers between devices with their start and end apart: 68, of which 17 were waited for; matrix products, arithmetic and copies ran while one was open for 9% of the time, Pallas kernels for 44%

profile of v4, /device:TPU:0, one launch (start us, length us, event | category | flops | bytes accessed | tf_op | source)
XLA Modules:
  0.0 509.9 jit_solution(17533657406991665285)
XLA Ops:
  33.3 21.2 %collective-permute-done.8 = bf16[512,384]{1,0:T(8,128)(2,1)S(1)} collective-permute-done((bf16[512,384]{1,0:T(8,128)(2,1)S(1)}, bf16[512,384]{1,0:T(8,128)(2,1)S(1)}, u32[]{:S(2)}, u32[]{:S(2)}) %collective-permute-start.8) | collective-permute-done | bytes 393248 | tf_op jit(solution)/shard_map/ppermute | solution.py:901
  55.9 3.7 all-to-all-start
  62.4 5.4 %collective-permute-done.9 = bf16[1024,128]{1,0:T(8,128)(2,1)S(1)} collective-permute-done((bf16[1024,128]{1,0:T(8,128)(2,1)S(1)}, bf16[1024,128]{1,0:T(8,128)(2,1)S(1)}, u32[]{:S(2)}, u32[]{:S(2)}) %collective-permute-start.9) | collective-permute-done | bytes 262176 | tf_op jit(solution)/shard_map/ppermute | solution.py:898
  67.8 9.4 %collective-permute-done.11 = bf16[1024,256]{1,0:T(8,128)(2,1)S(1)} collective-permute-done((bf16[1024,256]{1,0:T(8,128)(2,1)S(1)}, bf16[1024,256]{1,0:T(8,128)(2,1)S(1)}, u32[]{:S(2)}, u32[]{:S(2)}) %collective-permute-start.11) | collective-permute-done | bytes 524320 | tf_op jit(solution)/shard_map/ppermute | solution.py:898
  79.8 11.0 %all-to-all-done = bf16[4,512,256]{2,1,0:T(8,128)(2,1)S(1)} async-done(((bf16[4,512,256]{2,1,0:T(8,128)(2,1)}), bf16[4,512,256]{2,1,0:T(8,128)(2,1)S(1)}, u32[]{:S(2)}, u32[]{:S(2)}) %all-to-all-start) | async-done | bytes 1048608 | tf_op jit(solution)/shard_map/all_to_all | solution.py:915
  93.1 8.5 %collective-permute-done.14.h.refs_18_ = bf16[2,1024,256]{2,1,0:T(8,128)(2,1)} collective-permute-done((bf16[2,1024,256]{2,1,0:T(8,128)(2,1)S(1)}, bf16[2,1024,256]{2,1,0:T(8,128)(2,1)}, u32[]{:S(2)}, u32[]{:S(2)}) %collective-permute-start.14) | collective-permute-done | bytes 1048608 | tf_op jit(solution)/shard_map/ppermute | solution.py:898
  101.7 6.5 %collective-permute-done.10 = bf16[2,1024,128]{2,1,0:T(8,128)(2,1)S(1)} collective-permute-done((bf16[2,1024,128]{2,1,0:T(8,128)(2,1)S(1)}, bf16[2,1024,128]{2,1,0:T(8,128)(2,1)S(1)}, u32[]{:S(2)}, u32[]{:S(2)}) %collective-permute-start.10) | collective-permute-done | bytes 524320 | tf_op jit(solution)/shard_map/ppermute | solution.py:898
  109.7 3.6 enter.1
  113.3 4.4 project.4
  118.9 4.4 project.5
  123.5 4.4 project.6
  129.1 4.3 project.7
  135.9 7.1 %attend.4 = (bf16[2,512,128]{2,1,0:T(8,128)(2,1)}, f32[2,2,512]{2,1,0:T(2,128)}) custom-call(bf16[2,512,128]{2,1,0:T(8,128)(2,1)} %get-tuple-element.235.refs_0_, bf16[2,512,256]{2,1,0:T(8,128)(2,1)} %get-tuple-element.159.refs_1_.refs_3_, bf16[2,512,256]{2,1,0:T(8,128)(2,1)} %copy-done.11), custom_call_target="tpu_custom_call" | custom-call | tf_op jit(solution)/shard_map/attend/pallas_call | solution.py:84
  143.8 7.1 %attend.5 = (bf16[2,512,128]{2,1,0:T(8,128)(2,1)}, f32[2,2,512]{2,1,0:T(2,128)}) custom-call(bf16[2,512,128]{2,1,0:T(8,128)(2,1)} %get-tuple-element.233.refs_0_, bf16[2,512,256]{2,1,0:T(8,128)(2,1)} %get-tuple-element.160.refs_1_.refs_3_, bf16[2,512,256]{2,1,0:T(8,128)(2,1)} %copy-done.10), custom_call_target="tpu_custom_call" | custom-call | tf_op jit(solution)/shard_map/attend/pallas_call | solution.py:84
  151.7 7.1 %attend.6 = (bf16[2,512,128]{2,1,0:T(8,128)(2,1)}, f32[2,2,512]{2,1,0:T(2,128)}) custom-call(bf16[2,512,128]{2,1,0:T(8,128)(2,1)} %get-tuple-element.206.refs_0_, bf16[2,512,256]{2,1,0:T(8,128)(2,1)} %get-tuple-element.165.refs_1_.refs_3_, bf16[2,512,256]{2,1,0:T(8,128)(2,1)} %copy-done.24), custom_call_target="tpu_custom_call" | custom-call | tf_op jit(solution)/shard_map/attend/pallas_call | solution.py:84
  159.6 7.1 %attend.7 = (bf16[2,512,128]{2,1,0:T(8,128)(2,1)}, f32[2,2,512]{2,1,0:T(2,128)}) custom-call(bf16[2,512,128]{2,1,0:T(8,128)(2,1)} %get-tuple-element.203.refs_0_, bf16[2,512,256]{2,1,0:T(8,128)(2,1)} %get-tuple-element.166.refs_1_.refs_3_, bf16[2,512,256]{2,1,0:T(8,128)(2,1)} %copy-done.25), custom_call_target="tpu_custom_call" | custom-call | tf_op jit(solution)/shard_map/attend/pallas_call | solution.py:84
  168.0 3.7 all-to-all-start.1
  173.4 9.7 %out.1 = (f32[512,1024]{1,0:T(8,128)}, f32[512,1024]{1,0:T(8,128)}, bf16[512,1024]{1,0:T(8,128)(2,1)}, bf16[1024,512]{1,0:T(8,128)(2,1)}) custom-call(s32[8,2]{1,0:T(8,128)} %concatenate.127.refs_0_, bf16[2,512,128]{2,1,0:T(8,128)(2,1)} %get-tuple-element.170.refs_1_.refs_4_, bf16[2,512,128]{2,1,0:T(8,128)(2,1)} %get-tuple-element.163.refs_2_.refs_4_, ...), custom_call_target="tpu_custom_call" | custom-call | tf_op jit(solution)/shard_map/out/pallas_call | solution.py:84
  183.1 19.9 %feed_forward.1 = (f32[4,512,1024]{2,1,0:T(8,128)}, bf16[4,512,1024]{2,1,0:T(8,128)(2,1)}, f32[512,1024]{1,0:T(8,128)}, bf16[512,1024]{1,0:T(8,128)(2,1)}) custom-call(bf16[512,1024]{1,0:T(8,128)(2,1)} %get-tuple-element.175.a, bf16[4,1024,2304]{2,1,0:T(8,128)(2,1)} %bitcast.247, bf16[4,1024,2304]{2,1,0:T(8,128)(2,1)} %bitcast.248, ...), custom_call_target="tpu_custom_call" | custom-call | tf_op jit(solution)/shard_map/feed_forward/pallas_call | solution.py:84
  204.1 3.9 enter_back.1
  208.0 18.4 %feed_back.2 = (bf16[2,1024,512]{2,1,0:T(8,128)(2,1)}, bf16[2,1024,512]{2,1,0:T(8,128)(2,1)}, bf16[2,1024,512]{2,1,0:T(8,128)(2,1)}, bf16[2,1024,512]{2,1,0:T(8,...) custom-call(s32[2,2]{1,0:T(2,128)} %copy-done.59, bf16[512,1024]{1,0:T(8,128)(2,1)} %get-tuple-element.188.refs_0_, ...), custom_call_target="tpu_custom_call" | custom-call | tf_op jit(solution)/shard_map/feed_back/pallas_call | solution.py:84
  227.6 24.6 %feed_back.3 = (bf16[2,1024,512]{2,1,0:T(8,128)(2,1)}, bf16[2,1024,512]{2,1,0:T(8,128)(2,1)}, bf16[2,1024,512]{2,1,0:T(8,128)(2,1)}, bf16[2,1024,512]{2,1,0:T(8,...) custom-call(s32[2,2]{1,0:T(2,128)} %copy-done.60, ...), custom_call_target="tpu_custom_call" | custom-call | tf_op jit(solution)/shard_map/feed_back/pallas_call | solution.py:84
  253.6 4.1 d_shrink.3
  259.4 3.4 d_expand.3
  264.0 8.1 %attended_back.1.refs_1_ = bf16[8,512,128]{2,1,0:T(8,128)(2,1)} custom-call(s32[2,8]{1,0:T(2,128)} %copy-done.65, bf16[512,1024]{1,0:T(8,128)(2,1)} %get-tuple-element.199.a, bf16[4,1024,2304]{2,1,0:T(8,128)(2,1)} %bitcast.253), custom_call_target="tpu_custom_call" | custom-call | tf_op jit(solution)/shard_map/attended_back/pallas_call | solution.py:84
  276.7 5.0 all-to-all-start.2
  284.6 10.8 %attend_back.6 = (bf16[2,512,128]{2,1,0:T(8,128)(2,1)}, f32[2,512,256]{2,1,0:T(8,128)}, bf16[2,512,256]{2,1,0:T(8,128)(2,1)}, f32[2,1,128]{2,1,0:T(1,128)}) custom-call(bf16[2,512,128]{2,1,0:T(8,128)(2,1)} %get-tuple-element.203.refs_0_, bf16[8,512,128]{2,1,0:T(8,128)(2,1)} %attended_back.1.refs_1_, f32[2,2,512]{2,1,0:T(2,128)} %get-tuple-element.204.refs_2_, ...), custom_call_target="tpu_custom_call" | custom-call | tf_op jit(solution)/shard_map/attend_back/pallas_call | solution.py:84
  295.4 10.6 %attend_back.7 = (bf16[2,512,128]{2,1,0:T(8,128)(2,1)}, f32[2,512,256]{2,1,0:T(8,128)}, bf16[2,512,256]{2,1,0:T(8,128)(2,1)}, f32[2,1,128]{2,1,0:T(1,128)}) custom-call(bf16[2,512,128]{2,1,0:T(8,128)(2,1)} %get-tuple-element.206.refs_0_, bf16[8,512,128]{2,1,0:T(8,128)(2,1)} %attended_back.1.refs_1_, f32[2,2,512]{2,1,0:T(2,128)} %get-tuple-element.207.refs_2_, ...), custom_call_target="tpu_custom_call" | custom-call | tf_op jit(solution)/shard_map/attend_back/pallas_call | solution.py:84
  307.2 3.4 collective-permute-done.28.refs_2_
  310.7 3.6 d_shrink.4
  320.5 5.5 %d_in.6 = (bf16[512,512]{1,0:T(8,128)(2,1)}, bf16[512,512]{1,0:T(8,128)(2,1)}, bf16[512,512]{1,0:T(8,128)(2,1)}, bf16[512,512]{1,0:T(8,128)(2,1)}) custom-call(bf16[1024,512]{1,0:T(8,128)(2,1)} %get-tuple-element.263.refs_0_, bf16[1024,512]{1,0:T(8,128)(2,1)} %get-tuple-element.212.refs_1_, bf16[2,512,128]{2,1,0:T(8,128)(2,1)} %get-tuple-element.205.refs_2_.refs_5_, ...), custom_call_target="tpu_custom_call" | custom-call | tf_op jit(solution)/shard_map/d_in/pallas_call | solution.py:84
  328.6 6.3 %attend_back.8 = (bf16[1,512,128]{2,1,0:T(8,128)(2,1)}, f32[1,512,256]{2,1,0:T(8,128)}, bf16[1,512,256]{2,1,0:T(8,128)(2,1)}, f32[1,1,128]{2,1,0:T(1,128)}) custom-call(bf16[2,512,128]{2,1,0:T(8,128)(2,1)} %get-tuple-element.233.refs_0_, bf16[8,512,128]{2,1,0:T(8,128)(2,1)} %attended_back.1.refs_1_, f32[2,2,512]{2,1,0:T(2,128)} %get-tuple-element.217.refs_2_, ...), custom_call_target="tpu_custom_call" | custom-call | tf_op jit(solution)/shard_map/attend_back/pallas_call | solution.py:84
  336.2 5.4 %d_in.7 = bf16[2,1024,512]{2,1,0:T(8,128)(2,1)} custom-call(bf16[1024,512]{1,0:T(8,128)(2,1)} %get-tuple-element.263.refs_0_, bf16[1024,512]{1,0:T(8,128)(2,1)} %get-tuple-element.212.refs_1_, bf16[2,512,128]{2,1,0:T(8,128)(2,1)} %get-tuple-element.208.refs_2_.refs_4_, bf16[2,512,256]{2,1,0:T(8,128)(2,1)} %add_convert_fusion.refs_3_.refs_10_, ...), custom_call_target="tpu_custom_call" | custom-call | tf_op jit(solution)/shard_map/d_in/pallas_call | solution.py:84
  341.6 6.2 %attend_back.9 = (bf16[1,512,128]{2,1,0:T(8,128)(2,1)}, f32[1,512,256]{2,1,0:T(8,128)}, bf16[1,512,256]{2,1,0:T(8,128)(2,1)}, f32[1,1,128]{2,1,0:T(1,128)}) custom-call(bf16[2,512,128]{2,1,0:T(8,128)(2,1)} %get-tuple-element.235.refs_0_, bf16[8,512,128]{2,1,0:T(8,128)(2,1)} %attended_back.1.refs_1_, f32[2,2,512]{2,1,0:T(2,128)} %get-tuple-element.226.refs_2_, ...), custom_call_target="tpu_custom_call" | custom-call | tf_op jit(solution)/shard_map/attend_back/pallas_call | solution.py:84
  347.9 3.3 d_shrink.5
  356.9 3.6 d_in.8
  360.5 6.3 %attend_back.10 = (bf16[1,512,128]{2,1,0:T(8,128)(2,1)}, f32[1,512,256]{2,1,0:T(8,128)}, bf16[1,512,256]{2,1,0:T(8,128)(2,1)}, f32[1,1,128]{2,1,0:T(1,128)}) custom-call(bf16[2,512,128]{2,1,0:T(8,128)(2,1)} %get-tuple-element.233.refs_0_, bf16[8,512,128]{2,1,0:T(8,128)(2,1)} %attended_back.1.refs_1_, f32[2,2,512]{2,1,0:T(2,128)} %get-tuple-element.217.refs_2_, ...), custom_call_target="tpu_custom_call" | custom-call | tf_op jit(solution)/shard_map/attend_back/pallas_call | solution.py:84
  366.8 6.3 %attend_back.11 = (bf16[1,512,128]{2,1,0:T(8,128)(2,1)}, f32[1,512,256]{2,1,0:T(8,128)}, bf16[1,512,256]{2,1,0:T(8,128)(2,1)}, f32[1,1,128]{2,1,0:T(1,128)}) custom-call(bf16[2,512,128]{2,1,0:T(8,128)(2,1)} %get-tuple-element.235.refs_0_, bf16[8,512,128]{2,1,0:T(8,128)(2,1)} %attended_back.1.refs_1_, f32[2,2,512]{2,1,0:T(2,128)} %get-tuple-element.226.refs_2_, ...), custom_call_target="tpu_custom_call" | custom-call | tf_op jit(solution)/shard_map/attend_back/pallas_call | solution.py:84
  373.9 3.7 collective-permute-done.37.refs_3_
  384.2 3.5 d_in.9
  388.1 13.0 %collective-permute-done.42.refs_7_ = bf16[2,1024,512]{2,1,0:T(8,128)(2,1)S(1)} collective-permute-done((bf16[2,1024,512]{2,1,0:T(8,128)(2,1)}, bf16[2,1024,512]{2,1,0:T(8,128)(2,1)S(1)}, u32[]{:S(2)}, u32[]{:S(2)}) %collective-permute-start.42) | collective-permute-done | bytes 2097184 | tf_op jit(solution)/shard_map/ppermute | solution.py:898
  402.4 4.3 d_in.10
  408.5 12.0 %tokens_back.1 = (bf16[512,1024]{1,0:T(8,128)(2,1)}, f32[2,1024]{1,0:T(2,128)}) custom-call(bf16[1,512,128]{2,1,0:T(8,128)(2,1)} %get-tuple-element.246.refs_0_.refs_2_, bf16[1,512,128]{2,1,0:T(8,128)(2,1)} %get-tuple-element.227.refs_2_.refs_1_, bf16[1,512,128]{2,1,0:T(8,128)(2,1)} %get-tuple-element.234.refs_2_, ...), custom_call_target="tpu_custom_call" | custom-call | tf_op jit(solution)/shard_map/tokens_back/pallas_call | solution.py:84
  427.8 4.8 all-to-all-start.3
  436.9 4.9 d_in.11
  443.5 3.8 collective-permute-done.49
  448.0 10.9 %all-to-all-done.3 = bf16[4,512,256]{2,1,0:T(8,128)(2,1)S(1)} async-done(((bf16[4,512,256]{2,1,0:T(8,128)(2,1)}), bf16[4,512,256]{2,1,0:T(8,128)(2,1)S(1)}, u32[]{:S(2)}, u32[]{:S(2)}) %all-to-all-start.3) | async-done | bytes 1048608 | tf_op jit(solution)/shard_map/all_to_all | solution.py:932
  494.0 6.5 %collective-permute-done.57 = bf16[256,512]{1,0:T(8,128)(2,1)S(1)} collective-permute-done((bf16[256,512]{1,0:T(8,128)(2,1)}, bf16[256,512]{1,0:T(8,128)(2,1)S(1)}, u32[]{:S(2)}, u32[]{:S(2)}) %collective-permute-start.57) | collective-permute-done | bytes 262176 | tf_op jit(solution)/shard_map/ppermute | solution.py:898
  (527 shorter events, 139.0 us)
Async XLA Ops:
  7.2 159.6 %all-gather.2.cloned.1.call-start = ((), (), s32[]{:S(2)}) async-start(), calls=%async_computation.7 | async-start | bytes 20054016 | tf_op jit(solution)/shard_map/all_gather | solution.py:804
  12.7 20.5 %collective-permute-start = (bf16[2,512,256]{2,1,0:T(8,128)(2,1)}, bf16[2,512,256]{2,1,0:T(8,128)(2,1)S(1)}, u32[]{:S(2)}, u32[]{:S(2)}) collective-permute-start(bf16[2,512,256]{2,1,0:T(8,128)(2,1)} %get-tuple-element.357), channel_id=1, source_target_pairs={{0,4},{4,0},{1,5},{5,1},{2,6},{6,2},{3,7},{7,3},{8,12},{12,8},{9,1... | collective-permute-start | bytes 1572872 | tf_op jit(solution)/shard_map/ppermute | solution.py:898
  13.6 17.5 %collective-permute-start.1 = (bf16[256,384]{1,0:T(8,128)(2,1)S(1)}, bf16[256,384]{1,0:T(8,128)(2,1)S(1)}, u32[]{:S(2)}, u32[]{:S(2)}) collective-permute-start(bf16[256,384]{1,0:T(8,128)(2,1)S(1)} %bitcast.282), channel_id=1, source_target_pairs={{0,1},{1,0},{2,3},{3,2},{4,5},{5,4},{6,7},{7,6},{8,9},{9,8},{10,11... | collective-permute-start | bytes 589832 | tf_op jit(solution)/shard_map/ppermute | solution.py:901
  31.1 23.4 %collective-permute-start.8 = (bf16[512,384]{1,0:T(8,128)(2,1)S(1)}, bf16[512,384]{1,0:T(8,128)(2,1)S(1)}, u32[]{:S(2)}, u32[]{:S(2)}) collective-permute-start(bf16[512,384]{1,0:T(8,128)(2,1)S(1)} %pad_maximum_fusion.12), channel_id=1, source_target_pairs={{0,2},{1,3},{2,0},{3,1},{4,6},{5,7},{6,4},{7,5},{8,10},{9,11},{10,... | collective-permute-start | bytes 1179656 | tf_op jit(solution)/shard_map/ppermute | solution.py:901
  55.9 34.9 %all-to-all-start = ((bf16[4,512,256]{2,1,0:T(8,128)(2,1)}), bf16[4,512,256]{2,1,0:T(8,128)(2,1)S(1)}, u32[]{:S(2)}, u32[]{:S(2)}) async-start(bf16[4,512,256]{2,1,0:T(8,128)(2,1)} %pad_maximum_fusion.2), calls=%async_computation | async-start | bytes 2097152 | tf_op jit(solution)/shard_map/all_to_all | solution.py:915
  59.7 17.5 %collective-permute-start.11 = (bf16[1024,256]{1,0:T(8,128)(2,1)S(1)}, bf16[1024,256]{1,0:T(8,128)(2,1)S(1)}, u32[]{:S(2)}, u32[]{:S(2)}) collective-permute-start(bf16[1024,256]{1,0:T(8,128)(2,1)S(1)} %get-tuple-element.359), channel_id=1, source_target_pairs={{0,8},{8,0},{1,9},{9,1},{2,10},{10,2},{3,11},{11,3},{4,12},{12,4},... | collective-permute-start | bytes 1572872 | tf_op jit(solution)/shard_map/ppermute | solution.py:898
  77.3 24.3 %collective-permute-start.14 = (bf16[2,1024,256]{2,1,0:T(8,128)(2,1)S(1)}, bf16[2,1024,256]{2,1,0:T(8,128)(2,1)}, u32[]{:S(2)}, u32[]{:S(2)}) collective-permute-start(bf16[2,1024,256]{2,1,0:T(8,128)(2,1)S(1)} %pad_maximum_fusion.3.h.refs_16_), channel_id=1, source_target_pairs={{0,16},{16,0},{1,17},{17,1},{2,18},{18,2},{3,19},{19,3},{4,20},{20... | collective-permute-start | bytes 3145736 | tf_op jit(solution)/shard_map/ppermute | solution.py:898
  79.7 54.2 %collective-permute-start.21 = (bf16[2,512,256]{2,1,0:T(8,128)(2,1)}, bf16[2,512,256]{2,1,0:T(8,128)(2,1)}, u32[]{:S(2)}, u32[]{:S(2)}) collective-permute-start(bf16[2,512,256]{2,1,0:T(8,128)(2,1)} %get-tuple-element.351), channel_id=1, source_target_pairs={{0,4},{4,0},{1,5},{5,1},{2,6},{6,2},{3,7},{7,3},{8,12},{12,8},{9,1... | collective-permute-start | bytes 1572872 | tf_op jit(solution)/shard_map/ppermute | solution.py:898
  91.9 16.2 %collective-permute-start.10 = (bf16[2,1024,128]{2,1,0:T(8,128)(2,1)S(1)}, bf16[2,1024,128]{2,1,0:T(8,128)(2,1)S(1)}, u32[]{:S(2)}, u32[]{:S(2)}) collective-permute-start(bf16[2,1024,128]{2,1,0:T(8,128)(2,1)S(1)} %pad_maximum_fusion.9), channel_id=1, source_target_pairs={{0,8},{8,0},{1,9},{9,1},{2,10},{10,2},{3,11},{11,3},{4,12},{12,4},... | collective-permute-start | bytes 1572872 | tf_op jit(solution)/shard_map/ppermute | solution.py:898
  93.0 24.7 %collective-permute-start.13 = (bf16[2,1024,256]{2,1,0:T(8,128)(2,1)S(1)}, bf16[2,1024,256]{2,1,0:T(8,128)(2,1)S(1)}, u32[]{:S(2)}, u32[]{:S(2)}) collective-permute-start(bf16[2,1024,256]{2,1,0:T(8,128)(2,1)S(1)} %pad_maximum_fusion.3.h.refs_16_), channel_id=1, source_target_pairs={{0,4},{4,0},{1,5},{5,1},{2,6},{6,2},{3,7},{7,3},{8,12},{12,8},{9,1... | collective-permute-start | bytes 3145736 | tf_op jit(solution)/shard_map/ppermute | solution.py:898
  101.6 26.3 %collective-permute-start.16 = (bf16[2,1024,256]{2,1,0:T(8,128)(2,1)}, bf16[2,1024,256]{2,1,0:T(8,128)(2,1)S(1)}, u32[]{:S(2)}, u32[]{:S(2)}) collective-permute-start(bf16[2,1024,256]{2,1,0:T(8,128)(2,1)} %collective-permute-done.14.h.refs_18_), channel_id=1, source_target_pairs={{0,4},{4,0},{1,5},{5,1},{2,6},{6,2},{3,7},{7,3},{8,12},{12,8},{9,1... | collective-permute-start | bytes 3145736 | tf_op jit(solution)/shard_map/ppermute | solution.py:898
  108.3 9.5 %collective-permute-start.12 = (bf16[2,1024,128]{2,1,0:T(8,128)(2,1)S(1)}, bf16[2,1024,128]{2,1,0:T(8,128)(2,1)S(1)}, u32[]{:S(2)}, u32[]{:S(2)}) collective-permute-start(bf16[2,1024,128]{2,1,0:T(8,128)(2,1)S(1)} %pad_maximum_fusion.10.g.refs_12_), channel_id=1, source_target_pairs={{0,4},{4,0},{1,5},{5,1},{2,6},{6,2},{3,7},{7,3},{8,12},{12,8},{9,1... | collective-permute-start | bytes 1572872 | tf_op jit(solution)/shard_map/ppermute | solution.py:898
  108.4 19.5 %collective-permute-start.15 = (bf16[2,1024,128]{2,1,0:T(8,128)(2,1)S(1)}, bf16[2,1024,128]{2,1,0:T(8,128)(2,1)S(1)}, u32[]{:S(2)}, u32[]{:S(2)}) collective-permute-start(bf16[2,1024,128]{2,1,0:T(8,128)(2,1)S(1)} %pad_maximum_fusion.11.g.refs_14_), channel_id=1, source_target_pairs={{0,4},{4,0},{1,5},{5,1},{2,6},{6,2},{3,7},{7,3},{8,12},{12,8},{9,1... | collective-permute-start | bytes 1572872 | tf_op jit(solution)/shard_map/ppermute | solution.py:898
  117.7 25.3 %collective-permute-start.18 = (bf16[2,512,256]{2,1,0:T(8,128)(2,1)}, bf16[2,512,256]{2,1,0:T(8,128)(2,1)S(1)}, u32[]{:S(2)}, u32[]{:S(2)}) collective-permute-start(bf16[2,512,256]{2,1,0:T(8,128)(2,1)} %get-tuple-element.159.refs_1_.refs_3_), channel_id=1, source_target_pairs={{0,4},{4,0},{1,5},{5,1},{2,6},{6,2},{3,7},{7,3},{8,12},{12,8},{9,1... | collective-permute-start | bytes 1572872 | tf_op jit(solution)/shard_map/ppermute | solution.py:898
  123.3 11.8 %collective-permute-start.17 = (bf16[2,512,256]{2,1,0:T(8,128)(2,1)}, bf16[2,512,256]{2,1,0:T(8,128)(2,1)S(1)}, u32[]{:S(2)}, u32[]{:S(2)}) collective-permute-start(bf16[2,512,256]{2,1,0:T(8,128)(2,1)} %get-tuple-element.160.refs_1_.refs_3_), channel_id=1, source_target_pairs={{0,4},{4,0},{1,5},{5,1},{2,6},{6,2},{3,7},{7,3},{8,12},{12,8},{9,1... | collective-permute-start | bytes 1572872 | tf_op jit(solution)/shard_map/ppermute | solution.py:898
  133.4 17.5 %collective-permute-start.19 = (bf16[2,512,256]{2,1,0:T(8,128)(2,1)}, bf16[2,512,256]{2,1,0:T(8,128)(2,1)S(1)}, u32[]{:S(2)}, u32[]{:S(2)}) collective-permute-start(bf16[2,512,256]{2,1,0:T(8,128)(2,1)} %get-tuple-element.166.refs_1_.refs_3_), channel_id=1, source_target_pairs={{0,4},{4,0},{1,5},{5,1},{2,6},{6,2},{3,7},{7,3},{8,12},{12,8},{9,1... | collective-permute-start | bytes 1572872 | tf_op jit(solution)/shard_map/ppermute | solution.py:898
  133.7 25.1 %collective-permute-start.20 = (bf16[2,512,256]{2,1,0:T(8,128)(2,1)S(1)}, bf16[2,512,256]{2,1,0:T(8,128)(2,1)S(1)}, u32[]{:S(2)}, u32[]{:S(2)}) collective-permute-start(bf16[2,512,256]{2,1,0:T(8,128)(2,1)S(1)} %copy-done.23), channel_id=1, source_target_pairs={{0,4},{4,0},{1,5},{5,1},{2,6},{6,2},{3,7},{7,3},{8,12},{12,8},{9,1... | collective-permute-start | bytes 1572872 | tf_op jit(solution)/shard_map/ppermute | solution.py:898
  168.0 35.0 %all-to-all-start.1 = ((bf16[4,512,256]{2,1,0:T(8,128)(2,1)}), bf16[4,512,256]{2,1,0:T(8,128)(2,1)S(1)}, u32[]{:S(2)}, u32[]{:S(2)}) async-start(bf16[4,512,256]{2,1,0:T(8,128)(2,1)} %pad_maximum_fusion.5), calls=%async_computation.1 | async-start | bytes 2097152 | tf_op jit(solution)/shard_map/all_to_all | solution.py:915
  226.4 25.8 %collective-permute-start.22 = (bf16[2,1024,512]{2,1,0:T(8,128)(2,1)}, bf16[2,1024,512]{2,1,0:T(8,128)(2,1)}, u32[]{:S(2)}, u32[]{:S(2)}) collective-permute-start(bf16[2,1024,512]{2,1,0:T(8,128)(2,1)} %get-tuple-element.187), channel_id=1, source_target_pairs={{0,4},{4,0},{1,5},{5,1},{2,6},{6,2},{3,7},{7,3},{8,12},{12,8},{9,1... | collective-permute-start | bytes 6291464 | tf_op jit(solution)/shard_map/ppermute | solution.py:898
  227.0 25.2 %collective-permute-start.23 = (bf16[2,1024,512]{2,1,0:T(8,128)(2,1)}, bf16[2,1024,512]{2,1,0:T(8,128)(2,1)S(1)}, u32[]{:S(2)}, u32[]{:S(2)}) collective-permute-start(bf16[2,1024,512]{2,1,0:T(8,128)(2,1)} %get-tuple-element.193), channel_id=1, source_target_pairs={{0,4},{4,0},{1,5},{5,1},{2,6},{6,2},{3,7},{7,3},{8,12},{12,8},{9,1... | collective-permute-start | bytes 6291464 | tf_op jit(solution)/shard_map/ppermute | solution.py:898
  227.1 25.2 %collective-permute-start.24 = (bf16[2,1024,512]{2,1,0:T(8,128)(2,1)}, bf16[2,1024,512]{2,1,0:T(8,128)(2,1)S(1)}, u32[]{:S(2)}, u32[]{:S(2)}) collective-permute-start(bf16[2,1024,512]{2,1,0:T(8,128)(2,1)} %get-tuple-element.194), channel_id=1, source_target_pairs={{0,4},{4,0},{1,5},{5,1},{2,6},{6,2},{3,7},{7,3},{8,12},{12,8},{9,1... | collective-permute-start | bytes 6291464 | tf_op jit(solution)/shard_map/ppermute | solution.py:898
  227.5 24.8 %collective-permute-start.25 = (bf16[2,1024,512]{2,1,0:T(8,128)(2,1)}, bf16[2,1024,512]{2,1,0:T(8,128)(2,1)S(1)}, u32[]{:S(2)}, u32[]{:S(2)}) collective-permute-start(bf16[2,1024,512]{2,1,0:T(8,128)(2,1)} %get-tuple-element.195), channel_id=1, source_target_pairs={{0,4},{4,0},{1,5},{5,1},{2,6},{6,2},{3,7},{7,3},{8,12},{12,8},{9,1... | collective-permute-start | bytes 6291464 | tf_op jit(solution)/shard_map/ppermute | solution.py:898
  257.7 49.5 %collective-permute-start.27 = (bf16[2,1024,512]{2,1,0:T(8,128)(2,1)}, bf16[2,1024,512]{2,1,0:T(8,128)(2,1)}, u32[]{:S(2)}, u32[]{:S(2)}) collective-permute-start(bf16[2,1024,512]{2,1,0:T(8,128)(2,1)} %d_shrink.3), channel_id=1, source_target_pairs={{0,8},{8,0},{1,9},{9,1},{2,10},{10,2},{3,11},{11,3},{4,12},{12,4},... | collective-permute-start | bytes 6291464 | tf_op jit(solution)/shard_map/ppermute | solution.py:898
  262.9 47.8 %collective-permute-start.28 = (bf16[2,1024,512]{2,1,0:T(8,128)(2,1)}, bf16[2,1024,512]{2,1,0:T(8,128)(2,1)S(1)}, u32[]{:S(2)}, u32[]{:S(2)}) collective-permute-start(bf16[2,1024,512]{2,1,0:T(8,128)(2,1)} %d_expand.3), channel_id=1, source_target_pairs={{0,16},{16,0},{1,17},{17,1},{2,18},{18,2},{3,19},{19,3},{4,20},{20... | collective-permute-start | bytes 6291464 | tf_op jit(solution)/shard_map/ppermute | solution.py:898
  276.7 30.6 %all-to-all-start.2 = ((bf16[4,512,256]{2,1,0:T(8,128)(2,1)}), bf16[4,512,256]{2,1,0:T(8,128)(2,1)}, u32[]{:S(2)}, u32[]{:S(2)}) async-start(bf16[4,512,256]{2,1,0:T(8,128)(2,1)} %bitcast.263), calls=%async_computation.2 | async-start | bytes 2097152 | tf_op jit(solution)/shard_map/all_to_all | solution.py:932
  281.7 126.8 %reduce-scatter.4.cloned.1.call-start = ((), (), s32[]{:S(2)}) async-start(), calls=%async_computation.8 | async-start | bytes 1310720 | tf_op jit(solution)/shard_map/reduce_scatter | solution.py:1080
  305.9 9.5 %collective-permute-start.29 = (bf16[2,512,256]{2,1,0:T(8,128)(2,1)}, bf16[2,512,256]{2,1,0:T(8,128)(2,1)}, u32[]{:S(2)}, u32[]{:S(2)}) collective-permute-start(bf16[2,512,256]{2,1,0:T(8,128)(2,1)} %get-tuple-element.214), channel_id=1, source_target_pairs={{0,4},{4,0},{1,5},{5,1},{2,6},{6,2},{3,7},{7,3},{8,12},{12,8},{9,1... | collective-permute-start | bytes 1572872 | tf_op jit(solution)/shard_map/ppermute | solution.py:898
  306.0 20.6 %collective-permute-start.30 = (bf16[2,512,256]{2,1,0:T(8,128)(2,1)}, bf16[2,512,256]{2,1,0:T(8,128)(2,1)S(1)}, u32[]{:S(2)}, u32[]{:S(2)}) collective-permute-start(bf16[2,512,256]{2,1,0:T(8,128)(2,1)} %get-tuple-element.221), channel_id=1, source_target_pairs={{0,4},{4,0},{1,5},{5,1},{2,6},{6,2},{3,7},{7,3},{8,12},{12,8},{9,1... | collective-permute-start | bytes 1572872 | tf_op jit(solution)/shard_map/ppermute | solution.py:898
  314.3 33.6 %collective-permute-start.35 = (bf16[1,1024,512]{2,1,0:T(8,128)(2,1)}, bf16[1,1024,512]{2,1,0:T(8,128)(2,1)}, u32[]{:S(2)}, u32[]{:S(2)}) collective-permute-start(bf16[1,1024,512]{2,1,0:T(8,128)(2,1)} %d_shrink.4), channel_id=1, source_target_pairs={{0,16},{16,0},{1,17},{17,1},{2,18},{18,2},{3,19},{19,3},{4,20},{20... | collective-permute-start | bytes 3145736 | tf_op jit(solution)/shard_map/ppermute | solution.py:898
  326.0 8.8 %collective-permute-start.31 = (bf16[512,512]{1,0:T(8,128)(2,1)}, bf16[512,512]{1,0:T(8,128)(2,1)S(1)}, u32[]{:S(2)}, u32[]{:S(2)}) collective-permute-start(bf16[512,512]{1,0:T(8,128)(2,1)} %get-tuple-element.215), channel_id=1, source_target_pairs={{0,4},{4,0},{1,5},{5,1},{2,6},{6,2},{3,7},{7,3},{8,12},{12,8},{9,1... | collective-permute-start | bytes 1572872 | tf_op jit(solution)/shard_map/ppermute | solution.py:898
  326.0 8.8 %collective-permute-start.32 = (bf16[512,512]{1,0:T(8,128)(2,1)}, bf16[512,512]{1,0:T(8,128)(2,1)S(1)}, u32[]{:S(2)}, u32[]{:S(2)}) collective-permute-start(bf16[512,512]{1,0:T(8,128)(2,1)} %get-tuple-element.222), channel_id=1, source_target_pairs={{0,4},{4,0},{1,5},{5,1},{2,6},{6,2},{3,7},{7,3},{8,12},{12,8},{9,1... | collective-permute-start | bytes 1572872 | tf_op jit(solution)/shard_map/ppermute | solution.py:898
  351.2 122.0 %reduce-scatter.8.cloned.1.call-start = ((), (), s32[]{:S(2)}) async-start(), calls=%async_computation.10 | async-start | bytes 1310720 | tf_op jit(solution)/shard_map/reduce_scatter | solution.py:1080
  352.3 25.4 %collective-permute-start.37 = (bf16[1,1024,512]{2,1,0:T(8,128)(2,1)}, bf16[1,1024,512]{2,1,0:T(8,128)(2,1)S(1)}, u32[]{:S(2)}, u32[]{:S(2)}) collective-permute-start(bf16[1,1024,512]{2,1,0:T(8,128)(2,1)} %d_expand.4), channel_id=1, source_target_pairs={{0,8},{8,0},{1,9},{9,1},{2,10},{10,2},{3,11},{11,3},{4,12},{12,4},... | collective-permute-start | bytes 3145736 | tf_op jit(solution)/shard_map/ppermute | solution.py:898
  352.7 20.9 %collective-permute-start.39 = (bf16[1,512,256]{2,1,0:T(8,128)(2,1)}, bf16[1,512,256]{2,1,0:T(8,128)(2,1)S(1)}, u32[]{:S(2)}, u32[]{:S(2)}) collective-permute-start(bf16[1,512,256]{2,1,0:T(8,128)(2,1)} %get-tuple-element.244), channel_id=1, source_target_pairs={{0,4},{4,0},{1,5},{5,1},{2,6},{6,2},{3,7},{7,3},{8,12},{12,8},{9,1... | collective-permute-start | bytes 786440 | tf_op jit(solution)/shard_map/ppermute | solution.py:898
  353.3 47.8 %collective-permute-start.42 = (bf16[2,1024,512]{2,1,0:T(8,128)(2,1)}, bf16[2,1024,512]{2,1,0:T(8,128)(2,1)S(1)}, u32[]{:S(2)}, u32[]{:S(2)}) collective-permute-start(bf16[2,1024,512]{2,1,0:T(8,128)(2,1)} %d_in.7), channel_id=1, source_target_pairs={{0,16},{16,0},{1,17},{17,1},{2,18},{18,2},{3,19},{19,3},{4,20},{20... | collective-permute-start | bytes 6291464 | tf_op jit(solution)/shard_map/ppermute | solution.py:898
  356.2 68.6 %collective-permute-start.26 = (bf16[2,512,256]{2,1,0:T(8,128)(2,1)}, bf16[2,512,256]{2,1,0:T(8,128)(2,1)}, u32[]{:S(2)}, u32[]{:S(2)}) collective-permute-start(bf16[2,512,256]{2,1,0:T(8,128)(2,1)} %dynamic-slice_bitcast_fusion.1), channel_id=1, source_target_pairs={{0,4},{4,0},{1,5},{5,1},{2,6},{6,2},{3,7},{7,3},{8,12},{12,8},{9,1... | collective-permute-start | bytes 1572872 | tf_op jit(solution)/shard_map/ppermute | solution.py:898
  373.8 14.3 %collective-permute-start.40 = (bf16[512,512]{1,0:T(8,128)(2,1)}, bf16[512,512]{1,0:T(8,128)(2,1)}, u32[]{:S(2)}, u32[]{:S(2)}) collective-permute-start(bf16[512,512]{1,0:T(8,128)(2,1)} %get-tuple-element.232), channel_id=1, source_target_pairs={{0,4},{4,0},{1,5},{5,1},{2,6},{6,2},{3,7},{7,3},{8,12},{12,8},{9,1... | collective-permute-start | bytes 1572872 | tf_op jit(solution)/shard_map/ppermute | solution.py:898
  406.7 29.3 %collective-permute-start.48 = (bf16[1,1024,512]{2,1,0:T(8,128)(2,1)}, bf16[1,1024,512]{2,1,0:T(8,128)(2,1)}, u32[]{:S(2)}, u32[]{:S(2)}) collective-permute-start(bf16[1,1024,512]{2,1,0:T(8,128)(2,1)} %d_in.10), channel_id=1, source_target_pairs={{0,8},{8,0},{1,9},{9,1},{2,10},{10,2},{3,11},{11,3},{4,12},{12,4},... | collective-permute-start | bytes 3145736 | tf_op jit(solution)/shard_map/ppermute | solution.py:898
  426.1 10.0 %collective-permute-start.46 = (bf16[512,512]{1,0:T(8,128)(2,1)}, bf16[512,512]{1,0:T(8,128)(2,1)S(1)}, u32[]{:S(2)}, u32[]{:S(2)}) collective-permute-start(bf16[512,512]{1,0:T(8,128)(2,1)} %get-tuple-element.241), channel_id=1, source_target_pairs={{0,4},{4,0},{1,5},{5,1},{2,6},{6,2},{3,7},{7,3},{8,12},{12,8},{9,1... | collective-permute-start | bytes 1572872 | tf_op jit(solution)/shard_map/ppermute | solution.py:898
  426.7 9.4 %collective-permute-start.47 = (bf16[512,512]{1,0:T(8,128)(2,1)}, bf16[512,512]{1,0:T(8,128)(2,1)}, u32[]{:S(2)}, u32[]{:S(2)}) collective-permute-start(bf16[512,512]{1,0:T(8,128)(2,1)} %get-tuple-element.264), channel_id=1, source_target_pairs={{0,4},{4,0},{1,5},{5,1},{2,6},{6,2},{3,7},{7,3},{8,12},{12,8},{9,1... | collective-permute-start | bytes 1572872 | tf_op jit(solution)/shard_map/ppermute | solution.py:898
  427.8 31.1 %all-to-all-start.3 = ((bf16[4,512,256]{2,1,0:T(8,128)(2,1)}), bf16[4,512,256]{2,1,0:T(8,128)(2,1)S(1)}, u32[]{:S(2)}, u32[]{:S(2)}) async-start(bf16[4,512,256]{2,1,0:T(8,128)(2,1)} %bitcast.240), calls=%async_computation.4 | async-start | bytes 2097152 | tf_op jit(solution)/shard_map/all_to_all | solution.py:932
  432.6 57.3 %reduce-scatter.6.cloned.1.call-start = ((), (), s32[]{:S(2)}) async-start(), calls=%async_computation.9 | async-start | bytes 1310720 | tf_op jit(solution)/shard_map/reduce_scatter | solution.py:1080
  465.4 10.7 %collective-permute-start.53 = (f32[64,128]{1,0:T(8,128)S(1)}, f32[64,128]{1,0:T(8,128)S(1)}, u32[]{:S(2)}, u32[]{:S(2)}) collective-permute-start(f32[64,128]{1,0:T(8,128)S(1)} %get-tuple-element.414), channel_id=1, source_target_pairs={{0,3},{1,2},{2,1},{3,0},{4,7},{5,6},{6,5},{7,4},{8,11},{9,10},{10,... | collective-permute-start | bytes 98312 | tf_op jit(solution)/shard_map/ppermute | solution.py:901
  466.9 9.1 %collective-permute-start.52 = (f32[64,128]{1,0:T(8,128)S(1)}, f32[64,128]{1,0:T(8,128)S(1)}, u32[]{:S(2)}, u32[]{:S(2)}) collective-permute-start(f32[64,128]{1,0:T(8,128)S(1)} %get-tuple-element.413), channel_id=1, source_target_pairs={{0,2},{1,3},{2,0},{3,1},{4,6},{5,7},{6,4},{7,5},{8,10},{9,11},{10,... | collective-permute-start | bytes 98312 | tf_op jit(solution)/shard_map/ppermute | solution.py:901
  466.9 9.2 %collective-permute-start.51 = (f32[64,128]{1,0:T(8,128)S(1)}, f32[64,128]{1,0:T(8,128)S(1)}, u32[]{:S(2)}, u32[]{:S(2)}) collective-permute-start(f32[64,128]{1,0:T(8,128)S(1)} %get-tuple-element.412), channel_id=1, source_target_pairs={{0,1},{1,0},{2,3},{3,2},{4,5},{5,4},{6,7},{7,6},{8,9},{9,8},{10,11... | collective-permute-start | bytes 98312 | tf_op jit(solution)/shard_map/ppermute | solution.py:901
  472.3 13.1 %collective-permute-start.59 = (bf16[256,512]{1,0:T(8,128)(2,1)}, bf16[256,512]{1,0:T(8,128)(2,1)S(1)}, u32[]{:S(2)}, u32[]{:S(2)}) collective-permute-start(bf16[256,512]{1,0:T(8,128)(2,1)} %gate.13), channel_id=1, source_target_pairs={{0,16},{16,0},{1,17},{17,1},{2,18},{18,2},{3,19},{19,3},{4,20},{20... | collective-permute-start | bytes 786440 | tf_op jit(solution)/shard_map/ppermute | solution.py:898
  474.9 10.5 %collective-permute-start.58 = (bf16[256,512]{1,0:T(8,128)(2,1)}, bf16[256,512]{1,0:T(8,128)(2,1)S(1)}, u32[]{:S(2)}, u32[]{:S(2)}) collective-permute-start(bf16[256,512]{1,0:T(8,128)(2,1)} %gate.14), channel_id=1, source_target_pairs={{0,16},{16,0},{1,17},{17,1},{2,18},{18,2},{3,19},{19,3},{4,20},{20... | collective-permute-start | bytes 786440 | tf_op jit(solution)/shard_map/ppermute | solution.py:898
  491.6 8.9 %collective-permute-start.57 = (bf16[256,512]{1,0:T(8,128)(2,1)}, bf16[256,512]{1,0:T(8,128)(2,1)S(1)}, u32[]{:S(2)}, u32[]{:S(2)}) collective-permute-start(bf16[256,512]{1,0:T(8,128)(2,1)} %gate.15), channel_id=1, source_target_pairs={{0,16},{16,0},{1,17},{17,1},{2,18},{18,2},{3,19},{19,3},{4,20},{20... | collective-permute-start | bytes 786440 | tf_op jit(solution)/shard_map/ppermute | solution.py:898
  (105 other events, 667.3 us)
Sparse Core Ops, SparseCore 0:
  11.9 141.0 all-gather.1
  351.3 26.7 reduce-scatter.3
  382.0 26.8 reduce-scatter.7
  462.6 26.5 reduce-scatter.5

commit v5 on v4

--- a/solution.py
+++ b/solution.py
@@ -985,10 +985,10 @@
         near = after(near, one_pair)
         far = self.swap(near, "dp")
         kv = [near, self.swap(near, "core"), far, self.swap(far, "core")]
-        one_pair, held = lax.optimization_barrier((one_pair, held))
         got = self.swap(one_pair, "y")
         near = jnp.stack([one_pair[0], got[0]])
         far = jnp.stack([one_pair[1], got[1]])
+        near, held = lax.optimization_barrier((near, held))
         queries = [near, self.swap(near, "core"), far, self.swap(far, "core")]
         return queries, kv, held
 

time: 515 us -> 506 us (0.983)
  waiting for transfers between devices: 111 us -> 98.6 us
    all_to_all x2, waiting for transfers between devices: 11 us -> 0.01 us  [scatter(): pieces = lax.all_to_all(jnp.stack(pieces), 'lat', 0, 0, tiled=True)]
    unnamed x184 -> x180, local copies, waits for them, and re-layouts: 18.7 us -> 18.2 us
  transfers between devices with their start and end apart: 68 -> 68, of which waited for: 17 -> 14; matrix products, arithmetic and copies ran while one was open for 9% -> 10% of each run, Pallas kernels for 44% -> 44%
where the time goes in v5:
time: 506 us; the launch traced here: 501 us
  Pallas kernels  254 us (50%)
  waiting for transfers between devices  98.6 us (19%)
  starting transfers between devices  63.2 us (12%)
  local copies, waits for them, and re-layouts  42.1 us (8%)
  other arithmetic  25.8 us (5%)
  between operations  16 us (3%)
    pallas_call x42, Pallas kernels, ordered(): found = run(first, *others) if table is None else run(table, first, *others)  254 us
    ppermute x49, waiting for transfers between devices, swap(): return lax.ppermute(values, axis, [(0, 1), (1, 0)])  64.1 us
    ppermute x49, starting transfers between devices, swap(): return lax.ppermute(values, axis, [(0, 1), (1, 0)])  27.2 us
    ppermute x11, waiting for transfers between devices, along(): return lax.ppermute(values, 'lat', [(i, i ^ bits) for i in range(4)])  23.4 us
    unnamed x180, local copies, waits for them, and re-layouts  18.2 us
    ppermute x11, starting transfers between devices, along(): return lax.ppermute(values, 'lat', [(i, i ^ bits) for i in range(4)])  17.1 us
    all_to_all x2, waiting for transfers between devices, collect_start(): return [lax.all_to_all(pieces, 'lat', 0, 0, tiled=True)]  11 us
    all_to_all x2, starting transfers between devices, collect_start(): return [lax.all_to_all(pieces, 'lat', 0, 0, tiled=True)]  10.2 us
  transfers between devices with their start and end apart: 68, of which 14 were waited for; matrix products, arithmetic and copies ran while one was open for 10% of the time, Pallas kernels for 44%

profile of v5, /device:TPU:0, one launch (start us, length us, event | category | flops | bytes accessed | tf_op | source)
XLA Modules:
  0.0 501.2 jit_solution(2560358537185699410)
XLA Ops:
  33.3 21.2 %collective-permute-done.8 = bf16[512,384]{1,0:T(8,128)(2,1)S(1)} collective-permute-done((bf16[512,384]{1,0:T(8,128)(2,1)S(1)}, bf16[512,384]{1,0:T(8,128)(2,1)S(1)}, u32[]{:S(2)}, u32[]{:S(2)}) %collective-permute-start.8) | collective-permute-done | bytes 393248 | tf_op jit(solution)/shard_map/ppermute | solution.py:901
  58.6 4.4 all-to-all-start
  63.2 10.5 %collective-permute-done.11 = bf16[1024,256]{1,0:T(8,128)(2,1)S(1)} collective-permute-done((bf16[1024,256]{1,0:T(8,128)(2,1)S(1)}, bf16[1024,256]{1,0:T(8,128)(2,1)S(1)}, u32[]{:S(2)}, u32[]{:S(2)}) %collective-permute-start.11) | collective-permute-done | bytes 524320 | tf_op jit(solution)/shard_map/ppermute | solution.py:898
  79.1 19.1 %collective-permute-done.14.h.refs_18_ = bf16[2,1024,256]{2,1,0:T(8,128)(2,1)} collective-permute-done((bf16[2,1024,256]{2,1,0:T(8,128)(2,1)S(1)}, bf16[2,1024,256]{2,1,0:T(8,128)(2,1)}, u32[]{:S(2)}, u32[]{:S(2)}) %collective-permute-start.14) | collective-permute-done | bytes 1048608 | tf_op jit(solution)/shard_map/ppermute | solution.py:898
  102.3 3.6 enter.1
  105.9 4.4 project.4
  111.6 4.3 project.5
  115.9 4.4 project.6
  120.4 4.4 project.7
  127.3 7.1 %attend.4 = (bf16[2,512,128]{2,1,0:T(8,128)(2,1)}, f32[2,2,512]{2,1,0:T(2,128)}) custom-call(bf16[2,512,128]{2,1,0:T(8,128)(2,1)} %get-tuple-element.235.refs_0_, bf16[2,512,256]{2,1,0:T(8,128)(2,1)} %get-tuple-element.159.refs_1_.refs_3_, bf16[2,512,256]{2,1,0:T(8,128)(2,1)} %copy-done.11), custom_call_target="tpu_custom_call" | custom-call | tf_op jit(solution)/shard_map/attend/pallas_call | solution.py:84
  135.2 7.1 %attend.5 = (bf16[2,512,128]{2,1,0:T(8,128)(2,1)}, f32[2,2,512]{2,1,0:T(2,128)}) custom-call(bf16[2,512,128]{2,1,0:T(8,128)(2,1)} %get-tuple-element.233.refs_0_, bf16[2,512,256]{2,1,0:T(8,128)(2,1)} %get-tuple-element.160.refs_1_.refs_3_, bf16[2,512,256]{2,1,0:T(8,128)(2,1)} %copy-done.10), custom_call_target="tpu_custom_call" | custom-call | tf_op jit(solution)/shard_map/attend/pallas_call | solution.py:84
  143.2 7.1 %attend.6 = (bf16[2,512,128]{2,1,0:T(8,128)(2,1)}, f32[2,2,512]{2,1,0:T(2,128)}) custom-call(bf16[2,512,128]{2,1,0:T(8,128)(2,1)} %get-tuple-element.206.refs_0_, bf16[2,512,256]{2,1,0:T(8,128)(2,1)} %get-tuple-element.165.refs_1_.refs_3_, bf16[2,512,256]{2,1,0:T(8,128)(2,1)} %copy-done.21), custom_call_target="tpu_custom_call" | custom-call | tf_op jit(solution)/shard_map/attend/pallas_call | solution.py:84
  151.1 7.1 %attend.7 = (bf16[2,512,128]{2,1,0:T(8,128)(2,1)}, f32[2,2,512]{2,1,0:T(2,128)}) custom-call(bf16[2,512,128]{2,1,0:T(8,128)(2,1)} %get-tuple-element.203.refs_0_, bf16[2,512,256]{2,1,0:T(8,128)(2,1)} %get-tuple-element.166.refs_1_.refs_3_, bf16[2,512,256]{2,1,0:T(8,128)(2,1)} %copy-done.22), custom_call_target="tpu_custom_call" | custom-call | tf_op jit(solution)/shard_map/attend/pallas_call | solution.py:84
  159.5 3.7 all-to-all-start.1
  164.9 9.7 %out.1 = (f32[512,1024]{1,0:T(8,128)}, f32[512,1024]{1,0:T(8,128)}, bf16[512,1024]{1,0:T(8,128)(2,1)}, bf16[1024,512]{1,0:T(8,128)(2,1)}) custom-call(s32[8,2]{1,0:T(8,128)} %concatenate.127.refs_0_, bf16[2,512,128]{2,1,0:T(8,128)(2,1)} %get-tuple-element.170.refs_1_.refs_4_, bf16[2,512,128]{2,1,0:T(8,128)(2,1)} %get-tuple-element.163.refs_2_.refs_4_, ...), custom_call_target="tpu_custom_call" | custom-call | tf_op jit(solution)/shard_map/out/pallas_call | solution.py:84
  174.6 19.9 %feed_forward.1 = (f32[4,512,1024]{2,1,0:T(8,128)}, bf16[4,512,1024]{2,1,0:T(8,128)(2,1)}, f32[512,1024]{1,0:T(8,128)}, bf16[512,1024]{1,0:T(8,128)(2,1)}) custom-call(bf16[512,1024]{1,0:T(8,128)(2,1)} %get-tuple-element.175.a, bf16[4,1024,2304]{2,1,0:T(8,128)(2,1)} %bitcast.247, bf16[4,1024,2304]{2,1,0:T(8,128)(2,1)} %bitcast.248, ...), custom_call_target="tpu_custom_call" | custom-call | tf_op jit(solution)/shard_map/feed_forward/pallas_call | solution.py:84
  195.6 3.9 enter_back.1
  199.5 18.4 %feed_back.2 = (bf16[2,1024,512]{2,1,0:T(8,128)(2,1)}, bf16[2,1024,512]{2,1,0:T(8,128)(2,1)}, bf16[2,1024,512]{2,1,0:T(8,128)(2,1)}, bf16[2,1024,512]{2,1,0:T(8,...) custom-call(s32[2,2]{1,0:T(2,128)} %copy-done.57, bf16[512,1024]{1,0:T(8,128)(2,1)} %get-tuple-element.188.refs_0_, ...), custom_call_target="tpu_custom_call" | custom-call | tf_op jit(solution)/shard_map/feed_back/pallas_call | solution.py:84
  219.0 24.6 %feed_back.3 = (bf16[2,1024,512]{2,1,0:T(8,128)(2,1)}, bf16[2,1024,512]{2,1,0:T(8,128)(2,1)}, bf16[2,1024,512]{2,1,0:T(8,128)(2,1)}, bf16[2,1024,512]{2,1,0:T(8,...) custom-call(s32[2,2]{1,0:T(2,128)} %copy-done.58, ...), custom_call_target="tpu_custom_call" | custom-call | tf_op jit(solution)/shard_map/feed_back/pallas_call | solution.py:84
  245.0 4.1 d_shrink.3
  250.9 3.4 d_expand.3
  255.3 8.1 %attended_back.1.refs_1_ = bf16[8,512,128]{2,1,0:T(8,128)(2,1)} custom-call(s32[2,8]{1,0:T(2,128)} %copy-done.63, bf16[512,1024]{1,0:T(8,128)(2,1)} %get-tuple-element.199.a, bf16[4,1024,2304]{2,1,0:T(8,128)(2,1)} %bitcast.253), custom_call_target="tpu_custom_call" | custom-call | tf_op jit(solution)/shard_map/attended_back/pallas_call | solution.py:84
  268.0 5.1 %all-to-all-start.2 = ((bf16[4,512,256]{2,1,0:T(8,128)(2,1)}), bf16[4,512,256]{2,1,0:T(8,128)(2,1)}, u32[]{:S(2)}, u32[]{:S(2)}) async-start(bf16[4,512,256]{2,1,0:T(8,128)(2,1)} %bitcast.263), calls=%async_computation.2 | async-start | bytes 2097152 | tf_op jit(solution)/shard_map/all_to_all | solution.py:932
  275.9 10.8 %attend_back.6 = (bf16[2,512,128]{2,1,0:T(8,128)(2,1)}, f32[2,512,256]{2,1,0:T(8,128)}, bf16[2,512,256]{2,1,0:T(8,128)(2,1)}, f32[2,1,128]{2,1,0:T(1,128)}) custom-call(bf16[2,512,128]{2,1,0:T(8,128)(2,1)} %get-tuple-element.203.refs_0_, bf16[8,512,128]{2,1,0:T(8,128)(2,1)} %attended_back.1.refs_1_, f32[2,2,512]{2,1,0:T(2,128)} %get-tuple-element.204.refs_2_, ...), custom_call_target="tpu_custom_call" | custom-call | tf_op jit(solution)/shard_map/attend_back/pallas_call | solution.py:84
  286.7 10.6 %attend_back.7 = (bf16[2,512,128]{2,1,0:T(8,128)(2,1)}, f32[2,512,256]{2,1,0:T(8,128)}, bf16[2,512,256]{2,1,0:T(8,128)(2,1)}, f32[2,1,128]{2,1,0:T(1,128)}) custom-call(bf16[2,512,128]{2,1,0:T(8,128)(2,1)} %get-tuple-element.206.refs_0_, bf16[8,512,128]{2,1,0:T(8,128)(2,1)} %attended_back.1.refs_1_, f32[2,2,512]{2,1,0:T(2,128)} %get-tuple-element.207.refs_2_, ...), custom_call_target="tpu_custom_call" | custom-call | tf_op jit(solution)/shard_map/attend_back/pallas_call | solution.py:84
  298.6 3.3 collective-permute-done.28.refs_2_
  301.8 3.6 d_shrink.4
  308.7 2.8 d_expand.4
  311.5 5.5 %d_in.6 = (bf16[512,512]{1,0:T(8,128)(2,1)}, bf16[512,512]{1,0:T(8,128)(2,1)}, bf16[512,512]{1,0:T(8,128)(2,1)}, bf16[512,512]{1,0:T(8,128)(2,1)}) custom-call(bf16[1024,512]{1,0:T(8,128)(2,1)} %get-tuple-element.263.refs_0_, bf16[1024,512]{1,0:T(8,128)(2,1)} %get-tuple-element.212.refs_1_, bf16[2,512,128]{2,1,0:T(8,128)(2,1)} %get-tuple-element.205.refs_2_.refs_5_, ...), custom_call_target="tpu_custom_call" | custom-call | tf_op jit(solution)/shard_map/d_in/pallas_call | solution.py:84
  319.6 6.3 %attend_back.8 = (bf16[1,512,128]{2,1,0:T(8,128)(2,1)}, f32[1,512,256]{2,1,0:T(8,128)}, bf16[1,512,256]{2,1,0:T(8,128)(2,1)}, f32[1,1,128]{2,1,0:T(1,128)}) custom-call(bf16[2,512,128]{2,1,0:T(8,128)(2,1)} %get-tuple-element.233.refs_0_, bf16[8,512,128]{2,1,0:T(8,128)(2,1)} %attended_back.1.refs_1_, f32[2,2,512]{2,1,0:T(2,128)} %get-tuple-element.217.refs_2_, ...), custom_call_target="tpu_custom_call" | custom-call | tf_op jit(solution)/shard_map/attend_back/pallas_call | solution.py:84
  327.2 5.4 %d_in.7 = bf16[2,1024,512]{2,1,0:T(8,128)(2,1)} custom-call(bf16[1024,512]{1,0:T(8,128)(2,1)} %get-tuple-element.263.refs_0_, bf16[1024,512]{1,0:T(8,128)(2,1)} %get-tuple-element.212.refs_1_, bf16[2,512,128]{2,1,0:T(8,128)(2,1)} %get-tuple-element.208.refs_2_.refs_4_, bf16[2,512,256]{2,1,0:T(8,128)(2,1)} %add_convert_fusion.refs_3_.refs_10_, ...), custom_call_target="tpu_custom_call" | custom-call | tf_op jit(solution)/shard_map/d_in/pallas_call | solution.py:84
  332.6 6.2 %attend_back.9 = (bf16[1,512,128]{2,1,0:T(8,128)(2,1)}, f32[1,512,256]{2,1,0:T(8,128)}, bf16[1,512,256]{2,1,0:T(8,128)(2,1)}, f32[1,1,128]{2,1,0:T(1,128)}) custom-call(bf16[2,512,128]{2,1,0:T(8,128)(2,1)} %get-tuple-element.235.refs_0_, bf16[8,512,128]{2,1,0:T(8,128)(2,1)} %attended_back.1.refs_1_, f32[2,2,512]{2,1,0:T(2,128)} %get-tuple-element.226.refs_2_, ...), custom_call_target="tpu_custom_call" | custom-call | tf_op jit(solution)/shard_map/attend_back/pallas_call | solution.py:84
  338.9 3.3 d_shrink.5
  348.4 3.6 d_in.8
  351.9 6.3 %attend_back.10 = (bf16[1,512,128]{2,1,0:T(8,128)(2,1)}, f32[1,512,256]{2,1,0:T(8,128)}, bf16[1,512,256]{2,1,0:T(8,128)(2,1)}, f32[1,1,128]{2,1,0:T(1,128)}) custom-call(bf16[2,512,128]{2,1,0:T(8,128)(2,1)} %get-tuple-element.233.refs_0_, bf16[8,512,128]{2,1,0:T(8,128)(2,1)} %attended_back.1.refs_1_, f32[2,2,512]{2,1,0:T(2,128)} %get-tuple-element.217.refs_2_, ...), custom_call_target="tpu_custom_call" | custom-call | tf_op jit(solution)/shard_map/attend_back/pallas_call | solution.py:84
  358.2 6.3 %attend_back.11 = (bf16[1,512,128]{2,1,0:T(8,128)(2,1)}, f32[1,512,256]{2,1,0:T(8,128)}, bf16[1,512,256]{2,1,0:T(8,128)(2,1)}, f32[1,1,128]{2,1,0:T(1,128)}) custom-call(bf16[2,512,128]{2,1,0:T(8,128)(2,1)} %get-tuple-element.235.refs_0_, bf16[8,512,128]{2,1,0:T(8,128)(2,1)} %attended_back.1.refs_1_, f32[2,2,512]{2,1,0:T(2,128)} %get-tuple-element.226.refs_2_, ...), custom_call_target="tpu_custom_call" | custom-call | tf_op jit(solution)/shard_map/attend_back/pallas_call | solution.py:84
  365.3 3.3 collective-permute-done.37.refs_3_
  369.6 3.2 d_expand.5
  375.2 3.5 d_in.9
  379.2 13.2 %collective-permute-done.42.refs_7_ = bf16[2,1024,512]{2,1,0:T(8,128)(2,1)S(1)} collective-permute-done((bf16[2,1024,512]{2,1,0:T(8,128)(2,1)}, bf16[2,1024,512]{2,1,0:T(8,128)(2,1)S(1)}, u32[]{:S(2)}, u32[]{:S(2)}) %collective-permute-start.42) | collective-permute-done | bytes 2097184 | tf_op jit(solution)/shard_map/ppermute | solution.py:898
  393.7 4.3 d_in.10
  399.5 12.0 %tokens_back.1 = (bf16[512,1024]{1,0:T(8,128)(2,1)}, f32[2,1024]{1,0:T(2,128)}) custom-call(bf16[1,512,128]{2,1,0:T(8,128)(2,1)} %get-tuple-element.246.refs_0_.refs_2_, bf16[1,512,128]{2,1,0:T(8,128)(2,1)} %get-tuple-element.227.refs_2_.refs_1_, bf16[1,512,128]{2,1,0:T(8,128)(2,1)} %get-tuple-element.234.refs_2_, ...), custom_call_target="tpu_custom_call" | custom-call | tf_op jit(solution)/shard_map/tokens_back/pallas_call | solution.py:84
  418.8 5.1 %all-to-all-start.3 = ((bf16[4,512,256]{2,1,0:T(8,128)(2,1)}), bf16[4,512,256]{2,1,0:T(8,128)(2,1)S(1)}, u32[]{:S(2)}, u32[]{:S(2)}) async-start(bf16[4,512,256]{2,1,0:T(8,128)(2,1)} %bitcast.240), calls=%async_computation.4 | async-start | bytes 2097152 | tf_op jit(solution)/shard_map/all_to_all | solution.py:932
  428.2 4.9 d_in.11
  435.1 3.6 collective-permute-done.49
  439.4 10.8 %all-to-all-done.3 = bf16[4,512,256]{2,1,0:T(8,128)(2,1)S(1)} async-done(((bf16[4,512,256]{2,1,0:T(8,128)(2,1)}), bf16[4,512,256]{2,1,0:T(8,128)(2,1)S(1)}, u32[]{:S(2)}, u32[]{:S(2)}) %all-to-all-start.3) | async-done | bytes 1048608 | tf_op jit(solution)/shard_map/all_to_all | solution.py:932
  458.2 2.9 collective-permute-start.51
  485.6 6.3 %collective-permute-done.57 = bf16[256,512]{1,0:T(8,128)(2,1)S(1)} collective-permute-done((bf16[256,512]{1,0:T(8,128)(2,1)}, bf16[256,512]{1,0:T(8,128)(2,1)S(1)}, u32[]{:S(2)}, u32[]{:S(2)}) %collective-permute-start.57) | collective-permute-done | bytes 262176 | tf_op jit(solution)/shard_map/ppermute | solution.py:898
  (522 shorter events, 132.2 us)
Async XLA Ops:
  7.2 151.1 %all-gather.2.cloned.1.call-start = ((), (), s32[]{:S(2)}) async-start(), calls=%async_computation.7 | async-start | bytes 20054016 | tf_op jit(solution)/shard_map/all_gather | solution.py:804
  12.7 20.5 %collective-permute-start = (bf16[2,512,256]{2,1,0:T(8,128)(2,1)}, bf16[2,512,256]{2,1,0:T(8,128)(2,1)S(1)}, u32[]{:S(2)}, u32[]{:S(2)}) collective-permute-start(bf16[2,512,256]{2,1,0:T(8,128)(2,1)} %get-tuple-element.357), channel_id=1, source_target_pairs={{0,4},{4,0},{1,5},{5,1},{2,6},{6,2},{3,7},{7,3},{8,12},{12,8},{9,1... | collective-permute-start | bytes 1572872 | tf_op jit(solution)/shard_map/ppermute | solution.py:898
  13.6 17.5 %collective-permute-start.1 = (bf16[256,384]{1,0:T(8,128)(2,1)S(1)}, bf16[256,384]{1,0:T(8,128)(2,1)S(1)}, u32[]{:S(2)}, u32[]{:S(2)}) collective-permute-start(bf16[256,384]{1,0:T(8,128)(2,1)S(1)} %bitcast.283), channel_id=1, source_target_pairs={{0,1},{1,0},{2,3},{3,2},{4,5},{5,4},{6,7},{7,6},{8,9},{9,8},{10,11... | collective-permute-start | bytes 589832 | tf_op jit(solution)/shard_map/ppermute | solution.py:901
  31.1 23.4 %collective-permute-start.8 = (bf16[512,384]{1,0:T(8,128)(2,1)S(1)}, bf16[512,384]{1,0:T(8,128)(2,1)S(1)}, u32[]{:S(2)}, u32[]{:S(2)}) collective-permute-start(bf16[512,384]{1,0:T(8,128)(2,1)S(1)} %pad_maximum_fusion.12), channel_id=1, source_target_pairs={{0,2},{1,3},{2,0},{3,1},{4,6},{5,7},{6,4},{7,5},{8,10},{9,11},{10,... | collective-permute-start | bytes 1179656 | tf_op jit(solution)/shard_map/ppermute | solution.py:901
  54.8 19.0 %collective-permute-start.11 = (bf16[1024,256]{1,0:T(8,128)(2,1)S(1)}, bf16[1024,256]{1,0:T(8,128)(2,1)S(1)}, u32[]{:S(2)}, u32[]{:S(2)}) collective-permute-start(bf16[1024,256]{1,0:T(8,128)(2,1)S(1)} %get-tuple-element.359), channel_id=1, source_target_pairs={{0,8},{8,0},{1,9},{9,1},{2,10},{10,2},{3,11},{11,3},{4,12},{12,4},... | collective-permute-start | bytes 1572872 | tf_op jit(solution)/shard_map/ppermute | solution.py:898
  58.6 40.3 %all-to-all-start = ((bf16[4,512,256]{2,1,0:T(8,128)(2,1)}), bf16[4,512,256]{2,1,0:T(8,128)(2,1)}, u32[]{:S(2)}, u32[]{:S(2)}) async-start(bf16[4,512,256]{2,1,0:T(8,128)(2,1)} %pad_maximum_fusion.2), calls=%async_computation | async-start | bytes 2097152 | tf_op jit(solution)/shard_map/all_to_all | solution.py:915
  75.7 22.5 %collective-permute-start.14 = (bf16[2,1024,256]{2,1,0:T(8,128)(2,1)S(1)}, bf16[2,1024,256]{2,1,0:T(8,128)(2,1)}, u32[]{:S(2)}, u32[]{:S(2)}) collective-permute-start(bf16[2,1024,256]{2,1,0:T(8,128)(2,1)S(1)} %pad_maximum_fusion.3.h.refs_16_), channel_id=1, source_target_pairs={{0,16},{16,0},{1,17},{17,1},{2,18},{18,2},{3,19},{19,3},{4,20},{20... | collective-permute-start | bytes 3145736 | tf_op jit(solution)/shard_map/ppermute | solution.py:898
  77.4 48.0 %collective-permute-start.21 = (bf16[2,512,256]{2,1,0:T(8,128)(2,1)}, bf16[2,512,256]{2,1,0:T(8,128)(2,1)}, u32[]{:S(2)}, u32[]{:S(2)}) collective-permute-start(bf16[2,512,256]{2,1,0:T(8,128)(2,1)} %get-tuple-element.351), channel_id=1, source_target_pairs={{0,4},{4,0},{1,5},{5,1},{2,6},{6,2},{3,7},{7,3},{8,12},{12,8},{9,1... | collective-permute-start | bytes 1572872 | tf_op jit(solution)/shard_map/ppermute | solution.py:898
  77.4 20.8 %collective-permute-start.10 = (bf16[2,1024,128]{2,1,0:T(8,128)(2,1)S(1)}, bf16[2,1024,128]{2,1,0:T(8,128)(2,1)S(1)}, u32[]{:S(2)}, u32[]{:S(2)}) collective-permute-start(bf16[2,1024,128]{2,1,0:T(8,128)(2,1)S(1)} %pad_maximum_fusion.9), channel_id=1, source_target_pairs={{0,8},{8,0},{1,9},{9,1},{2,10},{10,2},{3,11},{11,3},{4,12},{12,4},... | collective-permute-start | bytes 1572872 | tf_op jit(solution)/shard_map/ppermute | solution.py:898
  78.8 31.5 %collective-permute-start.13 = (bf16[2,1024,256]{2,1,0:T(8,128)(2,1)S(1)}, bf16[2,1024,256]{2,1,0:T(8,128)(2,1)}, u32[]{:S(2)}, u32[]{:S(2)}) collective-permute-start(bf16[2,1024,256]{2,1,0:T(8,128)(2,1)S(1)} %pad_maximum_fusion.3.h.refs_16_), channel_id=1, source_target_pairs={{0,4},{4,0},{1,5},{5,1},{2,6},{6,2},{3,7},{7,3},{8,12},{12,8},{9,1... | collective-permute-start | bytes 3145736 | tf_op jit(solution)/shard_map/ppermute | solution.py:898
  98.2 22.2 %collective-permute-start.16 = (bf16[2,1024,256]{2,1,0:T(8,128)(2,1)}, bf16[2,1024,256]{2,1,0:T(8,128)(2,1)}, u32[]{:S(2)}, u32[]{:S(2)}) collective-permute-start(bf16[2,1024,256]{2,1,0:T(8,128)(2,1)} %collective-permute-done.14.h.refs_18_), channel_id=1, source_target_pairs={{0,4},{4,0},{1,5},{5,1},{2,6},{6,2},{3,7},{7,3},{8,12},{12,8},{9,1... | collective-permute-start | bytes 3145736 | tf_op jit(solution)/shard_map/ppermute | solution.py:898
  98.3 22.0 %collective-permute-start.15 = (bf16[2,1024,128]{2,1,0:T(8,128)(2,1)S(1)}, bf16[2,1024,128]{2,1,0:T(8,128)(2,1)}, u32[]{:S(2)}, u32[]{:S(2)}) collective-permute-start(bf16[2,1024,128]{2,1,0:T(8,128)(2,1)S(1)} %pad_maximum_fusion.11.g.refs_14_), channel_id=1, source_target_pairs={{0,4},{4,0},{1,5},{5,1},{2,6},{6,2},{3,7},{7,3},{8,12},{12,8},{9,1... | collective-permute-start | bytes 1572872 | tf_op jit(solution)/shard_map/ppermute | solution.py:898
  101.5 9.3 %collective-permute-start.12 = (bf16[2,1024,128]{2,1,0:T(8,128)(2,1)S(1)}, bf16[2,1024,128]{2,1,0:T(8,128)(2,1)S(1)}, u32[]{:S(2)}, u32[]{:S(2)}) collective-permute-start(bf16[2,1024,128]{2,1,0:T(8,128)(2,1)S(1)} %pad_maximum_fusion.10.g.refs_12_), channel_id=1, source_target_pairs={{0,4},{4,0},{1,5},{5,1},{2,6},{6,2},{3,7},{7,3},{8,12},{12,8},{9,1... | collective-permute-start | bytes 1572872 | tf_op jit(solution)/shard_map/ppermute | solution.py:898
  110.3 24.2 %collective-permute-start.18 = (bf16[2,512,256]{2,1,0:T(8,128)(2,1)}, bf16[2,512,256]{2,1,0:T(8,128)(2,1)S(1)}, u32[]{:S(2)}, u32[]{:S(2)}) collective-permute-start(bf16[2,512,256]{2,1,0:T(8,128)(2,1)} %get-tuple-element.159.refs_1_.refs_3_), channel_id=1, source_target_pairs={{0,4},{4,0},{1,5},{5,1},{2,6},{6,2},{3,7},{7,3},{8,12},{12,8},{9,1... | collective-permute-start | bytes 1572872 | tf_op jit(solution)/shard_map/ppermute | solution.py:898
  115.9 10.6 %collective-permute-start.17 = (bf16[2,512,256]{2,1,0:T(8,128)(2,1)}, bf16[2,512,256]{2,1,0:T(8,128)(2,1)S(1)}, u32[]{:S(2)}, u32[]{:S(2)}) collective-permute-start(bf16[2,512,256]{2,1,0:T(8,128)(2,1)} %get-tuple-element.160.refs_1_.refs_3_), channel_id=1, source_target_pairs={{0,4},{4,0},{1,5},{5,1},{2,6},{6,2},{3,7},{7,3},{8,12},{12,8},{9,1... | collective-permute-start | bytes 1572872 | tf_op jit(solution)/shard_map/ppermute | solution.py:898
  124.8 17.6 %collective-permute-start.19 = (bf16[2,512,256]{2,1,0:T(8,128)(2,1)}, bf16[2,512,256]{2,1,0:T(8,128)(2,1)S(1)}, u32[]{:S(2)}, u32[]{:S(2)}) collective-permute-start(bf16[2,512,256]{2,1,0:T(8,128)(2,1)} %get-tuple-element.166.refs_1_.refs_3_), channel_id=1, source_target_pairs={{0,4},{4,0},{1,5},{5,1},{2,6},{6,2},{3,7},{7,3},{8,12},{12,8},{9,1... | collective-permute-start | bytes 1572872 | tf_op jit(solution)/shard_map/ppermute | solution.py:898
  125.3 25.0 %collective-permute-start.20 = (bf16[2,512,256]{2,1,0:T(8,128)(2,1)S(1)}, bf16[2,512,256]{2,1,0:T(8,128)(2,1)S(1)}, u32[]{:S(2)}, u32[]{:S(2)}) collective-permute-start(bf16[2,512,256]{2,1,0:T(8,128)(2,1)S(1)} %copy-done.20), channel_id=1, source_target_pairs={{0,4},{4,0},{1,5},{5,1},{2,6},{6,2},{3,7},{7,3},{8,12},{12,8},{9,1... | collective-permute-start | bytes 1572872 | tf_op jit(solution)/shard_map/ppermute | solution.py:898
  159.5 35.0 %all-to-all-start.1 = ((bf16[4,512,256]{2,1,0:T(8,128)(2,1)}), bf16[4,512,256]{2,1,0:T(8,128)(2,1)S(1)}, u32[]{:S(2)}, u32[]{:S(2)}) async-start(bf16[4,512,256]{2,1,0:T(8,128)(2,1)} %pad_maximum_fusion.5), calls=%async_computation.1 | async-start | bytes 2097152 | tf_op jit(solution)/shard_map/all_to_all | solution.py:915
  217.9 25.7 %collective-permute-start.22 = (bf16[2,1024,512]{2,1,0:T(8,128)(2,1)}, bf16[2,1024,512]{2,1,0:T(8,128)(2,1)}, u32[]{:S(2)}, u32[]{:S(2)}) collective-permute-start(bf16[2,1024,512]{2,1,0:T(8,128)(2,1)} %get-tuple-element.187), channel_id=1, source_target_pairs={{0,4},{4,0},{1,5},{5,1},{2,6},{6,2},{3,7},{7,3},{8,12},{12,8},{9,1... | collective-permute-start | bytes 6291464 | tf_op jit(solution)/shard_map/ppermute | solution.py:898
  218.4 25.2 %collective-permute-start.23 = (bf16[2,1024,512]{2,1,0:T(8,128)(2,1)}, bf16[2,1024,512]{2,1,0:T(8,128)(2,1)S(1)}, u32[]{:S(2)}, u32[]{:S(2)}) collective-permute-start(bf16[2,1024,512]{2,1,0:T(8,128)(2,1)} %get-tuple-element.193), channel_id=1, source_target_pairs={{0,4},{4,0},{1,5},{5,1},{2,6},{6,2},{3,7},{7,3},{8,12},{12,8},{9,1... | collective-permute-start | bytes 6291464 | tf_op jit(solution)/shard_map/ppermute | solution.py:898
  218.5 25.2 %collective-permute-start.24 = (bf16[2,1024,512]{2,1,0:T(8,128)(2,1)}, bf16[2,1024,512]{2,1,0:T(8,128)(2,1)S(1)}, u32[]{:S(2)}, u32[]{:S(2)}) collective-permute-start(bf16[2,1024,512]{2,1,0:T(8,128)(2,1)} %get-tuple-element.194), channel_id=1, source_target_pairs={{0,4},{4,0},{1,5},{5,1},{2,6},{6,2},{3,7},{7,3},{8,12},{12,8},{9,1... | collective-permute-start | bytes 6291464 | tf_op jit(solution)/shard_map/ppermute | solution.py:898
  218.9 24.7 %collective-permute-start.25 = (bf16[2,1024,512]{2,1,0:T(8,128)(2,1)}, bf16[2,1024,512]{2,1,0:T(8,128)(2,1)S(1)}, u32[]{:S(2)}, u32[]{:S(2)}) collective-permute-start(bf16[2,1024,512]{2,1,0:T(8,128)(2,1)} %get-tuple-element.195), channel_id=1, source_target_pairs={{0,4},{4,0},{1,5},{5,1},{2,6},{6,2},{3,7},{7,3},{8,12},{12,8},{9,1... | collective-permute-start | bytes 6291464 | tf_op jit(solution)/shard_map/ppermute | solution.py:898
  249.1 49.5 %collective-permute-start.27 = (bf16[2,1024,512]{2,1,0:T(8,128)(2,1)}, bf16[2,1024,512]{2,1,0:T(8,128)(2,1)}, u32[]{:S(2)}, u32[]{:S(2)}) collective-permute-start(bf16[2,1024,512]{2,1,0:T(8,128)(2,1)} %d_shrink.3), channel_id=1, source_target_pairs={{0,8},{8,0},{1,9},{9,1},{2,10},{10,2},{3,11},{11,3},{4,12},{12,4},... | collective-permute-start | bytes 6291464 | tf_op jit(solution)/shard_map/ppermute | solution.py:898
  254.3 47.5 %collective-permute-start.28 = (bf16[2,1024,512]{2,1,0:T(8,128)(2,1)}, bf16[2,1024,512]{2,1,0:T(8,128)(2,1)S(1)}, u32[]{:S(2)}, u32[]{:S(2)}) collective-permute-start(bf16[2,1024,512]{2,1,0:T(8,128)(2,1)} %d_expand.3), channel_id=1, source_target_pairs={{0,16},{16,0},{1,17},{17,1},{2,18},{18,2},{3,19},{19,3},{4,20},{20... | collective-permute-start | bytes 6291464 | tf_op jit(solution)/shard_map/ppermute | solution.py:898
  268.0 30.6 %all-to-all-start.2 = ((bf16[4,512,256]{2,1,0:T(8,128)(2,1)}), bf16[4,512,256]{2,1,0:T(8,128)(2,1)}, u32[]{:S(2)}, u32[]{:S(2)}) async-start(bf16[4,512,256]{2,1,0:T(8,128)(2,1)} %bitcast.263), calls=%async_computation.2 | async-start | bytes 2097152 | tf_op jit(solution)/shard_map/all_to_all | solution.py:932
  273.0 126.4 %reduce-scatter.4.cloned.1.call-start = ((), (), s32[]{:S(2)}) async-start(), calls=%async_computation.8 | async-start | bytes 1310720 | tf_op jit(solution)/shard_map/reduce_scatter | solution.py:1080
  297.3 9.2 %collective-permute-start.29 = (bf16[2,512,256]{2,1,0:T(8,128)(2,1)}, bf16[2,512,256]{2,1,0:T(8,128)(2,1)}, u32[]{:S(2)}, u32[]{:S(2)}) collective-permute-start(bf16[2,512,256]{2,1,0:T(8,128)(2,1)} %get-tuple-element.214), channel_id=1, source_target_pairs={{0,4},{4,0},{1,5},{5,1},{2,6},{6,2},{3,7},{7,3},{8,12},{12,8},{9,1... | collective-permute-start | bytes 1572872 | tf_op jit(solution)/shard_map/ppermute | solution.py:898
  297.3 20.3 %collective-permute-start.30 = (bf16[2,512,256]{2,1,0:T(8,128)(2,1)}, bf16[2,512,256]{2,1,0:T(8,128)(2,1)S(1)}, u32[]{:S(2)}, u32[]{:S(2)}) collective-permute-start(bf16[2,512,256]{2,1,0:T(8,128)(2,1)} %get-tuple-element.221), channel_id=1, source_target_pairs={{0,4},{4,0},{1,5},{5,1},{2,6},{6,2},{3,7},{7,3},{8,12},{12,8},{9,1... | collective-permute-start | bytes 1572872 | tf_op jit(solution)/shard_map/ppermute | solution.py:898
  305.4 33.4 %collective-permute-start.35 = (bf16[1,1024,512]{2,1,0:T(8,128)(2,1)}, bf16[1,1024,512]{2,1,0:T(8,128)(2,1)}, u32[]{:S(2)}, u32[]{:S(2)}) collective-permute-start(bf16[1,1024,512]{2,1,0:T(8,128)(2,1)} %d_shrink.4), channel_id=1, source_target_pairs={{0,16},{16,0},{1,17},{17,1},{2,18},{18,2},{3,19},{19,3},{4,20},{20... | collective-permute-start | bytes 3145736 | tf_op jit(solution)/shard_map/ppermute | solution.py:898
  317.0 8.8 %collective-permute-start.31 = (bf16[512,512]{1,0:T(8,128)(2,1)}, bf16[512,512]{1,0:T(8,128)(2,1)S(1)}, u32[]{:S(2)}, u32[]{:S(2)}) collective-permute-start(bf16[512,512]{1,0:T(8,128)(2,1)} %get-tuple-element.215), channel_id=1, source_target_pairs={{0,4},{4,0},{1,5},{5,1},{2,6},{6,2},{3,7},{7,3},{8,12},{12,8},{9,1... | collective-permute-start | bytes 1572872 | tf_op jit(solution)/shard_map/ppermute | solution.py:898
  317.0 8.8 %collective-permute-start.32 = (bf16[512,512]{1,0:T(8,128)(2,1)}, bf16[512,512]{1,0:T(8,128)(2,1)S(1)}, u32[]{:S(2)}, u32[]{:S(2)}) collective-permute-start(bf16[512,512]{1,0:T(8,128)(2,1)} %get-tuple-element.222), channel_id=1, source_target_pairs={{0,4},{4,0},{1,5},{5,1},{2,6},{6,2},{3,7},{7,3},{8,12},{12,8},{9,1... | collective-permute-start | bytes 1572872 | tf_op jit(solution)/shard_map/ppermute | solution.py:898
  342.2 122.5 %reduce-scatter.8.cloned.1.call-start = ((), (), s32[]{:S(2)}) async-start(), calls=%async_computation.10 | async-start | bytes 1310720 | tf_op jit(solution)/shard_map/reduce_scatter | solution.py:1080
  343.3 25.3 %collective-permute-start.37 = (bf16[1,1024,512]{2,1,0:T(8,128)(2,1)}, bf16[1,1024,512]{2,1,0:T(8,128)(2,1)S(1)}, u32[]{:S(2)}, u32[]{:S(2)}) collective-permute-start(bf16[1,1024,512]{2,1,0:T(8,128)(2,1)} %d_expand.4), channel_id=1, source_target_pairs={{0,8},{8,0},{1,9},{9,1},{2,10},{10,2},{3,11},{11,3},{4,12},{12,4},... | collective-permute-start | bytes 3145736 | tf_op jit(solution)/shard_map/ppermute | solution.py:898
  344.0 21.0 %collective-permute-start.39 = (bf16[1,512,256]{2,1,0:T(8,128)(2,1)}, bf16[1,512,256]{2,1,0:T(8,128)(2,1)S(1)}, u32[]{:S(2)}, u32[]{:S(2)}) collective-permute-start(bf16[1,512,256]{2,1,0:T(8,128)(2,1)} %get-tuple-element.244), channel_id=1, source_target_pairs={{0,4},{4,0},{1,5},{5,1},{2,6},{6,2},{3,7},{7,3},{8,12},{12,8},{9,1... | collective-permute-start | bytes 786440 | tf_op jit(solution)/shard_map/ppermute | solution.py:898
  344.5 47.8 %collective-permute-start.42 = (bf16[2,1024,512]{2,1,0:T(8,128)(2,1)}, bf16[2,1024,512]{2,1,0:T(8,128)(2,1)S(1)}, u32[]{:S(2)}, u32[]{:S(2)}) collective-permute-start(bf16[2,1024,512]{2,1,0:T(8,128)(2,1)} %d_in.7), channel_id=1, source_target_pairs={{0,16},{16,0},{1,17},{17,1},{2,18},{18,2},{3,19},{19,3},{4,20},{20... | collective-permute-start | bytes 6291464 | tf_op jit(solution)/shard_map/ppermute | solution.py:898
  347.6 68.3 %collective-permute-start.26 = (bf16[2,512,256]{2,1,0:T(8,128)(2,1)}, bf16[2,512,256]{2,1,0:T(8,128)(2,1)}, u32[]{:S(2)}, u32[]{:S(2)}) collective-permute-start(bf16[2,512,256]{2,1,0:T(8,128)(2,1)} %dynamic-slice_bitcast_fusion.1), channel_id=1, source_target_pairs={{0,4},{4,0},{1,5},{5,1},{2,6},{6,2},{3,7},{7,3},{8,12},{12,8},{9,1... | collective-permute-start | bytes 1572872 | tf_op jit(solution)/shard_map/ppermute | solution.py:898
  365.3 13.9 %collective-permute-start.40 = (bf16[512,512]{1,0:T(8,128)(2,1)}, bf16[512,512]{1,0:T(8,128)(2,1)}, u32[]{:S(2)}, u32[]{:S(2)}) collective-permute-start(bf16[512,512]{1,0:T(8,128)(2,1)} %get-tuple-element.232), channel_id=1, source_target_pairs={{0,4},{4,0},{1,5},{5,1},{2,6},{6,2},{3,7},{7,3},{8,12},{12,8},{9,1... | collective-permute-start | bytes 1572872 | tf_op jit(solution)/shard_map/ppermute | solution.py:898
  398.0 29.4 %collective-permute-start.48 = (bf16[1,1024,512]{2,1,0:T(8,128)(2,1)}, bf16[1,1024,512]{2,1,0:T(8,128)(2,1)}, u32[]{:S(2)}, u32[]{:S(2)}) collective-permute-start(bf16[1,1024,512]{2,1,0:T(8,128)(2,1)} %d_in.10), channel_id=1, source_target_pairs={{0,8},{8,0},{1,9},{9,1},{2,10},{10,2},{3,11},{11,3},{4,12},{12,4},... | collective-permute-start | bytes 3145736 | tf_op jit(solution)/shard_map/ppermute | solution.py:898
  417.1 10.3 %collective-permute-start.46 = (bf16[512,512]{1,0:T(8,128)(2,1)}, bf16[512,512]{1,0:T(8,128)(2,1)S(1)}, u32[]{:S(2)}, u32[]{:S(2)}) collective-permute-start(bf16[512,512]{1,0:T(8,128)(2,1)} %get-tuple-element.241), channel_id=1, source_target_pairs={{0,4},{4,0},{1,5},{5,1},{2,6},{6,2},{3,7},{7,3},{8,12},{12,8},{9,1... | collective-permute-start | bytes 1572872 | tf_op jit(solution)/shard_map/ppermute | solution.py:898
  417.7 9.7 %collective-permute-start.47 = (bf16[512,512]{1,0:T(8,128)(2,1)}, bf16[512,512]{1,0:T(8,128)(2,1)}, u32[]{:S(2)}, u32[]{:S(2)}) collective-permute-start(bf16[512,512]{1,0:T(8,128)(2,1)} %get-tuple-element.264), channel_id=1, source_target_pairs={{0,4},{4,0},{1,5},{5,1},{2,6},{6,2},{3,7},{7,3},{8,12},{12,8},{9,1... | collective-permute-start | bytes 1572872 | tf_op jit(solution)/shard_map/ppermute | solution.py:898
  418.8 31.4 %all-to-all-start.3 = ((bf16[4,512,256]{2,1,0:T(8,128)(2,1)}), bf16[4,512,256]{2,1,0:T(8,128)(2,1)S(1)}, u32[]{:S(2)}, u32[]{:S(2)}) async-start(bf16[4,512,256]{2,1,0:T(8,128)(2,1)} %bitcast.240), calls=%async_computation.4 | async-start | bytes 2097152 | tf_op jit(solution)/shard_map/all_to_all | solution.py:932
  423.9 57.3 %reduce-scatter.6.cloned.1.call-start = ((), (), s32[]{:S(2)}) async-start(), calls=%async_computation.9 | async-start | bytes 1310720 | tf_op jit(solution)/shard_map/reduce_scatter | solution.py:1080
  456.7 10.7 %collective-permute-start.53 = (f32[64,128]{1,0:T(8,128)S(1)}, f32[64,128]{1,0:T(8,128)S(1)}, u32[]{:S(2)}, u32[]{:S(2)}) collective-permute-start(f32[64,128]{1,0:T(8,128)S(1)} %get-tuple-element.412), channel_id=1, source_target_pairs={{0,3},{1,2},{2,1},{3,0},{4,7},{5,6},{6,5},{7,4},{8,11},{9,10},{10,... | collective-permute-start | bytes 98312 | tf_op jit(solution)/shard_map/ppermute | solution.py:901
  458.2 9.1 %collective-permute-start.52 = (f32[64,128]{1,0:T(8,128)S(1)}, f32[64,128]{1,0:T(8,128)S(1)}, u32[]{:S(2)}, u32[]{:S(2)}) collective-permute-start(f32[64,128]{1,0:T(8,128)S(1)} %get-tuple-element.411), channel_id=1, source_target_pairs={{0,2},{1,3},{2,0},{3,1},{4,6},{5,7},{6,4},{7,5},{8,10},{9,11},{10,... | collective-permute-start | bytes 98312 | tf_op jit(solution)/shard_map/ppermute | solution.py:901
  458.2 9.2 %collective-permute-start.51 = (f32[64,128]{1,0:T(8,128)S(1)}, f32[64,128]{1,0:T(8,128)S(1)}, u32[]{:S(2)}, u32[]{:S(2)}) collective-permute-start(f32[64,128]{1,0:T(8,128)S(1)} %get-tuple-element.410), channel_id=1, source_target_pairs={{0,1},{1,0},{2,3},{3,2},{4,5},{5,4},{6,7},{7,6},{8,9},{9,8},{10,11... | collective-permute-start | bytes 98312 | tf_op jit(solution)/shard_map/ppermute | solution.py:901
  463.7 13.1 %collective-permute-start.59 = (bf16[256,512]{1,0:T(8,128)(2,1)}, bf16[256,512]{1,0:T(8,128)(2,1)S(1)}, u32[]{:S(2)}, u32[]{:S(2)}) collective-permute-start(bf16[256,512]{1,0:T(8,128)(2,1)} %gate.13), channel_id=1, source_target_pairs={{0,16},{16,0},{1,17},{17,1},{2,18},{18,2},{3,19},{19,3},{4,20},{20... | collective-permute-start | bytes 786440 | tf_op jit(solution)/shard_map/ppermute | solution.py:898
  466.4 10.3 %collective-permute-start.58 = (bf16[256,512]{1,0:T(8,128)(2,1)}, bf16[256,512]{1,0:T(8,128)(2,1)S(1)}, u32[]{:S(2)}, u32[]{:S(2)}) collective-permute-start(bf16[256,512]{1,0:T(8,128)(2,1)} %gate.14), channel_id=1, source_target_pairs={{0,16},{16,0},{1,17},{17,1},{2,18},{18,2},{3,19},{19,3},{4,20},{20... | collective-permute-start | bytes 786440 | tf_op jit(solution)/shard_map/ppermute | solution.py:898
  482.9 8.9 %collective-permute-start.57 = (bf16[256,512]{1,0:T(8,128)(2,1)}, bf16[256,512]{1,0:T(8,128)(2,1)S(1)}, u32[]{:S(2)}, u32[]{:S(2)}) collective-permute-start(bf16[256,512]{1,0:T(8,128)(2,1)} %gate.15), channel_id=1, source_target_pairs={{0,16},{16,0},{1,17},{17,1},{2,18},{18,2},{3,19},{19,3},{4,20},{20... | collective-permute-start | bytes 786440 | tf_op jit(solution)/shard_map/ppermute | solution.py:898
  (103 other events, 659.9 us)
Sparse Core Ops, SparseCore 0:
  11.9 140.4 all-gather.1
  342.3 27.2 reduce-scatter.3
  373.0 27.3 reduce-scatter.7
  454.1 26.3 reduce-scatter.5

commit v6 on v5

--- a/solution.py
+++ b/solution.py
@@ -970,13 +970,11 @@
         odd, high = self.z % 2 == 1, self.z >= 2
         got = self.along(part, 1)
         part = jnp.concatenate([jnp.where(odd, got, part), jnp.where(odd, part, got)], axis=0)
-        part, held = lax.optimization_barrier((part, held))
         got = self.along(part, 2)
         part = jnp.concatenate(
             [jnp.where(high, got, part), jnp.where(high, part, got)], axis=0
         )
-
-        return part, held
+        return lax.optimization_barrier((part, held))
 
     def gather(self, part, held):
         one, two = part[:, :LANES], part[:, LANES:]
@@ -1362,7 +1360,7 @@
         )
     row_sums = net.with_units(row_sums, expand_sums)
     col_sums = jnp.concatenate([sums_two[3:4], shrink_sum], axis=0)
-    tokens_back = net.collect_start(gate(tokens_back))
+    tokens_back = net.collect_start(tokens_back)
     small_steps = Steps(net.small(summed, row_sums, col_sums))
     in_steps.step()
     small_steps.step()

time: 506 us -> 505 us (level)
    pallas_call x42 -> x41, Pallas kernels: 254 us -> 252 us  [ordered(): found = run(first, *others) if table is None else run(table, first, *others)]
    unnamed x180 -> x178, local copies, waits for them, and re-layouts: 18.2 us -> 18.2 us
  transfers between devices with their start and end apart: 68 -> 68, of which waited for: 14 -> 15; matrix products, arithmetic and copies ran while one was open for 10% -> 10% of each run, Pallas kernels for 44% -> 44%
where the time goes in v6:
time: 505 us; the launch traced here: 500 us
  Pallas kernels  252 us (50%)
  waiting for transfers between devices  98.1 us (19%)
  starting transfers between devices  63.6 us (13%)
  local copies, waits for them, and re-layouts  42.1 us (8%)
  other arithmetic  26.6 us (5%)
  between operations  16.1 us (3%)
    pallas_call x41, Pallas kernels, ordered(): found = run(first, *others) if table is None else run(table, first, *others)  252 us
    ppermute x49, waiting for transfers between devices, swap(): return lax.ppermute(values, axis, [(0, 1), (1, 0)])  65.9 us
    ppermute x49, starting transfers between devices, swap(): return lax.ppermute(values, axis, [(0, 1), (1, 0)])  26.7 us
    ppermute x11, waiting for transfers between devices, along(): return lax.ppermute(values, 'lat', [(i, i ^ bits) for i in range(4)])  21.1 us
    unnamed x178, local copies, waits for them, and re-layouts  18.2 us
    ppermute x11, starting transfers between devices, along(): return lax.ppermute(values, 'lat', [(i, i ^ bits) for i in range(4)])  16.8 us
    all_to_all x2, waiting for transfers between devices, collect_start(): return [lax.all_to_all(pieces, 'lat', 0, 0, tiled=True)]  11.1 us
    all_to_all x2, starting transfers between devices, collect_start(): return [lax.all_to_all(pieces, 'lat', 0, 0, tiled=True)]  10.2 us
  transfers between devices with their start and end apart: 68, of which 15 were waited for; matrix products, arithmetic and copies ran while one was open for 10% of the time, Pallas kernels for 44%

profile of v6, /device:TPU:0, one launch (start us, length us, event | category | flops | bytes accessed | tf_op | source)
XLA Modules:
  0.0 499.7 jit_solution(8991066791325646211)
XLA Ops:
  31.6 19.8 %collective-permute-done.2 = bf16[512,384]{1,0:T(8,128)(2,1)S(1)} collective-permute-done((bf16[512,384]{1,0:T(8,128)(2,1)S(1)}, bf16[512,384]{1,0:T(8,128)(2,1)S(1)}, u32[]{:S(2)}, u32[]{:S(2)}) %collective-permute-start.2) | collective-permute-done | bytes 393248 | tf_op jit(solution)/shard_map/ppermute | solution.py:901
  55.9 4.4 all-to-all-start
  60.9 10.4 %collective-permute-done.11 = bf16[1024,256]{1,0:T(8,128)(2,1)S(1)} collective-permute-done((bf16[1024,256]{1,0:T(8,128)(2,1)S(1)}, bf16[1024,256]{1,0:T(8,128)(2,1)S(1)}, u32[]{:S(2)}, u32[]{:S(2)}) %collective-permute-start.11) | collective-permute-done | bytes 524320 | tf_op jit(solution)/shard_map/ppermute | solution.py:898
  76.8 19.9 %collective-permute-done.14.h.refs_18_ = bf16[2,1024,256]{2,1,0:T(8,128)(2,1)} collective-permute-done((bf16[2,1024,256]{2,1,0:T(8,128)(2,1)S(1)}, bf16[2,1024,256]{2,1,0:T(8,128)(2,1)}, u32[]{:S(2)}, u32[]{:S(2)}) %collective-permute-start.14) | collective-permute-done | bytes 1048608 | tf_op jit(solution)/shard_map/ppermute | solution.py:898
  100.8 3.6 enter.1
  104.4 4.4 project.4
  110.1 4.4 project.5
  114.5 4.4 project.6
  119.0 4.4 project.7
  126.0 7.1 %attend.4 = (bf16[2,512,128]{2,1,0:T(8,128)(2,1)}, f32[2,2,512]{2,1,0:T(2,128)}) custom-call(bf16[2,512,128]{2,1,0:T(8,128)(2,1)} %get-tuple-element.235.refs_0_, bf16[2,512,256]{2,1,0:T(8,128)(2,1)} %get-tuple-element.159.refs_1_.refs_3_, bf16[2,512,256]{2,1,0:T(8,128)(2,1)} %copy-done.11), custom_call_target="tpu_custom_call" | custom-call | tf_op jit(solution)/shard_map/attend/pallas_call | solution.py:84
  133.9 7.1 %attend.5 = (bf16[2,512,128]{2,1,0:T(8,128)(2,1)}, f32[2,2,512]{2,1,0:T(2,128)}) custom-call(bf16[2,512,128]{2,1,0:T(8,128)(2,1)} %get-tuple-element.233.refs_0_, bf16[2,512,256]{2,1,0:T(8,128)(2,1)} %get-tuple-element.160.refs_1_.refs_3_, bf16[2,512,256]{2,1,0:T(8,128)(2,1)} %copy-done.10), custom_call_target="tpu_custom_call" | custom-call | tf_op jit(solution)/shard_map/attend/pallas_call | solution.py:84
  141.8 7.1 %attend.6 = (bf16[2,512,128]{2,1,0:T(8,128)(2,1)}, f32[2,2,512]{2,1,0:T(2,128)}) custom-call(bf16[2,512,128]{2,1,0:T(8,128)(2,1)} %get-tuple-element.206.refs_0_, bf16[2,512,256]{2,1,0:T(8,128)(2,1)} %get-tuple-element.165.refs_1_.refs_3_, bf16[2,512,256]{2,1,0:T(8,128)(2,1)} %copy-done.20), custom_call_target="tpu_custom_call" | custom-call | tf_op jit(solution)/shard_map/attend/pallas_call | solution.py:84
  149.8 7.1 %attend.7 = (bf16[2,512,128]{2,1,0:T(8,128)(2,1)}, f32[2,2,512]{2,1,0:T(2,128)}) custom-call(bf16[2,512,128]{2,1,0:T(8,128)(2,1)} %get-tuple-element.203.refs_0_, bf16[2,512,256]{2,1,0:T(8,128)(2,1)} %get-tuple-element.166.refs_1_.refs_3_, bf16[2,512,256]{2,1,0:T(8,128)(2,1)} %copy-done.21), custom_call_target="tpu_custom_call" | custom-call | tf_op jit(solution)/shard_map/attend/pallas_call | solution.py:84
  158.2 4.9 all-to-all-start.1
  164.7 9.7 %out.1 = (f32[512,1024]{1,0:T(8,128)}, f32[512,1024]{1,0:T(8,128)}, bf16[512,1024]{1,0:T(8,128)(2,1)}, bf16[1024,512]{1,0:T(8,128)(2,1)}) custom-call(s32[8,2]{1,0:T(8,128)} %concatenate.127.refs_0_, bf16[2,512,128]{2,1,0:T(8,128)(2,1)} %get-tuple-element.170.refs_1_.refs_4_, bf16[2,512,128]{2,1,0:T(8,128)(2,1)} %get-tuple-element.163.refs_2_.refs_4_, ...), custom_call_target="tpu_custom_call" | custom-call | tf_op jit(solution)/shard_map/out/pallas_call | solution.py:84
  174.4 19.9 %feed_forward.1 = (f32[4,512,1024]{2,1,0:T(8,128)}, bf16[4,512,1024]{2,1,0:T(8,128)(2,1)}, f32[512,1024]{1,0:T(8,128)}, bf16[512,1024]{1,0:T(8,128)(2,1)}) custom-call(bf16[512,1024]{1,0:T(8,128)(2,1)} %get-tuple-element.175.a, bf16[4,1024,2304]{2,1,0:T(8,128)(2,1)} %bitcast.247, bf16[4,1024,2304]{2,1,0:T(8,128)(2,1)} %bitcast.248, ...), custom_call_target="tpu_custom_call" | custom-call | tf_op jit(solution)/shard_map/feed_forward/pallas_call | solution.py:84
  195.4 3.9 enter_back.1
  199.3 18.4 %feed_back.2 = (bf16[2,1024,512]{2,1,0:T(8,128)(2,1)}, bf16[2,1024,512]{2,1,0:T(8,128)(2,1)}, bf16[2,1024,512]{2,1,0:T(8,128)(2,1)}, bf16[2,1024,512]{2,1,0:T(8,...) custom-call(s32[2,2]{1,0:T(2,128)} %copy-done.56, bf16[512,1024]{1,0:T(8,128)(2,1)} %get-tuple-element.188.refs_0_, ...), custom_call_target="tpu_custom_call" | custom-call | tf_op jit(solution)/shard_map/feed_back/pallas_call | solution.py:84
  218.8 24.6 %feed_back.3 = (bf16[2,1024,512]{2,1,0:T(8,128)(2,1)}, bf16[2,1024,512]{2,1,0:T(8,128)(2,1)}, bf16[2,1024,512]{2,1,0:T(8,128)(2,1)}, bf16[2,1024,512]{2,1,0:T(8,...) custom-call(s32[2,2]{1,0:T(2,128)} %copy-done.57, ...), custom_call_target="tpu_custom_call" | custom-call | tf_op jit(solution)/shard_map/feed_back/pallas_call | solution.py:84
  244.7 4.1 d_shrink.3
  250.3 3.4 d_expand.3
  255.2 8.1 %attended_back.1.refs_1_ = bf16[8,512,128]{2,1,0:T(8,128)(2,1)} custom-call(s32[2,8]{1,0:T(2,128)} %copy-done.62, bf16[512,1024]{1,0:T(8,128)(2,1)} %get-tuple-element.199.a, bf16[4,1024,2304]{2,1,0:T(8,128)(2,1)} %bitcast.253), custom_call_target="tpu_custom_call" | custom-call | tf_op jit(solution)/shard_map/attended_back/pallas_call | solution.py:84
  267.9 5.1 %all-to-all-start.2 = ((bf16[4,512,256]{2,1,0:T(8,128)(2,1)}), bf16[4,512,256]{2,1,0:T(8,128)(2,1)}, u32[]{:S(2)}, u32[]{:S(2)}) async-start(bf16[4,512,256]{2,1,0:T(8,128)(2,1)} %bitcast.263), calls=%async_computation.2 | async-start | bytes 2097152 | tf_op jit(solution)/shard_map/all_to_all | solution.py:932
  275.8 10.7 %attend_back.6 = (bf16[2,512,128]{2,1,0:T(8,128)(2,1)}, f32[2,512,256]{2,1,0:T(8,128)}, bf16[2,512,256]{2,1,0:T(8,128)(2,1)}, f32[2,1,128]{2,1,0:T(1,128)}) custom-call(bf16[2,512,128]{2,1,0:T(8,128)(2,1)} %get-tuple-element.203.refs_0_, bf16[8,512,128]{2,1,0:T(8,128)(2,1)} %attended_back.1.refs_1_, f32[2,2,512]{2,1,0:T(2,128)} %get-tuple-element.204.refs_2_, ...), custom_call_target="tpu_custom_call" | custom-call | tf_op jit(solution)/shard_map/attend_back/pallas_call | solution.py:84
  286.5 10.6 %attend_back.7 = (bf16[2,512,128]{2,1,0:T(8,128)(2,1)}, f32[2,512,256]{2,1,0:T(8,128)}, bf16[2,512,256]{2,1,0:T(8,128)(2,1)}, f32[2,1,128]{2,1,0:T(1,128)}) custom-call(bf16[2,512,128]{2,1,0:T(8,128)(2,1)} %get-tuple-element.206.refs_0_, bf16[8,512,128]{2,1,0:T(8,128)(2,1)} %attended_back.1.refs_1_, f32[2,2,512]{2,1,0:T(2,128)} %get-tuple-element.207.refs_2_, ...), custom_call_target="tpu_custom_call" | custom-call | tf_op jit(solution)/shard_map/attend_back/pallas_call | solution.py:84
  298.5 2.8 collective-permute-done.28.refs_2_
  301.3 3.6 d_shrink.4
  308.7 2.8 d_expand.4
  311.5 5.5 %d_in.6 = (bf16[512,512]{1,0:T(8,128)(2,1)}, bf16[512,512]{1,0:T(8,128)(2,1)}, bf16[512,512]{1,0:T(8,128)(2,1)}, bf16[512,512]{1,0:T(8,128)(2,1)}) custom-call(bf16[1024,512]{1,0:T(8,128)(2,1)} %get-tuple-element.263.refs_0_, bf16[1024,512]{1,0:T(8,128)(2,1)} %get-tuple-element.212.refs_1_, bf16[2,512,128]{2,1,0:T(8,128)(2,1)} %get-tuple-element.205.refs_2_.refs_5_, ...), custom_call_target="tpu_custom_call" | custom-call | tf_op jit(solution)/shard_map/d_in/pallas_call | solution.py:84
  319.5 6.3 %attend_back.8 = (bf16[1,512,128]{2,1,0:T(8,128)(2,1)}, f32[1,512,256]{2,1,0:T(8,128)}, bf16[1,512,256]{2,1,0:T(8,128)(2,1)}, f32[1,1,128]{2,1,0:T(1,128)}) custom-call(bf16[2,512,128]{2,1,0:T(8,128)(2,1)} %get-tuple-element.233.refs_0_, bf16[8,512,128]{2,1,0:T(8,128)(2,1)} %attended_back.1.refs_1_, f32[2,2,512]{2,1,0:T(2,128)} %get-tuple-element.217.refs_2_, ...), custom_call_target="tpu_custom_call" | custom-call | tf_op jit(solution)/shard_map/attend_back/pallas_call | solution.py:84
  327.1 5.4 %d_in.7 = bf16[2,1024,512]{2,1,0:T(8,128)(2,1)} custom-call(bf16[1024,512]{1,0:T(8,128)(2,1)} %get-tuple-element.263.refs_0_, bf16[1024,512]{1,0:T(8,128)(2,1)} %get-tuple-element.212.refs_1_, bf16[2,512,128]{2,1,0:T(8,128)(2,1)} %get-tuple-element.208.refs_2_.refs_4_, bf16[2,512,256]{2,1,0:T(8,128)(2,1)} %add_convert_fusion.refs_3_.refs_10_, ...), custom_call_target="tpu_custom_call" | custom-call | tf_op jit(solution)/shard_map/d_in/pallas_call | solution.py:84
  332.6 6.2 %attend_back.9 = (bf16[1,512,128]{2,1,0:T(8,128)(2,1)}, f32[1,512,256]{2,1,0:T(8,128)}, bf16[1,512,256]{2,1,0:T(8,128)(2,1)}, f32[1,1,128]{2,1,0:T(1,128)}) custom-call(bf16[2,512,128]{2,1,0:T(8,128)(2,1)} %get-tuple-element.235.refs_0_, bf16[8,512,128]{2,1,0:T(8,128)(2,1)} %attended_back.1.refs_1_, f32[2,2,512]{2,1,0:T(2,128)} %get-tuple-element.226.refs_2_, ...), custom_call_target="tpu_custom_call" | custom-call | tf_op jit(solution)/shard_map/attend_back/pallas_call | solution.py:84
  338.8 3.3 d_shrink.5
  347.7 3.6 d_in.8
  351.3 6.3 %attend_back.10 = (bf16[1,512,128]{2,1,0:T(8,128)(2,1)}, f32[1,512,256]{2,1,0:T(8,128)}, bf16[1,512,256]{2,1,0:T(8,128)(2,1)}, f32[1,1,128]{2,1,0:T(1,128)}) custom-call(bf16[2,512,128]{2,1,0:T(8,128)(2,1)} %get-tuple-element.233.refs_0_, bf16[8,512,128]{2,1,0:T(8,128)(2,1)} %attended_back.1.refs_1_, f32[2,2,512]{2,1,0:T(2,128)} %get-tuple-element.217.refs_2_, ...), custom_call_target="tpu_custom_call" | custom-call | tf_op jit(solution)/shard_map/attend_back/pallas_call | solution.py:84
  357.6 6.3 %attend_back.11 = (bf16[1,512,128]{2,1,0:T(8,128)(2,1)}, f32[1,512,256]{2,1,0:T(8,128)}, bf16[1,512,256]{2,1,0:T(8,128)(2,1)}, f32[1,1,128]{2,1,0:T(1,128)}) custom-call(bf16[2,512,128]{2,1,0:T(8,128)(2,1)} %get-tuple-element.235.refs_0_, bf16[8,512,128]{2,1,0:T(8,128)(2,1)} %attended_back.1.refs_1_, f32[2,2,512]{2,1,0:T(2,128)} %get-tuple-element.226.refs_2_, ...), custom_call_target="tpu_custom_call" | custom-call | tf_op jit(solution)/shard_map/attend_back/pallas_call | solution.py:84
  364.7 3.9 collective-permute-done.37.refs_3_
  369.6 3.2 d_expand.5
  375.2 3.5 d_in.9
  379.1 13.2 %collective-permute-done.42.refs_7_ = bf16[2,1024,512]{2,1,0:T(8,128)(2,1)S(1)} collective-permute-done((bf16[2,1024,512]{2,1,0:T(8,128)(2,1)}, bf16[2,1024,512]{2,1,0:T(8,128)(2,1)S(1)}, u32[]{:S(2)}, u32[]{:S(2)}) %collective-permute-start.42) | collective-permute-done | bytes 2097184 | tf_op jit(solution)/shard_map/ppermute | solution.py:898
  393.6 4.3 d_in.10
  399.4 12.0 %tokens_back.1 = (bf16[512,1024]{1,0:T(8,128)(2,1)}, f32[2,1024]{1,0:T(2,128)}) custom-call(bf16[1,512,128]{2,1,0:T(8,128)(2,1)} %get-tuple-element.246.refs_0_.refs_2_, bf16[1,512,128]{2,1,0:T(8,128)(2,1)} %get-tuple-element.227.refs_2_.refs_1_, bf16[1,512,128]{2,1,0:T(8,128)(2,1)} %get-tuple-element.234.refs_2_, ...), custom_call_target="tpu_custom_call" | custom-call | tf_op jit(solution)/shard_map/tokens_back/pallas_call | solution.py:84
  417.3 5.1 %all-to-all-start.3 = ((bf16[4,512,256]{2,1,0:T(8,128)(2,1)}), bf16[4,512,256]{2,1,0:T(8,128)(2,1)S(1)}, u32[]{:S(2)}, u32[]{:S(2)}) async-start(bf16[4,512,256]{2,1,0:T(8,128)(2,1)} %bitcast.240), calls=%async_computation.4 | async-start | bytes 2097152 | tf_op jit(solution)/shard_map/all_to_all | solution.py:932
  426.7 4.8 d_in.11
  433.5 3.6 collective-permute-done.49
  437.8 10.9 %all-to-all-done.3 = bf16[4,512,256]{2,1,0:T(8,128)(2,1)S(1)} async-done(((bf16[4,512,256]{2,1,0:T(8,128)(2,1)}), bf16[4,512,256]{2,1,0:T(8,128)(2,1)S(1)}, u32[]{:S(2)}, u32[]{:S(2)}) %all-to-all-start.3) | async-done | bytes 1048608 | tf_op jit(solution)/shard_map/all_to_all | solution.py:932
  456.7 2.9 collective-permute-start.51
  483.5 6.8 %collective-permute-done.57 = bf16[256,512]{1,0:T(8,128)(2,1)S(1)} collective-permute-done((bf16[256,512]{1,0:T(8,128)(2,1)}, bf16[256,512]{1,0:T(8,128)(2,1)S(1)}, u32[]{:S(2)}, u32[]{:S(2)}) %collective-permute-start.57) | collective-permute-done | bytes 262176 | tf_op jit(solution)/shard_map/ppermute | solution.py:898
  (519 shorter events, 129.6 us)
Async XLA Ops:
  7.2 149.7 %all-gather.2.cloned.1.call-start = ((), (), s32[]{:S(2)}) async-start(), calls=%async_computation.7 | async-start | bytes 20054016 | tf_op jit(solution)/shard_map/all_gather | solution.py:804
  12.7 18.8 %collective-permute-start = (bf16[2,512,256]{2,1,0:T(8,128)(2,1)}, bf16[2,512,256]{2,1,0:T(8,128)(2,1)S(1)}, u32[]{:S(2)}, u32[]{:S(2)}) collective-permute-start(bf16[2,512,256]{2,1,0:T(8,128)(2,1)} %get-tuple-element.357), channel_id=1, source_target_pairs={{0,4},{4,0},{1,5},{5,1},{2,6},{6,2},{3,7},{7,3},{8,12},{12,8},{9,1... | collective-permute-start | bytes 1572872 | tf_op jit(solution)/shard_map/ppermute | solution.py:898
  13.6 14.2 %collective-permute-start.1 = (bf16[256,384]{1,0:T(8,128)(2,1)S(1)}, bf16[256,384]{1,0:T(8,128)(2,1)S(1)}, u32[]{:S(2)}, u32[]{:S(2)}) collective-permute-start(bf16[256,384]{1,0:T(8,128)(2,1)S(1)} %bitcast.283), channel_id=1, source_target_pairs={{0,1},{1,0},{2,3},{3,2},{4,5},{5,4},{6,7},{7,6},{8,9},{9,8},{10,11... | collective-permute-start | bytes 589832 | tf_op jit(solution)/shard_map/ppermute | solution.py:901
  27.9 23.5 %collective-permute-start.2 = (bf16[512,384]{1,0:T(8,128)(2,1)S(1)}, bf16[512,384]{1,0:T(8,128)(2,1)S(1)}, u32[]{:S(2)}, u32[]{:S(2)}) collective-permute-start(bf16[512,384]{1,0:T(8,128)(2,1)S(1)} %pad_maximum_fusion.12), channel_id=1, source_target_pairs={{0,2},{1,3},{2,0},{3,1},{4,6},{5,7},{6,4},{7,5},{8,10},{9,11},{10,... | collective-permute-start | bytes 1179656 | tf_op jit(solution)/shard_map/ppermute | solution.py:901
  51.7 19.5 %collective-permute-start.11 = (bf16[1024,256]{1,0:T(8,128)(2,1)S(1)}, bf16[1024,256]{1,0:T(8,128)(2,1)S(1)}, u32[]{:S(2)}, u32[]{:S(2)}) collective-permute-start(bf16[1024,256]{1,0:T(8,128)(2,1)S(1)} %get-tuple-element.359), channel_id=1, source_target_pairs={{0,8},{8,0},{1,9},{9,1},{2,10},{10,2},{3,11},{11,3},{4,12},{12,4},... | collective-permute-start | bytes 1572872 | tf_op jit(solution)/shard_map/ppermute | solution.py:898
  55.9 41.6 %all-to-all-start = ((bf16[4,512,256]{2,1,0:T(8,128)(2,1)}), bf16[4,512,256]{2,1,0:T(8,128)(2,1)}, u32[]{:S(2)}, u32[]{:S(2)}) async-start(bf16[4,512,256]{2,1,0:T(8,128)(2,1)} %pad_maximum_fusion.2), calls=%async_computation | async-start | bytes 2097152 | tf_op jit(solution)/shard_map/all_to_all | solution.py:915
  73.1 23.6 %collective-permute-start.14 = (bf16[2,1024,256]{2,1,0:T(8,128)(2,1)S(1)}, bf16[2,1024,256]{2,1,0:T(8,128)(2,1)}, u32[]{:S(2)}, u32[]{:S(2)}) collective-permute-start(bf16[2,1024,256]{2,1,0:T(8,128)(2,1)S(1)} %pad_maximum_fusion.3.h.refs_16_), channel_id=1, source_target_pairs={{0,16},{16,0},{1,17},{17,1},{2,18},{18,2},{3,19},{19,3},{4,20},{20... | collective-permute-start | bytes 3145736 | tf_op jit(solution)/shard_map/ppermute | solution.py:898
  74.6 49.3 %collective-permute-start.21 = (bf16[2,512,256]{2,1,0:T(8,128)(2,1)}, bf16[2,512,256]{2,1,0:T(8,128)(2,1)}, u32[]{:S(2)}, u32[]{:S(2)}) collective-permute-start(bf16[2,512,256]{2,1,0:T(8,128)(2,1)} %get-tuple-element.351), channel_id=1, source_target_pairs={{0,4},{4,0},{1,5},{5,1},{2,6},{6,2},{3,7},{7,3},{8,12},{12,8},{9,1... | collective-permute-start | bytes 1572872 | tf_op jit(solution)/shard_map/ppermute | solution.py:898
  74.7 22.0 %collective-permute-start.10 = (bf16[2,1024,128]{2,1,0:T(8,128)(2,1)S(1)}, bf16[2,1024,128]{2,1,0:T(8,128)(2,1)S(1)}, u32[]{:S(2)}, u32[]{:S(2)}) collective-permute-start(bf16[2,1024,128]{2,1,0:T(8,128)(2,1)S(1)} %pad_maximum_fusion.9), channel_id=1, source_target_pairs={{0,8},{8,0},{1,9},{9,1},{2,10},{10,2},{3,11},{11,3},{4,12},{12,4},... | collective-permute-start | bytes 1572872 | tf_op jit(solution)/shard_map/ppermute | solution.py:898
  76.5 32.3 %collective-permute-start.13 = (bf16[2,1024,256]{2,1,0:T(8,128)(2,1)S(1)}, bf16[2,1024,256]{2,1,0:T(8,128)(2,1)}, u32[]{:S(2)}, u32[]{:S(2)}) collective-permute-start(bf16[2,1024,256]{2,1,0:T(8,128)(2,1)S(1)} %pad_maximum_fusion.3.h.refs_16_), channel_id=1, source_target_pairs={{0,4},{4,0},{1,5},{5,1},{2,6},{6,2},{3,7},{7,3},{8,12},{12,8},{9,1... | collective-permute-start | bytes 3145736 | tf_op jit(solution)/shard_map/ppermute | solution.py:898
  96.7 22.2 %collective-permute-start.16 = (bf16[2,1024,256]{2,1,0:T(8,128)(2,1)}, bf16[2,1024,256]{2,1,0:T(8,128)(2,1)}, u32[]{:S(2)}, u32[]{:S(2)}) collective-permute-start(bf16[2,1024,256]{2,1,0:T(8,128)(2,1)} %collective-permute-done.14.h.refs_18_), channel_id=1, source_target_pairs={{0,4},{4,0},{1,5},{5,1},{2,6},{6,2},{3,7},{7,3},{8,12},{12,8},{9,1... | collective-permute-start | bytes 3145736 | tf_op jit(solution)/shard_map/ppermute | solution.py:898
  96.8 22.1 %collective-permute-start.15 = (bf16[2,1024,128]{2,1,0:T(8,128)(2,1)S(1)}, bf16[2,1024,128]{2,1,0:T(8,128)(2,1)}, u32[]{:S(2)}, u32[]{:S(2)}) collective-permute-start(bf16[2,1024,128]{2,1,0:T(8,128)(2,1)S(1)} %pad_maximum_fusion.11.g.refs_14_), channel_id=1, source_target_pairs={{0,4},{4,0},{1,5},{5,1},{2,6},{6,2},{3,7},{7,3},{8,12},{12,8},{9,1... | collective-permute-start | bytes 1572872 | tf_op jit(solution)/shard_map/ppermute | solution.py:898
  100.0 9.3 %collective-permute-start.12 = (bf16[2,1024,128]{2,1,0:T(8,128)(2,1)S(1)}, bf16[2,1024,128]{2,1,0:T(8,128)(2,1)S(1)}, u32[]{:S(2)}, u32[]{:S(2)}) collective-permute-start(bf16[2,1024,128]{2,1,0:T(8,128)(2,1)S(1)} %pad_maximum_fusion.10.g.refs_12_), channel_id=1, source_target_pairs={{0,4},{4,0},{1,5},{5,1},{2,6},{6,2},{3,7},{7,3},{8,12},{12,8},{9,1... | collective-permute-start | bytes 1572872 | tf_op jit(solution)/shard_map/ppermute | solution.py:898
  108.8 24.3 %collective-permute-start.18 = (bf16[2,512,256]{2,1,0:T(8,128)(2,1)}, bf16[2,512,256]{2,1,0:T(8,128)(2,1)S(1)}, u32[]{:S(2)}, u32[]{:S(2)}) collective-permute-start(bf16[2,512,256]{2,1,0:T(8,128)(2,1)} %get-tuple-element.159.refs_1_.refs_3_), channel_id=1, source_target_pairs={{0,4},{4,0},{1,5},{5,1},{2,6},{6,2},{3,7},{7,3},{8,12},{12,8},{9,1... | collective-permute-start | bytes 1572872 | tf_op jit(solution)/shard_map/ppermute | solution.py:898
  114.5 10.6 %collective-permute-start.17 = (bf16[2,512,256]{2,1,0:T(8,128)(2,1)}, bf16[2,512,256]{2,1,0:T(8,128)(2,1)S(1)}, u32[]{:S(2)}, u32[]{:S(2)}) collective-permute-start(bf16[2,512,256]{2,1,0:T(8,128)(2,1)} %get-tuple-element.160.refs_1_.refs_3_), channel_id=1, source_target_pairs={{0,4},{4,0},{1,5},{5,1},{2,6},{6,2},{3,7},{7,3},{8,12},{12,8},{9,1... | collective-permute-start | bytes 1572872 | tf_op jit(solution)/shard_map/ppermute | solution.py:898
  123.4 17.6 %collective-permute-start.19 = (bf16[2,512,256]{2,1,0:T(8,128)(2,1)}, bf16[2,512,256]{2,1,0:T(8,128)(2,1)S(1)}, u32[]{:S(2)}, u32[]{:S(2)}) collective-permute-start(bf16[2,512,256]{2,1,0:T(8,128)(2,1)} %get-tuple-element.166.refs_1_.refs_3_), channel_id=1, source_target_pairs={{0,4},{4,0},{1,5},{5,1},{2,6},{6,2},{3,7},{7,3},{8,12},{12,8},{9,1... | collective-permute-start | bytes 1572872 | tf_op jit(solution)/shard_map/ppermute | solution.py:898
  123.9 25.0 %collective-permute-start.20 = (bf16[2,512,256]{2,1,0:T(8,128)(2,1)S(1)}, bf16[2,512,256]{2,1,0:T(8,128)(2,1)S(1)}, u32[]{:S(2)}, u32[]{:S(2)}) collective-permute-start(bf16[2,512,256]{2,1,0:T(8,128)(2,1)S(1)} %copy-done.19), channel_id=1, source_target_pairs={{0,4},{4,0},{1,5},{5,1},{2,6},{6,2},{3,7},{7,3},{8,12},{12,8},{9,1... | collective-permute-start | bytes 1572872 | tf_op jit(solution)/shard_map/ppermute | solution.py:898
  158.2 36.1 %all-to-all-start.1 = ((bf16[4,512,256]{2,1,0:T(8,128)(2,1)}), bf16[4,512,256]{2,1,0:T(8,128)(2,1)S(1)}, u32[]{:S(2)}, u32[]{:S(2)}) async-start(bf16[4,512,256]{2,1,0:T(8,128)(2,1)} %pad_maximum_fusion.5), calls=%async_computation.1 | async-start | bytes 2097152 | tf_op jit(solution)/shard_map/all_to_all | solution.py:915
  217.7 25.7 %collective-permute-start.22 = (bf16[2,1024,512]{2,1,0:T(8,128)(2,1)}, bf16[2,1024,512]{2,1,0:T(8,128)(2,1)}, u32[]{:S(2)}, u32[]{:S(2)}) collective-permute-start(bf16[2,1024,512]{2,1,0:T(8,128)(2,1)} %get-tuple-element.187), channel_id=1, source_target_pairs={{0,4},{4,0},{1,5},{5,1},{2,6},{6,2},{3,7},{7,3},{8,12},{12,8},{9,1... | collective-permute-start | bytes 6291464 | tf_op jit(solution)/shard_map/ppermute | solution.py:898
  217.8 25.6 %collective-permute-start.23 = (bf16[2,1024,512]{2,1,0:T(8,128)(2,1)}, bf16[2,1024,512]{2,1,0:T(8,128)(2,1)S(1)}, u32[]{:S(2)}, u32[]{:S(2)}) collective-permute-start(bf16[2,1024,512]{2,1,0:T(8,128)(2,1)} %get-tuple-element.193), channel_id=1, source_target_pairs={{0,4},{4,0},{1,5},{5,1},{2,6},{6,2},{3,7},{7,3},{8,12},{12,8},{9,1... | collective-permute-start | bytes 6291464 | tf_op jit(solution)/shard_map/ppermute | solution.py:898
  218.2 25.2 %collective-permute-start.24 = (bf16[2,1024,512]{2,1,0:T(8,128)(2,1)}, bf16[2,1024,512]{2,1,0:T(8,128)(2,1)S(1)}, u32[]{:S(2)}, u32[]{:S(2)}) collective-permute-start(bf16[2,1024,512]{2,1,0:T(8,128)(2,1)} %get-tuple-element.194), channel_id=1, source_target_pairs={{0,4},{4,0},{1,5},{5,1},{2,6},{6,2},{3,7},{7,3},{8,12},{12,8},{9,1... | collective-permute-start | bytes 6291464 | tf_op jit(solution)/shard_map/ppermute | solution.py:898
  218.3 25.1 %collective-permute-start.25 = (bf16[2,1024,512]{2,1,0:T(8,128)(2,1)}, bf16[2,1024,512]{2,1,0:T(8,128)(2,1)S(1)}, u32[]{:S(2)}, u32[]{:S(2)}) collective-permute-start(bf16[2,1024,512]{2,1,0:T(8,128)(2,1)} %get-tuple-element.195), channel_id=1, source_target_pairs={{0,4},{4,0},{1,5},{5,1},{2,6},{6,2},{3,7},{7,3},{8,12},{12,8},{9,1... | collective-permute-start | bytes 6291464 | tf_op jit(solution)/shard_map/ppermute | solution.py:898
  248.9 49.6 %collective-permute-start.27 = (bf16[2,1024,512]{2,1,0:T(8,128)(2,1)}, bf16[2,1024,512]{2,1,0:T(8,128)(2,1)}, u32[]{:S(2)}, u32[]{:S(2)}) collective-permute-start(bf16[2,1024,512]{2,1,0:T(8,128)(2,1)} %d_shrink.3), channel_id=1, source_target_pairs={{0,8},{8,0},{1,9},{9,1},{2,10},{10,2},{3,11},{11,3},{4,12},{12,4},... | collective-permute-start | bytes 6291464 | tf_op jit(solution)/shard_map/ppermute | solution.py:898
  253.7 47.5 %collective-permute-start.28 = (bf16[2,1024,512]{2,1,0:T(8,128)(2,1)}, bf16[2,1024,512]{2,1,0:T(8,128)(2,1)S(1)}, u32[]{:S(2)}, u32[]{:S(2)}) collective-permute-start(bf16[2,1024,512]{2,1,0:T(8,128)(2,1)} %d_expand.3), channel_id=1, source_target_pairs={{0,16},{16,0},{1,17},{17,1},{2,18},{18,2},{3,19},{19,3},{4,20},{20... | collective-permute-start | bytes 6291464 | tf_op jit(solution)/shard_map/ppermute | solution.py:898
  267.9 30.6 %all-to-all-start.2 = ((bf16[4,512,256]{2,1,0:T(8,128)(2,1)}), bf16[4,512,256]{2,1,0:T(8,128)(2,1)}, u32[]{:S(2)}, u32[]{:S(2)}) async-start(bf16[4,512,256]{2,1,0:T(8,128)(2,1)} %bitcast.263), calls=%async_computation.2 | async-start | bytes 2097152 | tf_op jit(solution)/shard_map/all_to_all | solution.py:932
  273.0 126.4 %reduce-scatter.4.cloned.1.call-start = ((), (), s32[]{:S(2)}) async-start(), calls=%async_computation.8 | async-start | bytes 1310720 | tf_op jit(solution)/shard_map/reduce_scatter | solution.py:1078
  297.1 9.3 %collective-permute-start.29 = (bf16[2,512,256]{2,1,0:T(8,128)(2,1)}, bf16[2,512,256]{2,1,0:T(8,128)(2,1)}, u32[]{:S(2)}, u32[]{:S(2)}) collective-permute-start(bf16[2,512,256]{2,1,0:T(8,128)(2,1)} %get-tuple-element.214), channel_id=1, source_target_pairs={{0,4},{4,0},{1,5},{5,1},{2,6},{6,2},{3,7},{7,3},{8,12},{12,8},{9,1... | collective-permute-start | bytes 1572872 | tf_op jit(solution)/shard_map/ppermute | solution.py:898
  297.2 20.4 %collective-permute-start.30 = (bf16[2,512,256]{2,1,0:T(8,128)(2,1)}, bf16[2,512,256]{2,1,0:T(8,128)(2,1)S(1)}, u32[]{:S(2)}, u32[]{:S(2)}) collective-permute-start(bf16[2,512,256]{2,1,0:T(8,128)(2,1)} %get-tuple-element.221), channel_id=1, source_target_pairs={{0,4},{4,0},{1,5},{5,1},{2,6},{6,2},{3,7},{7,3},{8,12},{12,8},{9,1... | collective-permute-start | bytes 1572872 | tf_op jit(solution)/shard_map/ppermute | solution.py:898
  304.9 34.0 %collective-permute-start.35 = (bf16[1,1024,512]{2,1,0:T(8,128)(2,1)}, bf16[1,1024,512]{2,1,0:T(8,128)(2,1)}, u32[]{:S(2)}, u32[]{:S(2)}) collective-permute-start(bf16[1,1024,512]{2,1,0:T(8,128)(2,1)} %d_shrink.4), channel_id=1, source_target_pairs={{0,16},{16,0},{1,17},{17,1},{2,18},{18,2},{3,19},{19,3},{4,20},{20... | collective-permute-start | bytes 3145736 | tf_op jit(solution)/shard_map/ppermute | solution.py:898
  317.0 8.8 %collective-permute-start.32 = (bf16[512,512]{1,0:T(8,128)(2,1)}, bf16[512,512]{1,0:T(8,128)(2,1)S(1)}, u32[]{:S(2)}, u32[]{:S(2)}) collective-permute-start(bf16[512,512]{1,0:T(8,128)(2,1)} %get-tuple-element.222), channel_id=1, source_target_pairs={{0,4},{4,0},{1,5},{5,1},{2,6},{6,2},{3,7},{7,3},{8,12},{12,8},{9,1... | collective-permute-start | bytes 1572872 | tf_op jit(solution)/shard_map/ppermute | solution.py:898
  342.2 120.5 %reduce-scatter.8.cloned.1.call-start = ((), (), s32[]{:S(2)}) async-start(), calls=%async_computation.10 | async-start | bytes 1310720 | tf_op jit(solution)/shard_map/reduce_scatter | solution.py:1078
  343.3 25.4 %collective-permute-start.37 = (bf16[1,1024,512]{2,1,0:T(8,128)(2,1)}, bf16[1,1024,512]{2,1,0:T(8,128)(2,1)S(1)}, u32[]{:S(2)}, u32[]{:S(2)}) collective-permute-start(bf16[1,1024,512]{2,1,0:T(8,128)(2,1)} %d_expand.4), channel_id=1, source_target_pairs={{0,8},{8,0},{1,9},{9,1},{2,10},{10,2},{3,11},{11,3},{4,12},{12,4},... | collective-permute-start | bytes 3145736 | tf_op jit(solution)/shard_map/ppermute | solution.py:898
  343.9 20.5 %collective-permute-start.39 = (bf16[1,512,256]{2,1,0:T(8,128)(2,1)}, bf16[1,512,256]{2,1,0:T(8,128)(2,1)S(1)}, u32[]{:S(2)}, u32[]{:S(2)}) collective-permute-start(bf16[1,512,256]{2,1,0:T(8,128)(2,1)} %get-tuple-element.244), channel_id=1, source_target_pairs={{0,4},{4,0},{1,5},{5,1},{2,6},{6,2},{3,7},{7,3},{8,12},{12,8},{9,1... | collective-permute-start | bytes 786440 | tf_op jit(solution)/shard_map/ppermute | solution.py:898
  344.5 47.8 %collective-permute-start.42 = (bf16[2,1024,512]{2,1,0:T(8,128)(2,1)}, bf16[2,1024,512]{2,1,0:T(8,128)(2,1)S(1)}, u32[]{:S(2)}, u32[]{:S(2)}) collective-permute-start(bf16[2,1024,512]{2,1,0:T(8,128)(2,1)} %d_in.7), channel_id=1, source_target_pairs={{0,16},{16,0},{1,17},{17,1},{2,18},{18,2},{3,19},{19,3},{4,20},{20... | collective-permute-start | bytes 6291464 | tf_op jit(solution)/shard_map/ppermute | solution.py:898
  347.0 67.3 %collective-permute-start.26 = (bf16[2,512,256]{2,1,0:T(8,128)(2,1)}, bf16[2,512,256]{2,1,0:T(8,128)(2,1)}, u32[]{:S(2)}, u32[]{:S(2)}) collective-permute-start(bf16[2,512,256]{2,1,0:T(8,128)(2,1)} %dynamic-slice_bitcast_fusion.1), channel_id=1, source_target_pairs={{0,4},{4,0},{1,5},{5,1},{2,6},{6,2},{3,7},{7,3},{8,12},{12,8},{9,1... | collective-permute-start | bytes 1572872 | tf_op jit(solution)/shard_map/ppermute | solution.py:898
  363.9 9.0 %collective-permute-start.38 = (bf16[1,512,256]{2,1,0:T(8,128)(2,1)}, bf16[1,512,256]{2,1,0:T(8,128)(2,1)}, u32[]{:S(2)}, u32[]{:S(2)}) collective-permute-start(bf16[1,512,256]{2,1,0:T(8,128)(2,1)} %get-tuple-element.240), channel_id=1, source_target_pairs={{0,4},{4,0},{1,5},{5,1},{2,6},{6,2},{3,7},{7,3},{8,12},{12,8},{9,1... | collective-permute-start | bytes 786440 | tf_op jit(solution)/shard_map/ppermute | solution.py:898
  364.6 14.5 %collective-permute-start.40 = (bf16[512,512]{1,0:T(8,128)(2,1)}, bf16[512,512]{1,0:T(8,128)(2,1)}, u32[]{:S(2)}, u32[]{:S(2)}) collective-permute-start(bf16[512,512]{1,0:T(8,128)(2,1)} %get-tuple-element.232), channel_id=1, source_target_pairs={{0,4},{4,0},{1,5},{5,1},{2,6},{6,2},{3,7},{7,3},{8,12},{12,8},{9,1... | collective-permute-start | bytes 1572872 | tf_op jit(solution)/shard_map/ppermute | solution.py:898
  398.0 27.9 %collective-permute-start.48 = (bf16[1,1024,512]{2,1,0:T(8,128)(2,1)}, bf16[1,1024,512]{2,1,0:T(8,128)(2,1)}, u32[]{:S(2)}, u32[]{:S(2)}) collective-permute-start(bf16[1,1024,512]{2,1,0:T(8,128)(2,1)} %d_in.10), channel_id=1, source_target_pairs={{0,8},{8,0},{1,9},{9,1},{2,10},{10,2},{3,11},{11,3},{4,12},{12,4},... | collective-permute-start | bytes 3145736 | tf_op jit(solution)/shard_map/ppermute | solution.py:898
  415.6 10.3 %collective-permute-start.46 = (bf16[512,512]{1,0:T(8,128)(2,1)}, bf16[512,512]{1,0:T(8,128)(2,1)S(1)}, u32[]{:S(2)}, u32[]{:S(2)}) collective-permute-start(bf16[512,512]{1,0:T(8,128)(2,1)} %get-tuple-element.241), channel_id=1, source_target_pairs={{0,4},{4,0},{1,5},{5,1},{2,6},{6,2},{3,7},{7,3},{8,12},{12,8},{9,1... | collective-permute-start | bytes 1572872 | tf_op jit(solution)/shard_map/ppermute | solution.py:898
  416.1 9.7 %collective-permute-start.47 = (bf16[512,512]{1,0:T(8,128)(2,1)}, bf16[512,512]{1,0:T(8,128)(2,1)}, u32[]{:S(2)}, u32[]{:S(2)}) collective-permute-start(bf16[512,512]{1,0:T(8,128)(2,1)} %get-tuple-element.264), channel_id=1, source_target_pairs={{0,4},{4,0},{1,5},{5,1},{2,6},{6,2},{3,7},{7,3},{8,12},{12,8},{9,1... | collective-permute-start | bytes 1572872 | tf_op jit(solution)/shard_map/ppermute | solution.py:898
  417.3 31.5 %all-to-all-start.3 = ((bf16[4,512,256]{2,1,0:T(8,128)(2,1)}), bf16[4,512,256]{2,1,0:T(8,128)(2,1)S(1)}, u32[]{:S(2)}, u32[]{:S(2)}) async-start(bf16[4,512,256]{2,1,0:T(8,128)(2,1)} %bitcast.240), calls=%async_computation.4 | async-start | bytes 2097152 | tf_op jit(solution)/shard_map/all_to_all | solution.py:932
  422.4 57.3 %reduce-scatter.6.cloned.1.call-start = ((), (), s32[]{:S(2)}) async-start(), calls=%async_computation.9 | async-start | bytes 1310720 | tf_op jit(solution)/shard_map/reduce_scatter | solution.py:1078
  455.2 10.7 %collective-permute-start.53 = (f32[64,128]{1,0:T(8,128)S(1)}, f32[64,128]{1,0:T(8,128)S(1)}, u32[]{:S(2)}, u32[]{:S(2)}) collective-permute-start(f32[64,128]{1,0:T(8,128)S(1)} %get-tuple-element.412), channel_id=1, source_target_pairs={{0,3},{1,2},{2,1},{3,0},{4,7},{5,6},{6,5},{7,4},{8,11},{9,10},{10,... | collective-permute-start | bytes 98312 | tf_op jit(solution)/shard_map/ppermute | solution.py:901
  456.7 9.1 %collective-permute-start.52 = (f32[64,128]{1,0:T(8,128)S(1)}, f32[64,128]{1,0:T(8,128)S(1)}, u32[]{:S(2)}, u32[]{:S(2)}) collective-permute-start(f32[64,128]{1,0:T(8,128)S(1)} %get-tuple-element.411), channel_id=1, source_target_pairs={{0,2},{1,3},{2,0},{3,1},{4,6},{5,7},{6,4},{7,5},{8,10},{9,11},{10,... | collective-permute-start | bytes 98312 | tf_op jit(solution)/shard_map/ppermute | solution.py:901
  456.7 9.2 %collective-permute-start.51 = (f32[64,128]{1,0:T(8,128)S(1)}, f32[64,128]{1,0:T(8,128)S(1)}, u32[]{:S(2)}, u32[]{:S(2)}) collective-permute-start(f32[64,128]{1,0:T(8,128)S(1)} %get-tuple-element.410), channel_id=1, source_target_pairs={{0,1},{1,0},{2,3},{3,2},{4,5},{5,4},{6,7},{7,6},{8,9},{9,8},{10,11... | collective-permute-start | bytes 98312 | tf_op jit(solution)/shard_map/ppermute | solution.py:901
  462.1 13.1 %collective-permute-start.59 = (bf16[256,512]{1,0:T(8,128)(2,1)}, bf16[256,512]{1,0:T(8,128)(2,1)S(1)}, u32[]{:S(2)}, u32[]{:S(2)}) collective-permute-start(bf16[256,512]{1,0:T(8,128)(2,1)} %gate.11), channel_id=1, source_target_pairs={{0,16},{16,0},{1,17},{17,1},{2,18},{18,2},{3,19},{19,3},{4,20},{20... | collective-permute-start | bytes 786440 | tf_op jit(solution)/shard_map/ppermute | solution.py:898
  464.4 10.9 %collective-permute-start.58 = (bf16[256,512]{1,0:T(8,128)(2,1)}, bf16[256,512]{1,0:T(8,128)(2,1)S(1)}, u32[]{:S(2)}, u32[]{:S(2)}) collective-permute-start(bf16[256,512]{1,0:T(8,128)(2,1)} %gate.12), channel_id=1, source_target_pairs={{0,16},{16,0},{1,17},{17,1},{2,18},{18,2},{3,19},{19,3},{4,20},{20... | collective-permute-start | bytes 786440 | tf_op jit(solution)/shard_map/ppermute | solution.py:898
  481.4 8.9 %collective-permute-start.57 = (bf16[256,512]{1,0:T(8,128)(2,1)}, bf16[256,512]{1,0:T(8,128)(2,1)S(1)}, u32[]{:S(2)}, u32[]{:S(2)}) collective-permute-start(bf16[256,512]{1,0:T(8,128)(2,1)} %gate.13), channel_id=1, source_target_pairs={{0,16},{16,0},{1,17},{17,1},{2,18},{18,2},{3,19},{19,3},{4,20},{20... | collective-permute-start | bytes 786440 | tf_op jit(solution)/shard_map/ppermute | solution.py:898
  (102 other events, 660.9 us)
Sparse Core Ops, SparseCore 0:
  11.9 140.6 all-gather.1
  342.3 26.7 reduce-scatter.3
  373.0 26.8 reduce-scatter.7
  452.1 26.8 reduce-scatter.5
